TPU v7x, 32 devices: a whole 2x2x4 slice. The times are simulated.
32 devices in a mesh: batch: 4 (over y, core), order: 8 (over z, x).
Axes of the slice: x: 2, y: 2, z: 4, core: 2. Of those that a mesh axis runs over, the one named last changes fastest.
Arguments:
- series: float32 [512, 23040], P('order', 'batch'), may hold values from -6 to 6
- norm_gain: float32 [512], P('order'), may hold values from 0.1 to 1.9
- mode_in: float32 [2, 32, 4, 512], P(None, None, None, 'order'), may hold values from -0.25 to 0.25
- mode_out: float32 [2, 32, 4, 512], P(None, None, None, 'order'), may hold values from -9 to 9
- lengths: int32 [32], P('batch'), may hold values from 96 to 720, as said below
- grad_out: float32 [512, 23040], P('order', 'batch'), may hold values from -6 to 6
Outputs:
- layer_out: float32 [512, 23040], P('order', 'batch')
- grad_series: float32 [512, 23040], P('order', 'batch')
- grad_gain: float32 [512], P('order')
- grad_mode_in: float32 [2, 32, 4, 512], P(None, None, None, 'order')
- grad_mode_out: float32 [2, 32, 4, 512], P(None, None, None, 'order')
- stream_rms: float32 [3], replicated
Inputs may be any that keep to these rules, and one draw needn't show every extreme that they name: `lengths`: A window's valid steps are its first steps; each length is one of 96, 336 and 720.
All inputs are finite; a program needn't handle non-finite values.
Results may differ from a plain program's by a relative error of at most 0.0003.
Values sent between devices are 32-bit elements; how exact they have to be, the bound alone decides.
No kernel may reach another device: no remote copies, remote signals or barrier semaphores. Data moves between devices by JAX's collectives and lax.ppermute only.
A program may use at most 256 MiB of HBM per device.

v0:
```python
import math

import jax
import jax.numpy as jnp
from jax import lax
from jax.sharding import PartitionSpec as P

ORDER = 256
LEN = 720


precise_mode = lax.Precision.HIGHEST
epsilon = 1e-06


def legendre_rows(order_count, steps_count):
    positions = jnp.arange(steps_count, dtype=jnp.float32)
    coords = 1.0 - (2.0 * positions + 1.0) / steps_count
    first_row = jnp.ones((steps_count,), jnp.float32)

    def advance(carry, degree):
        earlier, current = carry
        following = ((2.0 * degree + 1.0) * coords * current - degree * earlier) / (degree + 1.0)
        return ((current, following), following)

    degrees = jnp.arange(1, order_count - 1, dtype=jnp.float32)
    final_pair, higher = lax.scan(advance, (first_row, coords), degrees)
    stacked = jnp.concatenate([first_row[None], coords[None], higher], axis=0)
    scaling = jnp.sqrt((2.0 * jnp.arange(order_count, dtype=jnp.float32) + 1.0) / steps_count)
    return stacked * scaling[:, None]


def phase_tables(mode_count, steps_count):
    mode_ids = jnp.arange(mode_count, dtype=jnp.int32)
    positions = jnp.arange(steps_count, dtype=jnp.int32)
    turns = mode_ids[:, None] * positions[None, :] % steps_count
    angle = 2.0 * math.pi / steps_count * turns.astype(jnp.float32)
    return (jnp.cos(angle), jnp.sin(angle))


def projection_table(legendre, mode_count, steps_count):
    cosine_table, sine_table = phase_tables(mode_count, steps_count)
    cum_real = jnp.cumsum(legendre[:, None, :] * cosine_table[None], axis=2)
    cum_imag = -jnp.cumsum(legendre[:, None, :] * sine_table[None], axis=2)
    real_back = jnp.flip(cum_real, axis=2)
    imag_back = jnp.flip(cum_imag, axis=2)
    inv_root = 1.0 / math.sqrt(steps_count)
    table_real = (cosine_table[None] * real_back + sine_table[None] * imag_back) * inv_root
    table_imag = (cosine_table[None] * imag_back - sine_table[None] * real_back) * inv_root
    return jnp.concatenate([table_real, table_imag], axis=1)


def readout_weights(mode_count, steps_count):
    mode_ids = jnp.arange(mode_count, dtype=jnp.int32)
    turns = mode_ids * (steps_count - 1) % steps_count
    angle = 2.0 * math.pi / steps_count * turns.astype(jnp.float32)
    factor = jnp.where(mode_ids == 0, 1.0, 2.0).astype(jnp.float32) / math.sqrt(steps_count)
    return (factor * jnp.cos(angle), -factor * jnp.sin(angle))


def mix_in(coeffs, weights):
    mode_count = weights.shape[1]
    coeff_real = coeffs[:, :, :mode_count]
    coeff_imag = coeffs[:, :, mode_count:]
    real_part = jnp.einsum(
        "bnmd,mrd->bnmr", coeff_real, weights[0], precision=precise_mode
    ) - jnp.einsum("bnmd,mrd->bnmr", coeff_imag, weights[1], precision=precise_mode)
    imag_part = jnp.einsum(
        "bnmd,mrd->bnmr", coeff_real, weights[1], precision=precise_mode
    ) + jnp.einsum("bnmd,mrd->bnmr", coeff_imag, weights[0], precision=precise_mode)
    return (real_part, imag_part)


def mix_out(rank_real, rank_imag, weights):
    out_real = jnp.einsum(
        "bnmr,mrd->bnmd", rank_real, weights[0], precision=precise_mode
    ) - jnp.einsum("bnmr,mrd->bnmd", rank_imag, weights[1], precision=precise_mode)
    out_imag = jnp.einsum(
        "bnmr,mrd->bnmd", rank_real, weights[1], precision=precise_mode
    ) + jnp.einsum("bnmr,mrd->bnmd", rank_imag, weights[0], precision=precise_mode)
    return (out_real, out_imag)


def back_out(grad_real, grad_imag, rank_real, rank_imag, weights):
    rank_grad_real = jnp.einsum(
        "bnmd,mrd->bnmr", grad_real, weights[0], precision=precise_mode
    ) + jnp.einsum("bnmd,mrd->bnmr", grad_imag, weights[1], precision=precise_mode)
    rank_grad_imag = jnp.einsum(
        "bnmd,mrd->bnmr", grad_imag, weights[0], precision=precise_mode
    ) - jnp.einsum("bnmd,mrd->bnmr", grad_real, weights[1], precision=precise_mode)
    weight_real = jnp.einsum(
        "bnmr,bnmd->mrd", rank_real, grad_real, precision=precise_mode
    ) + jnp.einsum("bnmr,bnmd->mrd", rank_imag, grad_imag, precision=precise_mode)
    weight_imag = jnp.einsum(
        "bnmr,bnmd->mrd", rank_real, grad_imag, precision=precise_mode
    ) - jnp.einsum("bnmr,bnmd->mrd", rank_imag, grad_real, precision=precise_mode)
    return (rank_grad_real, rank_grad_imag, jnp.stack([weight_real, weight_imag]))


def back_in(rank_grad_real, rank_grad_imag, coeffs, weights):
    mode_count = weights.shape[1]
    coeff_real = coeffs[:, :, :mode_count]
    coeff_imag = coeffs[:, :, mode_count:]
    grad_coeff_real = jnp.einsum(
        "bnmr,mrd->bnmd", rank_grad_real, weights[0], precision=precise_mode
    ) + jnp.einsum("bnmr,mrd->bnmd", rank_grad_imag, weights[1], precision=precise_mode)
    grad_coeff_imag = jnp.einsum(
        "bnmr,mrd->bnmd", rank_grad_imag, weights[0], precision=precise_mode
    ) - jnp.einsum("bnmr,mrd->bnmd", rank_grad_real, weights[1], precision=precise_mode)
    weight_real = jnp.einsum(
        "bnmd,bnmr->mrd", coeff_real, rank_grad_real, precision=precise_mode
    ) + jnp.einsum("bnmd,bnmr->mrd", coeff_imag, rank_grad_imag, precision=precise_mode)
    weight_imag = jnp.einsum(
        "bnmd,bnmr->mrd", coeff_real, rank_grad_imag, precision=precise_mode
    ) - jnp.einsum("bnmd,bnmr->mrd", coeff_imag, rank_grad_real, precision=precise_mode)
    grad_coeffs = jnp.concatenate([grad_coeff_real, grad_coeff_imag], axis=2)
    return (grad_coeffs, jnp.stack([weight_real, weight_imag]))


def local(series, norm_gain, mode_in, mode_out, lengths, grad_out):
    steps_count = LEN
    local_width = series.shape[0]
    local_windows = series.shape[1] // steps_count
    order_devices = lax.axis_size("order")
    mode_count = mode_in.shape[1]
    full_width = local_width * order_devices
    stored_shape = series.shape
    inputs = series.reshape(local_width, local_windows, steps_count)
    cotangent = grad_out.reshape(local_width, local_windows, steps_count)
    legendre = legendre_rows(ORDER, steps_count)
    read_real, read_imag = readout_weights(mode_count, steps_count)
    valid_mask = (jnp.arange(steps_count, dtype=jnp.int32)[None, :] < lengths[:, None]).astype(
        jnp.float32
    )
    masked = valid_mask[None]
    squares_local = jnp.sum(inputs * inputs, axis=0)
    row_mean = lax.psum(squares_local, "order") / full_width
    inv_rms = lax.rsqrt(row_mean + epsilon)
    scaled = inputs * inv_rms[None]
    normed = masked * norm_gain[:, None, None] * scaled
    grad_branch = masked * cotangent
    local_order = ORDER // order_devices
    first_index = lax.axis_index("order") * local_order
    legendre_part = lax.dynamic_slice_in_dim(legendre, first_index, local_order, 0)
    proj_table = projection_table(legendre_part, mode_count, steps_count)
    recon_rows = jnp.flip(legendre_part, axis=1)
    weights_in, weights_out = (
        lax.all_gather(mode_in, "order", axis=3, tiled=True),
        lax.all_gather(mode_out, "order", axis=3, tiled=True),
    )
    coeffs = jnp.einsum(
        "nks,dbs->bnkd",
        proj_table,
        lax.all_gather(normed, "order", axis=0, tiled=True),
        precision=precise_mode,
    )
    rank_real, rank_imag = mix_in(coeffs, weights_in)
    out_real, out_imag = mix_out(rank_real, rank_imag, weights_out)
    readout = jnp.einsum("m,bnmd->bnd", read_real, out_real, precision=precise_mode) + jnp.einsum(
        "m,bnmd->bnd", read_imag, out_imag, precision=precise_mode
    )
    partial_field = jnp.einsum("nt,bnd->dbt", recon_rows, readout, precision=precise_mode)
    branch = masked * lax.psum_scatter(partial_field, "order", scatter_dimension=0, tiled=True)
    grad_read = jnp.einsum(
        "nt,dbt->bnd",
        recon_rows,
        lax.all_gather(grad_branch, "order", axis=0, tiled=True),
        precision=precise_mode,
    )
    grad_real = read_real[None, None, :, None] * grad_read[:, :, None, :]
    grad_imag = read_imag[None, None, :, None] * grad_read[:, :, None, :]
    rank_grad_real, rank_grad_imag, out_weight_part = back_out(
        grad_real, grad_imag, rank_real, rank_imag, weights_out
    )
    grad_coeffs, in_weight_part = back_in(rank_grad_real, rank_grad_imag, coeffs, weights_in)
    normed_part = jnp.einsum("nks,bnkd->dbs", proj_table, grad_coeffs, precision=precise_mode)
    grad_normed, in_weight_grad, out_weight_grad = (
        lax.psum_scatter(normed_part, "order", scatter_dimension=0, tiled=True),
        lax.psum_scatter(in_weight_part, "order", scatter_dimension=3, tiled=True),
        lax.psum_scatter(out_weight_part, "order", scatter_dimension=3, tiled=True),
    )
    layer_out = inputs + branch
    gain_part = jnp.sum(masked * scaled * grad_normed, axis=(1, 2))
    grad_scaled = masked * norm_gain[:, None, None] * grad_normed
    inner_local = jnp.sum(grad_scaled * inputs, axis=0)
    inner = lax.psum(inner_local, "order")
    grad_series = cotangent + inv_rms[None] * (
        grad_scaled - inputs * (inv_rms * inv_rms * inner / full_width)[None]
    )
    grad_gain, grad_mode_in, grad_mode_out = lax.psum(
        (gain_part, in_weight_grad, out_weight_grad), "batch"
    )
    count_term = jnp.where(lax.axis_index("order") == 0, jnp.sum(lengths).astype(jnp.float32), 0.0)
    sum_in = jnp.sum(masked * inputs * inputs)
    sum_branch = jnp.sum(masked * branch * branch)
    sum_out = jnp.sum(masked * layer_out * layer_out)
    total_in, total_branch, total_out, total_count = lax.psum(
        (sum_in, sum_branch, sum_out, count_term), ("batch", "order")
    )
    denominator = total_count * full_width
    stream_rms = jnp.stack(
        [
            jnp.sqrt(total_in / denominator),
            jnp.sqrt(total_branch / denominator),
            jnp.sqrt(total_out / denominator),
        ]
    )
    return (
        layer_out.reshape(stored_shape),
        grad_series.reshape(stored_shape),
        grad_gain,
        grad_mode_in,
        grad_mode_out,
        stream_rms,
    )


def solution(mesh):
    in_specs = (
        P("order", "batch"),
        P("order"),
        P(None, None, None, "order"),
        P(None, None, None, "order"),
        P("batch"),
        P("order", "batch"),
    )
    out_specs = (
        P("order", "batch"),
        P("order", "batch"),
        P("order"),
        P(None, None, None, "order"),
        P(None, None, None, "order"),
        P(),
    )
    return jax.shard_map(local, mesh=mesh, in_specs=in_specs, out_specs=out_specs, check_vma=False)
```

profile of v0, /device:TPU:0, one launch (start us, length us, event | category | flops | bytes accessed | tf_op | source)
XLA Modules:
  0.0 2611.2 jit_solution(10838401631587556636)
XLA Ops:
  12.6 38.8 %psum.63 = f32[8,720]{1,0:T(8,128)S(1)} all-reduce(f32[8,720]{1,0:T(8,128)S(1)} %reduce_sum.66), channel_id=1, replica_groups=mesh['batch'=4,'order'=8] {'order'}, use_global_device_ids=true, to_apply=%region_1.2 | all-reduce | flops 5760 | bytes 46080 | tf_op jit(solution)/shard_map/psum | solution.py:137
  58.1 683.4 %while.15 = (s32[]{:T(128)}, f32[720]{0:T(1024)S(1)}, f32[720]{0:T(1024)S(1)}, f32[254,720]{1,0:T(8,128)S(1)}, f32[254]{0:T(256)S(1)}, /*index=5*/s32[]{:T(128)}, f32[]{:T(128)}, f32[]{:T(128)}, s32[]{:T(128)}) while((s32[]{:T(128)}, f32[720]{0:T(1024)S(1)}, f32[720]{0:T(1024)S(1)}, f32[254,720]{1,0:T(8,128)S(1)}, ...), condition=%wide.region_3.4_spmd.clone, body=%wide.region_2.3_spmd.clone.sunk | while | flops 6485 | bytes 31845 | solution.py:27
  747.8 96.4 %reduce-window.16 = f32[32,32,6,128]{3,1,2,0:T(8,128)S(1)} reduce-window(f32[32,32,6,128]{3,1,2,0:T(8,128)} %bitcast.223, f32[]{:T(128)} %constant.35.clone.1), window={size=1x1x1x128 pad=0_0x0_0x0_0x127_0}, to_apply=%region_6.7 | reduce-window | flops 99876864 | bytes 6291460 | tf_op jit(solution)/shard_map/reduce-window.2
  859.8 96.4 %reduce-window.14 = f32[32,32,6,128]{3,1,2,0:T(8,128)S(1)} reduce-window(f32[32,32,6,128]{3,1,2,0:T(8,128)} %bitcast.225, f32[]{:T(128)} %constant.35.clone.1), window={size=1x1x1x128 pad=0_0x0_0x0_0x127_0}, to_apply=%region_4.5 | reduce-window | flops 99876864 | bytes 6291460 | tf_op jit(solution)/shard_map/reduce-window
  973.4 41.5 %all_gather.14 = f32[2,32,4,512]{1,2,0,3:T(4,128)S(1)} all-gather(f32[2,32,4,64]{1,2,0,3:T(4,128)S(1)} %copy.66), channel_id=1, replica_groups=mesh['batch'=4,'order'=8] {'order'}, dimensions={3}, use_global_device_ids=true | all-gather | bytes 589824 | tf_op jit(solution)/shard_map/all_gather | solution.py:149
  1017.6 40.8 %all_gather.13 = f32[2,32,4,512]{1,2,0,3:T(4,128)S(1)} all-gather(f32[2,32,4,64]{1,2,0,3:T(4,128)S(1)} %copy.61), channel_id=1, replica_groups=mesh['batch'=4,'order'=8] {'order'}, dimensions={3}, use_global_device_ids=true | all-gather | bytes 589824 | tf_op jit(solution)/shard_map/all_gather | solution.py:148
  1087.9 91.7 %fusion.9 = f32[32,8,32,4]{2,3,1,0:T(4,128)S(1)} fusion(f32[32]{0:T(128)S(1)} %sine_multiply_fusion, f32[8,32,512]{2,1,0:T(8,128)S(1)} %convolution_bitcast_fusion.2, f32[1,32,4,512]{3,2,1,0:T(4,128)S(1)} %copy-done.14), kind=kOutput, calls=%fused_computation.9 | convolution fusion | flops 205520896 | bytes 917632 | tf_op jit(solution)/shard_map/bnmd,mrd->bnmr/dot_general | solution.py:88
  1179.6 91.7 %fusion.11 = f32[32,8,32,4]{2,3,1,0:T(4,128)S(1)} fusion(f32[32]{0:T(128)S(1)} %sine_multiply_fusion, f32[8,32,512]{2,1,0:T(8,128)S(1)} %convolution_bitcast_fusion.2, f32[1,32,4,512]{3,2,1,0:T(4,128)S(1)} %copy-done.12), kind=kOutput, calls=%fused_computation.11 | convolution fusion | flops 205520896 | bytes 917632 | tf_op jit(solution)/shard_map/bnmd,mrd->bnmr/dot_general | solution.py:87
  1271.2 91.7 %fusion.80 = f32[8,32,32,4]{1,3,0,2:T(4,128)S(1)} fusion(f32[32,8,32,4]{2,3,1,0:T(4,128)S(1)} %fusion.9, f32[8,32,512]{2,1,0:T(8,128)S(1)} %convolution_bitcast_fusion.2, f32[32]{0:T(128)S(1)} %cosine_multiply_fusion, f32[1,32,4,512]{3,2,1,0:T(4,128)S(1)} %copy-done.12), kind=kOutput, calls=%fused_computation.102 | convolution fusion | flops 205553664 | bytes 1048704 | tf_op jit(solution)/shard_map/bnmd,mrd->bnmr/dot_general | solution.py:90
  1362.9 91.7 %fusion.74 = f32[8,32,32,4]{1,3,0,2:T(4,128)S(1)} fusion(f32[32,8,32,4]{2,3,1,0:T(4,128)S(1)} %fusion.11, f32[8,32,512]{2,1,0:T(8,128)S(1)} %convolution_bitcast_fusion.2, f32[32]{0:T(128)S(1)} %cosine_multiply_fusion, f32[1,32,4,512]{3,2,1,0:T(4,128)S(1)} %copy-done.14), kind=kOutput, calls=%fused_computation.100 | convolution fusion | flops 205553664 | bytes 1048704 | tf_op jit(solution)/shard_map/bnmd,mrd->bnmr/dot_general | solution.py:85
  1454.6 15.9 fusion.156
  1470.6 15.9 fusion.158
  1486.5 87.2 %convolution_bitcast_fusion = f32[8,32,64,512]{3,2,1,0:T(8,128)} fusion(f32[512,8,720]{2,0,1:T(8,128)} %all-gather.3.cloned.1.call-done, f32[32,32,720]{2,1,0:T(8,128)S(1)} %subtract_multiply_fusion.1, f32[32,32,720]{2,1,0:T(8,128)} %copy-done.5), kind=kOutput, calls=%fused_computation.49 | convolution fusion | flops 72479047680 | bytes 51249152 | tf_op jit(solution)/shard_map/nks,dbs->bnkd/dot_general | solution.py:151
  1573.8 17.4 fusion.202
  1591.1 25.6 fusion.98
  1616.8 25.8 fusion.95
  1642.6 38.0 %fusion.33 = f32[32,8,32,4]{2,3,1,0:T(4,128)S(1)} fusion(f32[8,32,32,512]{3,2,1,0:T(8,128)S(1)} %get-tuple-element.78, f32[1,32,4,512]{3,2,1,0:T(4,128)S(1)} %copy.113), kind=kOutput, calls=%fused_computation.37 | convolution fusion | flops 201326592 | bytes 17170432 | tf_op jit(solution)/shard_map/bnmd,mrd->bnmr/dot_general | solution.py:70
  1680.6 38.4 %fusion.35 = f32[32,8,32,4]{2,3,1,0:T(4,128)S(1)} fusion(f32[8,32,32,512]{3,2,1,0:T(8,128)S(1)} %get-tuple-element.78, f32[1,32,4,512]{3,2,1,0:T(4,128)S(1)} %copy-done.10), kind=kOutput, calls=%fused_computation.39 | convolution fusion | flops 201326592 | bytes 17170432 | tf_op jit(solution)/shard_map/bnmd,mrd->bnmr/dot_general | solution.py:67
  1719.0 18.8 subtract_bitcast_fusion
  1737.8 44.2 %fusion.86 = f32[8,32,32,4]{1,3,0,2:T(4,128)S(1)} fusion(f32[32,8,32,4]{2,3,1,0:T(4,128)S(1)} %fusion.35, f32[8,32,32,512]{3,2,1,0:T(8,128)} %get-tuple-element.77, f32[1,32,4,512]{3,2,1,0:T(4,128)S(1)} %copy.113), kind=kOutput, calls=%fused_computation.104 | convolution fusion | flops 201359360 | bytes 17301504 | tf_op jit(solution)/shard_map/bnmd,mrd->bnmr/dot_general | solution.py:65
  1782.0 38.3 %fusion.92 = f32[8,32,32,4]{1,3,0,2:T(4,128)S(1)} fusion(f32[32,8,32,4]{2,3,1,0:T(4,128)S(1)} %fusion.33, f32[8,32,32,512]{3,2,1,0:T(8,128)S(1)} %bitcast.220, f32[1,32,4,512]{3,2,1,0:T(4,128)S(1)} %copy-done.10), kind=kOutput, calls=%fused_computation.106 | convolution fusion | flops 201359360 | bytes 17301504 | tf_op jit(solution)/shard_map/bnmd,mrd->bnmr/dot_general | solution.py:68
  1820.4 17.8 fusion.134
  1838.2 17.8 fusion.140
  1870.0 15.7 reshape.179
  1958.9 18.5 add_bitcast_fusion
  1977.5 110.9 %fusion.63 = f32[512,8,720]{2,0,1:T(8,128)} fusion(f32[32,64,720,1]{2,1,0,3:T(8,128)} %maximum_bitcast_fusion, f32[8,32,32,512]{3,1,0,2:T(8,128)} %subtract_bitcast_fusion, f32[8,32,32,512]{3,1,0,2:T(8,128)} %add_bitcast_fusion), kind=kOutput, calls=%fused_computation.69 | convolution fusion | flops 72485961728 | bytes 51249152 | tf_op jit(solution)/shard_map/nks,bnkd->dbs/dot_general | solution.py:176
  2116.5 16.1 add_bitcast_fusion.1
  2132.6 22.6 fusion.25
  2214.9 80.3 %reduce-scatter.11.cloned.1.call-done = f32[64,8,720]{2,0,1:T(8,128)} async-done(((f32[512,8,720]{2,0,1:T(8,128)}), f32[64,8,720]{2,0,1:T(8,128)}) %reduce-scatter.11.cloned.1.call-update) | async-done | bytes 1474576 | tf_op jit(solution)/shard_map/reduce_scatter | solution.py:178
  2295.2 209.9 %reduce-scatter.9.cloned.1.call-done = f32[64,8,720]{2,0,1:T(8,128)} async-done(((f32[512,8,720]{2,0,1:T(8,128)}), f32[64,8,720]{2,0,1:T(8,128)}) %reduce-scatter.9.cloned.1.call-update) | async-done | bytes 1474576 | tf_op jit(solution)/shard_map/reduce_scatter | solution.py:163
  2513.7 35.5 %psum.64 = f32[8,720]{1,0:T(8,128)S(1)} all-reduce(f32[8,720]{1,0:T(8,128)S(1)} %get-tuple-element.52), channel_id=1, replica_groups=mesh['batch'=4,'order'=8] {'order'}, use_global_device_ids=true, to_apply=%region_11.12 | all-reduce | flops 5760 | bytes 46080 | tf_op jit(solution)/shard_map/psum | solution.py:186
  2560.6 37.2 %all-reduce.2 = (f32[]{:T(128)}, f32[]{:T(128)}, f32[]{:T(128)}, f32[]{:T(128)}) all-reduce(f32[]{:T(128)} %get-tuple-element.56, f32[]{:T(128)S(6)} %select_n.71, f32[]{:T(128)} %get-tuple-element.55, f32[]{:T(128)} %get-tuple-element.53), channel_id=1, replica_groups=mesh['batch'=4,'order'=8] {'batch','order'}, use_global_device_ids=true, to_apply=%region_25.26 | all-reduce | flops 4 | bytes 32 | tf_op jit(solution)/shard_map/psum | solution.py:197
  (1705 shorter events, 622.1 us)
Async XLA Ops:
  7.2 1065.4 %all-gather.5.cloned.1.call-start = ((), (), s32[]{:S(2)}) async-start(), calls=%async_computation.6 | async-start | bytes 14155776 | tf_op jit(solution)/shard_map/all_gather | solution.py:167
  8.8 45.8 %copy-start.22 = (f32[8,720]{1,0:T(8,128)}, f32[8,720]{1,0:T(8,128)S(1)}, u32[]{:S(2)}) copy-start(f32[8,720]{1,0:T(8,128)S(1)} %fusion.182) | copy-start | bytes 69124
  11.3 46.0 %copy-start = (f32[64,8,720]{2,1,0:T(8,128)}, f32[64,8,720]{2,1,0:T(8,128)S(1)}, u32[]{:S(2)}) copy-start(f32[64,8,720]{2,1,0:T(8,128)S(1)} %reshape.151) | copy-start | bytes 4423684
  11.3 43.3 %copy-start.30 = (f32[64]{0:T(128)S(1)}, f32[64]{0:T(128)}, u32[]{:S(2)}) copy-start(f32[64]{0:T(128)} %param.9) | copy-start | bytes 772
  57.3 1429.2 %all-gather.3.cloned.1.call-start = ((), (), s32[]{:S(2)}) async-start(), calls=%async_computation.4 | async-start | bytes 14155776 | tf_op jit(solution)/shard_map/all_gather | solution.py:154
  58.1 2141.4 %reduce-scatter.13.cloned.1.call-start = ((), (), s32[]{:S(2)}) async-start(), calls=%async_computation.8 | async-start | bytes 589824
  965.2 8.1 copy-start.28
  1072.6 15.3 copy-start.14
  1087.9 275.0 %copy-start.20 = (f32[8,32,512]{2,1,0:T(8,128)}, f32[8,32,512]{2,1,0:T(8,128)S(1)}, u32[]{:S(2)}) copy-start(f32[8,32,512]{2,1,0:T(8,128)S(1)} %convolution_bitcast_fusion.2) | copy-start | bytes 1572868
  1087.9 91.7 %copy-start.12 = (f32[1,32,4,512]{3,2,1,0:T(4,128)S(1)}, f32[1,32,4,512]{3,2,1,0:T(4,128)}, u32[]{:S(2)}) copy-start(f32[1,32,4,512]{3,2,1,0:T(4,128)} %copy.116) | copy-start | bytes 786436
  1362.9 91.7 %copy-start.6 = (f32[8,32,32,4]{1,3,0,2:T(4,128)}, f32[8,32,32,4]{1,3,0,2:T(4,128)S(1)}, u32[]{:S(2)}) copy-start(f32[8,32,32,4]{1,3,0,2:T(4,128)S(1)} %fusion.80) | copy-start | bytes 393220
  1454.6 16.0 copy-start.8
  1573.7 17.4 copy-start.7
  1591.1 25.7 copy-start.9
  1642.6 38.0 %copy-start.10 = (f32[1,32,4,512]{3,2,1,0:T(4,128)S(1)}, f32[1,32,4,512]{3,2,1,0:T(4,128)}, u32[]{:S(2)}) copy-start(f32[1,32,4,512]{3,2,1,0:T(4,128)} %copy.114) | copy-start | bytes 786436
  1719.0 63.0 %slice-start = ((s8[16777216]{0:T(1024)(128)(4,1)}), s8[4194304]{0:T(1024)(128)(4,1)S(1)}, s32[]{:S(2)}) async-start(s8[16777216]{0:T(1024)(128)(4,1)} %bitcast.219), calls=%async_computation.11 | async-start | bytes 8388608
  1719.0 63.0 %slice-start.1 = ((s8[16777216]{0:T(1024)(128)(4,1)}), s8[4194304]{0:T(1024)(128)(4,1)S(1)}, s32[]{:S(2)}) async-start(s8[16777216]{0:T(1024)(128)(4,1)} %bitcast.219), calls=%async_computation.12 | async-start | bytes 8388608
  1719.0 63.0 %slice-start.2 = ((s8[16777216]{0:T(1024)(128)(4,1)}), s8[4194304]{0:T(1024)(128)(4,1)S(1)}, s32[]{:S(2)}) async-start(s8[16777216]{0:T(1024)(128)(4,1)} %bitcast.219), calls=%async_computation.13 | async-start | bytes 8388608
  1737.8 44.2 %slice-start.3 = ((s8[16777216]{0:T(1024)(128)(4,1)}), s8[4194304]{0:T(1024)(128)(4,1)S(1)}, s32[]{:S(2)}) async-start(s8[16777216]{0:T(1024)(128)(4,1)} %bitcast.219), calls=%async_computation.14 | async-start | bytes 8388608
  1870.0 15.8 copy-start.21
  1885.7 321.4 %reduce-scatter.15.cloned.1.call-start = ((), (), s32[]{:S(2)}) async-start(), calls=%async_computation.9 | async-start | bytes 589824
  1977.5 317.8 %reduce-scatter.11.cloned.1.call-start = ((), (), s32[]{:S(2)}) async-start(), calls=%async_computation.7 | async-start | bytes 14155776 | tf_op jit(solution)/shard_map/reduce_scatter | solution.py:178
  2088.4 14.4 copy-start.15
  2088.5 416.7 %reduce-scatter.9.cloned.1.call-start = ((), (), s32[]{:S(2)}) async-start(), calls=%async_computation.5 | async-start | bytes 14155776 | tf_op jit(solution)/shard_map/reduce_scatter | solution.py:163
  2169.2 15.3 copy-start.19
  2197.5 403.6 %all-reduce.6.cloned.1.call-start = ((), (), s32[]{:S(2)}) async-start(), calls=%async_computation.10 | async-start | bytes 524288 | tf_op jit(solution)/shard_map/psum | solution.py:190
  2203.8 301.4 %copy-start.1 = (f32[64,8,720]{2,1,0:T(8,128)S(1)}, f32[64,8,720]{2,1,0:T(8,128)}, u32[]{:S(2)}) copy-start(f32[64,8,720]{2,1,0:T(8,128)} %copy-done) | copy-start | bytes 4423684
  2203.8 301.4 %copy-start.23 = (f32[8,720]{1,0:T(8,128)S(1)}, f32[8,720]{1,0:T(8,128)}, u32[]{:S(2)}) copy-start(f32[8,720]{1,0:T(8,128)} %copy-done.22) | copy-start | bytes 69124
  2203.8 301.4 %copy-start.25 = (f32[8,720]{1,0:T(8,128)S(1)}, f32[8,720]{1,0:T(8,128)}, u32[]{:S(2)}) copy-start(f32[8,720]{1,0:T(8,128)} %copy-done.24) | copy-start | bytes 69124
  2203.8 301.4 %copy-start.31 = (f32[64]{0:T(128)S(1)}, f32[64]{0:T(128)}, u32[]{:S(2)}) copy-start(f32[64]{0:T(128)} %param.9) | copy-start | bytes 772
  2508.7 40.5 %copy-start.27 = (f32[8,720]{1,0:T(8,128)S(1)}, f32[8,720]{1,0:T(8,128)}, u32[]{:S(2)}) copy-start(f32[8,720]{1,0:T(8,128)} %copy-done.26) | copy-start | bytes 69124
  2508.7 40.5 %copy-start.3 = (f32[64,8,720]{2,1,0:T(8,128)S(1)}, f32[64,8,720]{2,1,0:T(8,128)}, u32[]{:S(2)}) copy-start(f32[64,8,720]{2,1,0:T(8,128)} %copy-done.2) | copy-start | bytes 4423684
  (12 other events, 32.0 us)
Sparse Core Ops, SparseCore 0:
  57.4 173.7 all-gather.4
  233.4 174.6 all-gather.2
  1885.9 61.2 reduce-scatter.12
  1977.6 61.2 reduce-scatter.14
  2088.6 206.6 reduce-scatter.10
  2298.7 206.4 reduce-scatter.8
  2508.1 31.1 all-reduce.5
where the time goes:
time: 2640 us; the launch traced here: 2610 us
  matrix products  1050 us (40%)
  other arithmetic  387 us (15%)
  loops' own time  342 us (13%)
  local copies, waits for them, and re-layouts  326 us (12%)
  waiting for transfers between devices  291 us (11%)
  blocking collectives  200 us (8%)
    another operation x1, loops' own time, legendre_rows(): final_pair, higher = lax.scan(advance, (first_row, coords), degrees)  342 us
    reduce_scatter x1, waiting for transfers between devices, local(): lax.psum_scatter(partial_field, 'order', scatter_dimension=0, tiled=True)  210 us
    another operation x6, other arithmetic  198 us
    div x254, other arithmetic, advance(): ((2.0 * degree + 1.0) * coords * current - degree * earlier) / (degree +...  168 us
    dynamic_slice x254, local copies, waits for them, and re-layouts, legendre_rows(): final_pair, higher = lax.scan(advance, (first_row, coords), degrees)  149 us
    dot_general x1, matrix products, local(): jnp.einsum('nks,bnkd->dbs', proj_table, grad_coeffs, precision=precise_mode)  111 us
    unnamed x94, local copies, waits for them, and re-layouts  101 us
    dot_general x1, matrix products, back_out(): jnp.einsum('bnmd,mrd->bnmr', grad_real, weights[0], precision=precise_mode)  91.7 us
  transfers between devices with their start and end apart: 7, of which 2 were waited for; matrix products, arithmetic and copies ran while one was open for 51% of the time, Pallas kernels for 0%

commit v1 on v0

v1 whole, which is shorter than its diff:
```python
import functools
import math

import jax
import jax.numpy as jnp
import numpy as np
from jax import lax
from jax.experimental import pallas as pl
from jax.experimental.pallas import tpu as pltpu
from jax.sharding import PartitionSpec as P

ORDER = 256
LEN = 720
LANES = 768
BLOCK = 256
epsilon = 1e-06
f32 = jnp.float32
bf16 = jnp.bfloat16


def legendre_rows():
    coords = 1.0 - (2.0 * np.arange(LEN) + 1.0) / LEN
    rows = [np.ones(LEN), coords]
    for k in range(1, ORDER - 1):
        rows.append(((2.0 * k + 1.0) * coords * rows[k] - k * rows[k - 1]) / (k + 1.0))
    table = np.stack(rows) * np.sqrt((2.0 * np.arange(ORDER) + 1.0) / LEN)[:, None]
    out = np.zeros((ORDER, LANES))
    out[:, :LEN] = table[:, ::-1]
    return out


def phase_rows(mode_count):
    modes = np.arange(mode_count)[:, None]
    steps = np.arange(LANES)[None, :]
    now = 2.0 * np.pi * ((modes * steps) % LEN) / LEN
    nxt = 2.0 * np.pi * ((modes * (steps + 1)) % LEN) / LEN
    root = 1.0 / math.sqrt(LEN)
    rows = np.stack([np.cos(now), np.sin(now), np.cos(nxt) * root, np.sin(nxt) * root])
    return rows.astype(np.float32)


def readout_rows(mode_count):
    modes = np.arange(mode_count)
    angle = 2.0 * np.pi * ((modes * (LEN - 1)) % LEN) / LEN
    factor = np.where(modes == 0, 1.0, 2.0) / math.sqrt(LEN)
    return (factor * np.cos(angle)).astype(np.float32), (-factor * np.sin(angle)).astype(np.float32)


def halves(table):
    high = table.astype(np.float32).astype(jnp.bfloat16)
    low = (table - high.astype(np.float64)).astype(np.float32).astype(jnp.bfloat16)
    return high, low


def split(x):
    high = x.astype(bf16)
    return high, (x - high.astype(f32)).astype(bf16)


def nn(a, b):
    return lax.dot_general(a, b, (((1,), (0,)), ((), ())), preferred_element_type=f32)


def nt(a, b):
    return lax.dot_general(a, b, (((1,), (1,)), ((), ())), preferred_element_type=f32)


def three(dot, a, b):
    return dot(a[0], b[0]) + dot(a[0], b[1]) + dot(a[1], b[0])


def deep(x):
    high, low = split(x)
    return jnp.concatenate([high, low, high], axis=0)


def stacked(weights, pair, rows):
    first = nn(weights, pair[0])
    return first[:rows] + first[rows:] + nn(weights[:rows], pair[1])


def stacked_nt(left, pair, rows):
    first = nt(left, pair[0])
    return first[:rows] + first[rows:] + nt(left[:rows], pair[1])


def rotate(real, imag, cos, sin):
    modes = cos.shape[0]
    shape = (real.shape[0] // modes, modes, real.shape[1])
    real, imag = real.reshape(shape), imag.reshape(shape)
    cos, sin = cos[None], sin[None]
    flat = (shape[0] * modes, shape[2])
    return (real * cos + imag * sin).reshape(flat), (imag * cos - real * sin).reshape(flat)


def triangle():
    row = lax.broadcasted_iota(jnp.int32, (BLOCK, BLOCK), 0)
    col = lax.broadcasted_iota(jnp.int32, (BLOCK, BLOCK), 1)
    return jnp.where(row <= col, 1.0, 0.0).astype(bf16)


def running_sum(x, tri):
    high, low = split(x)
    blocks, carry = [], None
    for b in range(LANES // BLOCK):
        at = slice(b * BLOCK, (b + 1) * BLOCK)
        block = nn(high[:, at], tri) + nn(low[:, at], tri)
        if carry is not None:
            block = block + carry
        carry = block[:, BLOCK - 1 : BLOCK]
        blocks.append(block)
    return jnp.concatenate(blocks, axis=1)


def running_sum_back(x, tri):
    high, low = split(x)
    blocks, carry = [], None
    for b in reversed(range(LANES // BLOCK)):
        at = slice(b * BLOCK, (b + 1) * BLOCK)
        block = nt(high[:, at], tri) + nt(low[:, at], tri)
        if carry is not None:
            block = block + carry
        carry = block[:, 0:1]
        blocks.append(block)
    return jnp.concatenate(blocks[::-1], axis=1)


def deal_kernel(split_at, with_squares, scal_ref, x_ref, *out_refs):
    own_ref, send_refs = out_refs[0], out_refs[1 : 1 + len(split_at) - 1]
    channels = x_ref.shape[0]
    windows = x_ref.shape[1] // LEN
    half = windows // 2
    lane = lax.broadcasted_iota(jnp.int32, (channels, LEN), 1)
    side = scal_ref[0]
    tail = jnp.zeros((channels, 128), f32)
    own_ref[:, :, LANES - 128 :] = jnp.zeros((half, channels, 128), f32)
    for ref in send_refs:
        ref[:, :, LANES - 128 :] = jnp.zeros((ref.shape[0], channels, 128), f32)
    if with_squares:
        squares_ref = out_refs[-1]
        squares_ref[...] = jnp.zeros(squares_ref.shape, f32)
    for w in range(windows):
        value = x_ref[:, w * LEN : (w + 1) * LEN]
        value = jnp.where(lane < scal_ref[2 + w], value, 0.0)
        if with_squares:
            squares_ref[w : w + 1, :LEN] = jnp.sum(value * value, axis=0, keepdims=True)
        j = w % half
        unit = max(u for u in range(len(split_at) - 1) if split_at[u] <= j)
        send_ref, at = send_refs[unit], j - split_at[unit]
        mine = side == (0 if w < half else 1)

        @pl.when(mine)
        def _():
            own_ref[j, :, :LEN] = value

        @pl.when(jnp.logical_not(mine))
        def _():
            send_ref[at, :, :LEN] = value


def weights_kernel(own_ref, rec_ref, down_own, down_rec, up_own, up_rec, down_both, up_both):
    channels = own_ref.shape[1] // 2
    pieces = []
    for ref, down, up in ((own_ref, down_own, up_own), (rec_ref, down_rec, up_rec)):
        high, low = split(ref[...])
        down[...] = jnp.concatenate([high[:, :channels], high[:, :channels], low[:, :channels]], axis=1)
        up[...] = jnp.concatenate([high[:, channels:], high[:, channels:], low[:, channels:]], axis=1)
        across = ref[...].T
        pieces.append(across)
    for k, ref in ((0, down_both), (1, up_both)):
        at = slice(k * channels, (k + 1) * channels)
        rows = jnp.concatenate([pieces[0][at], pieces[1][at]], axis=0)
        high, low = split(rows)
        ref[...] = jnp.concatenate([high, low], axis=0)


def read_kernel(own_ref, rec_ref, up_own, up_rec, leg_high, leg_low, out_ref):
    field = nn(up_own[...], deep(own_ref[0])) + nn(up_rec[...], deep(rec_ref[0]))
    out_ref[0] = three(nt, split(field), (leg_high[...], leg_low[...]))


def inverse_rms(ss_ref, row, full_width):
    return lax.rsqrt(ss_ref[pl.ds(row, 1), :] * (1.0 / full_width) + epsilon)


def rank_kernel(first, full_width, scal_ref, own_ref, rec_ref, ss_ref, down_own, down_rec, leg_high, leg_low, phase_ref, out_ref):
    half = scal_ref[0] * (ss_ref.shape[0] // 2)
    inv = inverse_rms(ss_ref, half + first + pl.program_id(0), full_width)
    mixed = nn(down_own[...], deep(own_ref[0] * inv)) + nn(down_rec[...], deep(rec_ref[0] * inv))
    part = mixed.shape[0] // 2
    real, imag = rotate(mixed[:part], mixed[part:], phase_ref[0], phase_ref[1])
    total = running_sum(jnp.concatenate([real, imag], axis=0), triangle())
    real, imag = rotate(total[:part], total[part:], phase_ref[2], -phase_ref[3])
    memory = jnp.concatenate([real, imag], axis=0)
    out_ref[0] = three(nt, split(memory), (leg_high[...], leg_low[...]))


def back_kernel(first, full_width, scal_ref, mid_ref, end_ref, own_ref, rec_ref, ss_ref, down_both, leg_high, leg_low, phase_ref, prev_ref, own_out, rec_out, grad_out, inner_out):
    step = pl.program_id(0)
    half = scal_ref[0] * (ss_ref.shape[0] // 2)
    row = half + first + step
    inv = inverse_rms(ss_ref, row, full_width)
    channels = own_ref.shape[1]
    total = jnp.where(scal_ref[1] == 1, end_ref[0], mid_ref[0])
    memory = three(nn, split(total), (leg_high[...], leg_low[...]))
    part = memory.shape[0] // 2
    real, imag = rotate(memory[:part], memory[part:], phase_ref[2], phase_ref[3])
    back = running_sum_back(jnp.concatenate([real, imag], axis=0), triangle())
    real, imag = rotate(back[:part], back[part:], phase_ref[0], -phase_ref[1])
    pair = split(jnp.concatenate([real, imag], axis=0))
    scaled = stacked(down_both[...], pair, 2 * channels)
    lane = lax.broadcasted_iota(jnp.int32, scaled.shape, 1)
    scaled = jnp.where(lane < scal_ref[2 + row], scaled, 0.0)
    own_out[0] = scaled[:channels]
    rec_out[0] = scaled[channels:]
    both = jnp.concatenate([own_ref[0], rec_ref[0]], axis=0)
    inner_out[0] = jnp.sum(scaled * both, axis=0, keepdims=True)
    high, low = split(both * inv)
    grads = stacked_nt(jnp.concatenate([high, low], axis=0), pair, 2 * channels)

    @pl.when(step == 0)
    def _():
        grad_out[...] = prev_ref[...] + grads

    @pl.when(step > 0)
    def _():
        grad_out[...] += grads


def branch_kernel(first, scal_ref, mid_ref, end_ref, ser_own, ser_rec, cot_own, cot_rec, up_both, leg_high, leg_low, prev_ref, own_out, rec_out, grad_out):
    step = pl.program_id(0)
    channels = ser_own.shape[1]
    rows = 2 * channels
    row = scal_ref[0] * ((scal_ref.shape[0] - 2) // 2) + first + step
    total = jnp.where(scal_ref[1] == 1, end_ref[0], mid_ref[0])
    field = three(nn, split(total), (leg_high[...], leg_low[...]))
    pair = split(field)
    branch = stacked(up_both[...], pair, rows)
    lane = lax.broadcasted_iota(jnp.int32, branch.shape, 1)
    branch = jnp.where(lane < scal_ref[2 + row], branch, 0.0)
    own_out[0] = branch[:channels]
    rec_out[0] = branch[channels:]
    high, low = split(jnp.concatenate([cot_own[0], cot_rec[0]], axis=0))
    grads = stacked_nt(jnp.concatenate([high, low], axis=0), pair, rows)
    series = jnp.concatenate([ser_own[0], ser_rec[0]], axis=0)
    stats = []
    for v in (series, branch, series + branch):
        v = jnp.sum(v * v, axis=0, keepdims=True)
        stats.append(v[:, :256] + v[:, 256:512] + v[:, 512:])
    stats = jnp.concatenate(stats + [jnp.zeros((5, 256), f32)], axis=0)
    grads = jnp.concatenate([grads, stats], axis=0)

    @pl.when(step == 0)
    def _():
        grad_out[...] = prev_ref[...] + grads

    @pl.when(step > 0)
    def _():
        grad_out[...] += grads


def layer_kernel(units, scal_ref, x_ref, *refs):
    own_refs, rec_refs, out_ref = refs[: len(units)], refs[len(units) : 2 * len(units)], refs[-1]
    windows = x_ref.shape[1] // LEN
    half = windows // 2
    first_side = scal_ref[0] == 0
    for w in range(windows):
        j = w % half
        u = max(k for k in range(len(units)) if units[k][0] <= j)
        mine = own_refs[u][j - units[u][0], :, :LEN]
        theirs = rec_refs[u][j - units[u][0], :, :LEN]
        value = jnp.where(first_side == (w < half), mine, theirs)
        at = slice(w * LEN, (w + 1) * LEN)
        out_ref[:, at] = x_ref[:, at] + value


def series_grad_kernel(units, full_width, scal_ref, cot_ref, x_ref, ss_ref, in_own, in_rec, *refs):
    own_refs, rec_refs, out_ref = refs[: len(units)], refs[len(units) : 2 * len(units)], refs[-1]
    windows = x_ref.shape[1] // LEN
    half = windows // 2
    first_side = scal_ref[0] == 0
    for w in range(windows):
        j = w % half
        u = max(k for k in range(len(units)) if units[k][0] <= j)
        mine = own_refs[u][j - units[u][0], :, :LEN]
        theirs = rec_refs[u][j - units[u][0], :, :LEN]
        keep = first_side == (w < half)
        scaled = jnp.where(keep, mine, theirs)
        inner = jnp.where(keep, in_own[j], in_rec[j])[:, :LEN]
        inv = inverse_rms(ss_ref, w, full_width)[:, :LEN]
        at = slice(w * LEN, (w + 1) * LEN)
        shift = inv * inv * inner * (1.0 / full_width)
        out_ref[:, at] = cot_ref[:, at] + inv * (scaled - x_ref[:, at] * shift)


def whole(shape):
    return pl.BlockSpec(shape, lambda *_: (0,) * len(shape))


SMEM = pl.BlockSpec(memory_space=pltpu.SMEM)
PARAMS = pltpu.CompilerParams(vmem_limit_bytes=48 * 1024 * 1024)


def window_spec(shape, offset):
    return pl.BlockSpec((1,) + shape[1:], lambda i: (i + offset,) + (0,) * (len(shape) - 1))


def cost(flops, byte_count):
    return pl.CostEstimate(flops=int(flops), bytes_accessed=int(byte_count), transcendentals=0)


def struct(shape, dtype=f32):
    return jax.ShapeDtypeStruct(shape, dtype)


def deal(array, scal, units, with_squares):
    channels = array.shape[0]
    windows = array.shape[1] // LEN
    half = windows // 2
    edges = [u[0] for u in units] + [half]
    shapes = [struct((half, channels, LANES))] + [struct((n, channels, LANES)) for _, n in units]
    if with_squares:
        shapes.append(struct((windows, LANES)))
    return pl.pallas_call(
        functools.partial(deal_kernel, edges, with_squares),
        out_shape=shapes,
        in_specs=[SMEM, whole(array.shape)],
        out_specs=[whole(s.shape) for s in shapes],
        grid=(1,),
        compiler_params=PARAMS,
        cost_estimate=cost(array.size * 4, array.size * 8),
    )(scal, array)


def prepare_weights(own, rec):
    rows, channels = own.shape[0], own.shape[1] // 2
    shapes = [struct((rows, 3 * channels), bf16)] * 4 + [struct((4 * channels, rows), bf16)] * 2
    return pl.pallas_call(
        weights_kernel,
        out_shape=shapes,
        in_specs=[whole(own.shape)] * 2,
        out_specs=[whole(s.shape) for s in shapes],
        grid=(1,),
        compiler_params=PARAMS,
        cost_estimate=cost(own.size * 8, own.size * 16),
    )(own, rec)


MATMUL = 2 * 256 * 256 * 256


def unit_call(kernel, unit, smem, arrays, consts, outs, units_of_work):
    first, count = unit
    specs = [SMEM] * len(smem)
    specs += [window_spec(a.shape, offset) for a, offset in arrays]
    specs += [whole(c.shape) for c in consts]
    out_specs, shapes = [], []
    for shape, per_window in outs:
        shapes.append(struct(shape))
        out_specs.append(window_spec(shape, 0) if per_window else whole(shape))
    moved = sum(a.size * 4 * count // a.shape[0] for a, _ in arrays) + sum(c.size * c.dtype.itemsize for c in consts)
    return pl.pallas_call(
        kernel,
        out_shape=shapes,
        in_specs=specs,
        out_specs=out_specs,
        grid=(count,),
        compiler_params=PARAMS,
        cost_estimate=cost(units_of_work * MATMUL * count, moved),
    )(*smem, *[a for a, _ in arrays], *consts)


def swap(x, axis, bit):
    size = lax.axis_size(axis)
    return lax.ppermute(x, axis, [(i, i ^ bit) for i in range(size)])


def add_over(x, axis, bits):
    for bit in bits:
        x = x + swap(x, axis, bit)
    return x


def bits_of(size, start=1):
    bits, bit = [], start
    while bit < size:
        bits.append(bit)
        bit *= 2
    return bits


def line_sum(x):
    size = lax.axis_size("order")
    if size != 8:
        lines = [[2 * i + side for i in range(size // 2)] for side in (0, 1)]
        total = lax.psum(x, "order", axis_index_groups=lines)
        return total, total
    inward = [(0, 2), (1, 3), (6, 4), (7, 5)]
    middle = [(2, 4), (3, 5), (4, 2), (5, 3)]
    outward = [(2, 0), (3, 1), (4, 6), (5, 7)]
    pair = x + lax.ppermute(x, "order", inward)
    total = pair + lax.ppermute(pair, "order", middle)
    return total, lax.ppermute(total, "order", outward)


UNITS = 2


def local(series, norm_gain, mode_in, mode_out, lengths, grad_out):
    channels = series.shape[0]
    windows = series.shape[1] // LEN
    half = windows // 2
    order_devices = lax.axis_size("order")
    batch_devices = lax.axis_size("batch")
    mode_count, rank_count = mode_in.shape[1], mode_in.shape[2]
    full_width = channels * order_devices
    rows = 2 * rank_count * mode_count
    per = half // UNITS
    units = [(u * per, per) for u in range(UNITS)]

    place = lax.axis_index("order")
    line = place // 2
    at_end = jnp.logical_or(line == 0, line == order_devices // 2 - 1)
    scal = jnp.concatenate([jnp.stack([place % 2, at_end.astype(jnp.int32)]), lengths])

    table_high, table_low = (jnp.asarray(h) for h in halves(legendre_rows()))
    phase = jnp.asarray(phase_rows(mode_count))
    read_real, read_imag = (jnp.asarray(r)[None, :, None] for r in readout_rows(mode_count))

    into = jnp.transpose(mode_in, (0, 2, 1, 3))
    outof = jnp.transpose(mode_out, (0, 2, 1, 3))
    second = jnp.stack([
        read_real * outof[0] + read_imag * outof[1],
        read_imag * outof[0] - read_real * outof[1],
    ])
    weights = jnp.concatenate(
        [(into * norm_gain).reshape(rows, channels), second.reshape(rows, channels)], axis=1
    )

    cot = deal(grad_out, scal, units, False)
    weights_rec = swap(weights, "order", 1)
    cot_own = cot[0]
    cot_rec = [swap(c, "order", 1) for c in cot[1:]]
    ser = deal(series, scal, units, True)
    squares = add_over(ser[-1], "order", bits_of(order_devices))
    ser_own = ser[0]
    ser_rec = [swap(s, "order", 1) for s in ser[1:-1]]
    down_own, down_rec, up_own, up_rec, down_both, up_both = prepare_weights(weights, weights_rec)

    grad_sums = []
    for u, (first, count) in enumerate(units):
        (read,) = unit_call(
            read_kernel, units[u], [], [(cot_own, first), (cot_rec[u], 0)],
            [up_own, up_rec, table_high, table_low], [((count, rows, ORDER), True)], 15,
        )
        grad_sums.append(line_sum(read))

    rank_sums = []
    for u, (first, count) in enumerate(units):
        (ranks,) = unit_call(
            functools.partial(rank_kernel, first, full_width), units[u], [scal], [(ser_own, first), (ser_rec[u], 0)],
            [squares, down_own, down_rec, table_high, table_low, phase], [((count, rows, ORDER), True)], 21,
        )
        rank_sums.append(line_sum(ranks))

    grad_in = jnp.zeros((2 * channels, rows), f32)
    scaled_own, scaled_rec, inner = [], [], []
    for u, (first, count) in enumerate(units):
        mine, theirs, grad_in, dots = unit_call(
            functools.partial(back_kernel, first, full_width), units[u], [scal],
            [(grad_sums[u][0], 0), (grad_sums[u][1], 0), (ser_own, first), (ser_rec[u], 0)],
            [squares, down_both, table_high, table_low, phase, grad_in],
            [((count, channels, LANES), True)] * 2 + [((2 * channels, rows), False), ((count, 1, LANES), True)], 24,
        )
        scaled_own.append(mine)
        scaled_rec.append(swap(theirs, "order", 1))
        inner.append(dots)
    inner = jnp.concatenate(inner, axis=0)
    if order_devices == 8:
        inner = add_over(inner, "order", bits_of(order_devices, 2))
    else:
        inner = line_sum(inner)[0]
    inner_rec = swap(inner, "order", 1)

    grad_series = pl.pallas_call(
        functools.partial(series_grad_kernel, units, full_width),
        out_shape=struct(series.shape),
        in_specs=[SMEM] + [whole(series.shape)] * 2 + [whole(squares.shape)] + [whole(inner.shape)] * 2 + [whole(s.shape) for s in scaled_own + scaled_rec],
        out_specs=whole(series.shape),
        grid=(1,),
        compiler_params=PARAMS,
        cost_estimate=cost(series.size * 8, series.size * 16),
    )(scal, grad_out, series, squares, inner, inner_rec, *scaled_own, *scaled_rec)

    row = lax.broadcasted_iota(jnp.int32, (2 * channels + 8, rows), 0)
    col = lax.broadcasted_iota(jnp.int32, (2 * channels + 8, rows), 1)
    here = jnp.logical_and(row == 2 * channels + 3, col == 0)
    grad_mix = jnp.where(here, jnp.sum(lengths).astype(f32), 0.0)
    branch_own, branch_rec = [], []
    for u, (first, count) in enumerate(units):
        mine, theirs, grad_mix = unit_call(
            functools.partial(branch_kernel, first), units[u], [scal],
            [(rank_sums[u][0], 0), (rank_sums[u][1], 0), (ser_own, first), (ser_rec[u], 0), (cot_own, first), (cot_rec[u], 0)],
            [up_both, table_high, table_low, grad_mix],
            [((count, channels, LANES), True)] * 2 + [((2 * channels + 8, rows), False)], 18,
        )
        branch_own.append(mine)
        branch_rec.append(swap(theirs, "order", 1))

    layer_out = pl.pallas_call(
        functools.partial(layer_kernel, units),
        out_shape=struct(series.shape),
        in_specs=[SMEM] + [whole(series.shape)] + [whole(b.shape) for b in branch_own + branch_rec],
        out_specs=whole(series.shape),
        grid=(1,),
        compiler_params=PARAMS,
        cost_estimate=cost(series.size * 2, series.size * 12),
    )(scal, series, *branch_own, *branch_rec)

    stats = grad_mix[2 * channels :]
    own_part = jnp.concatenate([grad_in[:channels], grad_mix[:channels], stats], axis=0)
    rec_part = jnp.concatenate([grad_in[channels:], grad_mix[channels : 2 * channels], stats], axis=0)
    sums = own_part + swap(rec_part, "order", 1)
    if batch_devices == 4:
        sums = add_over(sums, "batch", bits_of(batch_devices))
    else:
        sums = lax.psum(sums, "batch")
    stats = sums[2 * channels :]
    if order_devices == 8:
        stats = add_over(stats, "order", bits_of(order_devices, 2))
    else:
        stats = line_sum(stats)[0]

    into_sum, mix_sum = sums[:channels].T, sums[channels : 2 * channels].T
    shape = (2, rank_count, mode_count, channels)
    into_sum, mix_sum = into_sum.reshape(shape), mix_sum.reshape(shape)
    grad_gain = jnp.sum(into_sum * into, axis=(0, 1, 2))
    grad_mode_in = jnp.transpose(into_sum * norm_gain, (0, 2, 1, 3))
    grad_mode_out = jnp.transpose(
        jnp.stack([
            read_real * mix_sum[0] + read_imag * mix_sum[1],
            read_imag * mix_sum[0] - read_real * mix_sum[1],
        ]),
        (0, 2, 1, 3),
    )
    stats = jnp.sum(stats, axis=1)
    count = stats[3] * (1.0 / order_devices)
    stream_rms = jnp.sqrt(stats[:3] / (count * full_width))
    return layer_out, grad_series, grad_gain, grad_mode_in, grad_mode_out, stream_rms


def solution(mesh):
    wide = P("order", "batch")
    weight = P(None, None, None, "order")
    in_specs = (wide, P("order"), weight, weight, P("batch"), wide)
    out_specs = (wide, wide, P("order"), weight, weight, P())
    return jax.shard_map(local, mesh=mesh, in_specs=in_specs, out_specs=out_specs, check_vma=False)
```

time: 2640 us -> 182 us (0.07); the launches traced: 2610 us -> 181 us
  matrix products: 1050 us -> 0 us
  other arithmetic: 387 us -> 9.8 us
  loops' own time: 342 us -> 0 us
  local copies, waits for them, and re-layouts: 326 us -> 4.83 us
  blocking collectives: 200 us -> 0 us
  waiting for transfers between devices: 291 us -> 92.6 us
  starting transfers between devices: 0.29 us -> 39.6 us
  Pallas kernels: 0 us -> 31.8 us
    dot_general x30 -> x0, matrix products: 1050 us -> none  [the longest x1 111 us: local(): jnp.einsum('nks,bnkd->dbs', proj_table, grad_coeffs, precision=precise_mode)]
    another operation x1 -> x0, loops' own time: 342 us -> none  [legendre_rows(): final_pair, higher = lax.scan(advance, (first_row, coords), degrees)]
    reduce_scatter x2 -> x0, waiting for transfers between devices: 290 us -> none  [the longest x1 210 us: local(): lax.psum_scatter(partial_field, 'order', scatter_dimension=0, tiled=True)]
    another operation x9 -> x1, other arithmetic: 199 us -> 0.01 us  [local(): jnp.stack([read_real * outof[0] + read_imag * outof[1], read_imag * outof...]
    div x255 -> x0, other arithmetic: 168 us -> none  [the longest x254 168 us: advance(): ((2.0 * degree + 1.0) * coords * current - degree * earlier) / (degree +...]
    dynamic_slice x255 -> x0, local copies, waits for them, and re-layouts: 149 us -> none  [the longest x254 149 us: legendre_rows(): final_pair, higher = lax.scan(advance, (first_row, coords), degrees)]
    psum x4 -> x0, blocking collectives: 118 us -> none  [the longest x1 38.8 us: local(): row_mean = lax.psum(squares_local, 'order') / full_width]
    unnamed x94 -> x58, local copies, waits for them, and re-layouts: 101 us -> 3.91 us
  transfers between devices with their start and end apart: 7 -> 32, of which waited for: 2 -> 17; matrix products, arithmetic and copies ran while one was open for 51% -> 6% of each run, Pallas kernels for 0% -> 17%
where the time goes in v1:
time: 182 us; the launch traced here: 181 us
  waiting for transfers between devices  92.6 us (51%)
  starting transfers between devices  39.6 us (22%)
  Pallas kernels  31.8 us (17%)
  other arithmetic  9.8 us (5%)
  local copies, waits for them, and re-layouts  4.83 us (3%)
  between operations  2.74 us (2%)
    ppermute x20, waiting for transfers between devices, swap(): return lax.ppermute(x, axis, [(i, i ^ bit) for i in range(size)])  43.4 us
    ppermute x4, waiting for transfers between devices, line_sum(): return (total, lax.ppermute(total, 'order', outward))  25.1 us
    ppermute x4, waiting for transfers between devices, line_sum(): pair = x + lax.ppermute(x, 'order', inward)  24.1 us
    pallas_call x8, Pallas kernels, unit_call(): pl.pallas_call(kernel, out_shape=shapes, in_specs=specs, out_specs=out_sp...  23.3 us
    ppermute x20, starting transfers between devices, swap(): return lax.ppermute(x, axis, [(i, i ^ bit) for i in range(size)])  21.6 us
    ppermute x4, starting transfers between devices, line_sum(): pair = x + lax.ppermute(x, 'order', inward)  7.48 us
    ppermute x4, starting transfers between devices, line_sum(): return (total, lax.ppermute(total, 'order', outward))  5.35 us
    ppermute x4, starting transfers between devices, line_sum(): total = pair + lax.ppermute(pair, 'order', middle)  5.2 us
  transfers between devices with their start and end apart: 32, of which 17 were waited for; matrix products, arithmetic and copies ran while one was open for 6% of the time, Pallas kernels for 17%

profile of v1, /device:TPU:0, one launch (start us, length us, event | category | flops | bytes accessed | tf_op | source)
XLA Modules:
  0.0 181.4 jit_solution(10552796461587343818)
XLA Ops:
  2.8 1.6 shard_map.154
  4.4 3.0 %collective-permute-start = (f32[2,64,768]{2,1,0:T(8,128)S(1)}, f32[2,64,768]{2,1,0:T(8,128)S(1)}, u32[]{:S(2)}, u32[]{:S(2)}) collective-permute-start(f32[2,64,768]{2,1,0:T(8,128)S(1)} %get-tuple-element.34), channel_id=1, source_target_pairs={{0,1},{1,0},{2,3},{3,2},{4,5},{5,4},{6,7},{7,6},{8,9},{9,8},{10,11... | collective-permute-start | bytes 1179656 | tf_op jit(solution)/shard_map/ppermute | solution.py:375
  8.7 2.0 %collective-permute-start.4 = (f32[256,128]{1,0:T(8,128)S(1)}, f32[256,128]{1,0:T(8,128)S(1)}, u32[]{:S(2)}, u32[]{:S(2)}) collective-permute-start(f32[256,128]{1,0:T(8,128)S(1)} %pad_maximum_fusion.2.own_ref), channel_id=1, source_target_pairs={{0,1},{1,0},{2,3},{3,2},{4,5},{5,4},{6,7},{7,6},{8,9},{9,8},{10,11... | collective-permute-start | bytes 393224 | tf_op jit(solution)/shard_map/ppermute | solution.py:375
  12.4 2.0 %collective-permute-start.1 = (f32[8,768]{1,0:T(8,128)S(1)}, f32[8,768]{1,0:T(8,128)S(1)}, u32[]{:S(2)}, u32[]{:S(2)}) collective-permute-start(f32[8,768]{1,0:T(8,128)S(1)} %get-tuple-element.35), channel_id=1, source_target_pairs={{0,1},{1,0},{2,3},{3,2},{4,5},{5,4},{6,7},{7,6},{8,9},{9,8},{10,11... | collective-permute-start | bytes 73736 | tf_op jit(solution)/shard_map/ppermute | solution.py:375
  14.3 22.4 %collective-permute-done.1 = f32[8,768]{1,0:T(8,128)S(1)} collective-permute-done((f32[8,768]{1,0:T(8,128)S(1)}, f32[8,768]{1,0:T(8,128)S(1)}, u32[]{:S(2)}, u32[]{:S(2)}) %collective-permute-start.1) | collective-permute-done | bytes 24608 | tf_op jit(solution)/shard_map/ppermute | solution.py:375
  36.7 1.8 %collective-permute-start.2 = (f32[8,768]{1,0:T(8,128)S(1)}, f32[8,768]{1,0:T(8,128)S(1)}, u32[]{:S(2)}, u32[]{:S(2)}) collective-permute-start(f32[8,768]{1,0:T(8,128)S(1)} %add.74), channel_id=1, source_target_pairs={{0,2},{1,3},{2,0},{3,1},{4,6},{5,7},{6,4},{7,5},{8,10},{9,11},{10,... | collective-permute-start | bytes 73736 | tf_op jit(solution)/shard_map/ppermute | solution.py:375
  38.6 2.0 %collective-permute-done.2 = f32[8,768]{1,0:T(8,128)S(1)} collective-permute-done((f32[8,768]{1,0:T(8,128)S(1)}, f32[8,768]{1,0:T(8,128)S(1)}, u32[]{:S(2)}, u32[]{:S(2)}) %collective-permute-start.2) | collective-permute-done | bytes 24608 | tf_op jit(solution)/shard_map/ppermute | solution.py:375
  40.6 2.8 %collective-permute-start.3 = (f32[8,768]{1,0:T(8,128)S(1)}, f32[8,768]{1,0:T(8,128)S(1)}, u32[]{:S(2)}, u32[]{:S(2)}) collective-permute-start(f32[8,768]{1,0:T(8,128)S(1)} %add.75), channel_id=1, source_target_pairs={{0,4},{1,5},{2,6},{3,7},{4,0},{5,1},{6,2},{7,3},{8,12},{9,13},{10,... | collective-permute-start | bytes 73736 | tf_op jit(solution)/shard_map/ppermute | solution.py:375
  43.4 1.9 %collective-permute-done.3 = f32[8,768]{1,0:T(8,128)S(1)} collective-permute-done((f32[8,768]{1,0:T(8,128)S(1)}, f32[8,768]{1,0:T(8,128)S(1)}, u32[]{:S(2)}, u32[]{:S(2)}) %collective-permute-start.3) | collective-permute-done | bytes 24608 | tf_op jit(solution)/shard_map/ppermute | solution.py:375
  45.3 1.7 collective-permute-start.13
  47.3 3.5 %shard_map.156 = f32[2,256,256]{2,1,0:T(8,128)S(1)} custom-call(s32[10]{0:T(128)S(1)} %pad_add_fusion.scal_ref, f32[4,64,768]{2,1,0:T(8,128)S(1)} %get-tuple-element.33.own_ref.ser_own, f32[2,64,768]{2,1,0:T(8,128)S(1)} %collective-permute-done.rec_ref.ser_rec, f32[8,768]{1,0:T(8,128)S(1)} %add.76.ss_ref, bf16[256,192]{1,0:T(8,128)(2,1)S(1)} %get-tuple-element.36.down_own, ...), custom_call_target="tpu_custom_call" | custom-call | flops 1409286144 | bytes 2187264 | tf_op jit(solution)/shard_map/pallas_call | solution.py:362
  50.9 3.5 %collective-permute-start.5 = (f32[2,256,256]{2,1,0:T(8,128)S(1)}, f32[2,256,256]{2,1,0:T(8,128)S(1)}, u32[]{:S(2)}, u32[]{:S(2)}) collective-permute-start(f32[2,256,256]{2,1,0:T(8,128)S(1)} %shard_map.156), channel_id=1, source_target_pairs={{0,2},{1,3},{6,4},{7,5},{8,10},{9,11},{14,12},{15,13},{16,18},{17,... | collective-permute-start | bytes 1572872 | tf_op jit(solution)/shard_map/ppermute | solution.py:401
  54.4 3.5 %shard_map.159 = f32[2,256,256]{2,1,0:T(8,128)S(1)} custom-call(s32[10]{0:T(128)S(1)} %pad_add_fusion.scal_ref, f32[4,64,768]{2,1,0:T(8,128)S(1)} %get-tuple-element.33.own_ref.ser_own, f32[2,64,768]{2,1,0:T(8,128)S(1)} %collective-permute-done.9.rec_ref.ser_rec, f32[8,768]{1,0:T(8,128)S(1)} %add.76.ss_ref, bf16[256,192]{1,0:T(8,128)(2,1)S(1)} %get-tuple-element.36.down_own, ...), custom_call_target="tpu_custom_call" | custom-call | flops 1409286144 | bytes 2187264 | tf_op jit(solution)/shard_map/pallas_call | solution.py:362
  59.3 2.0 %shard_map.162 = f32[2,256,256]{2,1,0:T(8,128)S(1)} custom-call(f32[4,64,768]{2,1,0:T(8,128)S(1)} %get-tuple-element.38.cot_own.own_ref, f32[2,64,768]{2,1,0:T(8,128)S(1)} %collective-permute-done.8.cot_rec.rec_ref, bf16[256,192]{1,0:T(8,128)(2,1)S(1)} %get-tuple-element.48.up_own, bf16[256,192]{1,0:T(8,128)(2,1)S(1)} %get-tuple-element.49.up_rec, ...), custom_call_target="tpu_custom_call" | custom-call | flops 1006632960 | bytes 1769472 | tf_op jit(solution)/shard_map/pallas_call | solution.py:362
  62.7 2.0 %shard_map.164 = f32[2,256,256]{2,1,0:T(8,128)S(1)} custom-call(f32[4,64,768]{2,1,0:T(8,128)S(1)} %get-tuple-element.38.cot_own.own_ref, f32[2,64,768]{2,1,0:T(8,128)S(1)} %collective-permute-done.13.cot_rec.rec_ref, bf16[256,192]{1,0:T(8,128)(2,1)S(1)} %get-tuple-element.48.up_own, bf16[256,192]{1,0:T(8,128)(2,1)S(1)} %get-tuple-element.49.up_rec, ...), custom_call_target="tpu_custom_call" | custom-call | flops 1006632960 | bytes 1769472 | tf_op jit(solution)/shard_map/pallas_call | solution.py:362
  67.5 10.5 %collective-permute-done.10 = f32[2,256,256]{2,1,0:T(8,128)S(1)} collective-permute-done((f32[2,256,256]{2,1,0:T(8,128)S(1)}, f32[2,256,256]{2,1,0:T(8,128)S(1)}, u32[]{:S(2)}, u32[]{:S(2)}) %collective-permute-start.10) | collective-permute-done | bytes 524320 | tf_op jit(solution)/shard_map/ppermute | solution.py:401
  80.3 8.9 %collective-permute-done.16 = f32[2,256,256]{2,1,0:T(8,128)S(1)} collective-permute-done((f32[2,256,256]{2,1,0:T(8,128)S(1)}, f32[2,256,256]{2,1,0:T(8,128)S(1)}, u32[]{:S(2)}, u32[]{:S(2)}) %collective-permute-start.16) | collective-permute-done | bytes 524320 | tf_op jit(solution)/shard_map/ppermute | solution.py:401
  91.7 4.1 %collective-permute-done.19 = f32[2,256,256]{2,1,0:T(8,128)S(1)} collective-permute-done((f32[2,256,256]{2,1,0:T(8,128)S(1)}, f32[2,256,256]{2,1,0:T(8,128)S(1)}, u32[]{:S(2)}, u32[]{:S(2)}) %collective-permute-start.19) | collective-permute-done | bytes 524320 | tf_op jit(solution)/shard_map/ppermute | solution.py:401
  109.1 7.8 %collective-permute-done.7.end_ref = f32[2,256,256]{2,1,0:T(8,128)S(1)} collective-permute-done((f32[2,256,256]{2,1,0:T(8,128)S(1)}, f32[2,256,256]{2,1,0:T(8,128)S(1)}, u32[]{:S(2)}, u32[]{:S(2)}) %collective-permute-start.7) | collective-permute-done | bytes 524320 | tf_op jit(solution)/shard_map/ppermute | solution.py:403
  116.9 2.6 %shard_map.158 = (f32[2,64,768]{2,1,0:T(8,128)S(1)}, f32[2,64,768]{2,1,0:T(8,128)S(1)}, f32[136,256]{1,0:T(8,128)S(1)}) custom-call(s32[10]{0:T(128)S(1)} %pad_add_fusion.scal_ref, f32[2,256,256]{2,1,0:T(8,128)S(1)} %add.79.mid_ref, f32[2,256,256]{2,1,0:T(8,128)S(1)} %collective-permute-done.7.end_ref, f32[4,64,768]{2,1,0:T(8,128)S(1)} %get-tuple-element.33.own_ref.ser_own, ...), custom_call_target="tpu_custom_call" | custom-call | flops 1207959552 | bytes 3678208 | tf_op jit(solution)/shard_map/pallas_call | solution.py:362
  119.5 8.6 %collective-permute-done.12.end_ref = f32[2,256,256]{2,1,0:T(8,128)S(1)} collective-permute-done((f32[2,256,256]{2,1,0:T(8,128)S(1)}, f32[2,256,256]{2,1,0:T(8,128)S(1)}, u32[]{:S(2)}, u32[]{:S(2)}) %collective-permute-start.12) | collective-permute-done | bytes 524320 | tf_op jit(solution)/shard_map/ppermute | solution.py:403
  128.1 2.6 %shard_map.160 = (f32[2,64,768]{2,1,0:T(8,128)S(1)}, f32[2,64,768]{2,1,0:T(8,128)S(1)}, f32[136,256]{1,0:T(8,128)S(1)}) custom-call(s32[10]{0:T(128)S(1)} %pad_add_fusion.scal_ref, f32[2,256,256]{2,1,0:T(8,128)S(1)} %add.81.mid_ref, f32[2,256,256]{2,1,0:T(8,128)S(1)} %collective-permute-done.12.end_ref, f32[4,64,768]{2,1,0:T(8,128)S(1)} %get-tuple-element.33.own_ref.ser_own, ...), custom_call_target="tpu_custom_call" | custom-call | flops 1207959552 | bytes 3678208 | tf_op jit(solution)/shard_map/pallas_call | solution.py:362
  132.8 6.5 %collective-permute-done.18.end_ref = f32[2,256,256]{2,1,0:T(8,128)S(1)} collective-permute-done((f32[2,256,256]{2,1,0:T(8,128)S(1)}, f32[2,256,256]{2,1,0:T(8,128)S(1)}, u32[]{:S(2)}, u32[]{:S(2)}) %collective-permute-start.18) | collective-permute-done | bytes 524320 | tf_op jit(solution)/shard_map/ppermute | solution.py:403
  139.3 3.6 %shard_map.163 = (f32[2,64,768]{2,1,0:T(8,128)S(1)}, f32[2,64,768]{2,1,0:T(8,128)S(1)}, f32[128,256]{1,0:T(8,128)S(1)}, f32[2,1,768]{2,1,0:T(1,128)S(1)}) custom-call(s32[10]{0:T(128)S(1)} %pad_add_fusion.scal_ref, f32[2,256,256]{2,1,0:T(8,128)S(1)} %add.83.mid_ref, f32[2,256,256]{2,1,0:T(8,128)S(1)} %collective-permute-done.18.end_ref, ...), custom_call_target="tpu_custom_call" | custom-call | flops 1610612736 | bytes 3301376 | tf_op jit(solution)/shard_map/pallas_call | solution.py:362
  142.9 2.2 %collective-permute-done.21.end_ref = f32[2,256,256]{2,1,0:T(8,128)S(1)} collective-permute-done((f32[2,256,256]{2,1,0:T(8,128)S(1)}, f32[2,256,256]{2,1,0:T(8,128)S(1)}, u32[]{:S(2)}, u32[]{:S(2)}) %collective-permute-start.21) | collective-permute-done | bytes 524320 | tf_op jit(solution)/shard_map/ppermute | solution.py:403
  145.1 3.5 %shard_map.165 = (f32[2,64,768]{2,1,0:T(8,128)S(1)}, f32[2,64,768]{2,1,0:T(8,128)S(1)}, f32[128,256]{1,0:T(8,128)S(1)}, f32[2,1,768]{2,1,0:T(1,128)S(1)}) custom-call(s32[10]{0:T(128)S(1)} %pad_add_fusion.scal_ref, f32[2,256,256]{2,1,0:T(8,128)S(1)} %add.85.mid_ref, f32[2,256,256]{2,1,0:T(8,128)S(1)} %collective-permute-done.21.end_ref, ...), custom_call_target="tpu_custom_call" | custom-call | flops 1610612736 | bytes 3301376 | tf_op jit(solution)/shard_map/pallas_call | solution.py:362
  150.9 4.5 %collective-permute-done.27 = f32[136,256]{1,0:T(8,128)S(1)} collective-permute-done((f32[136,256]{1,0:T(8,128)S(1)}, f32[136,256]{1,0:T(8,128)S(1)}, u32[]{:S(2)}, u32[]{:S(2)}) %collective-permute-start.27) | collective-permute-done | bytes 139296 | tf_op jit(solution)/shard_map/ppermute | solution.py:375
  157.4 4.6 %collective-permute-done.23 = f32[4,1,768]{2,1,0:T(1,128)S(1)} collective-permute-done((f32[4,1,768]{2,1,0:T(1,128)S(1)}, f32[4,1,768]{2,1,0:T(1,128)S(1)}, u32[]{:S(2)}, u32[]{:S(2)}) %collective-permute-start.23) | collective-permute-done | bytes 12320 | tf_op jit(solution)/shard_map/ppermute | solution.py:375
  165.1 2.1 %shard_map.161 = f32[64,5760]{1,0:T(8,128)} custom-call(s32[10]{0:T(128)S(1)} %pad_add_fusion.scal_ref, f32[64,5760]{1,0:T(8,128)S(1)} %copy-done.1, f32[2,64,768]{2,1,0:T(8,128)S(1)} %get-tuple-element.41.refs_0_, f32[2,64,768]{2,1,0:T(8,128)S(1)} %get-tuple-element.45.refs_1_, f32[2,64,768]{2,1,0:T(8,128)S(1)} %collective-permute-done.14.refs_2_, ...), custom_call_target="tpu_custom_call" | custom-call | flops 737280 | bytes 4423680 | tf_op jit(solution)/shard_map/pallas_call | solution.py:510
  167.3 3.1 %shard_map.166 = f32[64,5760]{1,0:T(8,128)} custom-call(s32[10]{0:T(128)S(1)} %pad_add_fusion.scal_ref, f32[64,5760]{1,0:T(8,128)S(1)} %copy-done.2, f32[64,5760]{1,0:T(8,128)S(1)} %copy-done.1, f32[8,768]{1,0:T(8,128)S(1)} %add.76.ss_ref, f32[4,1,768]{2,1,0:T(1,128)S(1)} %add.87.in_own, f32[4,1,768]{2,1,0:T(1,128)S(1)} %collective-permute-done.24.in_rec, ...), custom_call_target="tpu_custom_call" | custom-call | flops 2949120 | bytes 5898240 | tf_op jit(solution)/shard_map/pallas_call | solution.py:485
  171.4 3.5 %collective-permute-done.30 = f32[8,256]{1,0:T(8,128)S(1)} collective-permute-done((f32[8,256]{1,0:T(8,128)S(1)}, f32[8,256]{1,0:T(8,128)S(1)}, u32[]{:S(2)}, u32[]{:S(2)}) %collective-permute-start.30) | collective-permute-done | bytes 8224 | tf_op jit(solution)/shard_map/ppermute | solution.py:375
  176.5 3.0 %collective-permute-done.31 = f32[8,256]{1,0:T(8,128)S(1)} collective-permute-done((f32[8,256]{1,0:T(8,128)S(1)}, f32[8,256]{1,0:T(8,128)S(1)}, u32[]{:S(2)}, u32[]{:S(2)}) %collective-permute-start.31) | collective-permute-done | bytes 8224 | tf_op jit(solution)/shard_map/ppermute | solution.py:375
  (148 shorter events, 41.2 us)
Async XLA Ops:
  4.4 42.9 %collective-permute-start = (f32[2,64,768]{2,1,0:T(8,128)S(1)}, f32[2,64,768]{2,1,0:T(8,128)S(1)}, u32[]{:S(2)}, u32[]{:S(2)}) collective-permute-start(f32[2,64,768]{2,1,0:T(8,128)S(1)} %get-tuple-element.34), channel_id=1, source_target_pairs={{0,1},{1,0},{2,3},{3,2},{4,5},{5,4},{6,7},{7,6},{8,9},{9,8},{10,11... | collective-permute-start | bytes 1179656 | tf_op jit(solution)/shard_map/ppermute | solution.py:375
  7.4 47.0 %collective-permute-start.9 = (f32[2,64,768]{2,1,0:T(8,128)S(1)}, f32[2,64,768]{2,1,0:T(8,128)S(1)}, u32[]{:S(2)}, u32[]{:S(2)}) collective-permute-start(f32[2,64,768]{2,1,0:T(8,128)S(1)} %get-tuple-element.42), channel_id=1, source_target_pairs={{0,1},{1,0},{2,3},{3,2},{4,5},{5,4},{6,7},{7,6},{8,9},{9,8},{10,11... | collective-permute-start | bytes 1179656 | tf_op jit(solution)/shard_map/ppermute | solution.py:375
  8.7 38.3 %collective-permute-start.4 = (f32[256,128]{1,0:T(8,128)S(1)}, f32[256,128]{1,0:T(8,128)S(1)}, u32[]{:S(2)}, u32[]{:S(2)}) collective-permute-start(f32[256,128]{1,0:T(8,128)S(1)} %pad_maximum_fusion.2.own_ref), channel_id=1, source_target_pairs={{0,1},{1,0},{2,3},{3,2},{4,5},{5,4},{6,7},{7,6},{8,9},{9,8},{10,11... | collective-permute-start | bytes 393224 | tf_op jit(solution)/shard_map/ppermute | solution.py:375
  12.2 47.1 %collective-permute-start.8 = (f32[2,64,768]{2,1,0:T(8,128)S(1)}, f32[2,64,768]{2,1,0:T(8,128)S(1)}, u32[]{:S(2)}, u32[]{:S(2)}) collective-permute-start(f32[2,64,768]{2,1,0:T(8,128)S(1)} %get-tuple-element.39), channel_id=1, source_target_pairs={{0,1},{1,0},{2,3},{3,2},{4,5},{5,4},{6,7},{7,6},{8,9},{9,8},{10,11... | collective-permute-start | bytes 1179656 | tf_op jit(solution)/shard_map/ppermute | solution.py:375
  12.4 24.3 %collective-permute-start.1 = (f32[8,768]{1,0:T(8,128)S(1)}, f32[8,768]{1,0:T(8,128)S(1)}, u32[]{:S(2)}, u32[]{:S(2)}) collective-permute-start(f32[8,768]{1,0:T(8,128)S(1)} %get-tuple-element.35), channel_id=1, source_target_pairs={{0,1},{1,0},{2,3},{3,2},{4,5},{5,4},{6,7},{7,6},{8,9},{9,8},{10,11... | collective-permute-start | bytes 73736 | tf_op jit(solution)/shard_map/ppermute | solution.py:375
  36.7 3.8 %collective-permute-start.2 = (f32[8,768]{1,0:T(8,128)S(1)}, f32[8,768]{1,0:T(8,128)S(1)}, u32[]{:S(2)}, u32[]{:S(2)}) collective-permute-start(f32[8,768]{1,0:T(8,128)S(1)} %add.74), channel_id=1, source_target_pairs={{0,2},{1,3},{2,0},{3,1},{4,6},{5,7},{6,4},{7,5},{8,10},{9,11},{10,... | collective-permute-start | bytes 73736 | tf_op jit(solution)/shard_map/ppermute | solution.py:375
  40.6 4.7 %collective-permute-start.3 = (f32[8,768]{1,0:T(8,128)S(1)}, f32[8,768]{1,0:T(8,128)S(1)}, u32[]{:S(2)}, u32[]{:S(2)}) collective-permute-start(f32[8,768]{1,0:T(8,128)S(1)} %add.75), channel_id=1, source_target_pairs={{0,4},{1,5},{2,6},{3,7},{4,0},{5,1},{6,2},{7,3},{8,12},{9,13},{10,... | collective-permute-start | bytes 73736 | tf_op jit(solution)/shard_map/ppermute | solution.py:375
  45.3 17.4 %collective-permute-start.13 = (f32[2,64,768]{2,1,0:T(8,128)S(1)}, f32[2,64,768]{2,1,0:T(8,128)S(1)}, u32[]{:S(2)}, u32[]{:S(2)}) collective-permute-start(f32[2,64,768]{2,1,0:T(8,128)S(1)} %get-tuple-element.43), channel_id=1, source_target_pairs={{0,1},{1,0},{2,3},{3,2},{4,5},{5,4},{6,7},{7,6},{8,9},{9,8},{10,11... | collective-permute-start | bytes 1179656 | tf_op jit(solution)/shard_map/ppermute | solution.py:375
  50.9 15.8 %collective-permute-start.5 = (f32[2,256,256]{2,1,0:T(8,128)S(1)}, f32[2,256,256]{2,1,0:T(8,128)S(1)}, u32[]{:S(2)}, u32[]{:S(2)}) collective-permute-start(f32[2,256,256]{2,1,0:T(8,128)S(1)} %shard_map.156), channel_id=1, source_target_pairs={{0,2},{1,3},{6,4},{7,5},{8,10},{9,11},{14,12},{15,13},{16,18},{17,... | collective-permute-start | bytes 1572872 | tf_op jit(solution)/shard_map/ppermute | solution.py:401
  58.0 20.0 %collective-permute-start.10 = (f32[2,256,256]{2,1,0:T(8,128)S(1)}, f32[2,256,256]{2,1,0:T(8,128)S(1)}, u32[]{:S(2)}, u32[]{:S(2)}) collective-permute-start(f32[2,256,256]{2,1,0:T(8,128)S(1)} %shard_map.159), channel_id=1, source_target_pairs={{0,2},{1,3},{6,4},{7,5},{8,10},{9,11},{14,12},{15,13},{16,18},{17,... | collective-permute-start | bytes 1572872 | tf_op jit(solution)/shard_map/ppermute | solution.py:401
  61.4 27.8 %collective-permute-start.16 = (f32[2,256,256]{2,1,0:T(8,128)S(1)}, f32[2,256,256]{2,1,0:T(8,128)S(1)}, u32[]{:S(2)}, u32[]{:S(2)}) collective-permute-start(f32[2,256,256]{2,1,0:T(8,128)S(1)} %shard_map.162), channel_id=1, source_target_pairs={{0,2},{1,3},{6,4},{7,5},{8,10},{9,11},{14,12},{15,13},{16,18},{17,... | collective-permute-start | bytes 1572872 | tf_op jit(solution)/shard_map/ppermute | solution.py:401
  64.8 31.0 %collective-permute-start.19 = (f32[2,256,256]{2,1,0:T(8,128)S(1)}, f32[2,256,256]{2,1,0:T(8,128)S(1)}, u32[]{:S(2)}, u32[]{:S(2)}) collective-permute-start(f32[2,256,256]{2,1,0:T(8,128)S(1)} %shard_map.164), channel_id=1, source_target_pairs={{0,2},{1,3},{6,4},{7,5},{8,10},{9,11},{14,12},{15,13},{16,18},{17,... | collective-permute-start | bytes 1572872 | tf_op jit(solution)/shard_map/ppermute | solution.py:401
  66.8 31.3 %collective-permute-start.6 = (f32[2,256,256]{2,1,0:T(8,128)S(1)}, f32[2,256,256]{2,1,0:T(8,128)S(1)}, u32[]{:S(2)}, u32[]{:S(2)}) collective-permute-start(f32[2,256,256]{2,1,0:T(8,128)S(1)} %add.78), channel_id=1, source_target_pairs={{2,4},{3,5},{4,2},{5,3},{10,12},{11,13},{12,10},{13,11},{18,20},{1... | collective-permute-start | bytes 1572872 | tf_op jit(solution)/shard_map/ppermute | solution.py:402
  78.8 22.0 %collective-permute-start.11 = (f32[2,256,256]{2,1,0:T(8,128)}, f32[2,256,256]{2,1,0:T(8,128)}, u32[]{:S(2)}, u32[]{:S(2)}) collective-permute-start(f32[2,256,256]{2,1,0:T(8,128)} %add.80), channel_id=1, source_target_pairs={{2,4},{3,5},{4,2},{5,3},{10,12},{11,13},{12,10},{13,11},{18,20},{1... | collective-permute-start | bytes 1572872 | tf_op jit(solution)/shard_map/ppermute | solution.py:402
  90.1 13.4 %collective-permute-start.17 = (f32[2,256,256]{2,1,0:T(8,128)}, f32[2,256,256]{2,1,0:T(8,128)}, u32[]{:S(2)}, u32[]{:S(2)}) collective-permute-start(f32[2,256,256]{2,1,0:T(8,128)} %add.82), channel_id=1, source_target_pairs={{2,4},{3,5},{4,2},{5,3},{10,12},{11,13},{12,10},{13,11},{18,20},{1... | collective-permute-start | bytes 1572872 | tf_op jit(solution)/shard_map/ppermute | solution.py:402
  96.7 9.5 %collective-permute-start.20 = (f32[2,256,256]{2,1,0:T(8,128)}, f32[2,256,256]{2,1,0:T(8,128)}, u32[]{:S(2)}, u32[]{:S(2)}) collective-permute-start(f32[2,256,256]{2,1,0:T(8,128)} %add.84), channel_id=1, source_target_pairs={{2,4},{3,5},{4,2},{5,3},{10,12},{11,13},{12,10},{13,11},{18,20},{1... | collective-permute-start | bytes 1572872 | tf_op jit(solution)/shard_map/ppermute | solution.py:402
  98.2 18.7 %collective-permute-start.7 = (f32[2,256,256]{2,1,0:T(8,128)S(1)}, f32[2,256,256]{2,1,0:T(8,128)S(1)}, u32[]{:S(2)}, u32[]{:S(2)}) collective-permute-start(f32[2,256,256]{2,1,0:T(8,128)S(1)} %add.79.mid_ref), channel_id=1, source_target_pairs={{2,0},{3,1},{4,6},{5,7},{10,8},{11,9},{12,14},{13,15},{18,16},{19,... | collective-permute-start | bytes 1572872 | tf_op jit(solution)/shard_map/ppermute | solution.py:403
  102.1 26.0 %collective-permute-start.12 = (f32[2,256,256]{2,1,0:T(8,128)S(1)}, f32[2,256,256]{2,1,0:T(8,128)S(1)}, u32[]{:S(2)}, u32[]{:S(2)}) collective-permute-start(f32[2,256,256]{2,1,0:T(8,128)S(1)} %add.81.mid_ref), channel_id=1, source_target_pairs={{2,0},{3,1},{4,6},{5,7},{10,8},{11,9},{12,14},{13,15},{18,16},{19,... | collective-permute-start | bytes 1572872 | tf_op jit(solution)/shard_map/ppermute | solution.py:403
  104.9 34.4 %collective-permute-start.18 = (f32[2,256,256]{2,1,0:T(8,128)S(1)}, f32[2,256,256]{2,1,0:T(8,128)S(1)}, u32[]{:S(2)}, u32[]{:S(2)}) collective-permute-start(f32[2,256,256]{2,1,0:T(8,128)S(1)} %add.83.mid_ref), channel_id=1, source_target_pairs={{2,0},{3,1},{4,6},{5,7},{10,8},{11,9},{12,14},{13,15},{18,16},{19,... | collective-permute-start | bytes 1572872 | tf_op jit(solution)/shard_map/ppermute | solution.py:403
  107.5 37.6 %collective-permute-start.21 = (f32[2,256,256]{2,1,0:T(8,128)S(1)}, f32[2,256,256]{2,1,0:T(8,128)S(1)}, u32[]{:S(2)}, u32[]{:S(2)}) collective-permute-start(f32[2,256,256]{2,1,0:T(8,128)S(1)} %add.85.mid_ref), channel_id=1, source_target_pairs={{2,0},{3,1},{4,6},{5,7},{10,8},{11,9},{12,14},{13,15},{18,16},{19,... | collective-permute-start | bytes 1572872 | tf_op jit(solution)/shard_map/ppermute | solution.py:403
  130.7 32.8 %collective-permute-start.14 = (f32[2,64,768]{2,1,0:T(8,128)S(1)}, f32[2,64,768]{2,1,0:T(8,128)S(1)}, u32[]{:S(2)}, u32[]{:S(2)}) collective-permute-start(f32[2,64,768]{2,1,0:T(8,128)S(1)} %get-tuple-element.46), channel_id=1, source_target_pairs={{0,1},{1,0},{2,3},{3,2},{4,5},{5,4},{6,7},{7,6},{8,9},{9,8},{10,11... | collective-permute-start | bytes 1179656 | tf_op jit(solution)/shard_map/ppermute | solution.py:375
  131.3 33.8 %collective-permute-start.15 = (f32[2,64,768]{2,1,0:T(8,128)S(1)}, f32[2,64,768]{2,1,0:T(8,128)S(1)}, u32[]{:S(2)}, u32[]{:S(2)}) collective-permute-start(f32[2,64,768]{2,1,0:T(8,128)S(1)} %get-tuple-element.47), channel_id=1, source_target_pairs={{0,1},{1,0},{2,3},{3,2},{4,5},{5,4},{6,7},{7,6},{8,9},{9,8},{10,11... | collective-permute-start | bytes 1179656 | tf_op jit(solution)/shard_map/ppermute | solution.py:375
  148.7 6.7 %collective-permute-start.27 = (f32[136,256]{1,0:T(8,128)S(1)}, f32[136,256]{1,0:T(8,128)S(1)}, u32[]{:S(2)}, u32[]{:S(2)}) collective-permute-start(f32[136,256]{1,0:T(8,128)S(1)} %pad_maximum_fusion), channel_id=1, source_target_pairs={{0,1},{1,0},{2,3},{3,2},{4,5},{5,4},{6,7},{7,6},{8,9},{9,8},{10,11... | collective-permute-start | bytes 417800 | tf_op jit(solution)/shard_map/ppermute | solution.py:375
  149.3 6.6 %collective-permute-start.22 = (f32[4,1,768]{2,1,0:T(1,128)S(1)}, f32[4,1,768]{2,1,0:T(1,128)S(1)}, u32[]{:S(2)}, u32[]{:S(2)}) collective-permute-start(f32[4,1,768]{2,1,0:T(1,128)S(1)} %constant_dynamic-update-slice_fusion), channel_id=1, source_target_pairs={{0,2},{1,3},{2,0},{3,1},{4,6},{5,7},{6,4},{7,5},{8,10},{9,11},{10,... | collective-permute-start | bytes 36872 | tf_op jit(solution)/shard_map/ppermute | solution.py:375
  149.3 17.9 %collective-permute-start.25 = (f32[2,64,768]{2,1,0:T(8,128)S(1)}, f32[2,64,768]{2,1,0:T(8,128)S(1)}, u32[]{:S(2)}, u32[]{:S(2)}) collective-permute-start(f32[2,64,768]{2,1,0:T(8,128)S(1)} %get-tuple-element.56), channel_id=1, source_target_pairs={{0,1},{1,0},{2,3},{3,2},{4,5},{5,4},{6,7},{7,6},{8,9},{9,8},{10,11... | collective-permute-start | bytes 1179656 | tf_op jit(solution)/shard_map/ppermute | solution.py:375
  155.4 11.9 %collective-permute-start.26 = (f32[2,64,768]{2,1,0:T(8,128)S(1)}, f32[2,64,768]{2,1,0:T(8,128)S(1)}, u32[]{:S(2)}, u32[]{:S(2)}) collective-permute-start(f32[2,64,768]{2,1,0:T(8,128)S(1)} %get-tuple-element.57), channel_id=1, source_target_pairs={{0,1},{1,0},{2,3},{3,2},{4,5},{5,4},{6,7},{7,6},{8,9},{9,8},{10,11... | collective-permute-start | bytes 1179656 | tf_op jit(solution)/shard_map/ppermute | solution.py:375
  155.9 1.4 collective-permute-start.28
  157.4 4.6 %collective-permute-start.23 = (f32[4,1,768]{2,1,0:T(1,128)S(1)}, f32[4,1,768]{2,1,0:T(1,128)S(1)}, u32[]{:S(2)}, u32[]{:S(2)}) collective-permute-start(f32[4,1,768]{2,1,0:T(1,128)S(1)} %add.86), channel_id=1, source_target_pairs={{0,4},{1,5},{2,6},{3,7},{4,0},{5,1},{6,2},{7,3},{8,12},{9,13},{10,... | collective-permute-start | bytes 36872 | tf_op jit(solution)/shard_map/ppermute | solution.py:375
  162.0 8.4 %collective-permute-start.29 = (f32[136,256]{1,0:T(8,128)S(1)}, f32[136,256]{1,0:T(8,128)S(1)}, u32[]{:S(2)}, u32[]{:S(2)}) collective-permute-start(f32[136,256]{1,0:T(8,128)S(1)} %add.89), channel_id=1, source_target_pairs={{0,16},{8,24},{16,0},{24,8},{1,17},{9,25},{17,1},{25,9},{2,18},{10... | collective-permute-start | bytes 417800 | tf_op jit(solution)/shard_map/ppermute | solution.py:375
  163.5 3.8 %collective-permute-start.24 = (f32[4,1,768]{2,1,0:T(1,128)S(1)}, f32[4,1,768]{2,1,0:T(1,128)S(1)}, u32[]{:S(2)}, u32[]{:S(2)}) collective-permute-start(f32[4,1,768]{2,1,0:T(1,128)S(1)} %add.87.in_own), channel_id=1, source_target_pairs={{0,1},{1,0},{2,3},{3,2},{4,5},{5,4},{6,7},{7,6},{8,9},{9,8},{10,11... | collective-permute-start | bytes 36872 | tf_op jit(solution)/shard_map/ppermute | solution.py:375
  171.3 3.7 %collective-permute-start.30 = (f32[8,256]{1,0:T(8,128)S(1)}, f32[8,256]{1,0:T(8,128)S(1)}, u32[]{:S(2)}, u32[]{:S(2)}) collective-permute-start(f32[8,256]{1,0:T(8,128)S(1)} %slice.69), channel_id=1, source_target_pairs={{0,2},{1,3},{2,0},{3,1},{4,6},{5,7},{6,4},{7,5},{8,10},{9,11},{10,... | collective-permute-start | bytes 24584 | tf_op jit(solution)/shard_map/ppermute | solution.py:375
  175.0 4.5 %collective-permute-start.31 = (f32[8,256]{1,0:T(8,128)S(1)}, f32[8,256]{1,0:T(8,128)S(1)}, u32[]{:S(2)}, u32[]{:S(2)}) collective-permute-start(f32[8,256]{1,0:T(8,128)S(1)} %slice_add_fusion), channel_id=1, source_target_pairs={{0,4},{1,5},{2,6},{3,7},{4,0},{5,1},{6,2},{7,3},{8,12},{9,13},{10,... | collective-permute-start | bytes 24584 | tf_op jit(solution)/shard_map/ppermute | solution.py:375
  (27 other events, 363.6 us)

commit v2 on v1

v2 whole, which is shorter than its diff:
```python
import functools
import math

import jax
import jax.numpy as jnp
import numpy as np
from jax import lax
from jax.experimental import pallas as pl
from jax.experimental.pallas import tpu as pltpu
from jax.sharding import PartitionSpec as P

ORDER = 256
LEN = 720
LANES = 768
BLOCK = 256
epsilon = 1e-06
f32 = jnp.float32
bf16 = jnp.bfloat16


def legendre_rows():
    coords = 1.0 - (2.0 * np.arange(LEN) + 1.0) / LEN
    rows = [np.ones(LEN), coords]
    for k in range(1, ORDER - 1):
        rows.append(((2.0 * k + 1.0) * coords * rows[k] - k * rows[k - 1]) / (k + 1.0))
    table = np.stack(rows) * np.sqrt((2.0 * np.arange(ORDER) + 1.0) / LEN)[:, None]
    out = np.zeros((ORDER, LANES))
    out[:, :LEN] = table[:, ::-1]
    return out


def phase_rows(mode_count):
    modes = np.arange(mode_count)[:, None]
    steps = np.arange(LANES)[None, :]
    now = 2.0 * np.pi * ((modes * steps) % LEN) / LEN
    nxt = 2.0 * np.pi * ((modes * (steps + 1)) % LEN) / LEN
    root = 1.0 / math.sqrt(LEN)
    rows = np.stack([np.cos(now), np.sin(now), np.cos(nxt) * root, np.sin(nxt) * root])
    return rows.astype(np.float32)


def halves(table):
    high = table.astype(np.float32).astype(jnp.bfloat16)
    low = (table - high.astype(np.float64)).astype(np.float32).astype(jnp.bfloat16)
    return high, low


def split(x):
    high = x.astype(bf16)
    return high, (x - high.astype(f32)).astype(bf16)


def nn(a, b):
    return lax.dot_general(a, b, (((1,), (0,)), ((), ())), preferred_element_type=f32)


def nt(a, b):
    return lax.dot_general(a, b, (((1,), (1,)), ((), ())), preferred_element_type=f32)


def three(dot, a, b):
    return dot(a[0], b[0]) + dot(a[0], b[1]) + dot(a[1], b[0])


def deep(x):
    high, low = split(x)
    return jnp.concatenate([high, low, high], axis=0)


def stacked(weights, pair, rows):
    first = nn(weights, pair[0])
    return first[:rows] + first[rows:] + nn(weights[:rows], pair[1])


def stacked_nt(left, pair, rows):
    first = nt(left, pair[0])
    return first[:rows] + first[rows:] + nt(left[:rows], pair[1])


def rotate(real, imag, cos, sin):
    modes = cos.shape[0]
    shape = (real.shape[0] // modes, modes, real.shape[1])
    real, imag = real.reshape(shape), imag.reshape(shape)
    cos, sin = cos[None], sin[None]
    flat = (shape[0] * modes, shape[2])
    return (real * cos + imag * sin).reshape(flat), (imag * cos - real * sin).reshape(flat)


def triangle():
    row = lax.broadcasted_iota(jnp.int32, (BLOCK, BLOCK), 0)
    col = lax.broadcasted_iota(jnp.int32, (BLOCK, BLOCK), 1)
    return jnp.where(row <= col, 1.0, 0.0).astype(bf16)


def running_sum(x, tri):
    high, low = split(x)
    blocks, carry = [], None
    for b in range(LANES // BLOCK):
        at = slice(b * BLOCK, (b + 1) * BLOCK)
        block = nn(high[:, at], tri) + nn(low[:, at], tri)
        if carry is not None:
            block = block + carry
        carry = block[:, BLOCK - 1 : BLOCK]
        blocks.append(block)
    return jnp.concatenate(blocks, axis=1)


def running_sum_back(x, tri):
    high, low = split(x)
    blocks, carry = [], None
    for b in reversed(range(LANES // BLOCK)):
        at = slice(b * BLOCK, (b + 1) * BLOCK)
        block = nt(high[:, at], tri) + nt(low[:, at], tri)
        if carry is not None:
            block = block + carry
        carry = block[:, 0:1]
        blocks.append(block)
    return jnp.concatenate(blocks[::-1], axis=1)


def side_of():
    return lax.rem(lax.axis_index("order"), 2)


def at_line_end(line_length):
    line = lax.div(lax.axis_index("order"), 2)
    return jnp.logical_or(line == 0, line == line_length - 1)


def locate(units, j):
    u = max(k for k in range(len(units)) if units[k][0] <= j)
    return u, j - units[u][0]


def chunk_ends(windows):
    return [-(-LEN * min(w + 2, windows) // 128) * 128 for w in range(0, windows, 2)]


def deal_windows(split_at, len_hbm, hbm_ref, len_ref, buffer, sems, out_refs, use):
    lengths_copy = pltpu.make_async_copy(len_hbm, len_ref, sems.at[0])
    lengths_copy.start()
    own_ref, send_refs = out_refs[0], out_refs[1:]
    channels = hbm_ref.shape[0]
    windows = hbm_ref.shape[1] // LEN
    half = windows // 2
    ends = chunk_ends(windows)
    copies = []
    for c, end in enumerate(ends):
        at = slice(ends[c - 1] if c else 0, end)
        copies.append(pltpu.make_async_copy(hbm_ref.at[:, at], buffer.at[:, at], sems.at[1 + c]))
        copies[-1].start()
    lane = lax.broadcasted_iota(jnp.int32, (channels, LEN), 1)
    side = side_of()
    for ref in out_refs:
        ref[:, :, LANES - 128 :] = jnp.zeros((ref.shape[0], channels, 128), f32)
    lengths_copy.wait()
    for w in range(windows):
        if w % 2 == 0:
            copies[w // 2].wait()
        value = buffer[:, w * LEN : (w + 1) * LEN]
        value = jnp.where(lane < len_ref[w], value, 0.0)
        use(w, value)
        unit, at = locate(split_at, w % half)
        send_ref = send_refs[unit]
        mine = side == (0 if w < half else 1)

        @pl.when(mine)
        def _():
            own_ref[w % half, :, :LEN] = value

        @pl.when(jnp.logical_not(mine))
        def _():
            send_ref[at, :, :LEN] = value


PACK = 48
STATS = 8


def readout_columns(modes, channels):
    mode = lax.broadcasted_iota(jnp.int32, (modes, channels), 0)
    angle = mode.astype(f32) * (2.0 * math.pi / LEN)
    factor = jnp.where(mode == 0, 1.0, 2.0) * (1.0 / math.sqrt(LEN))
    return factor * jnp.cos(angle), factor * jnp.sin(angle)


def front_kernel(units, len_hbm, in_hbm, out_hbm, gain_hbm, x_hbm, message_ref, *refs):
    out_refs, (len_ref, in_ref, out_ref, gain_ref, buffer, packed, sems, weight_sems) = refs[:-8], refs[-8:]
    windows = x_hbm.shape[1] // LEN
    weights = [(in_hbm, in_ref), (out_hbm, out_ref), (gain_hbm, gain_ref)]
    weights = [pltpu.make_async_copy(a, b, weight_sems.at[k]) for k, (a, b) in enumerate(weights)]
    for copy in weights:
        copy.start()
    message_ref[...] = jnp.zeros(message_ref.shape, f32)

    def use(w, value):
        message_ref[w : w + 1, :LEN] = jnp.sum(value * value, axis=0, keepdims=True)

    deal_windows(units, len_hbm, x_hbm, len_ref, buffer, sems, out_refs, use)
    for copy in weights:
        copy.wait()
    modes, ranks, channels = in_ref.shape[1:]
    packed[...] = jnp.zeros(packed.shape, f32)
    read_real, read_imag = readout_columns(modes, channels)
    for r in range(ranks):
        real, imag = out_ref[0, :, r, :], out_ref[1, :, r, :]
        second = (read_real * real + read_imag * imag, read_imag * real - read_real * imag)
        for part in range(2):
            at = slice((part * ranks + r) * modes, (part * ranks + r + 1) * modes)
            packed[at, :channels] = in_ref[part, :, r, :] * gain_ref[...]
            packed[at, channels : 2 * channels] = second[part]
    rows = packed.shape[0]
    for k in range(-(-rows // PACK)):
        count = min(PACK, rows - k * PACK)
        message_ref[windows : windows + count, k * 128 : (k + 1) * 128] = packed[k * PACK : k * PACK + count]


def unpack(message_ref, windows, rows):
    pieces = []
    for k in range(-(-rows // PACK)):
        count = min(PACK, rows - k * PACK)
        pieces.append(message_ref[windows : windows + count, k * 128 : (k + 1) * 128])
    return jnp.concatenate(pieces, axis=0)


def cot_kernel(units, len_hbm, x_hbm, *refs):
    deal_windows(units, len_hbm, x_hbm, *refs[-3:], refs[:-3], lambda w, value: None)


def weights_kernel(windows, own_ref, rec_ref, down_own, down_rec, up_own, up_rec, down_both, up_both):
    rows, channels = down_own.shape[0], down_own.shape[1] // 3
    pieces = []
    for ref, down, up in ((own_ref, down_own, up_own), (rec_ref, down_rec, up_rec)):
        packed = unpack(ref, windows, rows)
        high, low = split(packed)
        down[...] = jnp.concatenate([high[:, :channels], high[:, :channels], low[:, :channels]], axis=1)
        upper = slice(channels, 2 * channels)
        up[...] = jnp.concatenate([high[:, upper], high[:, upper], low[:, upper]], axis=1)
        pieces.append(packed.T)
    for k, ref in ((0, down_both), (1, up_both)):
        at = slice(k * channels, (k + 1) * channels)
        both = jnp.concatenate([pieces[0][at], pieces[1][at]], axis=0)
        high, low = split(both)
        ref[...] = jnp.concatenate([high, low], axis=0)


def read_kernel(own_ref, rec_ref, up_own, up_rec, leg_high, leg_low, out_ref):
    field = nn(up_own[...], deep(own_ref[0])) + nn(up_rec[...], deep(rec_ref[0]))
    out_ref[0] = three(nt, split(field), (leg_high[...], leg_low[...]))


def inverse_rms(ss_ref, row, full_width):
    return lax.rsqrt(ss_ref[pl.ds(row, 1), :] * (1.0 / full_width) + epsilon)


def rank_kernel(first, full_width, own_ref, rec_ref, ss_ref, down_own, down_rec, leg_high, leg_low, phase_ref, out_ref):
    half = side_of() * (ss_ref.shape[0] // 2)
    inv = inverse_rms(ss_ref, half + first + pl.program_id(0), full_width)
    mixed = nn(down_own[...], deep(own_ref[0] * inv)) + nn(down_rec[...], deep(rec_ref[0] * inv))
    part = mixed.shape[0] // 2
    real, imag = rotate(mixed[:part], mixed[part:], phase_ref[0], phase_ref[1])
    total = running_sum(jnp.concatenate([real, imag], axis=0), triangle())
    real, imag = rotate(total[:part], total[part:], phase_ref[2], -phase_ref[3])
    memory = jnp.concatenate([real, imag], axis=0)
    out_ref[0] = three(nt, split(memory), (leg_high[...], leg_low[...]))


def opening(refs, outs):
    return None if len(refs) == outs else refs[0], refs[-outs:]


def back_kernel(first, full_width, line_length, len_ref, mid_ref, end_ref, own_ref, rec_ref, ss_ref, down_both, leg_high, leg_low, phase_ref, *refs):
    prev_ref, (own_out, rec_out, grad_out, inner_out) = opening(refs, 4)
    step = pl.program_id(0)
    half = side_of() * (ss_ref.shape[0] // 2)
    row = half + first + step
    inv = inverse_rms(ss_ref, row, full_width)
    channels = own_ref.shape[1]
    total = jnp.where(at_line_end(line_length), end_ref[0], mid_ref[0])
    memory = three(nn, split(total), (leg_high[...], leg_low[...]))
    part = memory.shape[0] // 2
    real, imag = rotate(memory[:part], memory[part:], phase_ref[2], phase_ref[3])
    back = running_sum_back(jnp.concatenate([real, imag], axis=0), triangle())
    real, imag = rotate(back[:part], back[part:], phase_ref[0], -phase_ref[1])
    pair = split(jnp.concatenate([real, imag], axis=0))
    scaled = stacked(down_both[...], pair, 2 * channels)
    lane = lax.broadcasted_iota(jnp.int32, scaled.shape, 1)
    scaled = jnp.where(lane < len_ref[row], scaled, 0.0)
    own_out[0] = scaled[:channels]
    rec_out[0] = scaled[channels:]
    both = jnp.concatenate([own_ref[0], rec_ref[0]], axis=0)
    inner = jnp.sum(scaled * both, axis=0, keepdims=True)
    pieces = [inner[:, p * 256 : (p + 1) * 256] for p in range(LANES // 256)]
    inner_out[0] = jnp.concatenate(pieces + [jnp.zeros((STATS - len(pieces), 256), f32)], axis=0)
    high, low = split(both * inv)
    grads = stacked_nt(jnp.concatenate([high, low], axis=0), pair, 2 * channels)

    @pl.when(step == 0)
    def _():
        grad_out[...] = grads if prev_ref is None else prev_ref[...] + grads

    @pl.when(step > 0)
    def _():
        grad_out[...] += grads


def branch_kernel(first, line_length, len_ref, mid_ref, end_ref, ser_own, ser_rec, cot_own, cot_rec, up_both, leg_high, leg_low, *refs):
    prev_ref, (own_out, rec_out, grad_out) = opening(refs, 3)
    step = pl.program_id(0)
    channels = ser_own.shape[1]
    rows = 2 * channels
    row = side_of() * (len_ref.shape[0] // 2) + first + step
    total = jnp.where(at_line_end(line_length), end_ref[0], mid_ref[0])
    field = three(nn, split(total), (leg_high[...], leg_low[...]))
    pair = split(field)
    branch = stacked(up_both[...], pair, rows)
    lane = lax.broadcasted_iota(jnp.int32, branch.shape, 1)
    branch = jnp.where(lane < len_ref[row], branch, 0.0)
    own_out[0] = branch[:channels]
    rec_out[0] = branch[channels:]
    high, low = split(jnp.concatenate([cot_own[0], cot_rec[0]], axis=0))
    grads = stacked_nt(jnp.concatenate([high, low], axis=0), pair, rows)
    series = jnp.concatenate([ser_own[0], ser_rec[0]], axis=0)
    stats = []
    for v in (series, branch, series + branch):
        v = jnp.sum(jnp.sum(v * v, axis=0, keepdims=True), axis=1, keepdims=True)
        stats.append(jnp.broadcast_to(v, (1, grads.shape[1])))
    steps = functools.reduce(lambda a, b: a + b, [len_ref[w] for w in range(len_ref.shape[0])])
    steps = jnp.where(jnp.logical_and(first == 0, step == 0), steps, 0).astype(f32)
    stats.append(jnp.full((1, grads.shape[1]), steps, f32))
    stats = jnp.concatenate(stats + [jnp.zeros((4, grads.shape[1]), f32)], axis=0)
    grads = jnp.concatenate([grads, stats], axis=0)

    @pl.when(step == 0)
    def _():
        grad_out[...] = grads if prev_ref is None else prev_ref[...] + grads

    @pl.when(step > 0)
    def _():
        grad_out[...] += grads


def layer_kernel(units, x_ref, *refs):
    own_refs, rec_refs, out_ref = refs[: len(units)], refs[len(units) : 2 * len(units)], refs[-1]
    windows = x_ref.shape[1] // LEN
    half = windows // 2
    first_side = side_of() == 0
    for w in range(windows):
        u, j = locate(units, w % half)
        value = jnp.where(first_side == (w < half), own_refs[u][j], rec_refs[u][j])
        at = slice(w * LEN, (w + 1) * LEN)
        out_ref[:, at] = x_ref[:, at] + value[:, :LEN]


def inner_row(small_ref, j):
    row = STATS * (1 + j)
    return jnp.concatenate([small_ref[row + p : row + p + 1, :] for p in range(LANES // 256)], axis=1)


def series_grad_kernel(units, full_width, cot_ref, x_ref, ss_ref, in_own, in_rec, *refs):
    own_refs, rec_refs, out_ref = refs[: len(units)], refs[len(units) : 2 * len(units)], refs[-1]
    windows = x_ref.shape[1] // LEN
    half = windows // 2
    first_side = side_of() == 0
    for w in range(windows):
        u, j = locate(units, w % half)
        keep = first_side == (w < half)
        scaled = jnp.where(keep, own_refs[u][j], rec_refs[u][j])[:, :LEN]
        inner = jnp.where(keep, inner_row(in_own, w % half), inner_row(in_rec, w % half))[:, :LEN]
        inv = inverse_rms(ss_ref, w, full_width)[:, :LEN]
        at = slice(w * LEN, (w + 1) * LEN)
        shift = inv * inv * inner * (1.0 / full_width)
        out_ref[:, at] = cot_ref[:, at] + inv * (scaled - x_ref[:, at] * shift)


def close_kernel(share, own_ref, rec_ref, in_ref, gain_ref, grad_in_ref, grad_out_ref, grad_gain_ref, rms_ref):
    modes, ranks, channels = in_ref.shape[1:]
    sums = own_ref[...] + rec_ref[...]
    into, mix, stats = sums[:channels].T, sums[channels : 2 * channels].T, sums[2 * channels : 2 * channels + STATS]
    total = jnp.zeros((modes, channels), f32)
    read_real, read_imag = readout_columns(modes, channels)
    for r in range(ranks):
        pieces = []
        for part in range(2):
            at = slice((part * ranks + r) * modes, (part * ranks + r + 1) * modes)
            grad = into[at]
            total = total + grad * in_ref[part, :, r, :]
            grad_in_ref[part, :, r, :] = grad * gain_ref[...]
            pieces.append(mix[at])
        grad_out_ref[0, :, r, :] = read_real * pieces[0] + read_imag * pieces[1]
        grad_out_ref[1, :, r, :] = read_imag * pieces[0] - read_real * pieces[1]
    grad_gain_ref[...] = jnp.sum(total, axis=0, keepdims=True)
    rms = jnp.sqrt(stats * share / stats[3:4])
    for k in range(3):
        rms_ref[k] = rms[k, 0]


def whole(shape):
    return pl.BlockSpec(shape, lambda *_: (0,) * len(shape))


SMEM = pl.BlockSpec(memory_space=pltpu.SMEM)
PARAMS = pltpu.CompilerParams(vmem_limit_bytes=8 * 1024 * 1024)


def window_spec(shape, offset):
    return pl.BlockSpec((1,) + shape[1:], lambda i: (i + offset,) + (0,) * (len(shape) - 1))


def cost(flops, byte_count, weight=1):
    return pl.CostEstimate(flops=int(flops * weight), bytes_accessed=int(byte_count * weight), transcendentals=0)


def struct(shape, dtype=f32):
    return jax.ShapeDtypeStruct(shape, dtype)


def one_call(kernel, outs, args, smem=0, scalars_out=0):
    single = not isinstance(outs, list)
    shapes = [outs] if single else outs
    specs = [SMEM] * smem + [whole(a.shape) for a in args[smem:]]
    moved = sum(a.size * a.dtype.itemsize for a in args) + sum(math.prod(o.shape) * 4 for o in shapes)
    result = pl.pallas_call(
        kernel,
        out_shape=shapes,
        in_specs=specs,
        out_specs=[whole(o.shape) for o in shapes[: len(shapes) - scalars_out]] + [SMEM] * scalars_out,
        grid=(1,),
        compiler_params=PARAMS,
        cost_estimate=cost(moved, moved),
    )(*args)
    return result[0] if single else result


HBM = pl.BlockSpec(memory_space=pltpu.MemorySpace.HBM)


def in_hbm(arrays):
    return [pltpu.with_memory_space_constraint(a, pltpu.MemorySpace.HBM) for a in arrays]


def deal_scratch(array, lengths):
    windows = array.shape[1] // LEN
    return [pltpu.SMEM(lengths.shape, jnp.int32)], [
        pltpu.VMEM(array.shape, f32),
        pltpu.SemaphoreType.DMA((1 + len(chunk_ends(windows)),)),
    ]


def front(series, lengths, weights, units, rows):
    channels, windows = series.shape[0], series.shape[1] // LEN
    shapes = [struct((windows + PACK, LANES)), struct((windows // 2, channels, LANES))]
    shapes += [struct((n, channels, LANES)) for _, n in units]
    first, (buffer, sems) = deal_scratch(series, lengths)
    scratch = first + [pltpu.VMEM(a.shape, f32) for a in weights] + [buffer, pltpu.VMEM((rows, 128), f32), sems]
    return pl.pallas_call(
        functools.partial(front_kernel, units),
        out_shape=shapes,
        in_specs=[HBM] * (2 + len(weights)),
        out_specs=[whole(o.shape) for o in shapes],
        grid=(1,),
        scratch_shapes=scratch + [pltpu.SemaphoreType.DMA((len(weights),))],
        compiler_params=PARAMS,
        cost_estimate=cost(series.size * 4, series.size * 8),
    )(*in_hbm([lengths, *weights, series]))


def deal(array, lengths, units):
    channels, windows = array.shape[0], array.shape[1] // LEN
    shapes = [struct((windows // 2, channels, LANES))] + [struct((n, channels, LANES)) for _, n in units]
    first, rest = deal_scratch(array, lengths)
    return pl.pallas_call(
        functools.partial(cot_kernel, units),
        out_shape=shapes,
        in_specs=[HBM] * 2,
        out_specs=[whole(o.shape) for o in shapes],
        grid=(1,),
        scratch_shapes=first + rest,
        compiler_params=PARAMS,
        cost_estimate=cost(array.size * 4, array.size * 8),
    )(*in_hbm([lengths, array]))


def prepare_weights(own, rec, windows, rows, channels):
    shapes = [struct((rows, 3 * channels), bf16)] * 4 + [struct((4 * channels, rows), bf16)] * 2
    return one_call(functools.partial(weights_kernel, windows), shapes, [own, rec])


MATMUL = 2 * 256 * 256 * 256


def unit_call(kernel, unit, smem, arrays, consts, outs, units_of_work, carried=(), weight=1):
    count = unit[1]
    specs = [SMEM] * len(smem)
    specs += [window_spec(a.shape, offset) for a, offset in arrays]
    specs += [whole(c.shape) for c in consts]
    aliases = {len(specs) + k: out for k, (out, _) in enumerate(carried)}
    specs += [pl.BlockSpec(memory_space=pl.ANY)] * len(carried)
    out_specs, shapes = [], []
    for shape, offset in outs:
        shapes.append(struct(shape))
        out_specs.append(whole(shape) if offset is None else window_spec(shape, offset))
    moved = sum(a.size * 4 * count // a.shape[0] for a, _ in arrays) + sum(c.size * c.dtype.itemsize for c in consts)
    return pl.pallas_call(
        kernel,
        out_shape=shapes,
        in_specs=specs,
        out_specs=out_specs,
        grid=(count,),
        input_output_aliases=aliases,
        compiler_params=PARAMS,
        cost_estimate=cost(units_of_work * MATMUL * count, moved, weight),
    )(*smem, *[a for a, _ in arrays], *consts, *[a for _, a in carried])


def swap(x, axis, bit):
    size = lax.axis_size(axis)
    return lax.ppermute(x, axis, [(i, i ^ bit) for i in range(size)])


def add_over(x, axis, bits):
    for bit in bits:
        x = x + swap(x, axis, bit)
    return x


def bits_of(size, start=1):
    bits, bit = [], start
    while bit < size:
        bits.append(bit)
        bit *= 2
    return bits


def hop(x, pairs):
    return lax.ppermute(x, "order", [(2 * a + side, 2 * b + side) for a, b in pairs for side in (0, 1)])


def inward(x):
    size = lax.axis_size("order")
    if size == 8:
        return hop(x, [(0, 1), (3, 2)])
    return lax.psum(x, "order", axis_index_groups=[list(range(side, size, 2)) for side in (0, 1)])


def middle(x):
    return hop(x, [(1, 2), (2, 1)]) if lax.axis_size("order") == 8 else x


def outward(x):
    return hop(x, [(1, 0), (2, 3)]) if lax.axis_size("order") == 8 else x


def join(kept, came):
    return kept + came if lax.axis_size("order") == 8 else came


def after(x, tokens):
    tokens = tokens if isinstance(tokens, tuple) else (tokens,)
    return lax.optimization_barrier((x, *tokens))[0]


WEIGHT = ((3,10),(10,10),(10,10),(10,10))
COT = (2, 2)
SER = (4,)
READ = (2, 2)
RANK = (2, 2)
PLAN = (
    "q", "R0", "Q", "R1", "hm0", "K0", "hm1", "K1", "ho0", "zm0", "ho1", "B0", "zm1", "zo0", "s0",
    "B1", "zo1", "M0", "s1", "M1", "st1", "b0", "st2", "se", "G", "F1", "gc", "gy", "F2",
)


def units_of(half, counts):
    counts = counts if sum(counts) == half else (1,) * half
    return [(sum(counts[:u]), counts[u]) for u in range(len(counts))]


def local(series, norm_gain, mode_in, mode_out, lengths, grad_out):
    channels = series.shape[0]
    windows = series.shape[1] // LEN
    half = windows // 2
    order_devices = lax.axis_size("order")
    line_length = order_devices // 2
    mode_count, rank_count = mode_in.shape[1], mode_in.shape[2]
    full_width = channels * order_devices
    rows = 2 * rank_count * mode_count
    cot_units, ser_units = units_of(half, COT), units_of(half, SER)
    read_units, rank_units = units_of(half, READ), units_of(half, RANK)

    legendre = [jnp.asarray(h) for h in halves(legendre_rows())]
    phase = jnp.asarray(phase_rows(mode_count))
    gain = norm_gain.reshape(1, channels)

    message, ser_own, *ser_rec = front(series, lengths, [mode_in, mode_out, gain], ser_units, rows)
    with jax.named_scope("message_x"):
        message_rec = swap(message, "order", 1)
    cot_own, *cot_rec = deal(after(grad_out, message), lengths, cot_units)
    message_rec = after(message_rec, cot_own)
    with jax.named_scope("cot_x"):
        cot_rec = [swap(c if u == 0 else after(c, message_rec), "order", 1) for u, c in enumerate(cot_rec)]
    down_own, down_rec, up_own, up_rec, down_both, up_both = prepare_weights(message, message_rec, windows, rows, channels)
    with jax.named_scope("squares_z1"):
        squares = message[:windows] + message_rec[:windows]
        squares_rec = swap(squares, "order", 2)
    with jax.named_scope("ser_x"):
        ser_rec = [swap(after(c, message_rec), "order", 1) for c in ser_rec]

    def windows_of(own, received, units, first, count):
        u, offset = locate(units, first)
        v, _ = locate(units, first + count - 1)
        if u < v:
            return [(own, first), (jnp.concatenate(received[u : v + 1], axis=0), offset)]
        return [(own, first), (received[u], offset)]

    chains = {}
    backs, branches, kept = {}, {}, {}
    state = {"squares": squares, "squares_rec": squares_rec, "token": up_own}

    def sums_of(name, token):
        return [(chains[name], 0), (after(chains[name + "out"], token), 0)]

    def do_read(u, token):
        first, count = read_units[u]
        own, rec = windows_of(cot_own, cot_rec, cot_units, first, count)
        (out,) = unit_call(
            read_kernel, read_units[u], [], [own, (after(rec[0], token), rec[1])],
            [up_own, up_rec, *legendre], [((count, rows, ORDER), 0)], 15, weight=WEIGHT[0][u],
        )
        start("h", u, out, inward)
        return out

    def do_rank(u, token):
        first, count = rank_units[u]
        own, rec = windows_of(ser_own, ser_rec, ser_units, first, count)
        (out,) = unit_call(
            functools.partial(rank_kernel, first, full_width), rank_units[u], [], [own, (after(rec[0], token), rec[1])],
            [state["squares"], down_own, down_rec, *legendre, phase], [((count, rows, ORDER), 0)], 21, weight=WEIGHT[1][u],
        )
        start("z", u, out, inward)
        return out

    def start(kind, u, value, move):
        name = f"{kind}{u}"
        chains[name] = value
        with jax.named_scope(f"{name}_{move.__name__}"):
            chains[name + ("out" if move is outward else "")] = (value, move(value)) if move is not outward else move(value)

    def do_join(kind, u, move, token):
        value, came = chains[f"{kind}{u}"]
        value = join(value, after(came, token))
        start(kind, u, value, move)
        if move is outward:
            chains[f"{kind}{u}"] = value
        return value

    def do_back(u, token):
        first, count = read_units[u]
        previous = [state["grad_in"]] if "grad_in" in state else []
        mine, theirs, state["grad_in"], dots = unit_call(
            functools.partial(back_kernel, first, full_width, line_length), read_units[u], [lengths],
            [*sums_of(f"h{u}", token), *windows_of(ser_own, ser_rec, ser_units, first, count)],
            [state["squares"], down_both, *legendre, phase, *previous],
            [((count, channels, LANES), 0)] * 2 + [((2 * channels, rows), None), ((count, STATS, 256), 0)], 24, weight=WEIGHT[2][u],
        )
        with jax.named_scope("scaled_x"):
            backs[u] = (mine, swap(theirs, "order", 1), dots)
        return state["grad_in"]

    def do_mix(u, token):
        first, count = rank_units[u]
        previous = [state["grad_mix"]] if "grad_mix" in state else []
        mine, theirs, state["grad_mix"] = unit_call(
            functools.partial(branch_kernel, first, line_length), rank_units[u], [lengths],
            [*sums_of(f"z{u}", token), *windows_of(ser_own, ser_rec, ser_units, first, count), *windows_of(cot_own, cot_rec, cot_units, first, count)],
            [up_both, *legendre, *previous],
            [((count, channels, LANES), 0)] * 2 + [((2 * channels + 8, rows), None)], 18, weight=WEIGHT[3][u],
        )
        branches[u] = mine
        with jax.named_scope("branch_x"):
            kept[u] = swap(theirs, "order", 1)
        return state["grad_mix"]

    def do_grads(token):
        grad_in, grad_mix, small = state["grad_in"], state["grad_mix"], state["small"]
        state["own"] = jnp.concatenate([grad_in[:channels], grad_mix[:channels], small], axis=0)
        rec = jnp.concatenate([grad_in[channels:], grad_mix[channels : 2 * channels], small], axis=0)
        with jax.named_scope("grads_x"):
            state["rec"] = swap(after(rec, token), "order", 1)
        return rec

    def do_series(token):
        count = len(read_units)
        return one_call(
            functools.partial(series_grad_kernel, read_units, full_width), struct(series.shape),
            [grad_out, series, state["squares"], state["small"], after(state["small_rec"], token)]
            + [backs[u][0] for u in range(count)] + [backs[u][1] for u in range(count)],
        )

    def do_layer(token):
        count = len(rank_units)
        return one_call(
            functools.partial(layer_kernel, rank_units), struct(series.shape),
            [after(series, token)] + [branches[u] for u in range(count)] + [kept[u] for u in range(count)],
        )

    for step in PLAN:
        name, token = step.rstrip("0123456789"), state["token"]
        u = int(step[len(name) :] or 0)
        if name == "q":
            with jax.named_scope("squares_z2"):
                out = state["squares"] + after(state["squares_rec"], token)
                state["squares"] = add_over(out, "order", bits_of(order_devices, 4))
        elif name == "s":
            out = after(backs[u][1], token)
            backs[u] = (backs[u][0], out, backs[u][2])
        elif name == "b":
            out = kept[u] = after(kept[u], token)
        elif name == "Q":
            out = state["squares"] = after(state["squares"], token)
        elif name == "R":
            out = do_read(u, token)
        elif name == "K":
            out = do_rank(u, token)
        elif name in ("hm", "zm"):
            out = do_join(name[0], u, middle, token)
        elif name in ("ho", "zo"):
            out = do_join(name[0], u, outward, token)
        elif name == "B":
            out = do_back(u, token)
        elif name == "M":
            out = do_mix(u, token)
        elif name == "st":
            with jax.named_scope("stats_z"):
                if u == 1:
                    out = jnp.concatenate([state["grad_mix"][2 * channels :]] + [backs[k][2].reshape(-1, 256) for k in range(len(read_units))], axis=0)
                else:
                    out = state["small"] + after(state["small_rec"], token)
                state["small"], state["small_rec"] = out, swap(out, "order", 1 << u)
        elif name == "se":
            with jax.named_scope("stats_z"):
                out = state["small"] + after(state["small_rec"], token)
                state["small"] = out = add_over(out, "order", bits_of(order_devices, 8))
        elif name == "G":
            out = do_grads(token)
        elif name == "gc":
            with jax.named_scope("grads_core"):
                rec = after(state["rec"], token)
                state["small_rec"] = rec[2 * channels :]
                out = state["own"] + rec
                state["own"], state["rec"] = out, swap(out, "batch", 1)
        elif name == "gy":
            with jax.named_scope("grads_y"):
                out = state["own"] + after(state["rec"], token)
                out = add_over(out, "batch", bits_of(lax.axis_size("batch") // 2, 2))
                state["own"], state["rec"] = out, swap(out, "batch", lax.axis_size("batch") // 2)
        elif name == "F":
            out = state[step] = do_layer(token) if u == 1 else do_series(token)
        state["token"] = out
    grad_mode_in, grad_mode_out, grad_gain, stream_rms = one_call(
        functools.partial(close_kernel, order_devices / full_width),
        [struct(mode_in.shape), struct(mode_out.shape), struct((1, channels)), struct((3,))],
        [state["own"], after(state["rec"], state["token"]), mode_in, gain], scalars_out=1,
    )
    return state["F1"], state["F2"], grad_gain.reshape(channels), grad_mode_in, grad_mode_out, stream_rms


def solution(mesh):
    wide = P("order", "batch")
    weight = P(None, None, None, "order")
    in_specs = (wide, P("order"), weight, weight, P("batch"), wide)
    out_specs = (wide, wide, P("order"), weight, weight, P())
    return jax.shard_map(local, mesh=mesh, in_specs=in_specs, out_specs=out_specs, check_vma=False)
```

time: 182 us -> 130 us (0.71)
  waiting for transfers between devices: 92.6 us -> 51.7 us
  other arithmetic: 9.8 us -> 0.64 us
  local copies, waits for them, and re-layouts: 4.83 us -> 0.07 us
  starting transfers between devices: 39.6 us -> 43.7 us
    ppermute x12, waiting for transfers between devices: 49.3 us -> 21.8 us  [hop(): lax.ppermute(x, 'order', [(2 * a + side, 2 * b + side) for a, b in pairs...]
    ppermute x20 -> x15, waiting for transfers between devices: 43.4 us -> 29.9 us  [swap(): return lax.ppermute(x, axis, [(i, i ^ bit) for i in range(size)])]
    add x11 -> x14, other arithmetic: 6.9 us -> 0.62 us  [the longest x8 0.55 us: join(): return kept + came if lax.axis_size('order') == 8 else came]
    ppermute x12, starting transfers between devices: 18 us -> 23.6 us  [hop(): lax.ppermute(x, 'order', [(2 * a + side, 2 * b + side) for a, b in pairs...]
    unnamed x58 -> x16, local copies, waits for them, and re-layouts: 3.91 us -> 0.04 us
    ppermute x20 -> x15, starting transfers between devices: 21.6 us -> 20.1 us  [swap(): return lax.ppermute(x, axis, [(i, i ^ bit) for i in range(size)])]
    pallas_call x5 -> x6, Pallas kernels: 8.46 us -> 9.91 us  [the longest x4 5.36 us: one_call(): pl.pallas_call(kernel, out_shape=shapes, in_specs=specs, out_specs=[whole...]
  transfers between devices with their start and end apart: 32 -> 27, of which waited for: 17 -> 17; matrix products, arithmetic and copies ran while one was open for 6% -> 0% of each run, Pallas kernels for 17% -> 22%
where the time goes in v2:
time: 130 us; the launch traced here: 129 us
  waiting for transfers between devices  51.7 us (40%)
  starting transfers between devices  43.7 us (34%)
  Pallas kernels  32.2 us (25%)
    ppermute x15, waiting for transfers between devices, swap(): return lax.ppermute(x, axis, [(i, i ^ bit) for i in range(size)])  29.9 us
    ppermute x12, starting transfers between devices, hop(): lax.ppermute(x, 'order', [(2 * a + side, 2 * b + side) for a, b in pairs...  23.6 us
    pallas_call x8, Pallas kernels, unit_call(): pl.pallas_call(kernel, out_shape=shapes, in_specs=specs, out_specs=out_sp...  22.2 us
    ppermute x12, waiting for transfers between devices, hop(): lax.ppermute(x, 'order', [(2 * a + side, 2 * b + side) for a, b in pairs...  21.8 us
    ppermute x15, starting transfers between devices, swap(): return lax.ppermute(x, axis, [(i, i ^ bit) for i in range(size)])  20.1 us
    pallas_call x4, Pallas kernels, one_call(): pl.pallas_call(kernel, out_shape=shapes, in_specs=specs, out_specs=[whole...  5.36 us
  transfers between devices with their start and end apart: 27, of which 17 were waited for; matrix products, arithmetic and copies ran while one was open for 0% of the time, Pallas kernels for 22%

profile of v2, /device:TPU:0, one launch (start us, length us, event | category | flops | bytes accessed | tf_op | source)
XLA Modules:
  0.0 129.5 jit_solution(15833331751884399086)
XLA Ops:
  0.7 2.6 %shard_map.136 = (f32[56,768]{1,0:T(8,128)S(1)}, f32[4,64,768]{2,1,0:T(8,128)S(1)}, f32[4,64,768]{2,1,0:T(8,128)S(1)}) custom-call(s32[8]{0:T(128)} %len_ref.7, f32[2,32,4,64]{3,2,1,0:T(4,128)} %in_ref.1, f32[2,32,4,64]{3,2,1,0:T(4,128)} %out_hbm.1, f32[1,64]{1,0:T(1,128)} %bitcast.8, f32[64,5760]{1,0:T(8,128)} %x_ref.2), custom_call_target="tpu_custom_call" | custom-call | flops 1474560 | bytes 2949120 | tf_op jit(solution)/shard_map/pallas_call | solution.py:456
  3.2 3.0 %collective-permute-start = (f32[56,768]{1,0:T(8,128)S(1)}, f32[56,768]{1,0:T(8,128)S(1)}, u32[]{:S(2)}, u32[]{:S(2)}) collective-permute-start(f32[56,768]{1,0:T(8,128)S(1)} %get-tuple-element.69.own_ref), channel_id=1, source_target_pairs={{0,1},{1,0},{2,3},{3,2},{4,5},{5,4},{6,7},{7,6},{8,9},{9,8},{10,11... | collective-permute-start | bytes 516104 | tf_op jit(solution)/shard_map/message_x/ppermute | solution.py:518
  6.2 2.0 %shard_map.137 = (f32[4,64,768]{2,1,0:T(8,128)S(1)}, f32[2,64,768]{2,1,0:T(8,128)S(1)}, f32[2,64,768]{2,1,0:T(8,128)S(1)}) custom-call(s32[8]{0:T(128)} %len_ref.7, f32[64,5760]{1,0:T(8,128)} %cot_ref.1), custom_call_target="tpu_custom_call" | custom-call | flops 1474560 | bytes 2949120 | tf_op jit(solution)/shard_map/pallas_call | solution.py:472
  8.3 2.7 %collective-permute-done.rec_ref = f32[56,768]{1,0:T(8,128)S(1)} collective-permute-done((f32[56,768]{1,0:T(8,128)S(1)}, f32[56,768]{1,0:T(8,128)S(1)}, u32[]{:S(2)}, u32[]{:S(2)}) %collective-permute-start) | collective-permute-done | bytes 172064 | tf_op jit(solution)/shard_map/message_x/ppermute | solution.py:518
  11.0 2.5 %collective-permute-start.1 = (f32[2,64,768]{2,1,0:T(8,128)S(1)}, f32[2,64,768]{2,1,0:T(8,128)S(1)}, u32[]{:S(2)}, u32[]{:S(2)}) collective-permute-start(f32[2,64,768]{2,1,0:T(8,128)S(1)} %get-tuple-element.74), channel_id=1, source_target_pairs={{0,1},{1,0},{2,3},{3,2},{4,5},{5,4},{6,7},{7,6},{8,9},{9,8},{10,11... | collective-permute-start | bytes 1179656 | tf_op jit(solution)/shard_map/cot_x/ppermute | solution.py:518
  15.3 2.0 %collective-permute-done.2 = f32[8,768]{1,0:T(8,128)S(1)} collective-permute-done((f32[8,768]{1,0:T(8,128)S(1)}, f32[8,768]{1,0:T(8,128)S(1)}, u32[]{:S(2)}, u32[]{:S(2)}) %collective-permute-start.2) | collective-permute-done | bytes 24608 | tf_op jit(solution)/shard_map/squares_z1/ppermute | solution.py:518
  17.3 2.6 %collective-permute-start.3 = (f32[8,768]{1,0:T(8,128)S(1)}, f32[8,768]{1,0:T(8,128)S(1)}, u32[]{:S(2)}, u32[]{:S(2)}) collective-permute-start(f32[8,768]{1,0:T(8,128)S(1)} %add.46), channel_id=1, source_target_pairs={{0,4},{1,5},{2,6},{3,7},{4,0},{5,1},{6,2},{7,3},{8,12},{9,13},{10,... | collective-permute-start | bytes 73736 | tf_op jit(solution)/shard_map/squares_z2/ppermute | solution.py:518
  20.2 1.9 %collective-permute-done.3 = f32[8,768]{1,0:T(8,128)S(1)} collective-permute-done((f32[8,768]{1,0:T(8,128)S(1)}, f32[8,768]{1,0:T(8,128)S(1)}, u32[]{:S(2)}, u32[]{:S(2)}) %collective-permute-start.3) | collective-permute-done | bytes 24608 | tf_op jit(solution)/shard_map/squares_z2/ppermute | solution.py:518
  22.1 2.0 %shard_map.139 = f32[2,256,256]{2,1,0:T(8,128)S(1)} custom-call(f32[4,64,768]{2,1,0:T(8,128)S(1)} %get-tuple-element.71.own_ref.cot_own, f32[2,64,768]{2,1,0:T(8,128)S(1)} %collective-permute-done.4.rec_ref.cot_rec, bf16[256,192]{1,0:T(8,128)(2,1)S(1)} %get-tuple-element.75.up_own, bf16[256,192]{1,0:T(8,128)(2,1)S(1)} %get-tuple-element.79.up_rec, ...), custom_call_target="tpu_custom_call" | custom-call | flops 3019898880 | bytes 5308416 | tf_op jit(solution)/shard_map/pallas_call | solution.py:504
  24.1 3.5 %collective-permute-start.7 = (f32[2,256,256]{2,1,0:T(8,128)S(1)}, f32[2,256,256]{2,1,0:T(8,128)S(1)}, u32[]{:S(2)}, u32[]{:S(2)}) collective-permute-start(f32[2,256,256]{2,1,0:T(8,128)S(1)} %shard_map.139), channel_id=1, source_target_pairs={{0,2},{1,3},{6,4},{7,5},{8,10},{9,11},{14,12},{15,13},{16,18},{17,... | collective-permute-start | bytes 1572872 | tf_op jit(solution)/shard_map/h0_inward/ppermute | solution.py:536
  28.8 2.0 %shard_map.140 = f32[2,256,256]{2,1,0:T(8,128)S(1)} custom-call(f32[4,64,768]{2,1,0:T(8,128)S(1)} %get-tuple-element.71.own_ref.cot_own, f32[2,64,768]{2,1,0:T(8,128)S(1)} %collective-permute-done.1.rec_ref.cot_rec, bf16[256,192]{1,0:T(8,128)(2,1)S(1)} %get-tuple-element.75.up_own, bf16[256,192]{1,0:T(8,128)(2,1)S(1)} %get-tuple-element.79.up_rec, ...), custom_call_target="tpu_custom_call" | custom-call | flops 10066329600 | bytes 17694720 | tf_op jit(solution)/shard_map/pallas_call | solution.py:504
  30.8 3.6 %collective-permute-start.5 = (f32[2,256,256]{2,1,0:T(8,128)S(1)}, f32[2,256,256]{2,1,0:T(8,128)S(1)}, u32[]{:S(2)}, u32[]{:S(2)}) collective-permute-start(f32[2,256,256]{2,1,0:T(8,128)S(1)} %shard_map.140), channel_id=1, source_target_pairs={{0,2},{1,3},{6,4},{7,5},{8,10},{9,11},{14,12},{15,13},{16,18},{17,... | collective-permute-start | bytes 1572872 | tf_op jit(solution)/shard_map/h1_inward/ppermute | solution.py:536
  34.4 3.3 %collective-permute-done.7 = f32[2,256,256]{2,1,0:T(8,128)S(1)} collective-permute-done((f32[2,256,256]{2,1,0:T(8,128)S(1)}, f32[2,256,256]{2,1,0:T(8,128)S(1)}, u32[]{:S(2)}, u32[]{:S(2)}) %collective-permute-start.7) | collective-permute-done | bytes 524320 | tf_op jit(solution)/shard_map/h0_inward/ppermute | solution.py:536
  38.6 5.8 %collective-permute-done.6.rec_ref.ser_rec = f32[4,64,768]{2,1,0:T(8,128)S(1)} collective-permute-done((f32[4,64,768]{2,1,0:T(8,128)S(1)}, f32[4,64,768]{2,1,0:T(8,128)S(1)}, u32[]{:S(2)}, u32[]{:S(2)}) %collective-permute-start.6) | collective-permute-done | bytes 786464 | tf_op jit(solution)/shard_map/ser_x/ppermute | solution.py:518
  44.3 3.0 %shard_map.141 = f32[2,256,256]{2,1,0:T(8,128)S(1)} custom-call(f32[4,64,768]{2,1,0:T(8,128)S(1)} %get-tuple-element.82.own_ref.ser_own, f32[4,64,768]{2,1,0:T(8,128)S(1)} %collective-permute-done.6.rec_ref.ser_rec, f32[8,768]{1,0:T(8,128)S(1)} %add.47.ss_ref, bf16[256,192]{1,0:T(8,128)(2,1)S(1)} %get-tuple-element.87.down_own, ...), custom_call_target="tpu_custom_call" | custom-call | flops 14092861440 | bytes 21872640 | tf_op jit(solution)/shard_map/pallas_call | solution.py:504
  47.3 3.8 %collective-permute-start.9 = (f32[2,256,256]{2,1,0:T(8,128)S(1)}, f32[2,256,256]{2,1,0:T(8,128)S(1)}, u32[]{:S(2)}, u32[]{:S(2)}) collective-permute-start(f32[2,256,256]{2,1,0:T(8,128)S(1)} %shard_map.141), channel_id=1, source_target_pairs={{0,2},{1,3},{6,4},{7,5},{8,10},{9,11},{14,12},{15,13},{16,18},{17,... | collective-permute-start | bytes 1572872 | tf_op jit(solution)/shard_map/z0_inward/ppermute | solution.py:536
  51.9 3.0 %shard_map.142 = f32[2,256,256]{2,1,0:T(8,128)S(1)} custom-call(f32[4,64,768]{2,1,0:T(8,128)S(1)} %get-tuple-element.82.own_ref.ser_own, f32[4,64,768]{2,1,0:T(8,128)S(1)} %collective-permute-done.6.rec_ref.ser_rec, f32[8,768]{1,0:T(8,128)S(1)} %add.47.ss_ref, bf16[256,192]{1,0:T(8,128)(2,1)S(1)} %get-tuple-element.87.down_own, ...), custom_call_target="tpu_custom_call" | custom-call | flops 14092861440 | bytes 21872640 | tf_op jit(solution)/shard_map/pallas_call | solution.py:504
  56.3 4.6 %collective-permute-start.15 = (f32[2,256,256]{2,1,0:T(8,128)S(1)}, f32[2,256,256]{2,1,0:T(8,128)S(1)}, u32[]{:S(2)}, u32[]{:S(2)}) collective-permute-start(f32[2,256,256]{2,1,0:T(8,128)S(1)} %shard_map.142), channel_id=1, source_target_pairs={{0,2},{1,3},{6,4},{7,5},{8,10},{9,11},{14,12},{15,13},{16,18},{17,... | collective-permute-start | bytes 1572872 | tf_op jit(solution)/shard_map/z1_inward/ppermute | solution.py:536
  60.9 2.4 %collective-permute-done.9 = f32[2,256,256]{2,1,0:T(8,128)S(1)} collective-permute-done((f32[2,256,256]{2,1,0:T(8,128)S(1)}, f32[2,256,256]{2,1,0:T(8,128)S(1)}, u32[]{:S(2)}, u32[]{:S(2)}) %collective-permute-start.9) | collective-permute-done | bytes 524320 | tf_op jit(solution)/shard_map/z0_inward/ppermute | solution.py:536
  65.5 5.9 %collective-permute-done.12.end_ref = f32[2,256,256]{2,1,0:T(8,128)S(1)} collective-permute-done((f32[2,256,256]{2,1,0:T(8,128)S(1)}, f32[2,256,256]{2,1,0:T(8,128)S(1)}, u32[]{:S(2)}, u32[]{:S(2)}) %collective-permute-start.12) | collective-permute-done | bytes 524320 | tf_op jit(solution)/shard_map/h0_outward/ppermute | solution.py:536
  71.4 3.5 %shard_map.143 = (f32[2,64,768]{2,1,0:T(8,128)S(1)}, f32[2,64,768]{2,1,0:T(8,128)S(1)}, f32[128,256]{1,0:T(8,128)S(1)}, f32[2,8,256]{2,1,0:T(8,128)S(1)}) custom-call(s32[8]{0:T(128)S(1)} %copy-done.3, f32[2,256,256]{2,1,0:T(8,128)S(1)} %add.50.mid_ref, f32[2,256,256]{2,1,0:T(8,128)S(1)} %collective-permute-done.12.end_ref, ...), custom_call_target="tpu_custom_call" | custom-call | flops 16106127360 | bytes 31703040 | tf_op jit(solution)/shard_map/pallas_call | solution.py:504
  78.7 4.1 %collective-permute-done.13.refs_2_ = f32[2,64,768]{2,1,0:T(8,128)S(1)} collective-permute-done((f32[2,64,768]{2,1,0:T(8,128)S(1)}, f32[2,64,768]{2,1,0:T(8,128)S(1)}, u32[]{:S(2)}, u32[]{:S(2)}) %collective-permute-start.13) | collective-permute-done | bytes 393248 | tf_op jit(solution)/shard_map/scaled_x/ppermute | solution.py:518
  82.7 3.5 %shard_map.144 = (f32[2,64,768]{2,1,0:T(8,128)S(1)}, f32[2,64,768]{2,1,0:T(8,128)S(1)}, f32[128,256]{1,0:T(8,128)S(1)}, f32[2,8,256]{2,1,0:T(8,128)S(1)}) custom-call(s32[8]{0:T(128)S(1)} %copy-done.3, f32[2,256,256]{2,1,0:T(8,128)S(1)} %add.52.mid_ref, f32[2,256,256]{2,1,0:T(8,128)S(1)} %collective-permute-done.11.end_ref, ...), custom_call_target="tpu_custom_call" | custom-call | flops 16106127360 | bytes 33013760 | tf_op jit(solution)/shard_map/pallas_call | solution.py:504
  89.4 4.7 %collective-permute-done.19.end_ref = f32[2,256,256]{2,1,0:T(8,128)S(1)} collective-permute-done((f32[2,256,256]{2,1,0:T(8,128)S(1)}, f32[2,256,256]{2,1,0:T(8,128)S(1)}, u32[]{:S(2)}, u32[]{:S(2)}) %collective-permute-start.19) | collective-permute-done | bytes 524320 | tf_op jit(solution)/shard_map/z0_outward/ppermute | solution.py:536
  94.2 2.5 %shard_map.145 = (f32[2,64,768]{2,1,0:T(8,128)S(1)}, f32[2,64,768]{2,1,0:T(8,128)S(1)}, f32[136,256]{1,0:T(8,128)S(1)}) custom-call(s32[8]{0:T(128)S(1)} %copy-done.3, f32[2,256,256]{2,1,0:T(8,128)S(1)} %add.54.mid_ref, f32[2,256,256]{2,1,0:T(8,128)S(1)} %collective-permute-done.19.end_ref, f32[4,64,768]{2,1,0:T(8,128)S(1)} %get-tuple-element.82.own_ref.ser_own, ...), custom_call_target="tpu_custom_call" | custom-call | flops 12079595520 | bytes 35389440 | tf_op jit(solution)/shard_map/pallas_call | solution.py:504
  97.8 5.4 %collective-permute-done.17.end_ref = f32[2,256,256]{2,1,0:T(8,128)S(1)} collective-permute-done((f32[2,256,256]{2,1,0:T(8,128)S(1)}, f32[2,256,256]{2,1,0:T(8,128)S(1)}, u32[]{:S(2)}, u32[]{:S(2)}) %collective-permute-start.17) | collective-permute-done | bytes 524320 | tf_op jit(solution)/shard_map/z1_outward/ppermute | solution.py:536
  103.2 2.6 %shard_map.146 = (f32[2,64,768]{2,1,0:T(8,128)S(1)}, f32[2,64,768]{2,1,0:T(8,128)S(1)}, f32[136,256]{1,0:T(8,128)S(1)}) custom-call(s32[8]{0:T(128)S(1)} %copy-done.3, f32[2,256,256]{2,1,0:T(8,128)S(1)} %add.55.mid_ref, f32[2,256,256]{2,1,0:T(8,128)S(1)} %collective-permute-done.17.end_ref, f32[4,64,768]{2,1,0:T(8,128)S(1)} %get-tuple-element.82.own_ref.ser_own, ...), custom_call_target="tpu_custom_call" | custom-call | flops 12079595520 | bytes 36782080 | tf_op jit(solution)/shard_map/pallas_call | solution.py:504
  107.4 2.5 %collective-permute-done.20 = f32[40,256]{1,0:T(8,128)S(1)} collective-permute-done((f32[40,256]{1,0:T(8,128)S(1)}, f32[40,256]{1,0:T(8,128)S(1)}, u32[]{:S(2)}, u32[]{:S(2)}) %collective-permute-start.20) | collective-permute-done | bytes 40992 | tf_op jit(solution)/shard_map/stats_z/ppermute | solution.py:518
  111.1 3.7 %collective-permute-done.22 = f32[40,256]{1,0:T(8,128)S(1)} collective-permute-done((f32[40,256]{1,0:T(8,128)S(1)}, f32[40,256]{1,0:T(8,128)S(1)}, u32[]{:S(2)}, u32[]{:S(2)}) %collective-permute-start.22) | collective-permute-done | bytes 40992 | tf_op jit(solution)/shard_map/stats_z/ppermute | solution.py:518
  118.0 2.3 %collective-permute-done.24 = f32[168,256]{1,0:T(8,128)S(1)} collective-permute-done((f32[168,256]{1,0:T(8,128)S(1)}, f32[168,256]{1,0:T(8,128)S(1)}, u32[]{:S(2)}, u32[]{:S(2)}) %collective-permute-start.24) | collective-permute-done | bytes 172064 | tf_op jit(solution)/shard_map/grads_x/ppermute | solution.py:518
  123.4 2.6 %shard_map.148 = f32[64,5760]{1,0:T(8,128)} custom-call(f32[64,5760]{1,0:T(8,128)S(1)} %copy-done.1, f32[64,5760]{1,0:T(8,128)S(1)} %copy-done, f32[8,768]{1,0:T(8,128)S(1)} %add.47.ss_ref, f32[40,256]{1,0:T(8,128)S(1)} %add.57.in_own, f32[40,256]{1,0:T(8,128)S(1)} %slice.29.in_rec, f32[2,64,768]{2,1,0:T(8,128)S(1)} %get-tuple-element.125.refs_0_, ...), custom_call_target="tpu_custom_call" | custom-call | flops 6103040 | bytes 6103040 | tf_op jit(solution)/shard_map/pallas_call | solution.py:423
  126.0 2.3 %collective-permute-done.26.rec_ref = f32[168,256]{1,0:T(8,128)S(1)} collective-permute-done((f32[168,256]{1,0:T(8,128)S(1)}, f32[168,256]{1,0:T(8,128)S(1)}, u32[]{:S(2)}, u32[]{:S(2)}) %collective-permute-start.26) | collective-permute-done | bytes 172064 | tf_op jit(solution)/shard_map/grads_y/ppermute | solution.py:518
  (73 shorter events, 26.3 us)
Async XLA Ops:
  0.6 21.4 %copy-start.5 = (bf16[256,768]{1,0:T(8,128)(2,1)S(1)}, bf16[256,768]{1,0:T(8,128)(2,1)}, u32[]{:S(2)}) copy-start(bf16[256,768]{1,0:T(8,128)(2,1)} %constant.6.clone.leg_high) | copy-start | bytes 1179652
  0.6 21.4 %copy-start.6 = (bf16[256,768]{1,0:T(8,128)(2,1)S(1)}, bf16[256,768]{1,0:T(8,128)(2,1)}, u32[]{:S(2)}) copy-start(bf16[256,768]{1,0:T(8,128)(2,1)} %constant.7.clone.leg_low) | copy-start | bytes 1179652
  3.2 7.8 %collective-permute-start = (f32[56,768]{1,0:T(8,128)S(1)}, f32[56,768]{1,0:T(8,128)S(1)}, u32[]{:S(2)}, u32[]{:S(2)}) collective-permute-start(f32[56,768]{1,0:T(8,128)S(1)} %get-tuple-element.69.own_ref), channel_id=1, source_target_pairs={{0,1},{1,0},{2,3},{3,2},{4,5},{5,4},{6,7},{7,6},{8,9},{9,8},{10,11... | collective-permute-start | bytes 516104 | tf_op jit(solution)/shard_map/message_x/ppermute | solution.py:518
  8.2 13.8 %collective-permute-start.4 = (f32[2,64,768]{2,1,0:T(8,128)S(1)}, f32[2,64,768]{2,1,0:T(8,128)S(1)}, u32[]{:S(2)}, u32[]{:S(2)}) collective-permute-start(f32[2,64,768]{2,1,0:T(8,128)S(1)} %get-tuple-element.77), channel_id=1, source_target_pairs={{0,1},{1,0},{2,3},{3,2},{4,5},{5,4},{6,7},{7,6},{8,9},{9,8},{10,11... | collective-permute-start | bytes 1179656 | tf_op jit(solution)/shard_map/cot_x/ppermute | solution.py:518
  11.0 17.8 %collective-permute-start.1 = (f32[2,64,768]{2,1,0:T(8,128)S(1)}, f32[2,64,768]{2,1,0:T(8,128)S(1)}, u32[]{:S(2)}, u32[]{:S(2)}) collective-permute-start(f32[2,64,768]{2,1,0:T(8,128)S(1)} %get-tuple-element.74), channel_id=1, source_target_pairs={{0,1},{1,0},{2,3},{3,2},{4,5},{5,4},{6,7},{7,6},{8,9},{9,8},{10,11... | collective-permute-start | bytes 1179656 | tf_op jit(solution)/shard_map/cot_x/ppermute | solution.py:518
  13.5 3.8 %collective-permute-start.2 = (f32[8,768]{1,0:T(8,128)S(1)}, f32[8,768]{1,0:T(8,128)S(1)}, u32[]{:S(2)}, u32[]{:S(2)}) collective-permute-start(f32[8,768]{1,0:T(8,128)S(1)} %slice_add_fusion), channel_id=1, source_target_pairs={{0,2},{1,3},{2,0},{3,1},{4,6},{5,7},{6,4},{7,5},{8,10},{9,11},{10,... | collective-permute-start | bytes 73736 | tf_op jit(solution)/shard_map/squares_z1/ppermute | solution.py:518
  17.3 4.7 %collective-permute-start.3 = (f32[8,768]{1,0:T(8,128)S(1)}, f32[8,768]{1,0:T(8,128)S(1)}, u32[]{:S(2)}, u32[]{:S(2)}) collective-permute-start(f32[8,768]{1,0:T(8,128)S(1)} %add.46), channel_id=1, source_target_pairs={{0,4},{1,5},{2,6},{3,7},{4,0},{5,1},{6,2},{7,3},{8,12},{9,13},{10,... | collective-permute-start | bytes 73736 | tf_op jit(solution)/shard_map/squares_z2/ppermute | solution.py:518
  19.9 24.4 %collective-permute-start.6 = (f32[4,64,768]{2,1,0:T(8,128)S(1)}, f32[4,64,768]{2,1,0:T(8,128)S(1)}, u32[]{:S(2)}, u32[]{:S(2)}) collective-permute-start(f32[4,64,768]{2,1,0:T(8,128)S(1)} %get-tuple-element.84), channel_id=1, source_target_pairs={{0,1},{1,0},{2,3},{3,2},{4,5},{5,4},{6,7},{7,6},{8,9},{9,8},{10,11... | collective-permute-start | bytes 2359304 | tf_op jit(solution)/shard_map/ser_x/ppermute | solution.py:518
  24.1 13.7 %collective-permute-start.7 = (f32[2,256,256]{2,1,0:T(8,128)S(1)}, f32[2,256,256]{2,1,0:T(8,128)S(1)}, u32[]{:S(2)}, u32[]{:S(2)}) collective-permute-start(f32[2,256,256]{2,1,0:T(8,128)S(1)} %shard_map.139), channel_id=1, source_target_pairs={{0,2},{1,3},{6,4},{7,5},{8,10},{9,11},{14,12},{15,13},{16,18},{17,... | collective-permute-start | bytes 1572872 | tf_op jit(solution)/shard_map/h0_inward/ppermute | solution.py:536
  30.8 13.5 %copy-start.7 = (f32[4,32,768]{2,1,0:T(8,128)S(1)}, f32[4,32,768]{2,1,0:T(8,128)}, u32[]{:S(2)}) copy-start(f32[4,32,768]{2,1,0:T(8,128)} %constant.8.clone.phase_ref) | copy-start | bytes 1179652
  30.8 20.3 %collective-permute-start.5 = (f32[2,256,256]{2,1,0:T(8,128)S(1)}, f32[2,256,256]{2,1,0:T(8,128)S(1)}, u32[]{:S(2)}, u32[]{:S(2)}) collective-permute-start(f32[2,256,256]{2,1,0:T(8,128)S(1)} %shard_map.140), channel_id=1, source_target_pairs={{0,2},{1,3},{6,4},{7,5},{8,10},{9,11},{14,12},{15,13},{16,18},{17,... | collective-permute-start | bytes 1572872 | tf_op jit(solution)/shard_map/h1_inward/ppermute | solution.py:536
  37.9 17.1 %collective-permute-start.10 = (f32[2,256,256]{2,1,0:T(8,128)S(1)}, f32[2,256,256]{2,1,0:T(8,128)S(1)}, u32[]{:S(2)}, u32[]{:S(2)}) collective-permute-start(f32[2,256,256]{2,1,0:T(8,128)S(1)} %add.48), channel_id=1, source_target_pairs={{2,4},{3,5},{4,2},{5,3},{10,12},{11,13},{12,10},{13,11},{18,20},{1... | collective-permute-start | bytes 1572872 | tf_op jit(solution)/shard_map/h0_middle/ppermute | solution.py:536
  47.3 16.0 %collective-permute-start.9 = (f32[2,256,256]{2,1,0:T(8,128)S(1)}, f32[2,256,256]{2,1,0:T(8,128)S(1)}, u32[]{:S(2)}, u32[]{:S(2)}) collective-permute-start(f32[2,256,256]{2,1,0:T(8,128)S(1)} %shard_map.141), channel_id=1, source_target_pairs={{0,2},{1,3},{6,4},{7,5},{8,10},{9,11},{14,12},{15,13},{16,18},{17,... | collective-permute-start | bytes 1572872 | tf_op jit(solution)/shard_map/z0_inward/ppermute | solution.py:536
  51.2 12.9 %collective-permute-start.8 = (f32[2,256,256]{2,1,0:T(8,128)S(1)}, f32[2,256,256]{2,1,0:T(8,128)S(1)}, u32[]{:S(2)}, u32[]{:S(2)}) collective-permute-start(f32[2,256,256]{2,1,0:T(8,128)S(1)} %add.49), channel_id=1, source_target_pairs={{2,4},{3,5},{4,2},{5,3},{10,12},{11,13},{12,10},{13,11},{18,20},{1... | collective-permute-start | bytes 1572872 | tf_op jit(solution)/shard_map/h1_middle/ppermute | solution.py:536
  55.0 16.4 %copy-start.3 = (s32[8]{0:T(128)S(1)}, s32[8]{0:T(128)}, u32[]{:S(2)}) copy-start(s32[8]{0:T(128)} %len_ref.7) | copy-start | bytes 100
  55.0 16.4 %collective-permute-start.12 = (f32[2,256,256]{2,1,0:T(8,128)S(1)}, f32[2,256,256]{2,1,0:T(8,128)S(1)}, u32[]{:S(2)}, u32[]{:S(2)}) collective-permute-start(f32[2,256,256]{2,1,0:T(8,128)S(1)} %add.50.mid_ref), channel_id=1, source_target_pairs={{2,0},{3,1},{4,6},{5,7},{10,8},{11,9},{12,14},{13,15},{18,16},{19,... | collective-permute-start | bytes 1572872 | tf_op jit(solution)/shard_map/h0_outward/ppermute | solution.py:536
  56.3 20.2 %collective-permute-start.15 = (f32[2,256,256]{2,1,0:T(8,128)S(1)}, f32[2,256,256]{2,1,0:T(8,128)S(1)}, u32[]{:S(2)}, u32[]{:S(2)}) collective-permute-start(f32[2,256,256]{2,1,0:T(8,128)S(1)} %shard_map.142), channel_id=1, source_target_pairs={{0,2},{1,3},{6,4},{7,5},{8,10},{9,11},{14,12},{15,13},{16,18},{17,... | collective-permute-start | bytes 1572872 | tf_op jit(solution)/shard_map/z1_inward/ppermute | solution.py:536
  63.4 13.9 %collective-permute-start.14 = (f32[2,256,256]{2,1,0:T(8,128)S(1)}, f32[2,256,256]{2,1,0:T(8,128)S(1)}, u32[]{:S(2)}, u32[]{:S(2)}) collective-permute-start(f32[2,256,256]{2,1,0:T(8,128)S(1)} %add.51), channel_id=1, source_target_pairs={{2,4},{3,5},{4,2},{5,3},{10,12},{11,13},{12,10},{13,11},{18,20},{1... | collective-permute-start | bytes 1572872 | tf_op jit(solution)/shard_map/z0_middle/ppermute | solution.py:536
  64.2 18.6 %collective-permute-start.11 = (f32[2,256,256]{2,1,0:T(8,128)S(1)}, f32[2,256,256]{2,1,0:T(8,128)S(1)}, u32[]{:S(2)}, u32[]{:S(2)}) collective-permute-start(f32[2,256,256]{2,1,0:T(8,128)S(1)} %add.52.mid_ref), channel_id=1, source_target_pairs={{2,0},{3,1},{4,6},{5,7},{10,8},{11,9},{12,14},{13,15},{18,16},{19,... | collective-permute-start | bytes 1572872 | tf_op jit(solution)/shard_map/h1_outward/ppermute | solution.py:536
  74.9 7.8 %collective-permute-start.13 = (f32[2,64,768]{2,1,0:T(8,128)S(1)}, f32[2,64,768]{2,1,0:T(8,128)S(1)}, u32[]{:S(2)}, u32[]{:S(2)}) collective-permute-start(f32[2,64,768]{2,1,0:T(8,128)S(1)} %get-tuple-element.96), channel_id=1, source_target_pairs={{0,1},{1,0},{2,3},{3,2},{4,5},{5,4},{6,7},{7,6},{8,9},{9,8},{10,11... | collective-permute-start | bytes 1179656 | tf_op jit(solution)/shard_map/scaled_x/ppermute | solution.py:518
  76.6 11.3 %collective-permute-start.16 = (f32[2,256,256]{2,1,0:T(8,128)S(1)}, f32[2,256,256]{2,1,0:T(8,128)S(1)}, u32[]{:S(2)}, u32[]{:S(2)}) collective-permute-start(f32[2,256,256]{2,1,0:T(8,128)S(1)} %add.53), channel_id=1, source_target_pairs={{2,4},{3,5},{4,2},{5,3},{10,12},{11,13},{12,10},{13,11},{18,20},{1... | collective-permute-start | bytes 1572872 | tf_op jit(solution)/shard_map/z1_middle/ppermute | solution.py:536
  77.4 16.8 %collective-permute-start.19 = (f32[2,256,256]{2,1,0:T(8,128)S(1)}, f32[2,256,256]{2,1,0:T(8,128)S(1)}, u32[]{:S(2)}, u32[]{:S(2)}) collective-permute-start(f32[2,256,256]{2,1,0:T(8,128)S(1)} %add.54.mid_ref), channel_id=1, source_target_pairs={{2,0},{3,1},{4,6},{5,7},{10,8},{11,9},{12,14},{13,15},{18,16},{19,... | collective-permute-start | bytes 1572872 | tf_op jit(solution)/shard_map/z0_outward/ppermute | solution.py:536
  86.3 11.5 %collective-permute-start.18 = (f32[2,64,768]{2,1,0:T(8,128)S(1)}, f32[2,64,768]{2,1,0:T(8,128)S(1)}, u32[]{:S(2)}, u32[]{:S(2)}) collective-permute-start(f32[2,64,768]{2,1,0:T(8,128)S(1)} %get-tuple-element.104), channel_id=1, source_target_pairs={{0,1},{1,0},{2,3},{3,2},{4,5},{5,4},{6,7},{7,6},{8,9},{9,8},{10,11... | collective-permute-start | bytes 1179656 | tf_op jit(solution)/shard_map/scaled_x/ppermute | solution.py:518
  88.0 15.3 %collective-permute-start.17 = (f32[2,256,256]{2,1,0:T(8,128)S(1)}, f32[2,256,256]{2,1,0:T(8,128)S(1)}, u32[]{:S(2)}, u32[]{:S(2)}) collective-permute-start(f32[2,256,256]{2,1,0:T(8,128)S(1)} %add.55.mid_ref), channel_id=1, source_target_pairs={{2,0},{3,1},{4,6},{5,7},{10,8},{11,9},{12,14},{13,15},{18,16},{19,... | collective-permute-start | bytes 1572872 | tf_op jit(solution)/shard_map/z1_outward/ppermute | solution.py:536
  96.7 9.2 %collective-permute-start.21 = (f32[2,64,768]{2,1,0:T(8,128)S(1)}, f32[2,64,768]{2,1,0:T(8,128)S(1)}, u32[]{:S(2)}, u32[]{:S(2)}) collective-permute-start(f32[2,64,768]{2,1,0:T(8,128)S(1)} %get-tuple-element.113), channel_id=1, source_target_pairs={{0,1},{1,0},{2,3},{3,2},{4,5},{5,4},{6,7},{7,6},{8,9},{9,8},{10,11... | collective-permute-start | bytes 1179656 | tf_op jit(solution)/shard_map/branch_x/ppermute | solution.py:518
  103.2 13.1 %copy-start = (f32[64,5760]{1,0:T(8,128)S(1)}, f32[64,5760]{1,0:T(8,128)}, u32[]{:S(2)}) copy-start(f32[64,5760]{1,0:T(8,128)} %x_ref.2) | copy-start | bytes 4423684
  105.8 4.1 %collective-permute-start.20 = (f32[40,256]{1,0:T(8,128)S(1)}, f32[40,256]{1,0:T(8,128)S(1)}, u32[]{:S(2)}, u32[]{:S(2)}) collective-permute-start(f32[40,256]{1,0:T(8,128)S(1)} %pad_maximum_fusion.2), channel_id=1, source_target_pairs={{0,2},{1,3},{2,0},{3,1},{4,6},{5,7},{6,4},{7,5},{8,10},{9,11},{10,... | collective-permute-start | bytes 122888 | tf_op jit(solution)/shard_map/stats_z/ppermute | solution.py:518
  105.9 10.4 %collective-permute-start.23 = (f32[2,64,768]{2,1,0:T(8,128)S(1)}, f32[2,64,768]{2,1,0:T(8,128)S(1)}, u32[]{:S(2)}, u32[]{:S(2)}) collective-permute-start(f32[2,64,768]{2,1,0:T(8,128)S(1)} %get-tuple-element.120), channel_id=1, source_target_pairs={{0,1},{1,0},{2,3},{3,2},{4,5},{5,4},{6,7},{7,6},{8,9},{9,8},{10,11... | collective-permute-start | bytes 1179656 | tf_op jit(solution)/shard_map/branch_x/ppermute | solution.py:518
  109.9 4.9 %collective-permute-start.22 = (f32[40,256]{1,0:T(8,128)S(1)}, f32[40,256]{1,0:T(8,128)S(1)}, u32[]{:S(2)}, u32[]{:S(2)}) collective-permute-start(f32[40,256]{1,0:T(8,128)S(1)} %fusion.1), channel_id=1, source_target_pairs={{0,4},{1,5},{2,6},{3,7},{4,0},{5,1},{6,2},{7,3},{8,12},{9,13},{10,... | collective-permute-start | bytes 122888 | tf_op jit(solution)/shard_map/stats_z/ppermute | solution.py:518
  114.8 5.5 %collective-permute-start.24 = (f32[168,256]{1,0:T(8,128)S(1)}, f32[168,256]{1,0:T(8,128)S(1)}, u32[]{:S(2)}, u32[]{:S(2)}) collective-permute-start(f32[168,256]{1,0:T(8,128)S(1)} %pad_maximum_fusion.1), channel_id=1, source_target_pairs={{0,1},{1,0},{2,3},{3,2},{4,5},{5,4},{6,7},{7,6},{8,9},{9,8},{10,11... | collective-permute-start | bytes 516104 | tf_op jit(solution)/shard_map/grads_x/ppermute | solution.py:518
  120.3 1.5 %collective-permute-start.25 = (f32[168,256]{1,0:T(8,128)S(1)}, f32[168,256]{1,0:T(8,128)S(1)}, u32[]{:S(2)}, u32[]{:S(2)}) collective-permute-start(f32[168,256]{1,0:T(8,128)S(1)} %fusion), channel_id=1, source_target_pairs={{0,8},{8,0},{16,24},{24,16},{1,9},{9,1},{17,25},{25,17},{2,10},{10... | collective-permute-start | bytes 516104 | tf_op jit(solution)/shard_map/grads_core/ppermute | solution.py:518
  121.8 6.5 %collective-permute-start.26 = (f32[168,256]{1,0:T(8,128)S(1)}, f32[168,256]{1,0:T(8,128)S(1)}, u32[]{:S(2)}, u32[]{:S(2)}) collective-permute-start(f32[168,256]{1,0:T(8,128)S(1)} %add.59.own_ref), channel_id=1, source_target_pairs={{0,16},{8,24},{16,0},{24,8},{1,17},{9,25},{17,1},{25,9},{2,18},{10... | collective-permute-start | bytes 516104 | tf_op jit(solution)/shard_map/grads_y/ppermute | solution.py:518
  (3 other events, 16.8 us)

commit v3 on v2

--- a/solution.py
+++ b/solution.py
@@ -58,8 +58,15 @@
     return lax.dot_general(a, b, (((1,), (1,)), ((), ())), preferred_element_type=f32)
 
 
-def three(dot, a, b):
-    return dot(a[0], b[0]) + dot(a[0], b[1]) + dot(a[1], b[0])
+def three(dot, pairs, table):
+    rows = pairs[0][0].shape[0]
+    high = dot(jnp.concatenate([half for pair in pairs for half in pair], axis=0), table[0])
+    low = dot(jnp.concatenate([pair[0] for pair in pairs], axis=0), table[1])
+    out = []
+    for k in range(len(pairs)):
+        at = 2 * k * rows
+        out.append(high[at : at + rows] + high[at + rows : at + 2 * rows] + low[k * rows : (k + 1) * rows])
+    return out
 
 
 def deep(x):
@@ -92,30 +99,26 @@
     return jnp.where(row <= col, 1.0, 0.0).astype(bf16)
 
 
-def running_sum(x, tri):
-    high, low = split(x)
-    blocks, carry = [], None
-    for b in range(LANES // BLOCK):
-        at = slice(b * BLOCK, (b + 1) * BLOCK)
-        block = nn(high[:, at], tri) + nn(low[:, at], tri)
-        if carry is not None:
-            block = block + carry
-        carry = block[:, BLOCK - 1 : BLOCK]
-        blocks.append(block)
+def block_sums(dot, x):
+    rows, blocks = x.shape[0], LANES // BLOCK
+    halves_of = split(x)
+    stack = [half[:, b * BLOCK : (b + 1) * BLOCK] for half in halves_of for b in range(blocks)]
+    sums = dot(jnp.concatenate(stack, axis=0), triangle())
+    return [sums[b * rows : (b + 1) * rows] + sums[(blocks + b) * rows : (blocks + b + 1) * rows] for b in range(blocks)]
+
+
+def running_sum(x):
+    blocks = block_sums(nn, x)
+    for b in range(1, len(blocks)):
+        blocks[b] = blocks[b] + blocks[b - 1][:, BLOCK - 1 : BLOCK]
     return jnp.concatenate(blocks, axis=1)
 
 
-def running_sum_back(x, tri):
-    high, low = split(x)
-    blocks, carry = [], None
-    for b in reversed(range(LANES // BLOCK)):
-        at = slice(b * BLOCK, (b + 1) * BLOCK)
-        block = nt(high[:, at], tri) + nt(low[:, at], tri)
-        if carry is not None:
-            block = block + carry
-        carry = block[:, 0:1]
-        blocks.append(block)
-    return jnp.concatenate(blocks[::-1], axis=1)
+def running_sum_back(x):
+    blocks = block_sums(nt, x)
+    for b in reversed(range(len(blocks) - 1)):
+        blocks[b] = blocks[b] + blocks[b + 1][:, 0:1]
+    return jnp.concatenate(blocks, axis=1)
 
 
 def side_of():
@@ -184,9 +187,10 @@
     return factor * jnp.cos(angle), factor * jnp.sin(angle)
 
 
-def front_kernel(units, len_hbm, in_hbm, out_hbm, gain_hbm, x_hbm, message_ref, *refs):
+def front_kernel(units, line_length, len_hbm, in_hbm, out_hbm, gain_hbm, x_hbm, message_ref, end_ref, *refs):
     out_refs, (len_ref, in_ref, out_ref, gain_ref, buffer, packed, sems, weight_sems) = refs[:-8], refs[-8:]
     windows = x_hbm.shape[1] // LEN
+    end_ref[...] = jnp.where(at_line_end(line_length), jnp.ones(end_ref.shape, f32), 0.0)
     weights = [(in_hbm, in_ref), (out_hbm, out_ref), (gain_hbm, gain_ref)]
     weights = [pltpu.make_async_copy(a, b, weight_sems.at[k]) for k, (a, b) in enumerate(weights)]
     for copy in weights:
@@ -244,100 +248,97 @@
         ref[...] = jnp.concatenate([high, low], axis=0)
 
 
-def read_kernel(own_ref, rec_ref, up_own, up_rec, leg_high, leg_low, out_ref):
-    field = nn(up_own[...], deep(own_ref[0])) + nn(up_rec[...], deep(rec_ref[0]))
-    out_ref[0] = three(nt, split(field), (leg_high[...], leg_low[...]))
+def read_kernel(own_ref, rec_ref, up_own, up_rec, leg_high, leg_low, *out_refs):
+    pairs = []
+    for k in range(len(out_refs)):
+        pairs.append(split(nn(up_own[...], deep(own_ref[k])) + nn(up_rec[...], deep(rec_ref[k]))))
+    for ref, value in zip(out_refs, three(nt, pairs, (leg_high[...], leg_low[...]))):
+        ref[...] = value
 
 
 def inverse_rms(ss_ref, row, full_width):
     return lax.rsqrt(ss_ref[pl.ds(row, 1), :] * (1.0 / full_width) + epsilon)
 
 
-def rank_kernel(first, full_width, own_ref, rec_ref, ss_ref, down_own, down_rec, leg_high, leg_low, phase_ref, out_ref):
-    half = side_of() * (ss_ref.shape[0] // 2)
-    inv = inverse_rms(ss_ref, half + first + pl.program_id(0), full_width)
-    mixed = nn(down_own[...], deep(own_ref[0] * inv)) + nn(down_rec[...], deep(rec_ref[0] * inv))
-    part = mixed.shape[0] // 2
-    real, imag = rotate(mixed[:part], mixed[part:], phase_ref[0], phase_ref[1])
-    total = running_sum(jnp.concatenate([real, imag], axis=0), triangle())
-    real, imag = rotate(total[:part], total[part:], phase_ref[2], -phase_ref[3])
-    memory = jnp.concatenate([real, imag], axis=0)
-    out_ref[0] = three(nt, split(memory), (leg_high[...], leg_low[...]))
+def rank_kernel(first, full_width, own_ref, rec_ref, ss_ref, down_own, down_rec, leg_high, leg_low, phase_ref, *out_refs):
+    row = side_of() * (ss_ref.shape[0] // 2) + first
+    pairs = []
+    for k in range(len(out_refs)):
+        inv = inverse_rms(ss_ref, row + k, full_width)
+        mixed = nn(down_own[...], deep(own_ref[k] * inv)) + nn(down_rec[...], deep(rec_ref[k] * inv))
+        part = mixed.shape[0] // 2
+        real, imag = rotate(mixed[:part], mixed[part:], phase_ref[0], phase_ref[1])
+        total = running_sum(jnp.concatenate([real, imag], axis=0))
+        real, imag = rotate(total[:part], total[part:], phase_ref[2], -phase_ref[3])
+        pairs.append(split(jnp.concatenate([real, imag], axis=0)))
+    for ref, value in zip(out_refs, three(nt, pairs, (leg_high[...], leg_low[...]))):
+        ref[...] = value
+
+
+def totals(line_length, refs):
+    count, at_end = len(refs) // 2, at_line_end(line_length)
+    return [split(jnp.where(at_end, refs[count + k][...], refs[k][...])) for k in range(count)]
+
+
+def masked(value, length):
+    lane = lax.broadcasted_iota(jnp.int32, value.shape, 1)
+    return jnp.where(lane < length, value, 0.0)
 
 
 def opening(refs, outs):
-    return None if len(refs) == outs else refs[0], refs[-outs:]
-
-
-def back_kernel(first, full_width, line_length, len_ref, mid_ref, end_ref, own_ref, rec_ref, ss_ref, down_both, leg_high, leg_low, phase_ref, *refs):
-    prev_ref, (own_out, rec_out, grad_out, inner_out) = opening(refs, 4)
-    step = pl.program_id(0)
-    half = side_of() * (ss_ref.shape[0] // 2)
-    row = half + first + step
-    inv = inverse_rms(ss_ref, row, full_width)
+    return 0.0 if len(refs) == outs else refs[0][...], refs[-outs:]
+
+
+def back_kernel(first, full_width, line_length, len_ref, own_ref, rec_ref, *refs):
+    sums, refs = refs[: 2 * own_ref.shape[0]], refs[2 * own_ref.shape[0] :]
+    ss_ref, down_both, leg_high, leg_low, phase_ref, *refs = refs
+    grads, (own_out, rec_out, grad_out, inner_out) = opening(refs, 4)
+    row = side_of() * (ss_ref.shape[0] // 2) + first
     channels = own_ref.shape[1]
-    total = jnp.where(at_line_end(line_length), end_ref[0], mid_ref[0])
-    memory = three(nn, split(total), (leg_high[...], leg_low[...]))
-    part = memory.shape[0] // 2
-    real, imag = rotate(memory[:part], memory[part:], phase_ref[2], phase_ref[3])
-    back = running_sum_back(jnp.concatenate([real, imag], axis=0), triangle())
-    real, imag = rotate(back[:part], back[part:], phase_ref[0], -phase_ref[1])
-    pair = split(jnp.concatenate([real, imag], axis=0))
-    scaled = stacked(down_both[...], pair, 2 * channels)
-    lane = lax.broadcasted_iota(jnp.int32, scaled.shape, 1)
-    scaled = jnp.where(lane < len_ref[row], scaled, 0.0)
-    own_out[0] = scaled[:channels]
-    rec_out[0] = scaled[channels:]
-    both = jnp.concatenate([own_ref[0], rec_ref[0]], axis=0)
-    inner = jnp.sum(scaled * both, axis=0, keepdims=True)
-    pieces = [inner[:, p * 256 : (p + 1) * 256] for p in range(LANES // 256)]
-    inner_out[0] = jnp.concatenate(pieces + [jnp.zeros((STATS - len(pieces), 256), f32)], axis=0)
-    high, low = split(both * inv)
-    grads = stacked_nt(jnp.concatenate([high, low], axis=0), pair, 2 * channels)
-
-    @pl.when(step == 0)
-    def _():
-        grad_out[...] = grads if prev_ref is None else prev_ref[...] + grads
-
-    @pl.when(step > 0)
-    def _():
-        grad_out[...] += grads
-
-
-def branch_kernel(first, line_length, len_ref, mid_ref, end_ref, ser_own, ser_rec, cot_own, cot_rec, up_both, leg_high, leg_low, *refs):
-    prev_ref, (own_out, rec_out, grad_out) = opening(refs, 3)
-    step = pl.program_id(0)
+    for k, total in enumerate(totals(line_length, sums)):
+        (memory,) = three(nn, [total], (leg_high[...], leg_low[...]))
+        part = memory.shape[0] // 2
+        real, imag = rotate(memory[:part], memory[part:], phase_ref[2], phase_ref[3])
+        back = running_sum_back(jnp.concatenate([real, imag], axis=0))
+        real, imag = rotate(back[:part], back[part:], phase_ref[0], -phase_ref[1])
+        pair = split(jnp.concatenate([real, imag], axis=0))
+        scaled = masked(stacked(down_both[...], pair, 2 * channels), len_ref[row + k])
+        own_out[k] = scaled[:channels]
+        rec_out[k] = scaled[channels:]
+        both = jnp.concatenate([own_ref[k], rec_ref[k]], axis=0)
+        inner = jnp.sum(scaled * both, axis=0, keepdims=True)
+        pieces = [inner[:, p * 256 : (p + 1) * 256] for p in range(LANES // 256)]
+        inner_out[k] = jnp.concatenate(pieces + [jnp.zeros((STATS - len(pieces), 256), f32)], axis=0)
+        high, low = split(both * inverse_rms(ss_ref, row + k, full_width))
+        grads = grads + stacked_nt(jnp.concatenate([high, low], axis=0), pair, 2 * channels)
+    grad_out[...] = grads
+
+
+def branch_kernel(first, line_length, len_ref, ser_own, ser_rec, cot_own, cot_rec, *refs):
+    sums, refs = refs[: 2 * ser_own.shape[0]], refs[2 * ser_own.shape[0] :]
+    up_both, leg_high, leg_low, *refs = refs
+    before, (own_out, rec_out, grad_out) = opening(refs, 3)
     channels = ser_own.shape[1]
     rows = 2 * channels
-    row = side_of() * (len_ref.shape[0] // 2) + first + step
-    total = jnp.where(at_line_end(line_length), end_ref[0], mid_ref[0])
-    field = three(nn, split(total), (leg_high[...], leg_low[...]))
-    pair = split(field)
-    branch = stacked(up_both[...], pair, rows)
-    lane = lax.broadcasted_iota(jnp.int32, branch.shape, 1)
-    branch = jnp.where(lane < len_ref[row], branch, 0.0)
-    own_out[0] = branch[:channels]
-    rec_out[0] = branch[channels:]
-    high, low = split(jnp.concatenate([cot_own[0], cot_rec[0]], axis=0))
-    grads = stacked_nt(jnp.concatenate([high, low], axis=0), pair, rows)
-    series = jnp.concatenate([ser_own[0], ser_rec[0]], axis=0)
-    stats = []
-    for v in (series, branch, series + branch):
-        v = jnp.sum(jnp.sum(v * v, axis=0, keepdims=True), axis=1, keepdims=True)
-        stats.append(jnp.broadcast_to(v, (1, grads.shape[1])))
-    steps = functools.reduce(lambda a, b: a + b, [len_ref[w] for w in range(len_ref.shape[0])])
-    steps = jnp.where(jnp.logical_and(first == 0, step == 0), steps, 0).astype(f32)
-    stats.append(jnp.full((1, grads.shape[1]), steps, f32))
-    stats = jnp.concatenate(stats + [jnp.zeros((4, grads.shape[1]), f32)], axis=0)
-    grads = jnp.concatenate([grads, stats], axis=0)
-
-    @pl.when(step == 0)
-    def _():
-        grad_out[...] = grads if prev_ref is None else prev_ref[...] + grads
-
-    @pl.when(step > 0)
-    def _():
-        grad_out[...] += grads
+    windows = len_ref.shape[0]
+    row = side_of() * (windows // 2) + first
+    grads, stats = 0.0, [0.0, 0.0, 0.0]
+    for k, total in enumerate(totals(line_length, sums)):
+        pair = split(three(nn, [total], (leg_high[...], leg_low[...]))[0])
+        branch = masked(stacked(up_both[...], pair, rows), len_ref[row + k])
+        own_out[k] = branch[:channels]
+        rec_out[k] = branch[channels:]
+        high, low = split(jnp.concatenate([cot_own[k], cot_rec[k]], axis=0))
+        grads = grads + stacked_nt(jnp.concatenate([high, low], axis=0), pair, rows)
+        series = jnp.concatenate([ser_own[k], ser_rec[k]], axis=0)
+        for i, v in enumerate((series, branch, series + branch)):
+            stats[i] = stats[i] + jnp.sum(v * v, axis=0, keepdims=True)
+    width = grads.shape[1]
+    stats = [jnp.broadcast_to(jnp.sum(v, axis=1, keepdims=True), (1, width)) for v in stats]
+    steps = functools.reduce(lambda a, b: a + b, [len_ref[w] for w in range(windows)]) if first == 0 else 0
+    stats.append(jnp.full((1, width), steps, jnp.int32).astype(f32))
+    stats = jnp.concatenate(stats + [jnp.zeros((STATS - 4, width), f32)], axis=0)
+    grad_out[...] = before + jnp.concatenate([grads, stats], axis=0)
 
 
 def layer_kernel(units, x_ref, *refs):
@@ -403,10 +404,6 @@
 PARAMS = pltpu.CompilerParams(vmem_limit_bytes=8 * 1024 * 1024)
 
 
-def window_spec(shape, offset):
-    return pl.BlockSpec((1,) + shape[1:], lambda i: (i + offset,) + (0,) * (len(shape) - 1))
-
-
 def cost(flops, byte_count, weight=1):
     return pl.CostEstimate(flops=int(flops * weight), bytes_accessed=int(byte_count * weight), transcendentals=0)
 
@@ -447,14 +444,14 @@
     ]
 
 
-def front(series, lengths, weights, units, rows):
+def front(series, lengths, weights, units, rows, line_length):
     channels, windows = series.shape[0], series.shape[1] // LEN
-    shapes = [struct((windows + PACK, LANES)), struct((windows // 2, channels, LANES))]
+    shapes = [struct((windows + PACK, LANES)), struct((8, ORDER)), struct((windows // 2, channels, LANES))]
     shapes += [struct((n, channels, LANES)) for _, n in units]
     first, (buffer, sems) = deal_scratch(series, lengths)
     scratch = first + [pltpu.VMEM(a.shape, f32) for a in weights] + [buffer, pltpu.VMEM((rows, 128), f32), sems]
     return pl.pallas_call(
-        functools.partial(front_kernel, units),
+        functools.partial(front_kernel, units, line_length),
         out_shape=shapes,
         in_specs=[HBM] * (2 + len(weights)),
         out_specs=[whole(o.shape) for o in shapes],
@@ -489,28 +486,22 @@
 MATMUL = 2 * 256 * 256 * 256
 
 
-def unit_call(kernel, unit, smem, arrays, consts, outs, units_of_work, carried=(), weight=1):
+def unit_call(kernel, unit, smem, arrays, consts, outs, units_of_work, weight=1):
     count = unit[1]
     specs = [SMEM] * len(smem)
-    specs += [window_spec(a.shape, offset) for a, offset in arrays]
+    assert all(o % count == 0 for _, o in arrays)
+    specs += [pl.BlockSpec((count,) + a.shape[1:], lambda i, o=o // count, r=a.ndim - 1: (o,) + (0,) * r) for a, o in arrays]
     specs += [whole(c.shape) for c in consts]
-    aliases = {len(specs) + k: out for k, (out, _) in enumerate(carried)}
-    specs += [pl.BlockSpec(memory_space=pl.ANY)] * len(carried)
-    out_specs, shapes = [], []
-    for shape, offset in outs:
-        shapes.append(struct(shape))
-        out_specs.append(whole(shape) if offset is None else window_spec(shape, offset))
     moved = sum(a.size * 4 * count // a.shape[0] for a, _ in arrays) + sum(c.size * c.dtype.itemsize for c in consts)
     return pl.pallas_call(
         kernel,
-        out_shape=shapes,
+        out_shape=[struct(shape) for shape in outs],
         in_specs=specs,
-        out_specs=out_specs,
-        grid=(count,),
-        input_output_aliases=aliases,
+        out_specs=[whole(shape) for shape in outs],
+        grid=(1,),
         compiler_params=PARAMS,
         cost_estimate=cost(units_of_work * MATMUL * count, moved, weight),
-    )(*smem, *[a for a, _ in arrays], *consts, *[a for _, a in carried])
+    )(*smem, *[a for a, _ in arrays], *consts)
 
 
 def swap(x, axis, bit):
@@ -532,27 +523,19 @@
     return bits
 
 
-def hop(x, pairs):
-    return lax.ppermute(x, "order", [(2 * a + side, 2 * b + side) for a, b in pairs for side in (0, 1)])
-
-
-def inward(x):
+def cross(x):
+    batch, order = lax.axis_size("batch"), lax.axis_size("order")
+    pairs = []
+    for b in range(batch):
+        for o in range(order):
+            inner = o // 2 in (1, 2)
+            pairs.append((b * order + o, b * order + (o ^ 6) if inner else (b ^ 1) * order + o))
+    return lax.ppermute(x, ("batch", "order"), pairs)
+
+
+def line_sum(x):
     size = lax.axis_size("order")
-    if size == 8:
-        return hop(x, [(0, 1), (3, 2)])
     return lax.psum(x, "order", axis_index_groups=[list(range(side, size, 2)) for side in (0, 1)])
-
-
-def middle(x):
-    return hop(x, [(1, 2), (2, 1)]) if lax.axis_size("order") == 8 else x
-
-
-def outward(x):
-    return hop(x, [(1, 0), (2, 3)]) if lax.axis_size("order") == 8 else x
-
-
-def join(kept, came):
-    return kept + came if lax.axis_size("order") == 8 else came
 
 
 def after(x, tokens):
@@ -560,14 +543,18 @@
     return lax.optimization_barrier((x, *tokens))[0]
 
 
-WEIGHT = ((3,10),(10,10),(10,10),(10,10))
-COT = (2, 2)
-SER = (4,)
-READ = (2, 2)
+WEIGHT = ((10,) * 4, (10,) * 4, (10,) * 4, (10,) * 4)
+COT = (1, 1, 2)
+SER = (2, 2)
+READ = (1, 1, 2)
 RANK = (2, 2)
+BACK = (2, 2)
+MIX = (2, 1, 1)
+LAG = 3
 PLAN = (
-    "q", "R0", "Q", "R1", "hm0", "K0", "hm1", "K1", "ho0", "zm0", "ho1", "B0", "zm1", "zo0", "s0",
-    "B1", "zo1", "M0", "s1", "M1", "st1", "b0", "st2", "se", "G", "F1", "gc", "gy", "F2",
+    "q", "R0", "e0", "R1", "e1", "Q", "m0", "R2", "e2", "m1", "e3", "m2", "K0", "e4", "m3", "e5",
+    "m4", "K1", "e6", "m5", "B0", "e7", "m6", "e8", "m7", "s0", "B1", "e9", "M0", "e10", "M1",
+    "s1", "M2", "st1", "b0", "st2", "b1", "se", "G", "F1", "gc", "gy", "F2",
 )
 
 
@@ -587,12 +574,13 @@
     rows = 2 * rank_count * mode_count
     cot_units, ser_units = units_of(half, COT), units_of(half, SER)
     read_units, rank_units = units_of(half, READ), units_of(half, RANK)
+    back_units, mix_units = units_of(half, BACK), units_of(half, MIX)
 
     legendre = [jnp.asarray(h) for h in halves(legendre_rows())]
     phase = jnp.asarray(phase_rows(mode_count))
     gain = norm_gain.reshape(1, channels)
 
-    message, ser_own, *ser_rec = front(series, lengths, [mode_in, mode_out, gain], ser_units, rows)
+    message, end_mask, ser_own, *ser_rec = front(series, lengths, [mode_in, mode_out, gain], ser_units, rows, line_length)
     with jax.named_scope("message_x"):
         message_rec = swap(message, "order", 1)
     cot_own, *cot_rec = deal(after(grad_out, message), lengths, cot_units)
@@ -613,68 +601,83 @@
             return [(own, first), (jnp.concatenate(received[u : v + 1], axis=0), offset)]
         return [(own, first), (received[u], offset)]
 
-    chains = {}
+    chained = order_devices == 8
+    at_end = end_mask[:1] > 0.5
+    parts, pairs, sends, came, crossed = {}, {}, {}, {}, {}
     backs, branches, kept = {}, {}, {}
     state = {"squares": squares, "squares_rec": squares_rec, "token": up_own}
-
-    def sums_of(name, token):
-        return [(chains[name], 0), (after(chains[name + "out"], token), 0)]
 
     def do_read(u, token):
         first, count = read_units[u]
         own, rec = windows_of(cot_own, cot_rec, cot_units, first, count)
-        (out,) = unit_call(
+        outs = unit_call(
             read_kernel, read_units[u], [], [own, (after(rec[0], token), rec[1])],
-            [up_own, up_rec, *legendre], [((count, rows, ORDER), 0)], 15, weight=WEIGHT[0][u],
+            [up_own, up_rec, *legendre], [(rows, ORDER)] * count, 15, weight=WEIGHT[0][u],
         )
-        start("h", u, out, inward)
-        return out
+        for k in range(count):
+            parts[first + k] = outs[k]
+        return outs[0]
 
     def do_rank(u, token):
         first, count = rank_units[u]
         own, rec = windows_of(ser_own, ser_rec, ser_units, first, count)
-        (out,) = unit_call(
+        outs = unit_call(
             functools.partial(rank_kernel, first, full_width), rank_units[u], [], [own, (after(rec[0], token), rec[1])],
-            [state["squares"], down_own, down_rec, *legendre, phase], [((count, rows, ORDER), 0)], 21, weight=WEIGHT[1][u],
+            [state["squares"], down_own, down_rec, *legendre, phase], [(rows, ORDER)] * count, 21, weight=WEIGHT[1][u],
         )
-        start("z", u, out, inward)
+        for k in range(count):
+            parts[half + first + k] = outs[k]
+        return outs[0]
+
+    def do_swap(k, token):
+        if not chained:
+            if k < windows:
+                came[k + LAG] = sends[k + LAG] = line_sum(after(parts[k], token))
+            return token
+        done = k - LAG
+        if done < 0:
+            out = after(parts[k], token)
+        else:
+            out = pairs[done] + after(crossed[done], token)
+            if k < windows:
+                out = jnp.where(at_end, parts[k], out)
+        with jax.named_scope(f"e{k}"):
+            sends[k], came[k] = out, swap(out, "order", 2)
         return out
 
-    def start(kind, u, value, move):
-        name = f"{kind}{u}"
-        chains[name] = value
-        with jax.named_scope(f"{name}_{move.__name__}"):
-            chains[name + ("out" if move is outward else "")] = (value, move(value)) if move is not outward else move(value)
-
-    def do_join(kind, u, move, token):
-        value, came = chains[f"{kind}{u}"]
-        value = join(value, after(came, token))
-        start(kind, u, value, move)
-        if move is outward:
-            chains[f"{kind}{u}"] = value
-        return value
+    def do_cross(k, token):
+        if not chained:
+            return token
+        out = pairs[k] = parts[k] + after(came[k], token)
+        with jax.named_scope(f"m{k}"):
+            crossed[k] = cross(out)
+        return out
+
+    def sums_of(first, count, token):
+        at = range(first + LAG, first + LAG + count)
+        return [sends[k] for k in at] + [after(came[k], token) for k in at]
 
     def do_back(u, token):
-        first, count = read_units[u]
+        first, count = back_units[u]
         previous = [state["grad_in"]] if "grad_in" in state else []
         mine, theirs, state["grad_in"], dots = unit_call(
-            functools.partial(back_kernel, first, full_width, line_length), read_units[u], [lengths],
-            [*sums_of(f"h{u}", token), *windows_of(ser_own, ser_rec, ser_units, first, count)],
-            [state["squares"], down_both, *legendre, phase, *previous],
-            [((count, channels, LANES), 0)] * 2 + [((2 * channels, rows), None), ((count, STATS, 256), 0)], 24, weight=WEIGHT[2][u],
+            functools.partial(back_kernel, first, full_width, line_length), back_units[u], [lengths],
+            windows_of(ser_own, ser_rec, ser_units, first, count),
+            [*sums_of(first, count, token), state["squares"], down_both, *legendre, phase, *previous],
+            [(count, channels, LANES)] * 2 + [(2 * channels, rows), (count, STATS, 256)], 24, weight=WEIGHT[2][u],
         )
         with jax.named_scope("scaled_x"):
             backs[u] = (mine, swap(theirs, "order", 1), dots)
         return state["grad_in"]
 
     def do_mix(u, token):
-        first, count = rank_units[u]
+        first, count = mix_units[u]
         previous = [state["grad_mix"]] if "grad_mix" in state else []
         mine, theirs, state["grad_mix"] = unit_call(
-            functools.partial(branch_kernel, first, line_length), rank_units[u], [lengths],
-            [*sums_of(f"z{u}", token), *windows_of(ser_own, ser_rec, ser_units, first, count), *windows_of(cot_own, cot_rec, cot_units, first, count)],
-            [up_both, *legendre, *previous],
-            [((count, channels, LANES), 0)] * 2 + [((2 * channels + 8, rows), None)], 18, weight=WEIGHT[3][u],
+            functools.partial(branch_kernel, first, line_length), mix_units[u], [lengths],
+            [*windows_of(ser_own, ser_rec, ser_units, first, count), *windows_of(cot_own, cot_rec, cot_units, first, count)],
+            [*sums_of(half + first, count, token), up_both, *legendre, *previous],
+            [(count, channels, LANES)] * 2 + [(2 * channels + STATS, rows)], 18, weight=WEIGHT[3][u],
         )
         branches[u] = mine
         with jax.named_scope("branch_x"):
@@ -690,17 +693,17 @@
         return rec
 
     def do_series(token):
-        count = len(read_units)
+        count = len(back_units)
         return one_call(
-            functools.partial(series_grad_kernel, read_units, full_width), struct(series.shape),
+            functools.partial(series_grad_kernel, back_units, full_width), struct(series.shape),
             [grad_out, series, state["squares"], state["small"], after(state["small_rec"], token)]
             + [backs[u][0] for u in range(count)] + [backs[u][1] for u in range(count)],
         )
 
     def do_layer(token):
-        count = len(rank_units)
+        count = len(mix_units)
         return one_call(
-            functools.partial(layer_kernel, rank_units), struct(series.shape),
+            functools.partial(layer_kernel, mix_units), struct(series.shape),
             [after(series, token)] + [branches[u] for u in range(count)] + [kept[u] for u in range(count)],
         )
 
@@ -722,10 +725,10 @@
             out = do_read(u, token)
         elif name == "K":
             out = do_rank(u, token)
-        elif name in ("hm", "zm"):
-            out = do_join(name[0], u, middle, token)
-        elif name in ("ho", "zo"):
-            out = do_join(name[0], u, outward, token)
+        elif name == "e":
+            out = do_swap(u, token)
+        elif name == "m":
+            out = do_cross(u, token)
         elif name == "B":
             out = do_back(u, token)
         elif name == "M":
@@ -733,7 +736,7 @@
         elif name == "st":
             with jax.named_scope("stats_z"):
                 if u == 1:
-                    out = jnp.concatenate([state["grad_mix"][2 * channels :]] + [backs[k][2].reshape(-1, 256) for k in range(len(read_units))], axis=0)
+                    out = jnp.concatenate([state["grad_mix"][2 * channels :]] + [backs[k][2].reshape(-1, 256) for k in range(len(back_units))], axis=0)
                 else:
                     out = state["small"] + after(state["small_rec"], token)
                 state["small"], state["small_rec"] = out, swap(out, "order", 1 << u)

time: 130 us -> 117 us (0.900)
  waiting for transfers between devices: 51.7 us -> 40.2 us
  Pallas kernels: 32.2 us -> 30.2 us
    ppermute x15 -> x29, starting transfers between devices: 20.1 us -> 44.2 us  [swap(): return lax.ppermute(x, axis, [(i, i ^ bit) for i in range(size)])]
    ppermute x12 -> x8, starting transfers between devices: 23.6 us -> 0.57 us  [cross(): return lax.ppermute(x, ('batch', 'order'), pairs)]
    ppermute x12 -> x8, waiting for transfers between devices: 21.8 us -> 0.02 us  [cross(): return lax.ppermute(x, ('batch', 'order'), pairs)]
    ppermute x15 -> x29, waiting for transfers between devices: 29.9 us -> 40.2 us  [swap(): return lax.ppermute(x, axis, [(i, i ^ bit) for i in range(size)])]
    pallas_call x9 -> x11, Pallas kernels: 24.8 us -> 22.9 us  [the longest x10 20.3 us: unit_call(): pl.pallas_call(kernel, out_shape=[struct(shape) for shape in outs], in_sp...]
  transfers between devices with their start and end apart: 27 -> 37, of which waited for: 17 -> 19; matrix products, arithmetic and copies ran while one was open for 0% -> 1% of each run, Pallas kernels for 22% -> 23%
where the time goes in v3:
time: 117 us
  starting transfers between devices  44.7 us (38%)
  waiting for transfers between devices  40.2 us (34%)
  Pallas kernels  30.2 us (26%)
  between operations  1.21 us (1%)
    ppermute x29, starting transfers between devices, swap(): return lax.ppermute(x, axis, [(i, i ^ bit) for i in range(size)])  44.2 us
    ppermute x29, waiting for transfers between devices, swap(): return lax.ppermute(x, axis, [(i, i ^ bit) for i in range(size)])  40.2 us
    pallas_call x10, Pallas kernels, unit_call(): pl.pallas_call(kernel, out_shape=[struct(shape) for shape in outs], in_sp...  20.3 us
    pallas_call x4, Pallas kernels, one_call(): pl.pallas_call(kernel, out_shape=shapes, in_specs=specs, out_specs=[whole...  5.35 us
    pallas_call x1, Pallas kernels, front(): pl.pallas_call(functools.partial(front_kernel, units, line_length), out_s...  2.58 us
  transfers between devices with their start and end apart: 37, of which 19 were waited for; matrix products, arithmetic and copies ran while one was open for 1% of the time, Pallas kernels for 23%

profile of v3, /device:TPU:0, one launch (start us, length us, event | category | flops | bytes accessed | tf_op | source)
XLA Modules:
  0.0 117.3 jit_solution(2434990919065761969)
XLA Ops:
  0.7 2.6 %shard_map.136 = (f32[56,768]{1,0:T(8,128)S(1)}, f32[8,256]{1,0:T(8,128)S(1)}, f32[4,64,768]{2,1,0:T(8,128)S(1)}, f32[2,64,768]{2,1,0:T(8,128)S(1)}, f32[2,64,768]{2,1,0:T(8,128)S(1)}) custom-call(s32[8]{0:T(128)} %len_ref.9, f32[2,32,4,64]{3,2,1,0:T(4,128)} %in_ref.1, f32[2,32,4,64]{3,2,1,0:T(4,128)} %out_hbm.1, f32[1,64]{1,0:T(1,128)} %bitcast.8, ...), custom_call_target="tpu_custom_call" | custom-call | flops 1474560 | bytes 2949120 | tf_op jit(solution)/shard_map/pallas_call | solution.py:453
  3.2 3.0 %collective-permute-start = (f32[56,768]{1,0:T(8,128)S(1)}, f32[56,768]{1,0:T(8,128)S(1)}, u32[]{:S(2)}, u32[]{:S(2)}) collective-permute-start(f32[56,768]{1,0:T(8,128)S(1)} %get-tuple-element.102.own_ref), channel_id=1, source_target_pairs={{0,1},{1,0},{2,3},{3,2},{4,5},{5,4},{6,7},{7,6},{8,9},{9,8},{10,11... | collective-permute-start | bytes 516104 | tf_op jit(solution)/shard_map/message_x/ppermute | solution.py:509
  6.3 2.0 %shard_map.137 = (f32[4,64,768]{2,1,0:T(8,128)S(1)}, f32[1,64,768]{2,1,0:T(8,128)S(1)}, f32[1,64,768]{2,1,0:T(8,128)S(1)}, f32[2,64,768]{2,1,0:T(8,128)S(1)}) custom-call(s32[8]{0:T(128)} %len_ref.9, f32[64,5760]{1,0:T(8,128)} %cot_ref.1), custom_call_target="tpu_custom_call" | custom-call | flops 1474560 | bytes 2949120 | tf_op jit(solution)/shard_map/pallas_call | solution.py:469
  8.3 2.7 %collective-permute-done.rec_ref = f32[56,768]{1,0:T(8,128)S(1)} collective-permute-done((f32[56,768]{1,0:T(8,128)S(1)}, f32[56,768]{1,0:T(8,128)S(1)}, u32[]{:S(2)}, u32[]{:S(2)}) %collective-permute-start) | collective-permute-done | bytes 172064 | tf_op jit(solution)/shard_map/message_x/ppermute | solution.py:509
  11.0 1.8 %collective-permute-start.5 = (f32[8,768]{1,0:T(8,128)S(1)}, f32[8,768]{1,0:T(8,128)S(1)}, u32[]{:S(2)}, u32[]{:S(2)}) collective-permute-start(f32[8,768]{1,0:T(8,128)S(1)} %slice_add_fusion), channel_id=1, source_target_pairs={{0,2},{1,3},{2,0},{3,1},{4,6},{5,7},{6,4},{7,5},{8,10},{9,11},{10,... | collective-permute-start | bytes 73736 | tf_op jit(solution)/shard_map/squares_z1/ppermute | solution.py:509
  12.8 2.3 %collective-permute-start.8 = (f32[1,64,768]{2,1,0:T(8,128)S(1)}, f32[1,64,768]{2,1,0:T(8,128)S(1)}, u32[]{:S(2)}, u32[]{:S(2)}) collective-permute-start(f32[1,64,768]{2,1,0:T(8,128)S(1)} %get-tuple-element.119), channel_id=1, source_target_pairs={{0,1},{1,0},{2,3},{3,2},{4,5},{5,4},{6,7},{7,6},{8,9},{9,8},{10,11... | collective-permute-start | bytes 589832 | tf_op jit(solution)/shard_map/cot_x/ppermute | solution.py:509
  15.1 2.0 %collective-permute-start.2 = (f32[2,64,768]{2,1,0:T(8,128)S(1)}, f32[2,64,768]{2,1,0:T(8,128)S(1)}, u32[]{:S(2)}, u32[]{:S(2)}) collective-permute-start(f32[2,64,768]{2,1,0:T(8,128)S(1)} %get-tuple-element.109), channel_id=1, source_target_pairs={{0,1},{1,0},{2,3},{3,2},{4,5},{5,4},{6,7},{7,6},{8,9},{9,8},{10,11... | collective-permute-start | bytes 1179656 | tf_op jit(solution)/shard_map/ser_x/ppermute | solution.py:509
  17.4 2.7 %collective-permute-start.7 = (f32[8,768]{1,0:T(8,128)S(1)}, f32[8,768]{1,0:T(8,128)S(1)}, u32[]{:S(2)}, u32[]{:S(2)}) collective-permute-start(f32[8,768]{1,0:T(8,128)S(1)} %add.70), channel_id=1, source_target_pairs={{0,4},{1,5},{2,6},{3,7},{4,0},{5,1},{6,2},{7,3},{8,12},{9,13},{10,... | collective-permute-start | bytes 73736 | tf_op jit(solution)/shard_map/squares_z2/ppermute | solution.py:509
  24.0 4.7 %collective-permute-done.6 = f32[256,256]{1,0:T(8,128)S(1)} collective-permute-done((f32[256,256]{1,0:T(8,128)S(1)}, f32[256,256]{1,0:T(8,128)S(1)}, u32[]{:S(2)}, u32[]{:S(2)}) %collective-permute-start.6) | collective-permute-done | bytes 262176 | tf_op jit(solution)/shard_map/e0/ppermute | solution.py:509
  33.5 3.2 %collective-permute-start.13 = (f32[256,256]{1,0:T(8,128)S(1)}, f32[256,256]{1,0:T(8,128)S(1)}, u32[]{:S(2)}, u32[]{:S(2)}) collective-permute-start(f32[256,256]{1,0:T(8,128)S(1)} %add_select_fusion.4.refs_0_), channel_id=1, source_target_pairs={{0,2},{1,3},{2,0},{3,1},{4,6},{5,7},{6,4},{7,5},{8,10},{9,11},{10,... | collective-permute-start | bytes 786440 | tf_op jit(solution)/shard_map/e3/ppermute | solution.py:509
  36.7 3.1 %collective-permute-done.9 = f32[256,256]{1,0:T(8,128)S(1)} collective-permute-done((f32[256,256]{1,0:T(8,128)S(1)}, f32[256,256]{1,0:T(8,128)S(1)}, u32[]{:S(2)}, u32[]{:S(2)}) %collective-permute-start.9) | collective-permute-done | bytes 262176 | tf_op jit(solution)/shard_map/e2/ppermute | solution.py:509
  39.9 2.1 %shard_map.142 = (f32[256,256]{1,0:T(8,128)S(1)}, f32[256,256]{1,0:T(8,128)S(1)}) custom-call(f32[4,64,768]{2,1,0:T(8,128)S(1)} %get-tuple-element.100.own_ref.ser_own, f32[2,64,768]{2,1,0:T(8,128)S(1)} %collective-permute-done.2.rec_ref.ser_rec, f32[8,768]{1,0:T(8,128)S(1)} %add.71.ss_ref.refs_4_, bf16[256,192]{1,0:T(8,128)(2,1)S(1)} %get-tuple-element.132.down_own, ...), custom_call_target="tpu_custom_call" | custom-call | flops 14092861440 | bytes 21872640 | tf_op jit(solution)/shard_map/pallas_call | solution.py:496
  44.6 3.6 %collective-permute-start.17 = (f32[256,256]{1,0:T(8,128)S(1)}, f32[256,256]{1,0:T(8,128)S(1)}, u32[]{:S(2)}, u32[]{:S(2)}) collective-permute-start(f32[256,256]{1,0:T(8,128)S(1)} %add_select_fusion.2.refs_0_), channel_id=1, source_target_pairs={{0,2},{1,3},{2,0},{3,1},{4,6},{5,7},{6,4},{7,5},{8,10},{9,11},{10,... | collective-permute-start | bytes 786440 | tf_op jit(solution)/shard_map/e5/ppermute | solution.py:509
  48.2 3.1 %collective-permute-done.15.refs_3_ = f32[256,256]{1,0:T(8,128)S(1)} collective-permute-done((f32[256,256]{1,0:T(8,128)S(1)}, f32[256,256]{1,0:T(8,128)S(1)}, u32[]{:S(2)}, u32[]{:S(2)}) %collective-permute-start.15) | collective-permute-done | bytes 262176 | tf_op jit(solution)/shard_map/e4/ppermute | solution.py:509
  51.4 2.1 %shard_map.143 = (f32[256,256]{1,0:T(8,128)S(1)}, f32[256,256]{1,0:T(8,128)S(1)}) custom-call(f32[4,64,768]{2,1,0:T(8,128)S(1)} %get-tuple-element.100.own_ref.ser_own, f32[2,64,768]{2,1,0:T(8,128)S(1)} %collective-permute-done.1.rec_ref.ser_rec, f32[8,768]{1,0:T(8,128)S(1)} %add.71.ss_ref.refs_4_, bf16[256,192]{1,0:T(8,128)(2,1)S(1)} %get-tuple-element.132.down_own, ...), custom_call_target="tpu_custom_call" | custom-call | flops 14092861440 | bytes 21872640 | tf_op jit(solution)/shard_map/pallas_call | solution.py:496
  53.6 3.2 %collective-permute-start.22 = (f32[256,256]{1,0:T(8,128)S(1)}, f32[256,256]{1,0:T(8,128)S(1)}, u32[]{:S(2)}, u32[]{:S(2)}) collective-permute-start(f32[256,256]{1,0:T(8,128)S(1)} %add_select_fusion.1.refs_1_), channel_id=1, source_target_pairs={{0,2},{1,3},{2,0},{3,1},{4,6},{5,7},{6,4},{7,5},{8,10},{9,11},{10,... | collective-permute-start | bytes 786440 | tf_op jit(solution)/shard_map/e6/ppermute | solution.py:509
  56.9 3.7 %shard_map.144 = (f32[2,64,768]{2,1,0:T(8,128)S(1)}, f32[2,64,768]{2,1,0:T(8,128)S(1)}, f32[128,256]{1,0:T(8,128)S(1)}, f32[2,8,256]{2,1,0:T(8,128)S(1)}) custom-call(s32[8]{0:T(128)S(1)} %copy-done.3, f32[4,64,768]{2,1,0:T(8,128)S(1)} %get-tuple-element.100.own_ref.ser_own, f32[2,64,768]{2,1,0:T(8,128)S(1)} %collective-permute-done.2.rec_ref.ser_rec, ...), custom_call_target="tpu_custom_call" | custom-call | flops 16106127360 | bytes 31703040 | tf_op jit(solution)/shard_map/pallas_call | solution.py:496
  60.6 2.1 %collective-permute-start.18 = (f32[2,64,768]{2,1,0:T(8,128)S(1)}, f32[2,64,768]{2,1,0:T(8,128)S(1)}, u32[]{:S(2)}, u32[]{:S(2)}) collective-permute-start(f32[2,64,768]{2,1,0:T(8,128)S(1)} %get-tuple-element.147), channel_id=1, source_target_pairs={{0,1},{1,0},{2,3},{3,2},{4,5},{5,4},{6,7},{7,6},{8,9},{9,8},{10,11... | collective-permute-start | bytes 1179656 | tf_op jit(solution)/shard_map/scaled_x/ppermute | solution.py:509
  62.8 1.9 %collective-permute-start.20 = (f32[256,256]{1,0:T(8,128)S(1)}, f32[256,256]{1,0:T(8,128)S(1)}, u32[]{:S(2)}, u32[]{:S(2)}) collective-permute-start(f32[256,256]{1,0:T(8,128)S(1)} %add_select_fusion.refs_0_), channel_id=1, source_target_pairs={{0,2},{1,3},{2,0},{3,1},{4,6},{5,7},{6,4},{7,5},{8,10},{9,11},{10,... | collective-permute-start | bytes 786440 | tf_op jit(solution)/shard_map/e7/ppermute | solution.py:509
  64.9 2.1 %collective-permute-start.25 = (f32[256,256]{1,0:T(8,128)S(1)}, f32[256,256]{1,0:T(8,128)S(1)}, u32[]{:S(2)}, u32[]{:S(2)}) collective-permute-start(f32[256,256]{1,0:T(8,128)S(1)} %add.84.refs_1_), channel_id=1, source_target_pairs={{0,2},{1,3},{2,0},{3,1},{4,6},{5,7},{6,4},{7,5},{8,10},{9,11},{10,... | collective-permute-start | bytes 786440 | tf_op jit(solution)/shard_map/e8/ppermute | solution.py:509
  67.0 5.0 %collective-permute-done.20.refs_2_ = f32[256,256]{1,0:T(8,128)S(1)} collective-permute-done((f32[256,256]{1,0:T(8,128)S(1)}, f32[256,256]{1,0:T(8,128)S(1)}, u32[]{:S(2)}, u32[]{:S(2)}) %collective-permute-start.20) | collective-permute-done | bytes 262176 | tf_op jit(solution)/shard_map/e7/ppermute | solution.py:509
  72.5 3.9 %shard_map.145 = (f32[2,64,768]{2,1,0:T(8,128)S(1)}, f32[2,64,768]{2,1,0:T(8,128)S(1)}, f32[128,256]{1,0:T(8,128)S(1)}, f32[2,8,256]{2,1,0:T(8,128)S(1)}) custom-call(s32[8]{0:T(128)S(1)} %copy-done.3, f32[4,64,768]{2,1,0:T(8,128)S(1)} %get-tuple-element.100.own_ref.ser_own, f32[2,64,768]{2,1,0:T(8,128)S(1)} %collective-permute-done.1.rec_ref.ser_rec, ...), custom_call_target="tpu_custom_call" | custom-call | flops 16106127360 | bytes 33013760 | tf_op jit(solution)/shard_map/pallas_call | solution.py:496
  76.4 1.8 %collective-permute-start.27 = (f32[2,64,768]{2,1,0:T(8,128)S(1)}, f32[2,64,768]{2,1,0:T(8,128)S(1)}, u32[]{:S(2)}, u32[]{:S(2)}) collective-permute-start(f32[2,64,768]{2,1,0:T(8,128)S(1)} %get-tuple-element.164), channel_id=1, source_target_pairs={{0,1},{1,0},{2,3},{3,2},{4,5},{5,4},{6,7},{7,6},{8,9},{9,8},{10,11... | collective-permute-start | bytes 1179656 | tf_op jit(solution)/shard_map/scaled_x/ppermute | solution.py:509
  78.5 2.5 %shard_map.146 = (f32[2,64,768]{2,1,0:T(8,128)S(1)}, f32[2,64,768]{2,1,0:T(8,128)S(1)}, f32[136,256]{1,0:T(8,128)S(1)}) custom-call(s32[8]{0:T(128)S(1)} %copy-done.3, f32[4,64,768]{2,1,0:T(8,128)S(1)} %get-tuple-element.100.own_ref.ser_own, f32[2,64,768]{2,1,0:T(8,128)S(1)} %collective-permute-done.2.rec_ref.ser_rec, ...), custom_call_target="tpu_custom_call" | custom-call | flops 12079595520 | bytes 35389440 | tf_op jit(solution)/shard_map/pallas_call | solution.py:496
  81.0 2.1 %collective-permute-start.30 = (f32[2,64,768]{2,1,0:T(8,128)S(1)}, f32[2,64,768]{2,1,0:T(8,128)S(1)}, u32[]{:S(2)}, u32[]{:S(2)}) collective-permute-start(f32[2,64,768]{2,1,0:T(8,128)S(1)} %get-tuple-element.172), channel_id=1, source_target_pairs={{0,1},{1,0},{2,3},{3,2},{4,5},{5,4},{6,7},{7,6},{8,9},{9,8},{10,11... | collective-permute-start | bytes 1179656 | tf_op jit(solution)/shard_map/branch_x/ppermute | solution.py:509
  83.2 4.3 %collective-permute-done.28.refs_1_ = f32[256,256]{1,0:T(8,128)S(1)} collective-permute-done((f32[256,256]{1,0:T(8,128)S(1)}, f32[256,256]{1,0:T(8,128)S(1)}, u32[]{:S(2)}, u32[]{:S(2)}) %collective-permute-start.28) | collective-permute-done | bytes 262176 | tf_op jit(solution)/shard_map/e9/ppermute | solution.py:509
  89.1 2.5 %collective-permute-done.26.refs_1_ = f32[256,256]{1,0:T(8,128)S(1)} collective-permute-done((f32[256,256]{1,0:T(8,128)S(1)}, f32[256,256]{1,0:T(8,128)S(1)}, u32[]{:S(2)}, u32[]{:S(2)}) %collective-permute-start.26) | collective-permute-done | bytes 262176 | tf_op jit(solution)/shard_map/e10/ppermute | solution.py:509
  94.2 2.6 %collective-permute-done.30.refs_3_ = f32[2,64,768]{2,1,0:T(8,128)S(1)} collective-permute-done((f32[2,64,768]{2,1,0:T(8,128)S(1)}, f32[2,64,768]{2,1,0:T(8,128)S(1)}, u32[]{:S(2)}, u32[]{:S(2)}) %collective-permute-start.30) | collective-permute-done | bytes 393248 | tf_op jit(solution)/shard_map/branch_x/ppermute | solution.py:509
  99.5 1.8 %collective-permute-done.32.refs_4_ = f32[1,64,768]{2,1,0:T(8,128)S(1)} collective-permute-done((f32[1,64,768]{2,1,0:T(8,128)S(1)}, f32[1,64,768]{2,1,0:T(8,128)S(1)}, u32[]{:S(2)}, u32[]{:S(2)}) %collective-permute-start.32) | collective-permute-done | bytes 196640 | tf_op jit(solution)/shard_map/branch_x/ppermute | solution.py:509
  104.0 2.3 %collective-permute-done.33.refs_5_ = f32[1,64,768]{2,1,0:T(8,128)S(1)} collective-permute-done((f32[1,64,768]{2,1,0:T(8,128)S(1)}, f32[1,64,768]{2,1,0:T(8,128)S(1)}, u32[]{:S(2)}, u32[]{:S(2)}) %collective-permute-start.33) | collective-permute-done | bytes 196640 | tf_op jit(solution)/shard_map/branch_x/ppermute | solution.py:509
  111.3 2.5 %shard_map.150 = f32[64,5760]{1,0:T(8,128)} custom-call(f32[64,5760]{1,0:T(8,128)S(1)} %copy-done.1, f32[64,5760]{1,0:T(8,128)S(1)} %copy-done, f32[8,768]{1,0:T(8,128)S(1)} %add.71.ss_ref.refs_4_, f32[40,256]{1,0:T(8,128)S(1)} %add.89.in_own, f32[40,256]{1,0:T(8,128)S(1)} %slice.33.in_rec, f32[2,64,768]{2,1,0:T(8,128)S(1)} %get-tuple-element.187.refs_0_, ...), custom_call_target="tpu_custom_call" | custom-call | flops 6103040 | bytes 6103040 | tf_op jit(solution)/shard_map/pallas_call | solution.py:420
  113.8 2.3 %collective-permute-done.36.rec_ref = f32[168,256]{1,0:T(8,128)S(1)} collective-permute-done((f32[168,256]{1,0:T(8,128)S(1)}, f32[168,256]{1,0:T(8,128)S(1)}, u32[]{:S(2)}, u32[]{:S(2)}) %collective-permute-start.36) | collective-permute-done | bytes 172064 | tf_op jit(solution)/shard_map/grads_y/ppermute | solution.py:509
  (105 shorter events, 28.8 us)
Async XLA Ops:
  3.2 7.8 %collective-permute-start = (f32[56,768]{1,0:T(8,128)S(1)}, f32[56,768]{1,0:T(8,128)S(1)}, u32[]{:S(2)}, u32[]{:S(2)}) collective-permute-start(f32[56,768]{1,0:T(8,128)S(1)} %get-tuple-element.102.own_ref), channel_id=1, source_target_pairs={{0,1},{1,0},{2,3},{3,2},{4,5},{5,4},{6,7},{7,6},{8,9},{9,8},{10,11... | collective-permute-start | bytes 516104 | tf_op jit(solution)/shard_map/message_x/ppermute | solution.py:509
  8.2 11.8 %collective-permute-start.4 = (f32[1,64,768]{2,1,0:T(8,128)S(1)}, f32[1,64,768]{2,1,0:T(8,128)S(1)}, u32[]{:S(2)}, u32[]{:S(2)}) collective-permute-start(f32[1,64,768]{2,1,0:T(8,128)S(1)} %get-tuple-element.112), channel_id=1, source_target_pairs={{0,1},{1,0},{2,3},{3,2},{4,5},{5,4},{6,7},{7,6},{8,9},{9,8},{10,11... | collective-permute-start | bytes 589832 | tf_op jit(solution)/shard_map/cot_x/ppermute | solution.py:509
  11.0 6.3 %collective-permute-start.5 = (f32[8,768]{1,0:T(8,128)S(1)}, f32[8,768]{1,0:T(8,128)S(1)}, u32[]{:S(2)}, u32[]{:S(2)}) collective-permute-start(f32[8,768]{1,0:T(8,128)S(1)} %slice_add_fusion), channel_id=1, source_target_pairs={{0,2},{1,3},{2,0},{3,1},{4,6},{5,7},{6,4},{7,5},{8,10},{9,11},{10,... | collective-permute-start | bytes 73736 | tf_op jit(solution)/shard_map/squares_z1/ppermute | solution.py:509
  12.8 9.7 %collective-permute-start.8 = (f32[1,64,768]{2,1,0:T(8,128)S(1)}, f32[1,64,768]{2,1,0:T(8,128)S(1)}, u32[]{:S(2)}, u32[]{:S(2)}) collective-permute-start(f32[1,64,768]{2,1,0:T(8,128)S(1)} %get-tuple-element.119), channel_id=1, source_target_pairs={{0,1},{1,0},{2,3},{3,2},{4,5},{5,4},{6,7},{7,6},{8,9},{9,8},{10,11... | collective-permute-start | bytes 589832 | tf_op jit(solution)/shard_map/cot_x/ppermute | solution.py:509
  15.1 14.2 %collective-permute-start.3 = (f32[2,64,768]{2,1,0:T(8,128)S(1)}, f32[2,64,768]{2,1,0:T(8,128)S(1)}, u32[]{:S(2)}, u32[]{:S(2)}) collective-permute-start(f32[2,64,768]{2,1,0:T(8,128)S(1)} %get-tuple-element.111), channel_id=1, source_target_pairs={{0,1},{1,0},{2,3},{3,2},{4,5},{5,4},{6,7},{7,6},{8,9},{9,8},{10,11... | collective-permute-start | bytes 1179656 | tf_op jit(solution)/shard_map/cot_x/ppermute | solution.py:509
  15.1 24.8 %collective-permute-start.2 = (f32[2,64,768]{2,1,0:T(8,128)S(1)}, f32[2,64,768]{2,1,0:T(8,128)S(1)}, u32[]{:S(2)}, u32[]{:S(2)}) collective-permute-start(f32[2,64,768]{2,1,0:T(8,128)S(1)} %get-tuple-element.109), channel_id=1, source_target_pairs={{0,1},{1,0},{2,3},{3,2},{4,5},{5,4},{6,7},{7,6},{8,9},{9,8},{10,11... | collective-permute-start | bytes 1179656 | tf_op jit(solution)/shard_map/ser_x/ppermute | solution.py:509
  20.9 7.8 %collective-permute-start.6 = (f32[256,256]{1,0:T(8,128)S(1)}, f32[256,256]{1,0:T(8,128)S(1)}, u32[]{:S(2)}, u32[]{:S(2)}) collective-permute-start(f32[256,256]{1,0:T(8,128)S(1)} %shard_map.139), channel_id=1, source_target_pairs={{0,2},{1,3},{2,0},{3,1},{4,6},{5,7},{6,4},{7,5},{8,10},{9,11},{10,... | collective-permute-start | bytes 786440 | tf_op jit(solution)/shard_map/e0/ppermute | solution.py:509
  23.4 9.9 %collective-permute-start.11 = (f32[256,256]{1,0:T(8,128)S(1)}, f32[256,256]{1,0:T(8,128)S(1)}, u32[]{:S(2)}, u32[]{:S(2)}) collective-permute-start(f32[256,256]{1,0:T(8,128)S(1)} %shard_map.140), channel_id=1, source_target_pairs={{0,2},{1,3},{2,0},{3,1},{4,6},{5,7},{6,4},{7,5},{8,10},{9,11},{10,... | collective-permute-start | bytes 786440 | tf_op jit(solution)/shard_map/e1/ppermute | solution.py:509
  30.5 9.2 %collective-permute-start.9 = (f32[256,256]{1,0:T(8,128)S(1)}, f32[256,256]{1,0:T(8,128)S(1)}, u32[]{:S(2)}, u32[]{:S(2)}) collective-permute-start(f32[256,256]{1,0:T(8,128)S(1)} %get-tuple-element.126), channel_id=1, source_target_pairs={{0,2},{1,3},{2,0},{3,1},{4,6},{5,7},{6,4},{7,5},{8,10},{9,11},{10,... | collective-permute-start | bytes 786440 | tf_op jit(solution)/shard_map/e2/ppermute | solution.py:509
  31.9 19.5 %collective-permute-start.1 = (f32[2,64,768]{2,1,0:T(8,128)S(1)}, f32[2,64,768]{2,1,0:T(8,128)S(1)}, u32[]{:S(2)}, u32[]{:S(2)}) collective-permute-start(f32[2,64,768]{2,1,0:T(8,128)S(1)} %get-tuple-element.106), channel_id=1, source_target_pairs={{0,1},{1,0},{2,3},{3,2},{4,5},{5,4},{6,7},{7,6},{8,9},{9,8},{10,11... | collective-permute-start | bytes 1179656 | tf_op jit(solution)/shard_map/ser_x/ppermute | solution.py:509
  33.3 8.7 %collective-permute-start.14 = (f32[256,256]{1,0:T(8,128)S(1)}, f32[256,256]{1,0:T(8,128)S(1)}, u32[]{:S(2)}, u32[]{:S(2)}) collective-permute-start(f32[256,256]{1,0:T(8,128)S(1)} %add.73), channel_id=1, source_target_pairs={{0,8},{1,9},{2,4},{3,5},{4,2},{5,3},{6,14},{7,15},{8,0},{9,1},{10,... | collective-permute-start | bytes 786440 | tf_op jit(solution)/shard_map/m1/ppermute | solution.py:533
  33.5 10.9 %collective-permute-start.13 = (f32[256,256]{1,0:T(8,128)S(1)}, f32[256,256]{1,0:T(8,128)S(1)}, u32[]{:S(2)}, u32[]{:S(2)}) collective-permute-start(f32[256,256]{1,0:T(8,128)S(1)} %add_select_fusion.4.refs_0_), channel_id=1, source_target_pairs={{0,2},{1,3},{2,0},{3,1},{4,6},{5,7},{6,4},{7,5},{8,10},{9,11},{10,... | collective-permute-start | bytes 786440 | tf_op jit(solution)/shard_map/e3/ppermute | solution.py:509
  42.1 9.2 %collective-permute-start.15 = (f32[256,256]{1,0:T(8,128)S(1)}, f32[256,256]{1,0:T(8,128)S(1)}, u32[]{:S(2)}, u32[]{:S(2)}) collective-permute-start(f32[256,256]{1,0:T(8,128)S(1)} %add_select_fusion.3.refs_1_), channel_id=1, source_target_pairs={{0,2},{1,3},{2,0},{3,1},{4,6},{5,7},{6,4},{7,5},{8,10},{9,11},{10,... | collective-permute-start | bytes 786440 | tf_op jit(solution)/shard_map/e4/ppermute | solution.py:509
  44.5 9.1 %collective-permute-start.16 = (f32[256,256]{1,0:T(8,128)S(1)}, f32[256,256]{1,0:T(8,128)S(1)}, u32[]{:S(2)}, u32[]{:S(2)}) collective-permute-start(f32[256,256]{1,0:T(8,128)S(1)} %add.77), channel_id=1, source_target_pairs={{0,8},{1,9},{2,4},{3,5},{4,2},{5,3},{6,14},{7,15},{8,0},{9,1},{10,... | collective-permute-start | bytes 786440 | tf_op jit(solution)/shard_map/m3/ppermute | solution.py:533
  44.6 12.2 %collective-permute-start.17 = (f32[256,256]{1,0:T(8,128)S(1)}, f32[256,256]{1,0:T(8,128)S(1)}, u32[]{:S(2)}, u32[]{:S(2)}) collective-permute-start(f32[256,256]{1,0:T(8,128)S(1)} %add_select_fusion.2.refs_0_), channel_id=1, source_target_pairs={{0,2},{1,3},{2,0},{3,1},{4,6},{5,7},{6,4},{7,5},{8,10},{9,11},{10,... | collective-permute-start | bytes 786440 | tf_op jit(solution)/shard_map/e5/ppermute | solution.py:509
  51.3 11.4 %collective-permute-start.19 = (f32[256,256]{1,0:T(8,128)S(1)}, f32[256,256]{1,0:T(8,128)S(1)}, u32[]{:S(2)}, u32[]{:S(2)}) collective-permute-start(f32[256,256]{1,0:T(8,128)S(1)} %add.79), channel_id=1, source_target_pairs={{0,8},{1,9},{2,4},{3,5},{4,2},{5,3},{6,14},{7,15},{8,0},{9,1},{10,... | collective-permute-start | bytes 786440 | tf_op jit(solution)/shard_map/m4/ppermute | solution.py:533
  53.6 11.1 %collective-permute-start.22 = (f32[256,256]{1,0:T(8,128)S(1)}, f32[256,256]{1,0:T(8,128)S(1)}, u32[]{:S(2)}, u32[]{:S(2)}) collective-permute-start(f32[256,256]{1,0:T(8,128)S(1)} %add_select_fusion.1.refs_1_), channel_id=1, source_target_pairs={{0,2},{1,3},{2,0},{3,1},{4,6},{5,7},{6,4},{7,5},{8,10},{9,11},{10,... | collective-permute-start | bytes 786440 | tf_op jit(solution)/shard_map/e6/ppermute | solution.py:509
  56.8 8.0 %collective-permute-start.21 = (f32[256,256]{1,0:T(8,128)S(1)}, f32[256,256]{1,0:T(8,128)S(1)}, u32[]{:S(2)}, u32[]{:S(2)}) collective-permute-start(f32[256,256]{1,0:T(8,128)S(1)} %add.81), channel_id=1, source_target_pairs={{0,8},{1,9},{2,4},{3,5},{4,2},{5,3},{6,14},{7,15},{8,0},{9,1},{10,... | collective-permute-start | bytes 786440 | tf_op jit(solution)/shard_map/m5/ppermute | solution.py:533
  60.6 11.9 %collective-permute-start.18 = (f32[2,64,768]{2,1,0:T(8,128)S(1)}, f32[2,64,768]{2,1,0:T(8,128)S(1)}, u32[]{:S(2)}, u32[]{:S(2)}) collective-permute-start(f32[2,64,768]{2,1,0:T(8,128)S(1)} %get-tuple-element.147), channel_id=1, source_target_pairs={{0,1},{1,0},{2,3},{3,2},{4,5},{5,4},{6,7},{7,6},{8,9},{9,8},{10,11... | collective-permute-start | bytes 1179656 | tf_op jit(solution)/shard_map/scaled_x/ppermute | solution.py:509
  62.8 9.2 %collective-permute-start.20 = (f32[256,256]{1,0:T(8,128)S(1)}, f32[256,256]{1,0:T(8,128)S(1)}, u32[]{:S(2)}, u32[]{:S(2)}) collective-permute-start(f32[256,256]{1,0:T(8,128)S(1)} %add_select_fusion.refs_0_), channel_id=1, source_target_pairs={{0,2},{1,3},{2,0},{3,1},{4,6},{5,7},{6,4},{7,5},{8,10},{9,11},{10,... | collective-permute-start | bytes 786440 | tf_op jit(solution)/shard_map/e7/ppermute | solution.py:509
  64.8 13.4 %collective-permute-start.24 = (f32[256,256]{1,0:T(8,128)S(1)}, f32[256,256]{1,0:T(8,128)S(1)}, u32[]{:S(2)}, u32[]{:S(2)}) collective-permute-start(f32[256,256]{1,0:T(8,128)S(1)} %add.83), channel_id=1, source_target_pairs={{0,8},{1,9},{2,4},{3,5},{4,2},{5,3},{6,14},{7,15},{8,0},{9,1},{10,... | collective-permute-start | bytes 786440 | tf_op jit(solution)/shard_map/m6/ppermute | solution.py:533
  64.9 13.6 %collective-permute-start.25 = (f32[256,256]{1,0:T(8,128)S(1)}, f32[256,256]{1,0:T(8,128)S(1)}, u32[]{:S(2)}, u32[]{:S(2)}) collective-permute-start(f32[256,256]{1,0:T(8,128)S(1)} %add.84.refs_1_), channel_id=1, source_target_pairs={{0,2},{1,3},{2,0},{3,1},{4,6},{5,7},{6,4},{7,5},{8,10},{9,11},{10,... | collective-permute-start | bytes 786440 | tf_op jit(solution)/shard_map/e8/ppermute | solution.py:509
  72.0 11.1 %collective-permute-start.23 = (f32[256,256]{1,0:T(8,128)S(1)}, f32[256,256]{1,0:T(8,128)S(1)}, u32[]{:S(2)}, u32[]{:S(2)}) collective-permute-start(f32[256,256]{1,0:T(8,128)S(1)} %add.85), channel_id=1, source_target_pairs={{0,8},{1,9},{2,4},{3,5},{4,2},{5,3},{6,14},{7,15},{8,0},{9,1},{10,... | collective-permute-start | bytes 786440 | tf_op jit(solution)/shard_map/m7/ppermute | solution.py:533
  76.4 12.7 %collective-permute-start.27 = (f32[2,64,768]{2,1,0:T(8,128)S(1)}, f32[2,64,768]{2,1,0:T(8,128)S(1)}, u32[]{:S(2)}, u32[]{:S(2)}) collective-permute-start(f32[2,64,768]{2,1,0:T(8,128)S(1)} %get-tuple-element.164), channel_id=1, source_target_pairs={{0,1},{1,0},{2,3},{3,2},{4,5},{5,4},{6,7},{7,6},{8,9},{9,8},{10,11... | collective-permute-start | bytes 1179656 | tf_op jit(solution)/shard_map/scaled_x/ppermute | solution.py:509
  78.2 9.3 %collective-permute-start.28 = (f32[256,256]{1,0:T(8,128)S(1)}, f32[256,256]{1,0:T(8,128)S(1)}, u32[]{:S(2)}, u32[]{:S(2)}) collective-permute-start(f32[256,256]{1,0:T(8,128)S(1)} %add.86.refs_0_), channel_id=1, source_target_pairs={{0,2},{1,3},{2,0},{3,1},{4,6},{5,7},{6,4},{7,5},{8,10},{9,11},{10,... | collective-permute-start | bytes 786440 | tf_op jit(solution)/shard_map/e9/ppermute | solution.py:509
  81.0 15.8 %collective-permute-start.30 = (f32[2,64,768]{2,1,0:T(8,128)S(1)}, f32[2,64,768]{2,1,0:T(8,128)S(1)}, u32[]{:S(2)}, u32[]{:S(2)}) collective-permute-start(f32[2,64,768]{2,1,0:T(8,128)S(1)} %get-tuple-element.172), channel_id=1, source_target_pairs={{0,1},{1,0},{2,3},{3,2},{4,5},{5,4},{6,7},{7,6},{8,9},{9,8},{10,11... | collective-permute-start | bytes 1179656 | tf_op jit(solution)/shard_map/branch_x/ppermute | solution.py:509
  83.1 8.4 %collective-permute-start.26 = (f32[256,256]{1,0:T(8,128)S(1)}, f32[256,256]{1,0:T(8,128)S(1)}, u32[]{:S(2)}, u32[]{:S(2)}) collective-permute-start(f32[256,256]{1,0:T(8,128)S(1)} %add.87.refs_0_), channel_id=1, source_target_pairs={{0,2},{1,3},{2,0},{3,1},{4,6},{5,7},{6,4},{7,5},{8,10},{9,11},{10,... | collective-permute-start | bytes 786440 | tf_op jit(solution)/shard_map/e10/ppermute | solution.py:509
  93.5 7.8 %collective-permute-start.32 = (f32[1,64,768]{2,1,0:T(8,128)S(1)}, f32[1,64,768]{2,1,0:T(8,128)S(1)}, u32[]{:S(2)}, u32[]{:S(2)}) collective-permute-start(f32[1,64,768]{2,1,0:T(8,128)S(1)} %get-tuple-element.175), channel_id=1, source_target_pairs={{0,1},{1,0},{2,3},{3,2},{4,5},{5,4},{6,7},{7,6},{8,9},{9,8},{10,11... | collective-permute-start | bytes 589832 | tf_op jit(solution)/shard_map/branch_x/ppermute | solution.py:509
  97.2 5.2 %collective-permute-start.31 = (f32[40,256]{1,0:T(8,128)S(1)}, f32[40,256]{1,0:T(8,128)S(1)}, u32[]{:S(2)}, u32[]{:S(2)}) collective-permute-start(f32[40,256]{1,0:T(8,128)S(1)} %fusion.1), channel_id=1, source_target_pairs={{0,4},{1,5},{2,6},{3,7},{4,0},{5,1},{6,2},{7,3},{8,12},{9,13},{10,... | collective-permute-start | bytes 122888 | tf_op jit(solution)/shard_map/stats_z/ppermute | solution.py:509
  98.8 7.5 %collective-permute-start.33 = (f32[1,64,768]{2,1,0:T(8,128)S(1)}, f32[1,64,768]{2,1,0:T(8,128)S(1)}, u32[]{:S(2)}, u32[]{:S(2)}) collective-permute-start(f32[1,64,768]{2,1,0:T(8,128)S(1)} %get-tuple-element.182), channel_id=1, source_target_pairs={{0,1},{1,0},{2,3},{3,2},{4,5},{5,4},{6,7},{7,6},{8,9},{9,8},{10,11... | collective-permute-start | bytes 589832 | tf_op jit(solution)/shard_map/branch_x/ppermute | solution.py:509
  102.4 5.8 %collective-permute-start.34 = (f32[168,256]{1,0:T(8,128)S(1)}, f32[168,256]{1,0:T(8,128)S(1)}, u32[]{:S(2)}, u32[]{:S(2)}) collective-permute-start(f32[168,256]{1,0:T(8,128)S(1)} %pad_maximum_fusion.2), channel_id=1, source_target_pairs={{0,1},{1,0},{2,3},{3,2},{4,5},{5,4},{6,7},{7,6},{8,9},{9,8},{10,11... | collective-permute-start | bytes 516104 | tf_op jit(solution)/shard_map/grads_x/ppermute | solution.py:509
  109.7 6.5 %collective-permute-start.36 = (f32[168,256]{1,0:T(8,128)S(1)}, f32[168,256]{1,0:T(8,128)S(1)}, u32[]{:S(2)}, u32[]{:S(2)}) collective-permute-start(f32[168,256]{1,0:T(8,128)S(1)} %add.91.own_ref), channel_id=1, source_target_pairs={{0,16},{8,24},{16,0},{24,8},{1,17},{9,25},{17,1},{25,9},{2,18},{10... | collective-permute-start | bytes 516104 | tf_op jit(solution)/shard_map/grads_y/ppermute | solution.py:509
  (13 other events, 101.1 us)

commit v4 on v3

--- a/solution.py
+++ b/solution.py
@@ -354,7 +354,7 @@
 
 
 def inner_row(small_ref, j):
-    row = STATS * (1 + j)
+    row = STATS * j
     return jnp.concatenate([small_ref[row + p : row + p + 1, :] for p in range(LANES // 256)], axis=1)
 
 
@@ -374,10 +374,9 @@
         out_ref[:, at] = cot_ref[:, at] + inv * (scaled - x_ref[:, at] * shift)
 
 
-def close_kernel(share, own_ref, rec_ref, in_ref, gain_ref, grad_in_ref, grad_out_ref, grad_gain_ref, rms_ref):
+def close_kernel(sums_ref, in_ref, gain_ref, grad_in_ref, grad_out_ref, grad_gain_ref):
     modes, ranks, channels = in_ref.shape[1:]
-    sums = own_ref[...] + rec_ref[...]
-    into, mix, stats = sums[:channels].T, sums[channels : 2 * channels].T, sums[2 * channels : 2 * channels + STATS]
+    into, mix = sums_ref[:channels].T, sums_ref[channels : 2 * channels].T
     total = jnp.zeros((modes, channels), f32)
     read_real, read_imag = readout_columns(modes, channels)
     for r in range(ranks):
@@ -391,6 +390,10 @@
         grad_out_ref[0, :, r, :] = read_real * pieces[0] + read_imag * pieces[1]
         grad_out_ref[1, :, r, :] = read_imag * pieces[0] - read_real * pieces[1]
     grad_gain_ref[...] = jnp.sum(total, axis=0, keepdims=True)
+
+
+def rms_kernel(share, own_ref, rec_ref, rms_ref):
+    stats = own_ref[...] + rec_ref[...]
     rms = jnp.sqrt(stats * share / stats[3:4])
     for k in range(3):
         rms_ref[k] = rms[k, 0]
@@ -412,7 +415,7 @@
     return jax.ShapeDtypeStruct(shape, dtype)
 
 
-def one_call(kernel, outs, args, smem=0, scalars_out=0):
+def one_call(kernel, outs, args, smem=0, scalars_out=0, weight=1):
     single = not isinstance(outs, list)
     shapes = [outs] if single else outs
     specs = [SMEM] * smem + [whole(a.shape) for a in args[smem:]]
@@ -424,7 +427,7 @@
         out_specs=[whole(o.shape) for o in shapes[: len(shapes) - scalars_out]] + [SMEM] * scalars_out,
         grid=(1,),
         compiler_params=PARAMS,
-        cost_estimate=cost(moved, moved),
+        cost_estimate=cost(moved, moved, weight),
     )(*args)
     return result[0] if single else result
 
@@ -543,18 +546,20 @@
     return lax.optimization_barrier((x, *tokens))[0]
 
 
-WEIGHT = ((10,) * 4, (10,) * 4, (10,) * 4, (10,) * 4)
-COT = (1, 1, 2)
+WEIGHT = ((10,10,10,10),(10,10),(10,10),(10,10,10))
+COT = (1, 1, 1, 1)
 SER = (2, 2)
-READ = (1, 1, 2)
+READ = (1, 1, 1, 1)
 RANK = (2, 2)
 BACK = (2, 2)
 MIX = (2, 1, 1)
 LAG = 3
+EARLY = 2
 PLAN = (
-    "q", "R0", "e0", "R1", "e1", "Q", "m0", "R2", "e2", "m1", "e3", "m2", "K0", "e4", "m3", "e5",
-    "m4", "K1", "e6", "m5", "B0", "e7", "m6", "e8", "m7", "s0", "B1", "e9", "M0", "e10", "M1",
-    "s1", "M2", "st1", "b0", "st2", "b1", "se", "G", "F1", "gc", "gy", "F2",
+    "R0", "e0", "c2", "R1", "q", "e1", "c3", "x0", "m0", "R2", "e2", "Q", "m1", "R3", "x1", "e3",
+    "m2", "K0", "e4", "m3", "e5", "K1", "m4", "e6", "m5", "B0", "g0", "e7", "m6", "B1", "e8", "m7",
+    "i1", "g1", "e9", "s0", "M0", "y0", "e10", "i2", "s1", "M1", "ix", "y1", "M2", "G", "y2", "iy",
+    "b0", "gc", "b1", "gy", "F2", "ge", "st1", "b2", "CL", "st2", "F1",
 )
 
 
@@ -586,14 +591,12 @@
     cot_own, *cot_rec = deal(after(grad_out, message), lengths, cot_units)
     message_rec = after(message_rec, cot_own)
     with jax.named_scope("cot_x"):
-        cot_rec = [swap(c if u == 0 else after(c, message_rec), "order", 1) for u, c in enumerate(cot_rec)]
+        for u in range(EARLY):
+            cot_rec[u] = swap(cot_rec[u] if u == 0 else after(cot_rec[u], message_rec), "order", 1)
     down_own, down_rec, up_own, up_rec, down_both, up_both = prepare_weights(message, message_rec, windows, rows, channels)
     with jax.named_scope("squares_z1"):
         squares = message[:windows] + message_rec[:windows]
         squares_rec = swap(squares, "order", 2)
-    with jax.named_scope("ser_x"):
-        ser_rec = [swap(after(c, message_rec), "order", 1) for c in ser_rec]
-
     def windows_of(own, received, units, first, count):
         u, offset = locate(units, first)
         v, _ = locate(units, first + count - 1)
@@ -666,8 +669,7 @@
             [*sums_of(first, count, token), state["squares"], down_both, *legendre, phase, *previous],
             [(count, channels, LANES)] * 2 + [(2 * channels, rows), (count, STATS, 256)], 24, weight=WEIGHT[2][u],
         )
-        with jax.named_scope("scaled_x"):
-            backs[u] = (mine, swap(theirs, "order", 1), dots)
+        backs[u] = (mine, theirs, dots)
         return state["grad_in"]
 
     def do_mix(u, token):
@@ -679,15 +681,14 @@
             [*sums_of(half + first, count, token), up_both, *legendre, *previous],
             [(count, channels, LANES)] * 2 + [(2 * channels + STATS, rows)], 18, weight=WEIGHT[3][u],
         )
-        branches[u] = mine
-        with jax.named_scope("branch_x"):
-            kept[u] = swap(theirs, "order", 1)
+        branches[u], kept[u] = mine, theirs
         return state["grad_mix"]
 
     def do_grads(token):
-        grad_in, grad_mix, small = state["grad_in"], state["grad_mix"], state["small"]
-        state["own"] = jnp.concatenate([grad_in[:channels], grad_mix[:channels], small], axis=0)
-        rec = jnp.concatenate([grad_in[channels:], grad_mix[channels : 2 * channels], small], axis=0)
+        grad_in, grad_mix = state["grad_in"], state["grad_mix"]
+        stats = grad_mix[2 * channels :]
+        state["own"] = jnp.concatenate([grad_in[:channels], grad_mix[:channels], stats], axis=0)
+        rec = jnp.concatenate([grad_in[channels:], grad_mix[channels : 2 * channels], stats], axis=0)
         with jax.named_scope("grads_x"):
             state["rec"] = swap(after(rec, token), "order", 1)
         return rec
@@ -696,8 +697,8 @@
         count = len(back_units)
         return one_call(
             functools.partial(series_grad_kernel, back_units, full_width), struct(series.shape),
-            [grad_out, series, state["squares"], state["small"], after(state["small_rec"], token)]
-            + [backs[u][0] for u in range(count)] + [backs[u][1] for u in range(count)],
+            [grad_out, series, state["squares"], state["inner"], after(state["inner_rec"], token)]
+            + [backs[u][0] for u in range(count)] + [backs[u][1] for u in range(count)], weight=0.01,
         )
 
     def do_layer(token):
@@ -714,6 +715,14 @@
             with jax.named_scope("squares_z2"):
                 out = state["squares"] + after(state["squares_rec"], token)
                 state["squares"] = add_over(out, "order", bits_of(order_devices, 4))
+        elif name == "g":
+            out = token
+            with jax.named_scope(f"scaled{u}"):
+                backs[u] = (backs[u][0], swap(after(backs[u][1], token), "order", 1), backs[u][2])
+        elif name == "y":
+            out = token
+            with jax.named_scope(f"branch{u}"):
+                kept[u] = swap(after(kept[u], token), "order", 1)
         elif name == "s":
             out = after(backs[u][1], token)
             backs[u] = (backs[u][0], out, backs[u][2])
@@ -725,6 +734,11 @@
             out = do_read(u, token)
         elif name == "K":
             out = do_rank(u, token)
+        elif name in ("c", "x"):
+            out, sent = token, cot_rec if name == "c" else ser_rec
+            if u < len(sent):
+                with jax.named_scope("cot_x" if name == "c" else "ser_x"):
+                    sent[u] = swap(after(sent[u], token), "order", 1)
         elif name == "e":
             out = do_swap(u, token)
         elif name == "m":
@@ -733,38 +747,57 @@
             out = do_back(u, token)
         elif name == "M":
             out = do_mix(u, token)
+        elif name == "i":
+            with jax.named_scope(f"inner_z{u}"):
+                if u == 1:
+                    out = [after(backs[k][2], token).reshape(-1, 256) for k in range(len(back_units))]
+                    out = jnp.concatenate(out, axis=0)
+                else:
+                    out = state["inner"] + after(state["inner_rec"], token)
+                state["inner"], state["inner_rec"] = out, swap(out, "order", 1 << u)
+        elif name == "ix":
+            with jax.named_scope("inner_x"):
+                out = state["inner"] + after(state["inner_rec"], token)
+                out = add_over(out, "order", bits_of(order_devices, 8))
+                state["inner"], state["inner_rec"] = out, swap(out, "order", 1)
+        elif name == "iy":
+            out = state["inner_rec"] = after(state["inner_rec"], token)
         elif name == "st":
-            with jax.named_scope("stats_z"):
+            with jax.named_scope(f"stats_z{u}"):
                 if u == 1:
-                    out = jnp.concatenate([state["grad_mix"][2 * channels :]] + [backs[k][2].reshape(-1, 256) for k in range(len(back_units))], axis=0)
+                    out = state["own"][2 * channels :]
                 else:
-                    out = state["small"] + after(state["small_rec"], token)
-                state["small"], state["small_rec"] = out, swap(out, "order", 1 << u)
-        elif name == "se":
-            with jax.named_scope("stats_z"):
-                out = state["small"] + after(state["small_rec"], token)
-                state["small"] = out = add_over(out, "order", bits_of(order_devices, 8))
+                    out = state["stats"] + after(state["stats_rec"], token)
+                    out = add_over(out, "order", bits_of(order_devices // 2, 4))
+                step_bit = 2 if u == 1 else order_devices // 2
+                state["stats"], state["stats_rec"] = out, swap(out, "order", step_bit)
+        elif name == "CL":
+            state["close"] = one_call(
+                close_kernel, [struct(mode_in.shape), struct(mode_out.shape), struct((1, channels))],
+                [after(state["own"], token), mode_in, gain],
+            )
+            out = state["close"][0]
         elif name == "G":
             out = do_grads(token)
         elif name == "gc":
             with jax.named_scope("grads_core"):
-                rec = after(state["rec"], token)
-                state["small_rec"] = rec[2 * channels :]
-                out = state["own"] + rec
+                out = state["own"] + after(state["rec"], token)
                 state["own"], state["rec"] = out, swap(out, "batch", 1)
         elif name == "gy":
             with jax.named_scope("grads_y"):
                 out = state["own"] + after(state["rec"], token)
                 out = add_over(out, "batch", bits_of(lax.axis_size("batch") // 2, 2))
                 state["own"], state["rec"] = out, swap(out, "batch", lax.axis_size("batch") // 2)
+        elif name == "ge":
+            state["own"] = out = state["own"] + after(state["rec"], token)
         elif name == "F":
             out = state[step] = do_layer(token) if u == 1 else do_series(token)
         state["token"] = out
-    grad_mode_in, grad_mode_out, grad_gain, stream_rms = one_call(
-        functools.partial(close_kernel, order_devices / full_width),
-        [struct(mode_in.shape), struct(mode_out.shape), struct((1, channels)), struct((3,))],
-        [state["own"], after(state["rec"], state["token"]), mode_in, gain], scalars_out=1,
-    )
+    stream_rms = one_call(
+        functools.partial(rms_kernel, order_devices / full_width), [struct((3,))],
+        [state["stats"], after(state["stats_rec"], state["token"])], scalars_out=1,
+    )[0]
+    grad_mode_in, grad_mode_out, grad_gain = state["close"]
     return state["F1"], state["F2"], grad_gain.reshape(channels), grad_mode_in, grad_mode_out, stream_rms
 
 

time: 117 us -> 115 us (0.983)
  waiting for transfers between devices: 40.2 us -> 25.5 us
  starting transfers between devices: 44.7 us -> 55.7 us
    ppermute x29 -> x33, waiting for transfers between devices: 40.2 us -> 25.5 us  [swap(): return lax.ppermute(x, axis, [(i, i ^ bit) for i in range(size)])]
    ppermute x29 -> x33, starting transfers between devices: 44.2 us -> 55.1 us  [swap(): return lax.ppermute(x, axis, [(i, i ^ bit) for i in range(size)])]
    pallas_call x4 -> x5, Pallas kernels: 5.35 us -> 5.88 us  [one_call(): pl.pallas_call(kernel, out_shape=shapes, in_specs=specs, out_specs=[whole...]
    pallas_call x10 -> x11, Pallas kernels: 20.3 us -> 20.8 us  [unit_call(): pl.pallas_call(kernel, out_shape=[struct(shape) for shape in outs], in_sp...]
  transfers between devices with their start and end apart: 37 -> 41, of which waited for: 19 -> 14; matrix products, arithmetic and copies ran while one was open for 1% -> 1% of each run, Pallas kernels for 23% -> 24%
where the time goes in v4:
time: 115 us
  starting transfers between devices  55.7 us (48%)
  Pallas kernels  31.2 us (27%)
  waiting for transfers between devices  25.5 us (22%)
  between operations  1.23 us (1%)
    ppermute x33, starting transfers between devices, swap(): return lax.ppermute(x, axis, [(i, i ^ bit) for i in range(size)])  55.1 us
    ppermute x33, waiting for transfers between devices, swap(): return lax.ppermute(x, axis, [(i, i ^ bit) for i in range(size)])  25.5 us
    pallas_call x11, Pallas kernels, unit_call(): pl.pallas_call(kernel, out_shape=[struct(shape) for shape in outs], in_sp...  20.8 us
    pallas_call x5, Pallas kernels, one_call(): pl.pallas_call(kernel, out_shape=shapes, in_specs=specs, out_specs=[whole...  5.88 us
    pallas_call x1, Pallas kernels, front(): pl.pallas_call(functools.partial(front_kernel, units, line_length), out_s...  2.58 us
  transfers between devices with their start and end apart: 41, of which 14 were waited for; matrix products, arithmetic and copies ran while one was open for 1% of the time, Pallas kernels for 24%

profile of v4, /device:TPU:0, one launch (start us, length us, event | category | flops | bytes accessed | tf_op | source)
XLA Modules:
  0.0 114.6 jit_solution(5697713000562987683)
XLA Ops:
  0.7 2.6 %shard_map.136 = (f32[56,768]{1,0:T(8,128)S(1)}, f32[8,256]{1,0:T(8,128)S(1)}, f32[4,64,768]{2,1,0:T(8,128)S(1)}, f32[2,64,768]{2,1,0:T(8,128)S(1)}, f32[2,64,768]{2,1,0:T(8,128)S(1)}) custom-call(s32[8]{0:T(128)} %len_ref.9, f32[2,32,4,64]{3,2,1,0:T(4,128)} %in_ref.1, f32[2,32,4,64]{3,2,1,0:T(4,128)} %out_hbm.1, f32[1,64]{1,0:T(1,128)} %bitcast.8, ...), custom_call_target="tpu_custom_call" | custom-call | flops 1474560 | bytes 2949120 | tf_op jit(solution)/shard_map/pallas_call | solution.py:456
  3.2 3.0 %collective-permute-start = (f32[56,768]{1,0:T(8,128)S(1)}, f32[56,768]{1,0:T(8,128)S(1)}, u32[]{:S(2)}, u32[]{:S(2)}) collective-permute-start(f32[56,768]{1,0:T(8,128)S(1)} %get-tuple-element.114.own_ref), channel_id=1, source_target_pairs={{0,1},{1,0},{2,3},{3,2},{4,5},{5,4},{6,7},{7,6},{8,9},{9,8},{10,11... | collective-permute-start | bytes 516104 | tf_op jit(solution)/shard_map/message_x/ppermute | solution.py:512
  6.3 2.0 %shard_map.137 = (f32[4,64,768]{2,1,0:T(8,128)S(1)}, f32[1,64,768]{2,1,0:T(8,128)S(1)}, f32[1,64,768]{2,1,0:T(8,128)S(1)}, f32[1,64,768]{2,1,0:T(8,128)S(1)}, f32[1,64,768]{2,1,0:T(8,128)S(1)}) custom-call(s32[8]{0:T(128)} %len_ref.9, f32[64,5760]{1,0:T(8,128)} %cot_ref.1), custom_call_target="tpu_custom_call" | custom-call | flops 1474560 | bytes 2949120 | tf_op jit(solution)/shard_map/pallas_call | solution.py:472
  8.3 2.7 %collective-permute-done.rec_ref = f32[56,768]{1,0:T(8,128)S(1)} collective-permute-done((f32[56,768]{1,0:T(8,128)S(1)}, f32[56,768]{1,0:T(8,128)S(1)}, u32[]{:S(2)}, u32[]{:S(2)}) %collective-permute-start) | collective-permute-done | bytes 172064 | tf_op jit(solution)/shard_map/message_x/ppermute | solution.py:512
  11.0 2.5 %collective-permute-start.1 = (f32[1,64,768]{2,1,0:T(8,128)S(1)}, f32[1,64,768]{2,1,0:T(8,128)S(1)}, u32[]{:S(2)}, u32[]{:S(2)}) collective-permute-start(f32[1,64,768]{2,1,0:T(8,128)S(1)} %get-tuple-element.120), channel_id=1, source_target_pairs={{0,1},{1,0},{2,3},{3,2},{4,5},{5,4},{6,7},{7,6},{8,9},{9,8},{10,11... | collective-permute-start | bytes 589832 | tf_op jit(solution)/shard_map/cot_x/ppermute | solution.py:512
  17.0 1.6 %collective-permute-start.8 = (f32[256,256]{1,0:T(8,128)S(1)}, f32[256,256]{1,0:T(8,128)S(1)}, u32[]{:S(2)}, u32[]{:S(2)}) collective-permute-start(f32[256,256]{1,0:T(8,128)S(1)} %shard_map.139), channel_id=1, source_target_pairs={{0,2},{1,3},{2,0},{3,1},{4,6},{5,7},{6,4},{7,5},{8,10},{9,11},{10,... | collective-permute-start | bytes 786440 | tf_op jit(solution)/shard_map/e0/ppermute | solution.py:512
  21.2 2.7 %collective-permute-start.6 = (f32[8,768]{1,0:T(8,128)S(1)}, f32[8,768]{1,0:T(8,128)S(1)}, u32[]{:S(2)}, u32[]{:S(2)}) collective-permute-start(f32[8,768]{1,0:T(8,128)S(1)} %add.76), channel_id=1, source_target_pairs={{0,4},{1,5},{2,6},{3,7},{4,0},{5,1},{6,2},{7,3},{8,12},{9,13},{10,... | collective-permute-start | bytes 73736 | tf_op jit(solution)/shard_map/squares_z2/ppermute | solution.py:512
  23.9 1.7 %collective-permute-start.5 = (f32[256,256]{1,0:T(8,128)S(1)}, f32[256,256]{1,0:T(8,128)S(1)}, u32[]{:S(2)}, u32[]{:S(2)}) collective-permute-start(f32[256,256]{1,0:T(8,128)S(1)} %shard_map.140), channel_id=1, source_target_pairs={{0,2},{1,3},{2,0},{3,1},{4,6},{5,7},{6,4},{7,5},{8,10},{9,11},{10,... | collective-permute-start | bytes 786440 | tf_op jit(solution)/shard_map/e1/ppermute | solution.py:512
  28.7 2.6 %collective-permute-start.11 = (f32[256,256]{1,0:T(8,128)S(1)}, f32[256,256]{1,0:T(8,128)S(1)}, u32[]{:S(2)}, u32[]{:S(2)}) collective-permute-start(f32[256,256]{1,0:T(8,128)S(1)} %shard_map.141), channel_id=1, source_target_pairs={{0,2},{1,3},{2,0},{3,1},{4,6},{5,7},{6,4},{7,5},{8,10},{9,11},{10,... | collective-permute-start | bytes 786440 | tf_op jit(solution)/shard_map/e2/ppermute | solution.py:512
  31.5 1.9 %collective-permute-done.4.rec_ref.cot_rec = f32[1,64,768]{2,1,0:T(8,128)S(1)} collective-permute-done((f32[1,64,768]{2,1,0:T(8,128)S(1)}, f32[1,64,768]{2,1,0:T(8,128)S(1)}, u32[]{:S(2)}, u32[]{:S(2)}) %collective-permute-start.4) | collective-permute-done | bytes 196640 | tf_op jit(solution)/shard_map/cot_x/ppermute | solution.py:512
  34.3 1.7 %collective-permute-start.9 = (f32[2,64,768]{2,1,0:T(8,128)S(1)}, f32[2,64,768]{2,1,0:T(8,128)S(1)}, u32[]{:S(2)}, u32[]{:S(2)}) collective-permute-start(f32[2,64,768]{2,1,0:T(8,128)S(1)} %get-tuple-element.138), channel_id=1, source_target_pairs={{0,1},{1,0},{2,3},{3,2},{4,5},{5,4},{6,7},{7,6},{8,9},{9,8},{10,11... | collective-permute-start | bytes 1179656 | tf_op jit(solution)/shard_map/ser_x/ppermute | solution.py:512
  36.0 2.4 %collective-permute-start.14 = (f32[256,256]{1,0:T(8,128)S(1)}, f32[256,256]{1,0:T(8,128)S(1)}, u32[]{:S(2)}, u32[]{:S(2)}) collective-permute-start(f32[256,256]{1,0:T(8,128)S(1)} %add_select_fusion.4.refs_0_), channel_id=1, source_target_pairs={{0,2},{1,3},{2,0},{3,1},{4,6},{5,7},{6,4},{7,5},{8,10},{9,11},{10,... | collective-permute-start | bytes 786440 | tf_op jit(solution)/shard_map/e3/ppermute | solution.py:512
  38.5 2.3 %collective-permute-done.10.rec_ref.ser_rec = f32[2,64,768]{2,1,0:T(8,128)S(1)} collective-permute-done((f32[2,64,768]{2,1,0:T(8,128)S(1)}, f32[2,64,768]{2,1,0:T(8,128)S(1)}, u32[]{:S(2)}, u32[]{:S(2)}) %collective-permute-start.10) | collective-permute-done | bytes 393248 | tf_op jit(solution)/shard_map/ser_x/ppermute | solution.py:512
  40.8 2.1 %shard_map.143 = (f32[256,256]{1,0:T(8,128)S(1)}, f32[256,256]{1,0:T(8,128)S(1)}) custom-call(f32[4,64,768]{2,1,0:T(8,128)S(1)} %get-tuple-element.112.own_ref.ser_own, f32[2,64,768]{2,1,0:T(8,128)S(1)} %collective-permute-done.10.rec_ref.ser_rec, f32[8,768]{1,0:T(8,128)S(1)} %add.77.ss_ref.refs_4_, bf16[256,192]{1,0:T(8,128)(2,1)S(1)} %get-tuple-element.145.down_own, ...), custom_call_target="tpu_custom_call" | custom-call | flops 14092861440 | bytes 21872640 | tf_op jit(solution)/shard_map/pallas_call | solution.py:499
  42.9 1.8 %collective-permute-start.17 = (f32[256,256]{1,0:T(8,128)S(1)}, f32[256,256]{1,0:T(8,128)S(1)}, u32[]{:S(2)}, u32[]{:S(2)}) collective-permute-start(f32[256,256]{1,0:T(8,128)S(1)} %add_select_fusion.3.refs_1_), channel_id=1, source_target_pairs={{0,2},{1,3},{2,0},{3,1},{4,6},{5,7},{6,4},{7,5},{8,10},{9,11},{10,... | collective-permute-start | bytes 786440 | tf_op jit(solution)/shard_map/e4/ppermute | solution.py:512
  44.9 4.5 %collective-permute-start.18 = (f32[256,256]{1,0:T(8,128)S(1)}, f32[256,256]{1,0:T(8,128)S(1)}, u32[]{:S(2)}, u32[]{:S(2)}) collective-permute-start(f32[256,256]{1,0:T(8,128)S(1)} %add_select_fusion.2.refs_0_), channel_id=1, source_target_pairs={{0,2},{1,3},{2,0},{3,1},{4,6},{5,7},{6,4},{7,5},{8,10},{9,11},{10,... | collective-permute-start | bytes 786440 | tf_op jit(solution)/shard_map/e5/ppermute | solution.py:512
  49.4 2.1 %shard_map.144 = (f32[256,256]{1,0:T(8,128)S(1)}, f32[256,256]{1,0:T(8,128)S(1)}) custom-call(f32[4,64,768]{2,1,0:T(8,128)S(1)} %get-tuple-element.112.own_ref.ser_own, f32[2,64,768]{2,1,0:T(8,128)S(1)} %collective-permute-done.9.rec_ref.ser_rec, f32[8,768]{1,0:T(8,128)S(1)} %add.77.ss_ref.refs_4_, bf16[256,192]{1,0:T(8,128)(2,1)S(1)} %get-tuple-element.145.down_own, ...), custom_call_target="tpu_custom_call" | custom-call | flops 14092861440 | bytes 21872640 | tf_op jit(solution)/shard_map/pallas_call | solution.py:499
  51.6 3.2 %collective-permute-start.19 = (f32[256,256]{1,0:T(8,128)S(1)}, f32[256,256]{1,0:T(8,128)S(1)}, u32[]{:S(2)}, u32[]{:S(2)}) collective-permute-start(f32[256,256]{1,0:T(8,128)S(1)} %add_select_fusion.1.refs_1_), channel_id=1, source_target_pairs={{0,2},{1,3},{2,0},{3,1},{4,6},{5,7},{6,4},{7,5},{8,10},{9,11},{10,... | collective-permute-start | bytes 786440 | tf_op jit(solution)/shard_map/e6/ppermute | solution.py:512
  55.9 3.7 %shard_map.145 = (f32[2,64,768]{2,1,0:T(8,128)S(1)}, f32[2,64,768]{2,1,0:T(8,128)S(1)}, f32[128,256]{1,0:T(8,128)S(1)}, f32[2,8,256]{2,1,0:T(8,128)S(1)}) custom-call(s32[8]{0:T(128)S(1)} %copy-done.3, f32[4,64,768]{2,1,0:T(8,128)S(1)} %get-tuple-element.112.own_ref.ser_own, f32[2,64,768]{2,1,0:T(8,128)S(1)} %collective-permute-done.10.rec_ref.ser_rec, ...), custom_call_target="tpu_custom_call" | custom-call | flops 16106127360 | bytes 31703040 | tf_op jit(solution)/shard_map/pallas_call | solution.py:499
  60.4 2.8 %collective-permute-start.21 = (f32[256,256]{1,0:T(8,128)S(1)}, f32[256,256]{1,0:T(8,128)S(1)}, u32[]{:S(2)}, u32[]{:S(2)}) collective-permute-start(f32[256,256]{1,0:T(8,128)S(1)} %add_select_fusion.refs_0_), channel_id=1, source_target_pairs={{0,2},{1,3},{2,0},{3,1},{4,6},{5,7},{6,4},{7,5},{8,10},{9,11},{10,... | collective-permute-start | bytes 786440 | tf_op jit(solution)/shard_map/e7/ppermute | solution.py:512
  63.3 3.9 %shard_map.146 = (f32[2,64,768]{2,1,0:T(8,128)S(1)}, f32[2,64,768]{2,1,0:T(8,128)S(1)}, f32[128,256]{1,0:T(8,128)S(1)}, f32[2,8,256]{2,1,0:T(8,128)S(1)}) custom-call(s32[8]{0:T(128)S(1)} %copy-done.3, f32[4,64,768]{2,1,0:T(8,128)S(1)} %get-tuple-element.112.own_ref.ser_own, f32[2,64,768]{2,1,0:T(8,128)S(1)} %collective-permute-done.9.rec_ref.ser_rec, ...), custom_call_target="tpu_custom_call" | custom-call | flops 16106127360 | bytes 33013760 | tf_op jit(solution)/shard_map/pallas_call | solution.py:499
  69.1 2.3 %collective-permute-start.28 = (f32[32,256]{1,0:T(8,128)S(1)}, f32[32,256]{1,0:T(8,128)S(1)}, u32[]{:S(2)}, u32[]{:S(2)}) collective-permute-start(f32[32,256]{1,0:T(8,128)S(1)} %pad_maximum_fusion.2), channel_id=1, source_target_pairs={{0,2},{1,3},{2,0},{3,1},{4,6},{5,7},{6,4},{7,5},{8,10},{9,11},{10,... | collective-permute-start | bytes 98312 | tf_op jit(solution)/shard_map/inner_z1/ppermute | solution.py:512
  72.9 3.5 %collective-permute-done.26.refs_3_ = f32[256,256]{1,0:T(8,128)S(1)} collective-permute-done((f32[256,256]{1,0:T(8,128)S(1)}, f32[256,256]{1,0:T(8,128)S(1)}, u32[]{:S(2)}, u32[]{:S(2)}) %collective-permute-start.26) | collective-permute-done | bytes 262176 | tf_op jit(solution)/shard_map/e8/ppermute | solution.py:512
  76.5 2.5 %shard_map.147 = (f32[2,64,768]{2,1,0:T(8,128)S(1)}, f32[2,64,768]{2,1,0:T(8,128)S(1)}, f32[136,256]{1,0:T(8,128)S(1)}) custom-call(s32[8]{0:T(128)S(1)} %copy-done.3, f32[4,64,768]{2,1,0:T(8,128)S(1)} %get-tuple-element.112.own_ref.ser_own, f32[2,64,768]{2,1,0:T(8,128)S(1)} %collective-permute-done.10.rec_ref.ser_rec, ...), custom_call_target="tpu_custom_call" | custom-call | flops 12079595520 | bytes 35389440 | tf_op jit(solution)/shard_map/pallas_call | solution.py:499
  78.9 1.7 %collective-permute-start.33 = (f32[2,64,768]{2,1,0:T(8,128)S(1)}, f32[2,64,768]{2,1,0:T(8,128)S(1)}, u32[]{:S(2)}, u32[]{:S(2)}) collective-permute-start(f32[2,64,768]{2,1,0:T(8,128)S(1)} %get-tuple-element.193), channel_id=1, source_target_pairs={{0,1},{1,0},{2,3},{3,2},{4,5},{5,4},{6,7},{7,6},{8,9},{9,8},{10,11... | collective-permute-start | bytes 1179656 | tf_op jit(solution)/shard_map/branch0/ppermute | solution.py:512
  85.2 2.0 %collective-permute-done.29 = f32[32,256]{1,0:T(8,128)S(1)} collective-permute-done((f32[32,256]{1,0:T(8,128)S(1)}, f32[32,256]{1,0:T(8,128)S(1)}, u32[]{:S(2)}, u32[]{:S(2)}) %collective-permute-start.29) | collective-permute-done | bytes 32800 | tf_op jit(solution)/shard_map/inner_z2/ppermute | solution.py:512
  90.3 1.7 %collective-permute-start.32 = (f32[136,256]{1,0:T(8,128)S(1)}, f32[136,256]{1,0:T(8,128)S(1)}, u32[]{:S(2)}, u32[]{:S(2)}) collective-permute-start(f32[136,256]{1,0:T(8,128)S(1)} %pad_maximum_fusion.1), channel_id=1, source_target_pairs={{0,1},{1,0},{2,3},{3,2},{4,5},{5,4},{6,7},{7,6},{8,9},{9,8},{10,11... | collective-permute-start | bytes 417800 | tf_op jit(solution)/shard_map/grads_x/ppermute | solution.py:512
  94.0 3.6 %collective-permute-done.34.in_rec = f32[32,256]{1,0:T(8,128)S(1)} collective-permute-done((f32[32,256]{1,0:T(8,128)S(1)}, f32[32,256]{1,0:T(8,128)S(1)}, u32[]{:S(2)}, u32[]{:S(2)}) %collective-permute-start.34) | collective-permute-done | bytes 32800 | tf_op jit(solution)/shard_map/inner_x/ppermute | solution.py:512
  97.7 1.7 %collective-permute-start.39 = (f32[1,64,768]{2,1,0:T(8,128)S(1)}, f32[1,64,768]{2,1,0:T(8,128)S(1)}, u32[]{:S(2)}, u32[]{:S(2)}) collective-permute-start(f32[1,64,768]{2,1,0:T(8,128)S(1)} %get-tuple-element.206), channel_id=1, source_target_pairs={{0,1},{1,0},{2,3},{3,2},{4,5},{5,4},{6,7},{7,6},{8,9},{9,8},{10,11... | collective-permute-start | bytes 589832 | tf_op jit(solution)/shard_map/branch2/ppermute | solution.py:512
  102.0 2.6 %shard_map.150 = f32[64,5760]{1,0:T(8,128)} custom-call(f32[64,5760]{1,0:T(8,128)S(1)} %copy-done.1, f32[64,5760]{1,0:T(8,128)S(1)} %copy-done, f32[8,768]{1,0:T(8,128)S(1)} %add.77.ss_ref.refs_4_, f32[32,256]{1,0:T(8,128)S(1)} %add.95.in_own, f32[32,256]{1,0:T(8,128)S(1)} %collective-permute-done.34.in_rec, f32[2,64,768]{2,1,0:T(8,128)S(1)} %get-tuple-element.202.refs_0_, ...), custom_call_target="tpu_custom_call" | custom-call | flops 60866 | bytes 60866 | tf_op jit(solution)/shard_map/pallas_call | solution.py:423
  107.4 1.9 %collective-permute-done.38 = f32[8,256]{1,0:T(8,128)S(1)} collective-permute-done((f32[8,256]{1,0:T(8,128)S(1)}, f32[8,256]{1,0:T(8,128)S(1)}, u32[]{:S(2)}, u32[]{:S(2)}) %collective-permute-start.38) | collective-permute-done | bytes 8224 | tf_op jit(solution)/shard_map/stats_z1/ppermute | solution.py:512
  111.8 2.1 %collective-permute-done.40.rec_ref = f32[8,256]{1,0:T(8,128)S(1)} collective-permute-done((f32[8,256]{1,0:T(8,128)S(1)}, f32[8,256]{1,0:T(8,128)S(1)}, u32[]{:S(2)}, u32[]{:S(2)}) %collective-permute-start.40) | collective-permute-done | bytes 8224 | tf_op jit(solution)/shard_map/stats_z2/ppermute | solution.py:512
  (118 shorter events, 34.3 us)
Async XLA Ops:
  3.2 7.8 %collective-permute-start = (f32[56,768]{1,0:T(8,128)S(1)}, f32[56,768]{1,0:T(8,128)S(1)}, u32[]{:S(2)}, u32[]{:S(2)}) collective-permute-start(f32[56,768]{1,0:T(8,128)S(1)} %get-tuple-element.114.own_ref), channel_id=1, source_target_pairs={{0,1},{1,0},{2,3},{3,2},{4,5},{5,4},{6,7},{7,6},{8,9},{9,8},{10,11... | collective-permute-start | bytes 516104 | tf_op jit(solution)/shard_map/message_x/ppermute | solution.py:512
  8.2 7.9 %collective-permute-start.2 = (f32[1,64,768]{2,1,0:T(8,128)S(1)}, f32[1,64,768]{2,1,0:T(8,128)S(1)}, u32[]{:S(2)}, u32[]{:S(2)}) collective-permute-start(f32[1,64,768]{2,1,0:T(8,128)S(1)} %get-tuple-element.121), channel_id=1, source_target_pairs={{0,1},{1,0},{2,3},{3,2},{4,5},{5,4},{6,7},{7,6},{8,9},{9,8},{10,11... | collective-permute-start | bytes 589832 | tf_op jit(solution)/shard_map/cot_x/ppermute | solution.py:512
  11.0 9.2 %collective-permute-start.1 = (f32[1,64,768]{2,1,0:T(8,128)S(1)}, f32[1,64,768]{2,1,0:T(8,128)S(1)}, u32[]{:S(2)}, u32[]{:S(2)}) collective-permute-start(f32[1,64,768]{2,1,0:T(8,128)S(1)} %get-tuple-element.120), channel_id=1, source_target_pairs={{0,1},{1,0},{2,3},{3,2},{4,5},{5,4},{6,7},{7,6},{8,9},{9,8},{10,11... | collective-permute-start | bytes 589832 | tf_op jit(solution)/shard_map/cot_x/ppermute | solution.py:512
  13.5 7.7 %collective-permute-start.3 = (f32[8,768]{1,0:T(8,128)S(1)}, f32[8,768]{1,0:T(8,128)S(1)}, u32[]{:S(2)}, u32[]{:S(2)}) collective-permute-start(f32[8,768]{1,0:T(8,128)S(1)} %slice_add_fusion), channel_id=1, source_target_pairs={{0,2},{1,3},{2,0},{3,1},{4,6},{5,7},{6,4},{7,5},{8,10},{9,11},{10,... | collective-permute-start | bytes 73736 | tf_op jit(solution)/shard_map/squares_z1/ppermute | solution.py:512
  17.0 10.6 %collective-permute-start.8 = (f32[256,256]{1,0:T(8,128)S(1)}, f32[256,256]{1,0:T(8,128)S(1)}, u32[]{:S(2)}, u32[]{:S(2)}) collective-permute-start(f32[256,256]{1,0:T(8,128)S(1)} %shard_map.139), channel_id=1, source_target_pairs={{0,2},{1,3},{2,0},{3,1},{4,6},{5,7},{6,4},{7,5},{8,10},{9,11},{10,... | collective-permute-start | bytes 786440 | tf_op jit(solution)/shard_map/e0/ppermute | solution.py:512
  18.7 9.1 %collective-permute-start.7 = (f32[1,64,768]{2,1,0:T(8,128)S(1)}, f32[1,64,768]{2,1,0:T(8,128)S(1)}, u32[]{:S(2)}, u32[]{:S(2)}) collective-permute-start(f32[1,64,768]{2,1,0:T(8,128)S(1)} %get-tuple-element.131), channel_id=1, source_target_pairs={{0,1},{1,0},{2,3},{3,2},{4,5},{5,4},{6,7},{7,6},{8,9},{9,8},{10,11... | collective-permute-start | bytes 589832 | tf_op jit(solution)/shard_map/cot_x/ppermute | solution.py:512
  23.9 7.5 %collective-permute-start.5 = (f32[256,256]{1,0:T(8,128)S(1)}, f32[256,256]{1,0:T(8,128)S(1)}, u32[]{:S(2)}, u32[]{:S(2)}) collective-permute-start(f32[256,256]{1,0:T(8,128)S(1)} %shard_map.140), channel_id=1, source_target_pairs={{0,2},{1,3},{2,0},{3,1},{4,6},{5,7},{6,4},{7,5},{8,10},{9,11},{10,... | collective-permute-start | bytes 786440 | tf_op jit(solution)/shard_map/e1/ppermute | solution.py:512
  25.5 7.8 %collective-permute-start.4 = (f32[1,64,768]{2,1,0:T(8,128)S(1)}, f32[1,64,768]{2,1,0:T(8,128)S(1)}, u32[]{:S(2)}, u32[]{:S(2)}) collective-permute-start(f32[1,64,768]{2,1,0:T(8,128)S(1)} %get-tuple-element.129), channel_id=1, source_target_pairs={{0,1},{1,0},{2,3},{3,2},{4,5},{5,4},{6,7},{7,6},{8,9},{9,8},{10,11... | collective-permute-start | bytes 589832 | tf_op jit(solution)/shard_map/cot_x/ppermute | solution.py:512
  27.1 13.6 %collective-permute-start.10 = (f32[2,64,768]{2,1,0:T(8,128)S(1)}, f32[2,64,768]{2,1,0:T(8,128)S(1)}, u32[]{:S(2)}, u32[]{:S(2)}) collective-permute-start(f32[2,64,768]{2,1,0:T(8,128)S(1)} %get-tuple-element.141), channel_id=1, source_target_pairs={{0,1},{1,0},{2,3},{3,2},{4,5},{5,4},{6,7},{7,6},{8,9},{9,8},{10,11... | collective-permute-start | bytes 1179656 | tf_op jit(solution)/shard_map/ser_x/ppermute | solution.py:512
  27.7 8.2 %collective-permute-start.12 = (f32[256,256]{1,0:T(8,128)S(1)}, f32[256,256]{1,0:T(8,128)S(1)}, u32[]{:S(2)}, u32[]{:S(2)}) collective-permute-start(f32[256,256]{1,0:T(8,128)S(1)} %add.78), channel_id=1, source_target_pairs={{0,8},{1,9},{2,4},{3,5},{4,2},{5,3},{6,14},{7,15},{8,0},{9,1},{10,... | collective-permute-start | bytes 786440 | tf_op jit(solution)/shard_map/m0/ppermute | solution.py:536
  28.7 9.7 %collective-permute-start.11 = (f32[256,256]{1,0:T(8,128)S(1)}, f32[256,256]{1,0:T(8,128)S(1)}, u32[]{:S(2)}, u32[]{:S(2)}) collective-permute-start(f32[256,256]{1,0:T(8,128)S(1)} %shard_map.141), channel_id=1, source_target_pairs={{0,2},{1,3},{2,0},{3,1},{4,6},{5,7},{6,4},{7,5},{8,10},{9,11},{10,... | collective-permute-start | bytes 786440 | tf_op jit(solution)/shard_map/e2/ppermute | solution.py:512
  31.4 11.5 %collective-permute-start.15 = (f32[256,256]{1,0:T(8,128)S(1)}, f32[256,256]{1,0:T(8,128)S(1)}, u32[]{:S(2)}, u32[]{:S(2)}) collective-permute-start(f32[256,256]{1,0:T(8,128)S(1)} %add.79), channel_id=1, source_target_pairs={{0,8},{1,9},{2,4},{3,5},{4,2},{5,3},{6,14},{7,15},{8,0},{9,1},{10,... | collective-permute-start | bytes 786440 | tf_op jit(solution)/shard_map/m1/ppermute | solution.py:536
  34.3 15.1 %collective-permute-start.9 = (f32[2,64,768]{2,1,0:T(8,128)S(1)}, f32[2,64,768]{2,1,0:T(8,128)S(1)}, u32[]{:S(2)}, u32[]{:S(2)}) collective-permute-start(f32[2,64,768]{2,1,0:T(8,128)S(1)} %get-tuple-element.138), channel_id=1, source_target_pairs={{0,1},{1,0},{2,3},{3,2},{4,5},{5,4},{6,7},{7,6},{8,9},{9,8},{10,11... | collective-permute-start | bytes 1179656 | tf_op jit(solution)/shard_map/ser_x/ppermute | solution.py:512
  36.0 8.7 %collective-permute-start.14 = (f32[256,256]{1,0:T(8,128)S(1)}, f32[256,256]{1,0:T(8,128)S(1)}, u32[]{:S(2)}, u32[]{:S(2)}) collective-permute-start(f32[256,256]{1,0:T(8,128)S(1)} %add_select_fusion.4.refs_0_), channel_id=1, source_target_pairs={{0,2},{1,3},{2,0},{3,1},{4,6},{5,7},{6,4},{7,5},{8,10},{9,11},{10,... | collective-permute-start | bytes 786440 | tf_op jit(solution)/shard_map/e3/ppermute | solution.py:512
  42.9 8.5 %collective-permute-start.17 = (f32[256,256]{1,0:T(8,128)S(1)}, f32[256,256]{1,0:T(8,128)S(1)}, u32[]{:S(2)}, u32[]{:S(2)}) collective-permute-start(f32[256,256]{1,0:T(8,128)S(1)} %add_select_fusion.3.refs_1_), channel_id=1, source_target_pairs={{0,2},{1,3},{2,0},{3,1},{4,6},{5,7},{6,4},{7,5},{8,10},{9,11},{10,... | collective-permute-start | bytes 786440 | tf_op jit(solution)/shard_map/e4/ppermute | solution.py:512
  44.9 10.9 %collective-permute-start.18 = (f32[256,256]{1,0:T(8,128)S(1)}, f32[256,256]{1,0:T(8,128)S(1)}, u32[]{:S(2)}, u32[]{:S(2)}) collective-permute-start(f32[256,256]{1,0:T(8,128)S(1)} %add_select_fusion.2.refs_0_), channel_id=1, source_target_pairs={{0,2},{1,3},{2,0},{3,1},{4,6},{5,7},{6,4},{7,5},{8,10},{9,11},{10,... | collective-permute-start | bytes 786440 | tf_op jit(solution)/shard_map/e5/ppermute | solution.py:512
  51.5 8.9 %collective-permute-start.20 = (f32[256,256]{1,0:T(8,128)S(1)}, f32[256,256]{1,0:T(8,128)S(1)}, u32[]{:S(2)}, u32[]{:S(2)}) collective-permute-start(f32[256,256]{1,0:T(8,128)S(1)} %add.85), channel_id=1, source_target_pairs={{0,8},{1,9},{2,4},{3,5},{4,2},{5,3},{6,14},{7,15},{8,0},{9,1},{10,... | collective-permute-start | bytes 786440 | tf_op jit(solution)/shard_map/m4/ppermute | solution.py:536
  51.6 11.6 %collective-permute-start.19 = (f32[256,256]{1,0:T(8,128)S(1)}, f32[256,256]{1,0:T(8,128)S(1)}, u32[]{:S(2)}, u32[]{:S(2)}) collective-permute-start(f32[256,256]{1,0:T(8,128)S(1)} %add_select_fusion.1.refs_1_), channel_id=1, source_target_pairs={{0,2},{1,3},{2,0},{3,1},{4,6},{5,7},{6,4},{7,5},{8,10},{9,11},{10,... | collective-permute-start | bytes 786440 | tf_op jit(solution)/shard_map/e6/ppermute | solution.py:512
  55.8 11.4 %collective-permute-start.22 = (f32[256,256]{1,0:T(8,128)S(1)}, f32[256,256]{1,0:T(8,128)S(1)}, u32[]{:S(2)}, u32[]{:S(2)}) collective-permute-start(f32[256,256]{1,0:T(8,128)S(1)} %add.87), channel_id=1, source_target_pairs={{0,8},{1,9},{2,4},{3,5},{4,2},{5,3},{6,14},{7,15},{8,0},{9,1},{10,... | collective-permute-start | bytes 786440 | tf_op jit(solution)/shard_map/m5/ppermute | solution.py:536
  59.6 13.2 %collective-permute-start.24 = (f32[2,64,768]{2,1,0:T(8,128)S(1)}, f32[2,64,768]{2,1,0:T(8,128)S(1)}, u32[]{:S(2)}, u32[]{:S(2)}) collective-permute-start(f32[2,64,768]{2,1,0:T(8,128)S(1)} %get-tuple-element.170), channel_id=1, source_target_pairs={{0,1},{1,0},{2,3},{3,2},{4,5},{5,4},{6,7},{7,6},{8,9},{9,8},{10,11... | collective-permute-start | bytes 1179656 | tf_op jit(solution)/shard_map/scaled0/ppermute | solution.py:512
  60.4 8.5 %collective-permute-start.21 = (f32[256,256]{1,0:T(8,128)S(1)}, f32[256,256]{1,0:T(8,128)S(1)}, u32[]{:S(2)}, u32[]{:S(2)}) collective-permute-start(f32[256,256]{1,0:T(8,128)S(1)} %add_select_fusion.refs_0_), channel_id=1, source_target_pairs={{0,2},{1,3},{2,0},{3,1},{4,6},{5,7},{6,4},{7,5},{8,10},{9,11},{10,... | collective-permute-start | bytes 786440 | tf_op jit(solution)/shard_map/e7/ppermute | solution.py:512
  63.3 8.1 %collective-permute-start.25 = (f32[256,256]{1,0:T(8,128)S(1)}, f32[256,256]{1,0:T(8,128)S(1)}, u32[]{:S(2)}, u32[]{:S(2)}) collective-permute-start(f32[256,256]{1,0:T(8,128)S(1)} %add.89), channel_id=1, source_target_pairs={{0,8},{1,9},{2,4},{3,5},{4,2},{5,3},{6,14},{7,15},{8,0},{9,1},{10,... | collective-permute-start | bytes 786440 | tf_op jit(solution)/shard_map/m6/ppermute | solution.py:536
  67.3 9.2 %collective-permute-start.26 = (f32[256,256]{1,0:T(8,128)S(1)}, f32[256,256]{1,0:T(8,128)S(1)}, u32[]{:S(2)}, u32[]{:S(2)}) collective-permute-start(f32[256,256]{1,0:T(8,128)S(1)} %add.90.refs_1_), channel_id=1, source_target_pairs={{0,2},{1,3},{2,0},{3,1},{4,6},{5,7},{6,4},{7,5},{8,10},{9,11},{10,... | collective-permute-start | bytes 786440 | tf_op jit(solution)/shard_map/e8/ppermute | solution.py:512
  69.0 11.7 %collective-permute-start.23 = (f32[256,256]{1,0:T(8,128)S(1)}, f32[256,256]{1,0:T(8,128)S(1)}, u32[]{:S(2)}, u32[]{:S(2)}) collective-permute-start(f32[256,256]{1,0:T(8,128)S(1)} %add.91), channel_id=1, source_target_pairs={{0,8},{1,9},{2,4},{3,5},{4,2},{5,3},{6,14},{7,15},{8,0},{9,1},{10,... | collective-permute-start | bytes 786440 | tf_op jit(solution)/shard_map/m7/ppermute | solution.py:536
  69.1 13.2 %collective-permute-start.28 = (f32[32,256]{1,0:T(8,128)S(1)}, f32[32,256]{1,0:T(8,128)S(1)}, u32[]{:S(2)}, u32[]{:S(2)}) collective-permute-start(f32[32,256]{1,0:T(8,128)S(1)} %pad_maximum_fusion.2), channel_id=1, source_target_pairs={{0,2},{1,3},{2,0},{3,1},{4,6},{5,7},{6,4},{7,5},{8,10},{9,11},{10,... | collective-permute-start | bytes 98312 | tf_op jit(solution)/shard_map/inner_z1/ppermute | solution.py:512
  71.4 12.3 %collective-permute-start.31 = (f32[2,64,768]{2,1,0:T(8,128)S(1)}, f32[2,64,768]{2,1,0:T(8,128)S(1)}, u32[]{:S(2)}, u32[]{:S(2)}) collective-permute-start(f32[2,64,768]{2,1,0:T(8,128)S(1)} %get-tuple-element.184), channel_id=1, source_target_pairs={{0,1},{1,0},{2,3},{3,2},{4,5},{5,4},{6,7},{7,6},{8,9},{9,8},{10,11... | collective-permute-start | bytes 1179656 | tf_op jit(solution)/shard_map/scaled1/ppermute | solution.py:512
  72.8 10.9 %collective-permute-start.30 = (f32[256,256]{1,0:T(8,128)S(1)}, f32[256,256]{1,0:T(8,128)S(1)}, u32[]{:S(2)}, u32[]{:S(2)}) collective-permute-start(f32[256,256]{1,0:T(8,128)S(1)} %add.92.refs_0_), channel_id=1, source_target_pairs={{0,2},{1,3},{2,0},{3,1},{4,6},{5,7},{6,4},{7,5},{8,10},{9,11},{10,... | collective-permute-start | bytes 786440 | tf_op jit(solution)/shard_map/e9/ppermute | solution.py:512
  78.9 18.7 %collective-permute-start.33 = (f32[2,64,768]{2,1,0:T(8,128)S(1)}, f32[2,64,768]{2,1,0:T(8,128)S(1)}, u32[]{:S(2)}, u32[]{:S(2)}) collective-permute-start(f32[2,64,768]{2,1,0:T(8,128)S(1)} %get-tuple-element.193), channel_id=1, source_target_pairs={{0,1},{1,0},{2,3},{3,2},{4,5},{5,4},{6,7},{7,6},{8,9},{9,8},{10,11... | collective-permute-start | bytes 1179656 | tf_op jit(solution)/shard_map/branch0/ppermute | solution.py:512
  80.7 8.0 %collective-permute-start.27 = (f32[256,256]{1,0:T(8,128)S(1)}, f32[256,256]{1,0:T(8,128)S(1)}, u32[]{:S(2)}, u32[]{:S(2)}) collective-permute-start(f32[256,256]{1,0:T(8,128)S(1)} %add.93.refs_0_), channel_id=1, source_target_pairs={{0,2},{1,3},{2,0},{3,1},{4,6},{5,7},{6,4},{7,5},{8,10},{9,11},{10,... | collective-permute-start | bytes 786440 | tf_op jit(solution)/shard_map/e10/ppermute | solution.py:512
  90.3 7.4 %collective-permute-start.32 = (f32[136,256]{1,0:T(8,128)S(1)}, f32[136,256]{1,0:T(8,128)S(1)}, u32[]{:S(2)}, u32[]{:S(2)}) collective-permute-start(f32[136,256]{1,0:T(8,128)S(1)} %pad_maximum_fusion.1), channel_id=1, source_target_pairs={{0,1},{1,0},{2,3},{3,2},{4,5},{5,4},{6,7},{7,6},{8,9},{9,8},{10,11... | collective-permute-start | bytes 417800 | tf_op jit(solution)/shard_map/grads_x/ppermute | solution.py:512
  92.4 8.0 %collective-permute-start.36 = (f32[1,64,768]{2,1,0:T(8,128)S(1)}, f32[1,64,768]{2,1,0:T(8,128)S(1)}, u32[]{:S(2)}, u32[]{:S(2)}) collective-permute-start(f32[1,64,768]{2,1,0:T(8,128)S(1)} %get-tuple-element.198), channel_id=1, source_target_pairs={{0,1},{1,0},{2,3},{3,2},{4,5},{5,4},{6,7},{7,6},{8,9},{9,8},{10,11... | collective-permute-start | bytes 589832 | tf_op jit(solution)/shard_map/branch1/ppermute | solution.py:512
  97.7 8.7 %collective-permute-start.39 = (f32[1,64,768]{2,1,0:T(8,128)S(1)}, f32[1,64,768]{2,1,0:T(8,128)S(1)}, u32[]{:S(2)}, u32[]{:S(2)}) collective-permute-start(f32[1,64,768]{2,1,0:T(8,128)S(1)} %get-tuple-element.206), channel_id=1, source_target_pairs={{0,1},{1,0},{2,3},{3,2},{4,5},{5,4},{6,7},{7,6},{8,9},{9,8},{10,11... | collective-permute-start | bytes 589832 | tf_op jit(solution)/shard_map/branch2/ppermute | solution.py:512
  (17 other events, 123.4 us)

commit v5 on v4

--- a/solution.py
+++ b/solution.py
@@ -285,14 +285,15 @@
     return jnp.where(lane < length, value, 0.0)
 
 
-def opening(refs, outs):
-    return 0.0 if len(refs) == outs else refs[0][...], refs[-outs:]
+def opening(refs, outs, sums):
+    return [ref[...] for ref in refs[:-outs]] or [0.0] * sums, refs[-outs:]
 
 
 def back_kernel(first, full_width, line_length, len_ref, own_ref, rec_ref, *refs):
     sums, refs = refs[: 2 * own_ref.shape[0]], refs[2 * own_ref.shape[0] :]
     ss_ref, down_both, leg_high, leg_low, phase_ref, *refs = refs
-    grads, (own_out, rec_out, grad_out, inner_out) = opening(refs, 4)
+    before, (own_out, rec_out, grad_own, grad_rec, inner_out) = opening(refs, 5, 2)
+    grads = 0.0
     row = side_of() * (ss_ref.shape[0] // 2) + first
     channels = own_ref.shape[1]
     for k, total in enumerate(totals(line_length, sums)):
@@ -311,13 +312,14 @@
         inner_out[k] = jnp.concatenate(pieces + [jnp.zeros((STATS - len(pieces), 256), f32)], axis=0)
         high, low = split(both * inverse_rms(ss_ref, row + k, full_width))
         grads = grads + stacked_nt(jnp.concatenate([high, low], axis=0), pair, 2 * channels)
-    grad_out[...] = grads
+    grad_own[...] = before[0] + grads[:channels]
+    grad_rec[...] = before[1] + grads[channels:]
 
 
 def branch_kernel(first, line_length, len_ref, ser_own, ser_rec, cot_own, cot_rec, *refs):
     sums, refs = refs[: 2 * ser_own.shape[0]], refs[2 * ser_own.shape[0] :]
     up_both, leg_high, leg_low, *refs = refs
-    before, (own_out, rec_out, grad_out) = opening(refs, 3)
+    before, (own_out, rec_out, grad_own, grad_rec, stats_out) = opening(refs, 5, 3)
     channels = ser_own.shape[1]
     rows = 2 * channels
     windows = len_ref.shape[0]
@@ -338,19 +340,21 @@
     steps = functools.reduce(lambda a, b: a + b, [len_ref[w] for w in range(windows)]) if first == 0 else 0
     stats.append(jnp.full((1, width), steps, jnp.int32).astype(f32))
     stats = jnp.concatenate(stats + [jnp.zeros((STATS - 4, width), f32)], axis=0)
-    grad_out[...] = before + jnp.concatenate([grads, stats], axis=0)
+    grad_own[...] = before[0] + grads[:channels]
+    grad_rec[...] = before[1] + grads[channels:]
+    stats_out[...] = before[2] + stats
+
+
+def own_or_theirs(units, own_refs, rec_refs, w, half):
+    u, j = locate(units, w % half)
+    return jnp.where((side_of() == 0) == (w < half), own_refs[u][j], rec_refs[u][j])
 
 
 def layer_kernel(units, x_ref, *refs):
     own_refs, rec_refs, out_ref = refs[: len(units)], refs[len(units) : 2 * len(units)], refs[-1]
     windows = x_ref.shape[1] // LEN
-    half = windows // 2
-    first_side = side_of() == 0
-    for w in range(windows):
-        u, j = locate(units, w % half)
-        value = jnp.where(first_side == (w < half), own_refs[u][j], rec_refs[u][j])
-        at = slice(w * LEN, (w + 1) * LEN)
-        out_ref[:, at] = x_ref[:, at] + value[:, :LEN]
+    branches = [own_or_theirs(units, own_refs, rec_refs, w, windows // 2)[:, :LEN] for w in range(windows)]
+    out_ref[...] = x_ref[...] + jnp.concatenate(branches, axis=1)
 
 
 def inner_row(small_ref, j):
@@ -358,25 +362,28 @@
     return jnp.concatenate([small_ref[row + p : row + p + 1, :] for p in range(LANES // 256)], axis=1)
 
 
-def series_grad_kernel(units, full_width, cot_ref, x_ref, ss_ref, in_own, in_rec, *refs):
-    own_refs, rec_refs, out_ref = refs[: len(units)], refs[len(units) : 2 * len(units)], refs[-1]
-    windows = x_ref.shape[1] // LEN
+def series_grad_kernel(units, full_width, cot_ref, x_own, ss_ref, in_own, in_rec, *refs):
+    count = len(units)
+    own_refs, rec_refs, sent_refs, out_ref = refs[:count], refs[count : 2 * count], refs[2 * count : -1], refs[-1]
+    windows = cot_ref.shape[1] // LEN
     half = windows // 2
     first_side = side_of() == 0
+    sent = [(ref, k) for ref in sent_refs for k in range(ref.shape[0])]
+    shifts = []
     for w in range(windows):
-        u, j = locate(units, w % half)
         keep = first_side == (w < half)
-        scaled = jnp.where(keep, own_refs[u][j], rec_refs[u][j])[:, :LEN]
-        inner = jnp.where(keep, inner_row(in_own, w % half), inner_row(in_rec, w % half))[:, :LEN]
-        inv = inverse_rms(ss_ref, w, full_width)[:, :LEN]
-        at = slice(w * LEN, (w + 1) * LEN)
-        shift = inv * inv * inner * (1.0 / full_width)
-        out_ref[:, at] = cot_ref[:, at] + inv * (scaled - x_ref[:, at] * shift)
-
-
-def close_kernel(sums_ref, in_ref, gain_ref, grad_in_ref, grad_out_ref, grad_gain_ref):
+        scaled = own_or_theirs(units, own_refs, rec_refs, w, half)
+        ref, k = sent[w % half]
+        series = jnp.where(keep, x_own[w % half], ref[k])
+        inner = jnp.where(keep, inner_row(in_own, w % half), inner_row(in_rec, w % half))
+        inv = inverse_rms(ss_ref, w, full_width)
+        shifts.append((inv * (scaled - series * (inv * inv * inner * (1.0 / full_width))))[:, :LEN])
+    out_ref[...] = cot_ref[...] + jnp.concatenate(shifts, axis=1)
+
+
+def close_kernel(into_ref, mix_ref, in_ref, gain_ref, grad_in_ref, grad_out_ref, grad_gain_ref):
     modes, ranks, channels = in_ref.shape[1:]
-    into, mix = sums_ref[:channels].T, sums_ref[channels : 2 * channels].T
+    into, mix = into_ref[...].T, mix_ref[:channels].T
     total = jnp.zeros((modes, channels), f32)
     read_real, read_imag = readout_columns(modes, channels)
     for r in range(ranks):
@@ -558,8 +565,8 @@
 PLAN = (
     "R0", "e0", "c2", "R1", "q", "e1", "c3", "x0", "m0", "R2", "e2", "Q", "m1", "R3", "x1", "e3",
     "m2", "K0", "e4", "m3", "e5", "K1", "m4", "e6", "m5", "B0", "g0", "e7", "m6", "B1", "e8", "m7",
-    "i1", "g1", "e9", "s0", "M0", "y0", "e10", "i2", "s1", "M1", "ix", "y1", "M2", "G", "y2", "iy",
-    "b0", "gc", "b1", "gy", "F2", "ge", "st1", "b2", "CL", "st2", "F1",
+    "r", "e9", "g1", "i1", "rc", "s0", "M0", "y0", "e10", "i2", "M1", "s1", "ry", "ix", "y1", "M2",
+    "re", "G", "y2", "iy", "b0", "gc", "gy", "F2", "b1", "ge", "t1", "b2", "CL", "t2", "F1",
 )
 
 
@@ -585,7 +592,8 @@
     phase = jnp.asarray(phase_rows(mode_count))
     gain = norm_gain.reshape(1, channels)
 
-    message, end_mask, ser_own, *ser_rec = front(series, lengths, [mode_in, mode_out, gain], ser_units, rows, line_length)
+    message, end_mask, ser_own, *ser_sent = front(series, lengths, [mode_in, mode_out, gain], ser_units, rows, line_length)
+    ser_rec = list(ser_sent)
     with jax.named_scope("message_x"):
         message_rec = swap(message, "order", 1)
     cot_own, *cot_rec = deal(after(grad_out, message), lengths, cot_units)
@@ -662,43 +670,52 @@
 
     def do_back(u, token):
         first, count = back_units[u]
-        previous = [state["grad_in"]] if "grad_in" in state else []
-        mine, theirs, state["grad_in"], dots = unit_call(
+        mine, theirs, *sums, dots = unit_call(
             functools.partial(back_kernel, first, full_width, line_length), back_units[u], [lengths],
             windows_of(ser_own, ser_rec, ser_units, first, count),
-            [*sums_of(first, count, token), state["squares"], down_both, *legendre, phase, *previous],
-            [(count, channels, LANES)] * 2 + [(2 * channels, rows), (count, STATS, 256)], 24, weight=WEIGHT[2][u],
+            [*sums_of(first, count, token), state["squares"], down_both, *legendre, phase, *state.get("into", [])],
+            [(count, channels, LANES)] * 2 + [(channels, rows)] * 2 + [(count, STATS, 256)], 24, weight=WEIGHT[2][u],
         )
-        backs[u] = (mine, theirs, dots)
-        return state["grad_in"]
+        backs[u], state["into"] = (mine, theirs, dots), sums
+        return dots
 
     def do_mix(u, token):
         first, count = mix_units[u]
-        previous = [state["grad_mix"]] if "grad_mix" in state else []
-        mine, theirs, state["grad_mix"] = unit_call(
+        branches[u], kept[u], *state["mix"] = unit_call(
             functools.partial(branch_kernel, first, line_length), mix_units[u], [lengths],
             [*windows_of(ser_own, ser_rec, ser_units, first, count), *windows_of(cot_own, cot_rec, cot_units, first, count)],
-            [*sums_of(half + first, count, token), up_both, *legendre, *previous],
-            [(count, channels, LANES)] * 2 + [(2 * channels + STATS, rows)], 18, weight=WEIGHT[3][u],
+            [*sums_of(half + first, count, token), up_both, *legendre, *state.get("mix", [])],
+            [(count, channels, LANES)] * 2 + [(channels, rows)] * 2 + [(STATS, rows)], 18, weight=WEIGHT[3][u],
         )
-        branches[u], kept[u] = mine, theirs
-        return state["grad_mix"]
-
-    def do_grads(token):
-        grad_in, grad_mix = state["grad_in"], state["grad_mix"]
-        stats = grad_mix[2 * channels :]
-        state["own"] = jnp.concatenate([grad_in[:channels], grad_mix[:channels], stats], axis=0)
-        rec = jnp.concatenate([grad_in[channels:], grad_mix[channels : 2 * channels], stats], axis=0)
-        with jax.named_scope("grads_x"):
-            state["rec"] = swap(after(rec, token), "order", 1)
-        return rec
+        return state["mix"][2]
+
+    def reduce_step(key, letter, token):
+        kept_part, came_part = state[key]
+        out = kept_part if came_part is None else kept_part + after(came_part, token)
+        if came_part is None:
+            out = after(out, token)
+        order, batch = order_devices, lax.axis_size("batch")
+        axis, early, bit = {
+            "x": ("order", [], 1), "1": ("order", [], 2), "2": ("order", bits_of(order // 2, 4), order // 2),
+            "c": ("batch", [], 1), "y": ("batch", bits_of(batch // 2, 2), batch // 2), "e": ("", [], 0),
+        }[letter]
+        with jax.named_scope(f"{key}_{letter}"):
+            if axis:
+                out = add_over(out, axis, early)
+            state[key] = (out, swap(out, axis, bit) if axis else None)
+        return out
+
+    def start_sums(key, sums, token):
+        with jax.named_scope(f"{key}_x"):
+            state[key] = (sums[0], swap(after(sums[1], token), "order", 1))
+        return token
 
     def do_series(token):
         count = len(back_units)
         return one_call(
             functools.partial(series_grad_kernel, back_units, full_width), struct(series.shape),
-            [grad_out, series, state["squares"], state["inner"], after(state["inner_rec"], token)]
-            + [backs[u][0] for u in range(count)] + [backs[u][1] for u in range(count)], weight=0.01,
+            [grad_out, ser_own, state["squares"], state["inner"], after(state["inner_rec"], token)]
+            + [backs[u][0] for u in range(count)] + [backs[u][1] for u in range(count)] + ser_sent, weight=0.01,
         )
 
     def do_layer(token):
@@ -762,40 +779,28 @@
                 state["inner"], state["inner_rec"] = out, swap(out, "order", 1)
         elif name == "iy":
             out = state["inner_rec"] = after(state["inner_rec"], token)
-        elif name == "st":
-            with jax.named_scope(f"stats_z{u}"):
-                if u == 1:
-                    out = state["own"][2 * channels :]
-                else:
-                    out = state["stats"] + after(state["stats_rec"], token)
-                    out = add_over(out, "order", bits_of(order_devices // 2, 4))
-                step_bit = 2 if u == 1 else order_devices // 2
-                state["stats"], state["stats_rec"] = out, swap(out, "order", step_bit)
+        elif name == "t":
+            if "stats" not in state:
+                state["stats"] = (state["w"][0][channels:], None)
+            out = reduce_step("stats", str(u), token)
+        elif name in ("tx", "tc", "ty", "gc", "gy", "ge", "rc", "ry", "re"):
+            out = reduce_step({"t": "stats", "g": "w", "r": "r"}[name[0]], name[1], token)
+        elif name == "r":
+            out = start_sums("r", state["into"], token)
+        elif name == "G":
+            out = start_sums("w", [jnp.concatenate([part, state["mix"][2]], axis=0) for part in state["mix"][:2]], token)
         elif name == "CL":
             state["close"] = one_call(
                 close_kernel, [struct(mode_in.shape), struct(mode_out.shape), struct((1, channels))],
-                [after(state["own"], token), mode_in, gain],
+                [state["r"][0], after(state["w"][0], token), mode_in, gain],
             )
             out = state["close"][0]
-        elif name == "G":
-            out = do_grads(token)
-        elif name == "gc":
-            with jax.named_scope("grads_core"):
-                out = state["own"] + after(state["rec"], token)
-                state["own"], state["rec"] = out, swap(out, "batch", 1)
-        elif name == "gy":
-            with jax.named_scope("grads_y"):
-                out = state["own"] + after(state["rec"], token)
-                out = add_over(out, "batch", bits_of(lax.axis_size("batch") // 2, 2))
-                state["own"], state["rec"] = out, swap(out, "batch", lax.axis_size("batch") // 2)
-        elif name == "ge":
-            state["own"] = out = state["own"] + after(state["rec"], token)
         elif name == "F":
             out = state[step] = do_layer(token) if u == 1 else do_series(token)
         state["token"] = out
     stream_rms = one_call(
         functools.partial(rms_kernel, order_devices / full_width), [struct((3,))],
-        [state["stats"], after(state["stats_rec"], state["token"])], scalars_out=1,
+        [state["stats"][0], after(state["stats"][1], state["token"])], scalars_out=1,
     )[0]
     grad_mode_in, grad_mode_out, grad_gain = state["close"]
     return state["F1"], state["F2"], grad_gain.reshape(channels), grad_mode_in, grad_mode_out, stream_rms

time: 115 us -> 114 us (level)
  starting transfers between devices: 55.7 us -> 58.8 us
  waiting for transfers between devices: 25.5 us -> 22.7 us
    ppermute x33 -> x36, starting transfers between devices: 55.1 us -> 58.2 us  [swap(): return lax.ppermute(x, axis, [(i, i ^ bit) for i in range(size)])]
    ppermute x33 -> x36, waiting for transfers between devices: 25.5 us -> 22.7 us  [swap(): return lax.ppermute(x, axis, [(i, i ^ bit) for i in range(size)])]
  transfers between devices with their start and end apart: 41 -> 44, of which waited for: 14 -> 18; matrix products, arithmetic and copies ran while one was open for 1% -> 1% of each run, Pallas kernels for 24% -> 24%
where the time goes in v5:
time: 114 us
  starting transfers between devices  58.8 us (52%)
  Pallas kernels  30.4 us (27%)
  waiting for transfers between devices  22.7 us (20%)
  between operations  1.23 us (1%)
    ppermute x36, starting transfers between devices, swap(): return lax.ppermute(x, axis, [(i, i ^ bit) for i in range(size)])  58.2 us
    ppermute x36, waiting for transfers between devices, swap(): return lax.ppermute(x, axis, [(i, i ^ bit) for i in range(size)])  22.7 us
    pallas_call x11, Pallas kernels, unit_call(): pl.pallas_call(kernel, out_shape=[struct(shape) for shape in outs], in_sp...  20.8 us
    pallas_call x5, Pallas kernels, one_call(): pl.pallas_call(kernel, out_shape=shapes, in_specs=specs, out_specs=[whole...  5 us
    pallas_call x1, Pallas kernels, front(): pl.pallas_call(functools.partial(front_kernel, units, line_length), out_s...  2.58 us
  transfers between devices with their start and end apart: 44, of which 18 were waited for; matrix products, arithmetic and copies ran while one was open for 1% of the time, Pallas kernels for 24%

profile of v5, /device:TPU:0, one launch (start us, length us, event | category | flops | bytes accessed | tf_op | source)
XLA Modules:
  0.0 114.0 jit_solution(50143611937527277)
XLA Ops:
  0.7 2.6 %shard_map.136 = (f32[56,768]{1,0:T(8,128)S(1)}, f32[8,256]{1,0:T(8,128)S(1)}, f32[4,64,768]{2,1,0:T(8,128)S(1)}, f32[2,64,768]{2,1,0:T(8,128)S(1)}, f32[2,64,768]{2,1,0:T(8,128)S(1)}) custom-call(s32[8]{0:T(128)} %len_ref.9, f32[2,32,4,64]{3,2,1,0:T(4,128)} %in_ref.1, f32[2,32,4,64]{3,2,1,0:T(4,128)} %out_hbm.1, f32[1,64]{1,0:T(1,128)} %bitcast.8, ...), custom_call_target="tpu_custom_call" | custom-call | flops 1474560 | bytes 2949120 | tf_op jit(solution)/shard_map/pallas_call | solution.py:463
  3.2 3.0 %collective-permute-start = (f32[56,768]{1,0:T(8,128)S(1)}, f32[56,768]{1,0:T(8,128)S(1)}, u32[]{:S(2)}, u32[]{:S(2)}) collective-permute-start(f32[56,768]{1,0:T(8,128)S(1)} %get-tuple-element.127.own_ref), channel_id=1, source_target_pairs={{0,1},{1,0},{2,3},{3,2},{4,5},{5,4},{6,7},{7,6},{8,9},{9,8},{10,11... | collective-permute-start | bytes 516104 | tf_op jit(solution)/shard_map/message_x/ppermute | solution.py:519
  6.3 2.0 %shard_map.137 = (f32[4,64,768]{2,1,0:T(8,128)S(1)}, f32[1,64,768]{2,1,0:T(8,128)S(1)}, f32[1,64,768]{2,1,0:T(8,128)S(1)}, f32[1,64,768]{2,1,0:T(8,128)S(1)}, f32[1,64,768]{2,1,0:T(8,128)S(1)}) custom-call(s32[8]{0:T(128)} %len_ref.9, f32[64,5760]{1,0:T(8,128)} %cot_ref.1), custom_call_target="tpu_custom_call" | custom-call | flops 1474560 | bytes 2949120 | tf_op jit(solution)/shard_map/pallas_call | solution.py:479
  8.3 2.7 %collective-permute-done.rec_ref = f32[56,768]{1,0:T(8,128)S(1)} collective-permute-done((f32[56,768]{1,0:T(8,128)S(1)}, f32[56,768]{1,0:T(8,128)S(1)}, u32[]{:S(2)}, u32[]{:S(2)}) %collective-permute-start) | collective-permute-done | bytes 172064 | tf_op jit(solution)/shard_map/message_x/ppermute | solution.py:519
  11.0 2.5 %collective-permute-start.1 = (f32[1,64,768]{2,1,0:T(8,128)S(1)}, f32[1,64,768]{2,1,0:T(8,128)S(1)}, u32[]{:S(2)}, u32[]{:S(2)}) collective-permute-start(f32[1,64,768]{2,1,0:T(8,128)S(1)} %get-tuple-element.133), channel_id=1, source_target_pairs={{0,1},{1,0},{2,3},{3,2},{4,5},{5,4},{6,7},{7,6},{8,9},{9,8},{10,11... | collective-permute-start | bytes 589832 | tf_op jit(solution)/shard_map/cot_x/ppermute | solution.py:519
  17.0 1.6 %collective-permute-start.8 = (f32[256,256]{1,0:T(8,128)S(1)}, f32[256,256]{1,0:T(8,128)S(1)}, u32[]{:S(2)}, u32[]{:S(2)}) collective-permute-start(f32[256,256]{1,0:T(8,128)S(1)} %shard_map.139), channel_id=1, source_target_pairs={{0,2},{1,3},{2,0},{3,1},{4,6},{5,7},{6,4},{7,5},{8,10},{9,11},{10,... | collective-permute-start | bytes 786440 | tf_op jit(solution)/shard_map/e0/ppermute | solution.py:519
  21.2 2.7 %collective-permute-start.6 = (f32[8,768]{1,0:T(8,128)S(1)}, f32[8,768]{1,0:T(8,128)S(1)}, u32[]{:S(2)}, u32[]{:S(2)}) collective-permute-start(f32[8,768]{1,0:T(8,128)S(1)} %add.85), channel_id=1, source_target_pairs={{0,4},{1,5},{2,6},{3,7},{4,0},{5,1},{6,2},{7,3},{8,12},{9,13},{10,... | collective-permute-start | bytes 73736 | tf_op jit(solution)/shard_map/squares_z2/ppermute | solution.py:519
  23.9 1.7 %collective-permute-start.5 = (f32[256,256]{1,0:T(8,128)S(1)}, f32[256,256]{1,0:T(8,128)S(1)}, u32[]{:S(2)}, u32[]{:S(2)}) collective-permute-start(f32[256,256]{1,0:T(8,128)S(1)} %shard_map.140), channel_id=1, source_target_pairs={{0,2},{1,3},{2,0},{3,1},{4,6},{5,7},{6,4},{7,5},{8,10},{9,11},{10,... | collective-permute-start | bytes 786440 | tf_op jit(solution)/shard_map/e1/ppermute | solution.py:519
  28.6 2.7 %collective-permute-start.11 = (f32[256,256]{1,0:T(8,128)S(1)}, f32[256,256]{1,0:T(8,128)S(1)}, u32[]{:S(2)}, u32[]{:S(2)}) collective-permute-start(f32[256,256]{1,0:T(8,128)S(1)} %shard_map.141), channel_id=1, source_target_pairs={{0,2},{1,3},{2,0},{3,1},{4,6},{5,7},{6,4},{7,5},{8,10},{9,11},{10,... | collective-permute-start | bytes 786440 | tf_op jit(solution)/shard_map/e2/ppermute | solution.py:519
  31.4 2.0 %collective-permute-done.4.rec_ref.cot_rec = f32[1,64,768]{2,1,0:T(8,128)S(1)} collective-permute-done((f32[1,64,768]{2,1,0:T(8,128)S(1)}, f32[1,64,768]{2,1,0:T(8,128)S(1)}, u32[]{:S(2)}, u32[]{:S(2)}) %collective-permute-start.4) | collective-permute-done | bytes 196640 | tf_op jit(solution)/shard_map/cot_x/ppermute | solution.py:519
  34.3 1.7 %collective-permute-start.9 = (f32[2,64,768]{2,1,0:T(8,128)S(1)}, f32[2,64,768]{2,1,0:T(8,128)S(1)}, u32[]{:S(2)}, u32[]{:S(2)}) collective-permute-start(f32[2,64,768]{2,1,0:T(8,128)S(1)} %get-tuple-element.151.refs_5_), channel_id=1, source_target_pairs={{0,1},{1,0},{2,3},{3,2},{4,5},{5,4},{6,7},{7,6},{8,9},{9,8},{10,11... | collective-permute-start | bytes 1179656 | tf_op jit(solution)/shard_map/ser_x/ppermute | solution.py:519
  36.0 2.4 %collective-permute-start.14 = (f32[256,256]{1,0:T(8,128)S(1)}, f32[256,256]{1,0:T(8,128)S(1)}, u32[]{:S(2)}, u32[]{:S(2)}) collective-permute-start(f32[256,256]{1,0:T(8,128)S(1)} %add_select_fusion.4.refs_0_), channel_id=1, source_target_pairs={{0,2},{1,3},{2,0},{3,1},{4,6},{5,7},{6,4},{7,5},{8,10},{9,11},{10,... | collective-permute-start | bytes 786440 | tf_op jit(solution)/shard_map/e3/ppermute | solution.py:519
  38.5 2.4 %collective-permute-done.10.rec_ref.ser_rec = f32[2,64,768]{2,1,0:T(8,128)S(1)} collective-permute-done((f32[2,64,768]{2,1,0:T(8,128)S(1)}, f32[2,64,768]{2,1,0:T(8,128)S(1)}, u32[]{:S(2)}, u32[]{:S(2)}) %collective-permute-start.10) | collective-permute-done | bytes 393248 | tf_op jit(solution)/shard_map/ser_x/ppermute | solution.py:519
  41.0 2.1 %shard_map.143 = (f32[256,256]{1,0:T(8,128)S(1)}, f32[256,256]{1,0:T(8,128)S(1)}) custom-call(f32[4,64,768]{2,1,0:T(8,128)S(1)} %get-tuple-element.125.own_ref.ser_own.x_own, f32[2,64,768]{2,1,0:T(8,128)S(1)} %collective-permute-done.10.rec_ref.ser_rec, f32[8,768]{1,0:T(8,128)S(1)} %add.86.ss_ref.refs_4_, bf16[256,192]{1,0:T(8,128)(2,1)S(1)} %get-tuple-element.158.down_own, ...), custom_call_target="tpu_custom_call" | custom-call | flops 14092861440 | bytes 21872640 | tf_op jit(solution)/shard_map/pallas_call | solution.py:506
  43.1 1.6 %collective-permute-start.16 = (f32[256,256]{1,0:T(8,128)S(1)}, f32[256,256]{1,0:T(8,128)S(1)}, u32[]{:S(2)}, u32[]{:S(2)}) collective-permute-start(f32[256,256]{1,0:T(8,128)S(1)} %add_select_fusion.3.refs_1_), channel_id=1, source_target_pairs={{0,2},{1,3},{2,0},{3,1},{4,6},{5,7},{6,4},{7,5},{8,10},{9,11},{10,... | collective-permute-start | bytes 786440 | tf_op jit(solution)/shard_map/e4/ppermute | solution.py:519
  44.9 4.5 %collective-permute-start.18 = (f32[256,256]{1,0:T(8,128)S(1)}, f32[256,256]{1,0:T(8,128)S(1)}, u32[]{:S(2)}, u32[]{:S(2)}) collective-permute-start(f32[256,256]{1,0:T(8,128)S(1)} %add_select_fusion.2.refs_0_), channel_id=1, source_target_pairs={{0,2},{1,3},{2,0},{3,1},{4,6},{5,7},{6,4},{7,5},{8,10},{9,11},{10,... | collective-permute-start | bytes 786440 | tf_op jit(solution)/shard_map/e5/ppermute | solution.py:519
  49.4 2.1 %shard_map.144 = (f32[256,256]{1,0:T(8,128)S(1)}, f32[256,256]{1,0:T(8,128)S(1)}) custom-call(f32[4,64,768]{2,1,0:T(8,128)S(1)} %get-tuple-element.125.own_ref.ser_own.x_own, f32[2,64,768]{2,1,0:T(8,128)S(1)} %collective-permute-done.9.rec_ref.ser_rec, f32[8,768]{1,0:T(8,128)S(1)} %add.86.ss_ref.refs_4_, bf16[256,192]{1,0:T(8,128)(2,1)S(1)} %get-tuple-element.158.down_own, ...), custom_call_target="tpu_custom_call" | custom-call | flops 14092861440 | bytes 21872640 | tf_op jit(solution)/shard_map/pallas_call | solution.py:506
  51.7 3.2 %collective-permute-start.22 = (f32[256,256]{1,0:T(8,128)S(1)}, f32[256,256]{1,0:T(8,128)S(1)}, u32[]{:S(2)}, u32[]{:S(2)}) collective-permute-start(f32[256,256]{1,0:T(8,128)S(1)} %add_select_fusion.1.refs_1_), channel_id=1, source_target_pairs={{0,2},{1,3},{2,0},{3,1},{4,6},{5,7},{6,4},{7,5},{8,10},{9,11},{10,... | collective-permute-start | bytes 786440 | tf_op jit(solution)/shard_map/e6/ppermute | solution.py:519
  55.8 3.7 %shard_map.145 = (f32[2,64,768]{2,1,0:T(8,128)S(1)}, f32[2,64,768]{2,1,0:T(8,128)S(1)}, f32[64,256]{1,0:T(8,128)S(1)}, f32[64,256]{1,0:T(8,128)S(1)}, f32[2,8,256]{2,1,0:T(8,128)S(1)}) custom-call(s32[8]{0:T(128)S(1)} %copy-done.3, f32[4,64,768]{2,1,0:T(8,128)S(1)} %get-tuple-element.125.own_ref.ser_own.x_own, ...), custom_call_target="tpu_custom_call" | custom-call | flops 16106127360 | bytes 31703040 | tf_op jit(solution)/shard_map/pallas_call | solution.py:506
  60.6 2.8 %collective-permute-start.20 = (f32[256,256]{1,0:T(8,128)S(1)}, f32[256,256]{1,0:T(8,128)S(1)}, u32[]{:S(2)}, u32[]{:S(2)}) collective-permute-start(f32[256,256]{1,0:T(8,128)S(1)} %add_select_fusion.refs_0_), channel_id=1, source_target_pairs={{0,2},{1,3},{2,0},{3,1},{4,6},{5,7},{6,4},{7,5},{8,10},{9,11},{10,... | collective-permute-start | bytes 786440 | tf_op jit(solution)/shard_map/e7/ppermute | solution.py:519
  63.5 3.9 %shard_map.146 = (f32[2,64,768]{2,1,0:T(8,128)S(1)}, f32[2,64,768]{2,1,0:T(8,128)S(1)}, f32[64,256]{1,0:T(8,128)S(1)}, f32[64,256]{1,0:T(8,128)S(1)}, f32[2,8,256]{2,1,0:T(8,128)S(1)}) custom-call(s32[8]{0:T(128)S(1)} %copy-done.3, f32[4,64,768]{2,1,0:T(8,128)S(1)} %get-tuple-element.125.own_ref.ser_own.x_own, ...), custom_call_target="tpu_custom_call" | custom-call | flops 16106127360 | bytes 33013760 | tf_op jit(solution)/shard_map/pallas_call | solution.py:506
  70.6 2.2 %collective-permute-start.33 = (f32[256,256]{1,0:T(8,128)S(1)}, f32[256,256]{1,0:T(8,128)S(1)}, u32[]{:S(2)}, u32[]{:S(2)}) collective-permute-start(f32[256,256]{1,0:T(8,128)S(1)} %add.101.refs_0_), channel_id=1, source_target_pairs={{0,2},{1,3},{2,0},{3,1},{4,6},{5,7},{6,4},{7,5},{8,10},{9,11},{10,... | collective-permute-start | bytes 786440 | tf_op jit(solution)/shard_map/e9/ppermute | solution.py:519
  73.7 1.9 %collective-permute-start.29 = (f32[32,256]{1,0:T(8,128)S(1)}, f32[32,256]{1,0:T(8,128)S(1)}, u32[]{:S(2)}, u32[]{:S(2)}) collective-permute-start(f32[32,256]{1,0:T(8,128)S(1)} %pad_maximum_fusion.3), channel_id=1, source_target_pairs={{0,2},{1,3},{2,0},{3,1},{4,6},{5,7},{6,4},{7,5},{8,10},{9,11},{10,... | collective-permute-start | bytes 98312 | tf_op jit(solution)/shard_map/inner_z1/ppermute | solution.py:519
  78.1 2.5 %shard_map.147 = (f32[2,64,768]{2,1,0:T(8,128)S(1)}, f32[2,64,768]{2,1,0:T(8,128)S(1)}, f32[64,256]{1,0:T(8,128)S(1)}, f32[64,256]{1,0:T(8,128)S(1)}, f32[8,256]{1,0:T(8,128)S(1)}) custom-call(s32[8]{0:T(128)S(1)} %copy-done.3, f32[4,64,768]{2,1,0:T(8,128)S(1)} %get-tuple-element.125.own_ref.ser_own.x_own, ...), custom_call_target="tpu_custom_call" | custom-call | flops 12079595520 | bytes 35389440 | tf_op jit(solution)/shard_map/pallas_call | solution.py:506
  82.9 2.0 %collective-permute-start.30 = (f32[32,256]{1,0:T(8,128)S(1)}, f32[32,256]{1,0:T(8,128)S(1)}, u32[]{:S(2)}, u32[]{:S(2)}) collective-permute-start(f32[32,256]{1,0:T(8,128)S(1)} %fusion.1), channel_id=1, source_target_pairs={{0,4},{1,5},{2,6},{3,7},{4,0},{5,1},{6,2},{7,3},{8,12},{9,13},{10,... | collective-permute-start | bytes 98312 | tf_op jit(solution)/shard_map/inner_z2/ppermute | solution.py:519
  86.5 2.2 %collective-permute-done.32.refs_3_ = f32[2,64,768]{2,1,0:T(8,128)S(1)} collective-permute-done((f32[2,64,768]{2,1,0:T(8,128)S(1)}, f32[2,64,768]{2,1,0:T(8,128)S(1)}, u32[]{:S(2)}, u32[]{:S(2)}) %collective-permute-start.32) | collective-permute-done | bytes 393248 | tf_op jit(solution)/shard_map/scaled1/ppermute | solution.py:519
  88.7 1.6 %collective-permute-start.34 = (f32[64,256]{1,0:T(8,128)S(1)}, f32[64,256]{1,0:T(8,128)S(1)}, u32[]{:S(2)}, u32[]{:S(2)}) collective-permute-start(f32[64,256]{1,0:T(8,128)S(1)} %add.105), channel_id=1, source_target_pairs={{0,16},{8,24},{16,0},{24,8},{1,17},{9,25},{17,1},{25,9},{2,18},{10... | collective-permute-start | bytes 196616 | tf_op jit(solution)/shard_map/r_y/ppermute | solution.py:519
  93.0 1.6 %collective-permute-start.35 = (f32[72,256]{1,0:T(8,128)S(1)}, f32[72,256]{1,0:T(8,128)S(1)}, u32[]{:S(2)}, u32[]{:S(2)}) collective-permute-start(f32[72,256]{1,0:T(8,128)S(1)} %pad_maximum_fusion.1), channel_id=1, source_target_pairs={{0,1},{1,0},{2,3},{3,2},{4,5},{5,4},{6,7},{7,6},{8,9},{9,8},{10,11... | collective-permute-start | bytes 221192 | tf_op jit(solution)/shard_map/w_x/ppermute | solution.py:519
  97.1 2.0 %collective-permute-done.37.in_rec = f32[32,256]{1,0:T(8,128)S(1)} collective-permute-done((f32[32,256]{1,0:T(8,128)S(1)}, f32[32,256]{1,0:T(8,128)S(1)}, u32[]{:S(2)}, u32[]{:S(2)}) %collective-permute-start.37) | collective-permute-done | bytes 32800 | tf_op jit(solution)/shard_map/inner_x/ppermute | solution.py:519
  100.5 1.6 %collective-permute-start.39 = (f32[72,256]{1,0:T(8,128)S(1)}, f32[72,256]{1,0:T(8,128)S(1)}, u32[]{:S(2)}, u32[]{:S(2)}) collective-permute-start(f32[72,256]{1,0:T(8,128)S(1)} %add.109), channel_id=1, source_target_pairs={{0,16},{8,24},{16,0},{24,8},{1,17},{9,25},{17,1},{25,9},{2,18},{10... | collective-permute-start | bytes 221192 | tf_op jit(solution)/shard_map/w_y/ppermute | solution.py:519
  102.2 1.7 %shard_map.150 = f32[64,5760]{1,0:T(8,128)} custom-call(f32[64,5760]{1,0:T(8,128)S(1)} %copy-done, f32[4,64,768]{2,1,0:T(8,128)S(1)} %get-tuple-element.125.own_ref.ser_own.x_own, f32[8,768]{1,0:T(8,128)S(1)} %add.86.ss_ref.refs_4_, f32[32,256]{1,0:T(8,128)S(1)} %add.106.in_own, f32[32,256]{1,0:T(8,128)S(1)} %collective-permute-done.37.in_rec, ...), custom_call_target="tpu_custom_call" | custom-call | flops 61849 | bytes 61849 | tf_op jit(solution)/shard_map/pallas_call | solution.py:430
  108.7 1.8 %collective-permute-start.43 = (f32[8,256]{1,0:T(8,128)S(1)}, f32[8,256]{1,0:T(8,128)S(1)}, u32[]{:S(2)}, u32[]{:S(2)}) collective-permute-start(f32[8,256]{1,0:T(8,128)S(1)} %add.111.own_ref), channel_id=1, source_target_pairs={{0,4},{1,5},{2,6},{3,7},{4,0},{5,1},{6,2},{7,3},{8,12},{9,13},{10,... | collective-permute-start | bytes 24584 | tf_op jit(solution)/shard_map/stats_2/ppermute | solution.py:519
  (123 shorter events, 38.1 us)
Async XLA Ops:
  3.2 7.8 %collective-permute-start = (f32[56,768]{1,0:T(8,128)S(1)}, f32[56,768]{1,0:T(8,128)S(1)}, u32[]{:S(2)}, u32[]{:S(2)}) collective-permute-start(f32[56,768]{1,0:T(8,128)S(1)} %get-tuple-element.127.own_ref), channel_id=1, source_target_pairs={{0,1},{1,0},{2,3},{3,2},{4,5},{5,4},{6,7},{7,6},{8,9},{9,8},{10,11... | collective-permute-start | bytes 516104 | tf_op jit(solution)/shard_map/message_x/ppermute | solution.py:519
  8.2 7.9 %collective-permute-start.2 = (f32[1,64,768]{2,1,0:T(8,128)S(1)}, f32[1,64,768]{2,1,0:T(8,128)S(1)}, u32[]{:S(2)}, u32[]{:S(2)}) collective-permute-start(f32[1,64,768]{2,1,0:T(8,128)S(1)} %get-tuple-element.134), channel_id=1, source_target_pairs={{0,1},{1,0},{2,3},{3,2},{4,5},{5,4},{6,7},{7,6},{8,9},{9,8},{10,11... | collective-permute-start | bytes 589832 | tf_op jit(solution)/shard_map/cot_x/ppermute | solution.py:519
  11.0 9.2 %collective-permute-start.1 = (f32[1,64,768]{2,1,0:T(8,128)S(1)}, f32[1,64,768]{2,1,0:T(8,128)S(1)}, u32[]{:S(2)}, u32[]{:S(2)}) collective-permute-start(f32[1,64,768]{2,1,0:T(8,128)S(1)} %get-tuple-element.133), channel_id=1, source_target_pairs={{0,1},{1,0},{2,3},{3,2},{4,5},{5,4},{6,7},{7,6},{8,9},{9,8},{10,11... | collective-permute-start | bytes 589832 | tf_op jit(solution)/shard_map/cot_x/ppermute | solution.py:519
  13.5 7.6 %collective-permute-start.3 = (f32[8,768]{1,0:T(8,128)S(1)}, f32[8,768]{1,0:T(8,128)S(1)}, u32[]{:S(2)}, u32[]{:S(2)}) collective-permute-start(f32[8,768]{1,0:T(8,128)S(1)} %slice_add_fusion), channel_id=1, source_target_pairs={{0,2},{1,3},{2,0},{3,1},{4,6},{5,7},{6,4},{7,5},{8,10},{9,11},{10,... | collective-permute-start | bytes 73736 | tf_op jit(solution)/shard_map/squares_z1/ppermute | solution.py:519
  17.0 10.6 %collective-permute-start.8 = (f32[256,256]{1,0:T(8,128)S(1)}, f32[256,256]{1,0:T(8,128)S(1)}, u32[]{:S(2)}, u32[]{:S(2)}) collective-permute-start(f32[256,256]{1,0:T(8,128)S(1)} %shard_map.139), channel_id=1, source_target_pairs={{0,2},{1,3},{2,0},{3,1},{4,6},{5,7},{6,4},{7,5},{8,10},{9,11},{10,... | collective-permute-start | bytes 786440 | tf_op jit(solution)/shard_map/e0/ppermute | solution.py:519
  18.7 9.1 %collective-permute-start.7 = (f32[1,64,768]{2,1,0:T(8,128)S(1)}, f32[1,64,768]{2,1,0:T(8,128)S(1)}, u32[]{:S(2)}, u32[]{:S(2)}) collective-permute-start(f32[1,64,768]{2,1,0:T(8,128)S(1)} %get-tuple-element.144), channel_id=1, source_target_pairs={{0,1},{1,0},{2,3},{3,2},{4,5},{5,4},{6,7},{7,6},{8,9},{9,8},{10,11... | collective-permute-start | bytes 589832 | tf_op jit(solution)/shard_map/cot_x/ppermute | solution.py:519
  23.9 7.5 %collective-permute-start.5 = (f32[256,256]{1,0:T(8,128)S(1)}, f32[256,256]{1,0:T(8,128)S(1)}, u32[]{:S(2)}, u32[]{:S(2)}) collective-permute-start(f32[256,256]{1,0:T(8,128)S(1)} %shard_map.140), channel_id=1, source_target_pairs={{0,2},{1,3},{2,0},{3,1},{4,6},{5,7},{6,4},{7,5},{8,10},{9,11},{10,... | collective-permute-start | bytes 786440 | tf_op jit(solution)/shard_map/e1/ppermute | solution.py:519
  25.6 7.8 %collective-permute-start.4 = (f32[1,64,768]{2,1,0:T(8,128)S(1)}, f32[1,64,768]{2,1,0:T(8,128)S(1)}, u32[]{:S(2)}, u32[]{:S(2)}) collective-permute-start(f32[1,64,768]{2,1,0:T(8,128)S(1)} %get-tuple-element.142), channel_id=1, source_target_pairs={{0,1},{1,0},{2,3},{3,2},{4,5},{5,4},{6,7},{7,6},{8,9},{9,8},{10,11... | collective-permute-start | bytes 589832 | tf_op jit(solution)/shard_map/cot_x/ppermute | solution.py:519
  27.2 13.8 %collective-permute-start.10 = (f32[2,64,768]{2,1,0:T(8,128)S(1)}, f32[2,64,768]{2,1,0:T(8,128)S(1)}, u32[]{:S(2)}, u32[]{:S(2)}) collective-permute-start(f32[2,64,768]{2,1,0:T(8,128)S(1)} %get-tuple-element.154.refs_4_), channel_id=1, source_target_pairs={{0,1},{1,0},{2,3},{3,2},{4,5},{5,4},{6,7},{7,6},{8,9},{9,8},{10,11... | collective-permute-start | bytes 1179656 | tf_op jit(solution)/shard_map/ser_x/ppermute | solution.py:519
  27.7 8.3 %collective-permute-start.12 = (f32[256,256]{1,0:T(8,128)S(1)}, f32[256,256]{1,0:T(8,128)S(1)}, u32[]{:S(2)}, u32[]{:S(2)}) collective-permute-start(f32[256,256]{1,0:T(8,128)S(1)} %add.87), channel_id=1, source_target_pairs={{0,8},{1,9},{2,4},{3,5},{4,2},{5,3},{6,14},{7,15},{8,0},{9,1},{10,... | collective-permute-start | bytes 786440 | tf_op jit(solution)/shard_map/m0/ppermute | solution.py:543
  28.6 9.7 %collective-permute-start.11 = (f32[256,256]{1,0:T(8,128)S(1)}, f32[256,256]{1,0:T(8,128)S(1)}, u32[]{:S(2)}, u32[]{:S(2)}) collective-permute-start(f32[256,256]{1,0:T(8,128)S(1)} %shard_map.141), channel_id=1, source_target_pairs={{0,2},{1,3},{2,0},{3,1},{4,6},{5,7},{6,4},{7,5},{8,10},{9,11},{10,... | collective-permute-start | bytes 786440 | tf_op jit(solution)/shard_map/e2/ppermute | solution.py:519
  31.4 11.7 %collective-permute-start.15 = (f32[256,256]{1,0:T(8,128)S(1)}, f32[256,256]{1,0:T(8,128)S(1)}, u32[]{:S(2)}, u32[]{:S(2)}) collective-permute-start(f32[256,256]{1,0:T(8,128)S(1)} %add.88), channel_id=1, source_target_pairs={{0,8},{1,9},{2,4},{3,5},{4,2},{5,3},{6,14},{7,15},{8,0},{9,1},{10,... | collective-permute-start | bytes 786440 | tf_op jit(solution)/shard_map/m1/ppermute | solution.py:543
  34.3 15.0 %collective-permute-start.9 = (f32[2,64,768]{2,1,0:T(8,128)S(1)}, f32[2,64,768]{2,1,0:T(8,128)S(1)}, u32[]{:S(2)}, u32[]{:S(2)}) collective-permute-start(f32[2,64,768]{2,1,0:T(8,128)S(1)} %get-tuple-element.151.refs_5_), channel_id=1, source_target_pairs={{0,1},{1,0},{2,3},{3,2},{4,5},{5,4},{6,7},{7,6},{8,9},{9,8},{10,11... | collective-permute-start | bytes 1179656 | tf_op jit(solution)/shard_map/ser_x/ppermute | solution.py:519
  36.0 8.7 %collective-permute-start.14 = (f32[256,256]{1,0:T(8,128)S(1)}, f32[256,256]{1,0:T(8,128)S(1)}, u32[]{:S(2)}, u32[]{:S(2)}) collective-permute-start(f32[256,256]{1,0:T(8,128)S(1)} %add_select_fusion.4.refs_0_), channel_id=1, source_target_pairs={{0,2},{1,3},{2,0},{3,1},{4,6},{5,7},{6,4},{7,5},{8,10},{9,11},{10,... | collective-permute-start | bytes 786440 | tf_op jit(solution)/shard_map/e3/ppermute | solution.py:519
  43.1 8.4 %collective-permute-start.16 = (f32[256,256]{1,0:T(8,128)S(1)}, f32[256,256]{1,0:T(8,128)S(1)}, u32[]{:S(2)}, u32[]{:S(2)}) collective-permute-start(f32[256,256]{1,0:T(8,128)S(1)} %add_select_fusion.3.refs_1_), channel_id=1, source_target_pairs={{0,2},{1,3},{2,0},{3,1},{4,6},{5,7},{6,4},{7,5},{8,10},{9,11},{10,... | collective-permute-start | bytes 786440 | tf_op jit(solution)/shard_map/e4/ppermute | solution.py:519
  44.9 10.8 %collective-permute-start.18 = (f32[256,256]{1,0:T(8,128)S(1)}, f32[256,256]{1,0:T(8,128)S(1)}, u32[]{:S(2)}, u32[]{:S(2)}) collective-permute-start(f32[256,256]{1,0:T(8,128)S(1)} %add_select_fusion.2.refs_0_), channel_id=1, source_target_pairs={{0,2},{1,3},{2,0},{3,1},{4,6},{5,7},{6,4},{7,5},{8,10},{9,11},{10,... | collective-permute-start | bytes 786440 | tf_op jit(solution)/shard_map/e5/ppermute | solution.py:519
  51.5 9.1 %collective-permute-start.17 = (f32[256,256]{1,0:T(8,128)S(1)}, f32[256,256]{1,0:T(8,128)S(1)}, u32[]{:S(2)}, u32[]{:S(2)}) collective-permute-start(f32[256,256]{1,0:T(8,128)S(1)} %add.94), channel_id=1, source_target_pairs={{0,8},{1,9},{2,4},{3,5},{4,2},{5,3},{6,14},{7,15},{8,0},{9,1},{10,... | collective-permute-start | bytes 786440 | tf_op jit(solution)/shard_map/m4/ppermute | solution.py:543
  51.7 11.7 %collective-permute-start.22 = (f32[256,256]{1,0:T(8,128)S(1)}, f32[256,256]{1,0:T(8,128)S(1)}, u32[]{:S(2)}, u32[]{:S(2)}) collective-permute-start(f32[256,256]{1,0:T(8,128)S(1)} %add_select_fusion.1.refs_1_), channel_id=1, source_target_pairs={{0,2},{1,3},{2,0},{3,1},{4,6},{5,7},{6,4},{7,5},{8,10},{9,11},{10,... | collective-permute-start | bytes 786440 | tf_op jit(solution)/shard_map/e6/ppermute | solution.py:519
  55.7 11.7 %collective-permute-start.21 = (f32[256,256]{1,0:T(8,128)S(1)}, f32[256,256]{1,0:T(8,128)S(1)}, u32[]{:S(2)}, u32[]{:S(2)}) collective-permute-start(f32[256,256]{1,0:T(8,128)S(1)} %add.96), channel_id=1, source_target_pairs={{0,8},{1,9},{2,4},{3,5},{4,2},{5,3},{6,14},{7,15},{8,0},{9,1},{10,... | collective-permute-start | bytes 786440 | tf_op jit(solution)/shard_map/m5/ppermute | solution.py:543
  59.5 16.1 %collective-permute-start.24 = (f32[2,64,768]{2,1,0:T(8,128)S(1)}, f32[2,64,768]{2,1,0:T(8,128)S(1)}, u32[]{:S(2)}, u32[]{:S(2)}) collective-permute-start(f32[2,64,768]{2,1,0:T(8,128)S(1)} %get-tuple-element.185), channel_id=1, source_target_pairs={{0,1},{1,0},{2,3},{3,2},{4,5},{5,4},{6,7},{7,6},{8,9},{9,8},{10,11... | collective-permute-start | bytes 1179656 | tf_op jit(solution)/shard_map/scaled0/ppermute | solution.py:519
  60.6 8.5 %collective-permute-start.20 = (f32[256,256]{1,0:T(8,128)S(1)}, f32[256,256]{1,0:T(8,128)S(1)}, u32[]{:S(2)}, u32[]{:S(2)}) collective-permute-start(f32[256,256]{1,0:T(8,128)S(1)} %add_select_fusion.refs_0_), channel_id=1, source_target_pairs={{0,2},{1,3},{2,0},{3,1},{4,6},{5,7},{6,4},{7,5},{8,10},{9,11},{10,... | collective-permute-start | bytes 786440 | tf_op jit(solution)/shard_map/e7/ppermute | solution.py:519
  67.4 9.2 %collective-permute-start.27 = (f32[256,256]{1,0:T(8,128)S(1)}, f32[256,256]{1,0:T(8,128)S(1)}, u32[]{:S(2)}, u32[]{:S(2)}) collective-permute-start(f32[256,256]{1,0:T(8,128)S(1)} %add.99.refs_1_), channel_id=1, source_target_pairs={{0,2},{1,3},{2,0},{3,1},{4,6},{5,7},{6,4},{7,5},{8,10},{9,11},{10,... | collective-permute-start | bytes 786440 | tf_op jit(solution)/shard_map/e8/ppermute | solution.py:519
  69.1 11.5 %collective-permute-start.23 = (f32[256,256]{1,0:T(8,128)S(1)}, f32[256,256]{1,0:T(8,128)S(1)}, u32[]{:S(2)}, u32[]{:S(2)}) collective-permute-start(f32[256,256]{1,0:T(8,128)S(1)} %add.100), channel_id=1, source_target_pairs={{0,8},{1,9},{2,4},{3,5},{4,2},{5,3},{6,14},{7,15},{8,0},{9,1},{10,... | collective-permute-start | bytes 786440 | tf_op jit(solution)/shard_map/m7/ppermute | solution.py:543
  70.6 12.2 %collective-permute-start.33 = (f32[256,256]{1,0:T(8,128)S(1)}, f32[256,256]{1,0:T(8,128)S(1)}, u32[]{:S(2)}, u32[]{:S(2)}) collective-permute-start(f32[256,256]{1,0:T(8,128)S(1)} %add.101.refs_0_), channel_id=1, source_target_pairs={{0,2},{1,3},{2,0},{3,1},{4,6},{5,7},{6,4},{7,5},{8,10},{9,11},{10,... | collective-permute-start | bytes 786440 | tf_op jit(solution)/shard_map/e9/ppermute | solution.py:519
  73.7 8.8 %collective-permute-start.29 = (f32[32,256]{1,0:T(8,128)S(1)}, f32[32,256]{1,0:T(8,128)S(1)}, u32[]{:S(2)}, u32[]{:S(2)}) collective-permute-start(f32[32,256]{1,0:T(8,128)S(1)} %pad_maximum_fusion.3), channel_id=1, source_target_pairs={{0,2},{1,3},{2,0},{3,1},{4,6},{5,7},{6,4},{7,5},{8,10},{9,11},{10,... | collective-permute-start | bytes 98312 | tf_op jit(solution)/shard_map/inner_z1/ppermute | solution.py:519
  75.6 13.0 %collective-permute-start.31 = (f32[64,256]{1,0:T(8,128)S(1)}, f32[64,256]{1,0:T(8,128)S(1)}, u32[]{:S(2)}, u32[]{:S(2)}) collective-permute-start(f32[64,256]{1,0:T(8,128)S(1)} %add.102), channel_id=1, source_target_pairs={{0,8},{8,0},{16,24},{24,16},{1,9},{9,1},{17,25},{25,17},{2,10},{10... | collective-permute-start | bytes 196616 | tf_op jit(solution)/shard_map/r_c/ppermute | solution.py:519
  76.6 12.0 %collective-permute-start.32 = (f32[2,64,768]{2,1,0:T(8,128)S(1)}, f32[2,64,768]{2,1,0:T(8,128)S(1)}, u32[]{:S(2)}, u32[]{:S(2)}) collective-permute-start(f32[2,64,768]{2,1,0:T(8,128)S(1)} %get-tuple-element.201), channel_id=1, source_target_pairs={{0,1},{1,0},{2,3},{3,2},{4,5},{5,4},{6,7},{7,6},{8,9},{9,8},{10,11... | collective-permute-start | bytes 1179656 | tf_op jit(solution)/shard_map/scaled1/ppermute | solution.py:519
  80.6 18.6 %collective-permute-start.36 = (f32[2,64,768]{2,1,0:T(8,128)S(1)}, f32[2,64,768]{2,1,0:T(8,128)S(1)}, u32[]{:S(2)}, u32[]{:S(2)}) collective-permute-start(f32[2,64,768]{2,1,0:T(8,128)S(1)} %get-tuple-element.218), channel_id=1, source_target_pairs={{0,1},{1,0},{2,3},{3,2},{4,5},{5,4},{6,7},{7,6},{8,9},{9,8},{10,11... | collective-permute-start | bytes 1179656 | tf_op jit(solution)/shard_map/branch0/ppermute | solution.py:519
  82.5 8.6 %collective-permute-start.28 = (f32[256,256]{1,0:T(8,128)S(1)}, f32[256,256]{1,0:T(8,128)S(1)}, u32[]{:S(2)}, u32[]{:S(2)}) collective-permute-start(f32[256,256]{1,0:T(8,128)S(1)} %add.103.refs_0_), channel_id=1, source_target_pairs={{0,2},{1,3},{2,0},{3,1},{4,6},{5,7},{6,4},{7,5},{8,10},{9,11},{10,... | collective-permute-start | bytes 786440 | tf_op jit(solution)/shard_map/e10/ppermute | solution.py:519
  82.9 7.4 %collective-permute-start.30 = (f32[32,256]{1,0:T(8,128)S(1)}, f32[32,256]{1,0:T(8,128)S(1)}, u32[]{:S(2)}, u32[]{:S(2)}) collective-permute-start(f32[32,256]{1,0:T(8,128)S(1)} %fusion.1), channel_id=1, source_target_pairs={{0,4},{1,5},{2,6},{3,7},{4,0},{5,1},{6,2},{7,3},{8,12},{9,13},{10,... | collective-permute-start | bytes 98312 | tf_op jit(solution)/shard_map/inner_z2/ppermute | solution.py:519
  95.1 8.7 %collective-permute-start.40 = (f32[1,64,768]{2,1,0:T(8,128)S(1)}, f32[1,64,768]{2,1,0:T(8,128)S(1)}, u32[]{:S(2)}, u32[]{:S(2)}) collective-permute-start(f32[1,64,768]{2,1,0:T(8,128)S(1)} %get-tuple-element.224), channel_id=1, source_target_pairs={{0,1},{1,0},{2,3},{3,2},{4,5},{5,4},{6,7},{7,6},{8,9},{9,8},{10,11... | collective-permute-start | bytes 589832 | tf_op jit(solution)/shard_map/branch1/ppermute | solution.py:519
  96.6 9.8 %collective-permute-start.42 = (f32[1,64,768]{2,1,0:T(8,128)S(1)}, f32[1,64,768]{2,1,0:T(8,128)S(1)}, u32[]{:S(2)}, u32[]{:S(2)}) collective-permute-start(f32[1,64,768]{2,1,0:T(8,128)S(1)} %get-tuple-element.232), channel_id=1, source_target_pairs={{0,1},{1,0},{2,3},{3,2},{4,5},{5,4},{6,7},{7,6},{8,9},{9,8},{10,11... | collective-permute-start | bytes 589832 | tf_op jit(solution)/shard_map/branch2/ppermute | solution.py:519
  (20 other events, 129.9 us)

commit v6 on v5

--- a/solution.py
+++ b/solution.py
@@ -187,24 +187,17 @@
     return factor * jnp.cos(angle), factor * jnp.sin(angle)
 
 
-def front_kernel(units, line_length, len_hbm, in_hbm, out_hbm, gain_hbm, x_hbm, message_ref, end_ref, *refs):
-    out_refs, (len_ref, in_ref, out_ref, gain_ref, buffer, packed, sems, weight_sems) = refs[:-8], refs[-8:]
-    windows = x_hbm.shape[1] // LEN
+def pack_kernel(line_length, in_hbm, out_hbm, gain_hbm, message_ref, end_ref, in_ref, out_ref, gain_ref, packed, sems):
+    copies = [(in_hbm, in_ref), (out_hbm, out_ref), (gain_hbm, gain_ref)]
+    copies = [pltpu.make_async_copy(a, b, sems.at[k]) for k, (a, b) in enumerate(copies)]
+    for copy in copies:
+        copy.start()
     end_ref[...] = jnp.where(at_line_end(line_length), jnp.ones(end_ref.shape, f32), 0.0)
-    weights = [(in_hbm, in_ref), (out_hbm, out_ref), (gain_hbm, gain_ref)]
-    weights = [pltpu.make_async_copy(a, b, weight_sems.at[k]) for k, (a, b) in enumerate(weights)]
-    for copy in weights:
-        copy.start()
     message_ref[...] = jnp.zeros(message_ref.shape, f32)
-
-    def use(w, value):
-        message_ref[w : w + 1, :LEN] = jnp.sum(value * value, axis=0, keepdims=True)
-
-    deal_windows(units, len_hbm, x_hbm, len_ref, buffer, sems, out_refs, use)
-    for copy in weights:
+    packed[...] = jnp.zeros(packed.shape, f32)
+    for copy in copies:
         copy.wait()
     modes, ranks, channels = in_ref.shape[1:]
-    packed[...] = jnp.zeros(packed.shape, f32)
     read_real, read_imag = readout_columns(modes, channels)
     for r in range(ranks):
         real, imag = out_ref[0, :, r, :], out_ref[1, :, r, :]
@@ -216,14 +209,23 @@
     rows = packed.shape[0]
     for k in range(-(-rows // PACK)):
         count = min(PACK, rows - k * PACK)
-        message_ref[windows : windows + count, k * 128 : (k + 1) * 128] = packed[k * PACK : k * PACK + count]
-
-
-def unpack(message_ref, windows, rows):
+        message_ref[:count, k * 128 : (k + 1) * 128] = packed[k * PACK : k * PACK + count]
+
+
+def series_kernel(units, len_hbm, x_hbm, squares_ref, *refs):
+    squares_ref[...] = jnp.zeros(squares_ref.shape, f32)
+
+    def use(w, value):
+        squares_ref[w : w + 1, :LEN] = jnp.sum(value * value, axis=0, keepdims=True)
+
+    deal_windows(units, len_hbm, x_hbm, *refs[-3:], refs[:-3], use)
+
+
+def unpack(message_ref, rows):
     pieces = []
     for k in range(-(-rows // PACK)):
         count = min(PACK, rows - k * PACK)
-        pieces.append(message_ref[windows : windows + count, k * 128 : (k + 1) * 128])
+        pieces.append(message_ref[:count, k * 128 : (k + 1) * 128])
     return jnp.concatenate(pieces, axis=0)
 
 
@@ -231,11 +233,11 @@
     deal_windows(units, len_hbm, x_hbm, *refs[-3:], refs[:-3], lambda w, value: None)
 
 
-def weights_kernel(windows, own_ref, rec_ref, down_own, down_rec, up_own, up_rec, down_both, up_both):
+def weights_kernel(own_ref, rec_ref, down_own, down_rec, up_own, up_rec, down_both, up_both):
     rows, channels = down_own.shape[0], down_own.shape[1] // 3
     pieces = []
     for ref, down, up in ((own_ref, down_own, up_own), (rec_ref, down_rec, up_rec)):
-        packed = unpack(ref, windows, rows)
+        packed = unpack(ref, rows)
         high, low = split(packed)
         down[...] = jnp.concatenate([high[:, :channels], high[:, :channels], low[:, :channels]], axis=1)
         upper = slice(channels, 2 * channels)
@@ -454,43 +456,40 @@
     ]
 
 
-def front(series, lengths, weights, units, rows, line_length):
-    channels, windows = series.shape[0], series.shape[1] // LEN
-    shapes = [struct((windows + PACK, LANES)), struct((8, ORDER)), struct((windows // 2, channels, LANES))]
-    shapes += [struct((n, channels, LANES)) for _, n in units]
-    first, (buffer, sems) = deal_scratch(series, lengths)
-    scratch = first + [pltpu.VMEM(a.shape, f32) for a in weights] + [buffer, pltpu.VMEM((rows, 128), f32), sems]
+def pack(weights, rows, line_length):
+    shapes = [struct((PACK, LANES)), struct((8, ORDER))]
     return pl.pallas_call(
-        functools.partial(front_kernel, units, line_length),
+        functools.partial(pack_kernel, line_length),
         out_shape=shapes,
-        in_specs=[HBM] * (2 + len(weights)),
+        in_specs=[HBM] * len(weights),
         out_specs=[whole(o.shape) for o in shapes],
         grid=(1,),
-        scratch_shapes=scratch + [pltpu.SemaphoreType.DMA((len(weights),))],
+        scratch_shapes=[pltpu.VMEM(a.shape, f32) for a in weights]
+        + [pltpu.VMEM((rows, 128), f32), pltpu.SemaphoreType.DMA((len(weights),))],
         compiler_params=PARAMS,
-        cost_estimate=cost(series.size * 4, series.size * 8),
-    )(*in_hbm([lengths, *weights, series]))
-
-
-def deal(array, lengths, units):
+        cost_estimate=cost(rows * 1024, rows * 2048),
+    )(*in_hbm(weights))
+
+
+def deal(kernel, array, lengths, units, extra=()):
     channels, windows = array.shape[0], array.shape[1] // LEN
-    shapes = [struct((windows // 2, channels, LANES))] + [struct((n, channels, LANES)) for _, n in units]
+    shapes = [struct(shape) for shape in extra] + [struct((windows // 2, channels, LANES))] + [struct((n, channels, LANES)) for _, n in units]
     first, rest = deal_scratch(array, lengths)
     return pl.pallas_call(
-        functools.partial(cot_kernel, units),
+        functools.partial(kernel, units),
         out_shape=shapes,
         in_specs=[HBM] * 2,
         out_specs=[whole(o.shape) for o in shapes],
         grid=(1,),
         scratch_shapes=first + rest,
         compiler_params=PARAMS,
-        cost_estimate=cost(array.size * 4, array.size * 8),
+        cost_estimate=cost(array.size * 4, array.size * 8, DEAL),
     )(*in_hbm([lengths, array]))
 
 
-def prepare_weights(own, rec, windows, rows, channels):
+def prepare_weights(own, rec, rows, channels):
     shapes = [struct((rows, 3 * channels), bf16)] * 4 + [struct((4 * channels, rows), bf16)] * 2
-    return one_call(functools.partial(weights_kernel, windows), shapes, [own, rec])
+    return one_call(weights_kernel, shapes, [own, rec])
 
 
 MATMUL = 2 * 256 * 256 * 256
@@ -553,6 +552,7 @@
     return lax.optimization_barrier((x, *tokens))[0]
 
 
+DEAL = 1000
 WEIGHT = ((10,10,10,10),(10,10),(10,10),(10,10,10))
 COT = (1, 1, 1, 1)
 SER = (2, 2)
@@ -592,19 +592,25 @@
     phase = jnp.asarray(phase_rows(mode_count))
     gain = norm_gain.reshape(1, channels)
 
-    message, end_mask, ser_own, *ser_sent = front(series, lengths, [mode_in, mode_out, gain], ser_units, rows, line_length)
-    ser_rec = list(ser_sent)
+    message, end_mask = pack([mode_in, mode_out, gain], rows, line_length)
     with jax.named_scope("message_x"):
         message_rec = swap(message, "order", 1)
-    cot_own, *cot_rec = deal(after(grad_out, message), lengths, cot_units)
-    message_rec = after(message_rec, cot_own)
+    cot_own, *cot_rec = deal(cot_kernel, after(grad_out, message), lengths, cot_units)
     with jax.named_scope("cot_x"):
-        for u in range(EARLY):
-            cot_rec[u] = swap(cot_rec[u] if u == 0 else after(cot_rec[u], message_rec), "order", 1)
-    down_own, down_rec, up_own, up_rec, down_both, up_both = prepare_weights(message, message_rec, windows, rows, channels)
+        cot_rec[0] = swap(cot_rec[0], "order", 1)
+    squares, ser_own, *ser_sent = deal(series_kernel, after(series, cot_own), lengths, ser_units, [(windows, LANES)])
+    ser_rec = list(ser_sent)
+    with jax.named_scope("squares_x"):
+        squares_rec = swap(squares, "order", 1)
+    message_rec = after(message_rec, ser_own)
+    with jax.named_scope("cot_x"):
+        for u in range(1, EARLY):
+            cot_rec[u] = swap(after(cot_rec[u], message_rec), "order", 1)
+    down_own, down_rec, up_own, up_rec, down_both, up_both = prepare_weights(message, message_rec, rows, channels)
     with jax.named_scope("squares_z1"):
-        squares = message[:windows] + message_rec[:windows]
+        squares = squares + after(squares_rec, up_own)
         squares_rec = swap(squares, "order", 2)
+
     def windows_of(own, received, units, first, count):
         u, offset = locate(units, first)
         v, _ = locate(units, first + count - 1)
@@ -731,7 +737,7 @@
         if name == "q":
             with jax.named_scope("squares_z2"):
                 out = state["squares"] + after(state["squares_rec"], token)
-                state["squares"] = add_over(out, "order", bits_of(order_devices, 4))
+                state["squares"], state["squares_rec"] = out, swap(out, "order", 4)
         elif name == "g":
             out = token
             with jax.named_scope(f"scaled{u}"):
@@ -746,7 +752,8 @@
         elif name == "b":
             out = kept[u] = after(kept[u], token)
         elif name == "Q":
-            out = state["squares"] = after(state["squares"], token)
+            out = state["squares"] + after(state["squares_rec"], token)
+            state["squares"] = out = add_over(out, "order", bits_of(order_devices, 8))
         elif name == "R":
             out = do_read(u, token)
         elif name == "K":

time: 114 us -> 114 us (level)
  waiting for transfers between devices: 22.7 us -> 19.3 us
  starting transfers between devices: 58.8 us -> 61.3 us
    ppermute x36 -> x37, waiting for transfers between devices: 22.7 us -> 19.2 us  [swap(): return lax.ppermute(x, axis, [(i, i ^ bit) for i in range(size)])]
    ppermute x36 -> x37, starting transfers between devices: 58.2 us -> 60.7 us  [swap(): return lax.ppermute(x, axis, [(i, i ^ bit) for i in range(size)])]
    pallas_call x2 -> x3, Pallas kernels: 4.57 us -> 5.4 us  [the longest x2 4.17 us: deal(): pl.pallas_call(functools.partial(kernel, units), out_shape=shapes, in_spe...]
  transfers between devices with their start and end apart: 44 -> 45, of which waited for: 18 -> 15; matrix products, arithmetic and copies ran while one was open for 1% -> 1% of each run, Pallas kernels for 24% -> 26%
where the time goes in v6:
time: 114 us
  starting transfers between devices  61.3 us (54%)
  Pallas kernels  31.2 us (27%)
  waiting for transfers between devices  19.3 us (17%)
  between operations  1.26 us (1%)
    ppermute x37, starting transfers between devices, swap(): return lax.ppermute(x, axis, [(i, i ^ bit) for i in range(size)])  60.7 us
    pallas_call x11, Pallas kernels, unit_call(): pl.pallas_call(kernel, out_shape=[struct(shape) for shape in outs], in_sp...  20.8 us
    ppermute x37, waiting for transfers between devices, swap(): return lax.ppermute(x, axis, [(i, i ^ bit) for i in range(size)])  19.2 us
    pallas_call x5, Pallas kernels, one_call(): pl.pallas_call(kernel, out_shape=shapes, in_specs=specs, out_specs=[whole...  5 us
    pallas_call x2, Pallas kernels, deal(): pl.pallas_call(functools.partial(kernel, units), out_shape=shapes, in_spe...  4.17 us
  transfers between devices with their start and end apart: 45, of which 15 were waited for; matrix products, arithmetic and copies ran while one was open for 1% of the time, Pallas kernels for 26%

profile of v6, /device:TPU:0, one launch (start us, length us, event | category | flops | bytes accessed | tf_op | source)
XLA Modules:
  0.0 113.9 jit_solution(242458109600502813)
XLA Ops:
  1.9 3.0 %collective-permute-start = (f32[48,768]{1,0:T(8,128)S(1)}, f32[48,768]{1,0:T(8,128)S(1)}, u32[]{:S(2)}, u32[]{:S(2)}) collective-permute-start(f32[48,768]{1,0:T(8,128)S(1)} %get-tuple-element.128.own_ref), channel_id=1, source_target_pairs={{0,1},{1,0},{2,3},{3,2},{4,5},{5,4},{6,7},{7,6},{8,9},{9,8},{10,11... | collective-permute-start | bytes 442376 | tf_op jit(solution)/shard_map/message_x/ppermute | solution.py:518
  4.9 2.0 %shard_map.137 = (f32[4,64,768]{2,1,0:T(8,128)S(1)}, f32[1,64,768]{2,1,0:T(8,128)S(1)}, f32[1,64,768]{2,1,0:T(8,128)S(1)}, f32[1,64,768]{2,1,0:T(8,128)S(1)}, f32[1,64,768]{2,1,0:T(8,128)S(1)}) custom-call(s32[8]{0:T(128)} %len_ref.9, f32[64,5760]{1,0:T(8,128)} %cot_ref.1), custom_call_target="tpu_custom_call" | custom-call | flops 1474560000 | bytes 2949120000 | tf_op jit(solution)/shard_map/pallas_call | solution.py:478
  7.0 2.2 %shard_map.138 = (f32[8,768]{1,0:T(8,128)S(1)}, f32[4,64,768]{2,1,0:T(8,128)S(1)}, f32[2,64,768]{2,1,0:T(8,128)S(1)}, f32[2,64,768]{2,1,0:T(8,128)S(1)}) custom-call(s32[8]{0:T(128)} %len_ref.9, f32[64,5760]{1,0:T(8,128)} %x_ref), custom_call_target="tpu_custom_call" | custom-call | flops 1474560000 | bytes 2949120000 | tf_op jit(solution)/shard_map/pallas_call | solution.py:478
  9.2 2.1 %collective-permute-start.3 = (f32[8,768]{1,0:T(8,128)S(1)}, f32[8,768]{1,0:T(8,128)S(1)}, u32[]{:S(2)}, u32[]{:S(2)}) collective-permute-start(f32[8,768]{1,0:T(8,128)S(1)} %get-tuple-element.144), channel_id=1, source_target_pairs={{0,1},{1,0},{2,3},{3,2},{4,5},{5,4},{6,7},{7,6},{8,9},{9,8},{10,11... | collective-permute-start | bytes 73736 | tf_op jit(solution)/shard_map/squares_x/ppermute | solution.py:518
  11.8 2.9 %collective-permute-done.3 = f32[8,768]{1,0:T(8,128)S(1)} collective-permute-done((f32[8,768]{1,0:T(8,128)S(1)}, f32[8,768]{1,0:T(8,128)S(1)}, u32[]{:S(2)}, u32[]{:S(2)}) %collective-permute-start.3) | collective-permute-done | bytes 24608 | tf_op jit(solution)/shard_map/squares_x/ppermute | solution.py:518
  14.7 1.6 %collective-permute-start.4 = (f32[8,768]{1,0:T(8,128)S(1)}, f32[8,768]{1,0:T(8,128)S(1)}, u32[]{:S(2)}, u32[]{:S(2)}) collective-permute-start(f32[8,768]{1,0:T(8,128)S(1)} %add.84), channel_id=1, source_target_pairs={{0,2},{1,3},{2,0},{3,1},{4,6},{5,7},{6,4},{7,5},{8,10},{9,11},{10,... | collective-permute-start | bytes 73736 | tf_op jit(solution)/shard_map/squares_z1/ppermute | solution.py:518
  17.7 1.6 %collective-permute-start.8 = (f32[1,64,768]{2,1,0:T(8,128)S(1)}, f32[1,64,768]{2,1,0:T(8,128)S(1)}, u32[]{:S(2)}, u32[]{:S(2)}) collective-permute-start(f32[1,64,768]{2,1,0:T(8,128)S(1)} %get-tuple-element.150), channel_id=1, source_target_pairs={{0,1},{1,0},{2,3},{3,2},{4,5},{5,4},{6,7},{7,6},{8,9},{9,8},{10,11... | collective-permute-start | bytes 589832 | tf_op jit(solution)/shard_map/cot_x/ppermute | solution.py:518
  20.2 2.4 %collective-permute-start.7 = (f32[8,768]{1,0:T(8,128)S(1)}, f32[8,768]{1,0:T(8,128)S(1)}, u32[]{:S(2)}, u32[]{:S(2)}) collective-permute-start(f32[8,768]{1,0:T(8,128)S(1)} %add.85), channel_id=1, source_target_pairs={{0,4},{1,5},{2,6},{3,7},{4,0},{5,1},{6,2},{7,3},{8,12},{9,13},{10,... | collective-permute-start | bytes 73736 | tf_op jit(solution)/shard_map/squares_z2/ppermute | solution.py:518
  22.6 1.6 %collective-permute-start.6 = (f32[256,256]{1,0:T(8,128)S(1)}, f32[256,256]{1,0:T(8,128)S(1)}, u32[]{:S(2)}, u32[]{:S(2)}) collective-permute-start(f32[256,256]{1,0:T(8,128)S(1)} %shard_map.141), channel_id=1, source_target_pairs={{0,2},{1,3},{2,0},{3,1},{4,6},{5,7},{6,4},{7,5},{8,10},{9,11},{10,... | collective-permute-start | bytes 786440 | tf_op jit(solution)/shard_map/e1/ppermute | solution.py:518
  24.9 1.7 %collective-permute-start.11 = (f32[2,64,768]{2,1,0:T(8,128)S(1)}, f32[2,64,768]{2,1,0:T(8,128)S(1)}, u32[]{:S(2)}, u32[]{:S(2)}) collective-permute-start(f32[2,64,768]{2,1,0:T(8,128)S(1)} %get-tuple-element.160.refs_4_), channel_id=1, source_target_pairs={{0,1},{1,0},{2,3},{3,2},{4,5},{5,4},{6,7},{7,6},{8,9},{9,8},{10,11... | collective-permute-start | bytes 1179656 | tf_op jit(solution)/shard_map/ser_x/ppermute | solution.py:518
  27.6 4.4 %collective-permute-start.12 = (f32[256,256]{1,0:T(8,128)S(1)}, f32[256,256]{1,0:T(8,128)S(1)}, u32[]{:S(2)}, u32[]{:S(2)}) collective-permute-start(f32[256,256]{1,0:T(8,128)S(1)} %shard_map.142), channel_id=1, source_target_pairs={{0,2},{1,3},{2,0},{3,1},{4,6},{5,7},{6,4},{7,5},{8,10},{9,11},{10,... | collective-permute-start | bytes 786440 | tf_op jit(solution)/shard_map/e2/ppermute | solution.py:518
  33.8 3.9 %collective-permute-start.15 = (f32[256,256]{1,0:T(8,128)S(1)}, f32[256,256]{1,0:T(8,128)S(1)}, u32[]{:S(2)}, u32[]{:S(2)}) collective-permute-start(f32[256,256]{1,0:T(8,128)S(1)} %add_select_fusion.4.refs_0_), channel_id=1, source_target_pairs={{0,2},{1,3},{2,0},{3,1},{4,6},{5,7},{6,4},{7,5},{8,10},{9,11},{10,... | collective-permute-start | bytes 786440 | tf_op jit(solution)/shard_map/e3/ppermute | solution.py:518
  37.8 2.1 %shard_map.144 = (f32[256,256]{1,0:T(8,128)S(1)}, f32[256,256]{1,0:T(8,128)S(1)}) custom-call(f32[4,64,768]{2,1,0:T(8,128)S(1)} %get-tuple-element.132.own_ref.ser_own.x_own, f32[2,64,768]{2,1,0:T(8,128)S(1)} %collective-permute-done.11.rec_ref.ser_rec, f32[8,768]{1,0:T(8,128)S(1)} %add.87.ss_ref.refs_4_, bf16[256,192]{1,0:T(8,128)(2,1)S(1)} %get-tuple-element.164.down_own, ...), custom_call_target="tpu_custom_call" | custom-call | flops 14092861440 | bytes 21872640 | tf_op jit(solution)/shard_map/pallas_call | solution.py:505
  40.0 3.3 %collective-permute-start.17 = (f32[256,256]{1,0:T(8,128)S(1)}, f32[256,256]{1,0:T(8,128)S(1)}, u32[]{:S(2)}, u32[]{:S(2)}) collective-permute-start(f32[256,256]{1,0:T(8,128)S(1)} %add_select_fusion.3.refs_1_), channel_id=1, source_target_pairs={{0,2},{1,3},{2,0},{3,1},{4,6},{5,7},{6,4},{7,5},{8,10},{9,11},{10,... | collective-permute-start | bytes 786440 | tf_op jit(solution)/shard_map/e4/ppermute | solution.py:518
  43.4 4.4 %collective-permute-start.19 = (f32[256,256]{1,0:T(8,128)S(1)}, f32[256,256]{1,0:T(8,128)S(1)}, u32[]{:S(2)}, u32[]{:S(2)}) collective-permute-start(f32[256,256]{1,0:T(8,128)S(1)} %add_select_fusion.2.refs_0_), channel_id=1, source_target_pairs={{0,2},{1,3},{2,0},{3,1},{4,6},{5,7},{6,4},{7,5},{8,10},{9,11},{10,... | collective-permute-start | bytes 786440 | tf_op jit(solution)/shard_map/e5/ppermute | solution.py:518
  47.8 2.1 %shard_map.145 = (f32[256,256]{1,0:T(8,128)S(1)}, f32[256,256]{1,0:T(8,128)S(1)}) custom-call(f32[4,64,768]{2,1,0:T(8,128)S(1)} %get-tuple-element.132.own_ref.ser_own.x_own, f32[2,64,768]{2,1,0:T(8,128)S(1)} %collective-permute-done.10.rec_ref.ser_rec, f32[8,768]{1,0:T(8,128)S(1)} %add.87.ss_ref.refs_4_, bf16[256,192]{1,0:T(8,128)(2,1)S(1)} %get-tuple-element.164.down_own, ...), custom_call_target="tpu_custom_call" | custom-call | flops 14092861440 | bytes 21872640 | tf_op jit(solution)/shard_map/pallas_call | solution.py:505
  50.7 4.2 %collective-permute-start.23 = (f32[256,256]{1,0:T(8,128)S(1)}, f32[256,256]{1,0:T(8,128)S(1)}, u32[]{:S(2)}, u32[]{:S(2)}) collective-permute-start(f32[256,256]{1,0:T(8,128)S(1)} %add_select_fusion.1.refs_1_), channel_id=1, source_target_pairs={{0,2},{1,3},{2,0},{3,1},{4,6},{5,7},{6,4},{7,5},{8,10},{9,11},{10,... | collective-permute-start | bytes 786440 | tf_op jit(solution)/shard_map/e6/ppermute | solution.py:518
  55.0 3.7 %shard_map.146 = (f32[2,64,768]{2,1,0:T(8,128)S(1)}, f32[2,64,768]{2,1,0:T(8,128)S(1)}, f32[64,256]{1,0:T(8,128)S(1)}, f32[64,256]{1,0:T(8,128)S(1)}, f32[2,8,256]{2,1,0:T(8,128)S(1)}) custom-call(s32[8]{0:T(128)S(1)} %copy-done.4, f32[4,64,768]{2,1,0:T(8,128)S(1)} %get-tuple-element.132.own_ref.ser_own.x_own, ...), custom_call_target="tpu_custom_call" | custom-call | flops 16106127360 | bytes 31703040 | tf_op jit(solution)/shard_map/pallas_call | solution.py:505
  59.6 3.8 %collective-permute-start.21 = (f32[256,256]{1,0:T(8,128)S(1)}, f32[256,256]{1,0:T(8,128)S(1)}, u32[]{:S(2)}, u32[]{:S(2)}) collective-permute-start(f32[256,256]{1,0:T(8,128)S(1)} %add_select_fusion.refs_0_), channel_id=1, source_target_pairs={{0,2},{1,3},{2,0},{3,1},{4,6},{5,7},{6,4},{7,5},{8,10},{9,11},{10,... | collective-permute-start | bytes 786440 | tf_op jit(solution)/shard_map/e7/ppermute | solution.py:518
  63.6 3.9 %shard_map.147 = (f32[2,64,768]{2,1,0:T(8,128)S(1)}, f32[2,64,768]{2,1,0:T(8,128)S(1)}, f32[64,256]{1,0:T(8,128)S(1)}, f32[64,256]{1,0:T(8,128)S(1)}, f32[2,8,256]{2,1,0:T(8,128)S(1)}) custom-call(s32[8]{0:T(128)S(1)} %copy-done.4, f32[4,64,768]{2,1,0:T(8,128)S(1)} %get-tuple-element.132.own_ref.ser_own.x_own, ...), custom_call_target="tpu_custom_call" | custom-call | flops 16106127360 | bytes 33013760 | tf_op jit(solution)/shard_map/pallas_call | solution.py:505
  69.8 2.5 %collective-permute-start.34 = (f32[256,256]{1,0:T(8,128)S(1)}, f32[256,256]{1,0:T(8,128)S(1)}, u32[]{:S(2)}, u32[]{:S(2)}) collective-permute-start(f32[256,256]{1,0:T(8,128)S(1)} %add.101.refs_0_), channel_id=1, source_target_pairs={{0,2},{1,3},{2,0},{3,1},{4,6},{5,7},{6,4},{7,5},{8,10},{9,11},{10,... | collective-permute-start | bytes 786440 | tf_op jit(solution)/shard_map/e9/ppermute | solution.py:518
  72.7 2.2 %collective-permute-start.30 = (f32[32,256]{1,0:T(8,128)S(1)}, f32[32,256]{1,0:T(8,128)S(1)}, u32[]{:S(2)}, u32[]{:S(2)}) collective-permute-start(f32[32,256]{1,0:T(8,128)S(1)} %pad_maximum_fusion.3), channel_id=1, source_target_pairs={{0,2},{1,3},{2,0},{3,1},{4,6},{5,7},{6,4},{7,5},{8,10},{9,11},{10,... | collective-permute-start | bytes 98312 | tf_op jit(solution)/shard_map/inner_z1/ppermute | solution.py:518
  75.0 1.7 %collective-permute-done.28.refs_3_ = f32[256,256]{1,0:T(8,128)S(1)} collective-permute-done((f32[256,256]{1,0:T(8,128)S(1)}, f32[256,256]{1,0:T(8,128)S(1)}, u32[]{:S(2)}, u32[]{:S(2)}) %collective-permute-start.28) | collective-permute-done | bytes 262176 | tf_op jit(solution)/shard_map/e8/ppermute | solution.py:518
  78.2 2.5 %shard_map.148 = (f32[2,64,768]{2,1,0:T(8,128)S(1)}, f32[2,64,768]{2,1,0:T(8,128)S(1)}, f32[64,256]{1,0:T(8,128)S(1)}, f32[64,256]{1,0:T(8,128)S(1)}, f32[8,256]{1,0:T(8,128)S(1)}) custom-call(s32[8]{0:T(128)S(1)} %copy-done.4, f32[4,64,768]{2,1,0:T(8,128)S(1)} %get-tuple-element.132.own_ref.ser_own.x_own, ...), custom_call_target="tpu_custom_call" | custom-call | flops 12079595520 | bytes 35389440 | tf_op jit(solution)/shard_map/pallas_call | solution.py:505
  85.8 2.9 %collective-permute-done.33.refs_3_ = f32[2,64,768]{2,1,0:T(8,128)S(1)} collective-permute-done((f32[2,64,768]{2,1,0:T(8,128)S(1)}, f32[2,64,768]{2,1,0:T(8,128)S(1)}, u32[]{:S(2)}, u32[]{:S(2)}) %collective-permute-start.33) | collective-permute-done | bytes 393248 | tf_op jit(solution)/shard_map/scaled1/ppermute | solution.py:518
  88.7 1.6 %collective-permute-start.35 = (f32[64,256]{1,0:T(8,128)S(1)}, f32[64,256]{1,0:T(8,128)S(1)}, u32[]{:S(2)}, u32[]{:S(2)}) collective-permute-start(f32[64,256]{1,0:T(8,128)S(1)} %add.105), channel_id=1, source_target_pairs={{0,16},{8,24},{16,0},{24,8},{1,17},{9,25},{17,1},{25,9},{2,18},{10... | collective-permute-start | bytes 196616 | tf_op jit(solution)/shard_map/r_y/ppermute | solution.py:518
  93.1 1.6 %collective-permute-start.36 = (f32[72,256]{1,0:T(8,128)S(1)}, f32[72,256]{1,0:T(8,128)S(1)}, u32[]{:S(2)}, u32[]{:S(2)}) collective-permute-start(f32[72,256]{1,0:T(8,128)S(1)} %pad_maximum_fusion.1), channel_id=1, source_target_pairs={{0,1},{1,0},{2,3},{3,2},{4,5},{5,4},{6,7},{7,6},{8,9},{9,8},{10,11... | collective-permute-start | bytes 221192 | tf_op jit(solution)/shard_map/w_x/ppermute | solution.py:518
  97.2 1.9 %collective-permute-done.38.in_rec = f32[32,256]{1,0:T(8,128)S(1)} collective-permute-done((f32[32,256]{1,0:T(8,128)S(1)}, f32[32,256]{1,0:T(8,128)S(1)}, u32[]{:S(2)}, u32[]{:S(2)}) %collective-permute-start.38) | collective-permute-done | bytes 32800 | tf_op jit(solution)/shard_map/inner_x/ppermute | solution.py:518
  100.4 1.6 %collective-permute-start.40 = (f32[72,256]{1,0:T(8,128)S(1)}, f32[72,256]{1,0:T(8,128)S(1)}, u32[]{:S(2)}, u32[]{:S(2)}) collective-permute-start(f32[72,256]{1,0:T(8,128)S(1)} %add.109), channel_id=1, source_target_pairs={{0,16},{8,24},{16,0},{24,8},{1,17},{9,25},{17,1},{25,9},{2,18},{10... | collective-permute-start | bytes 221192 | tf_op jit(solution)/shard_map/w_y/ppermute | solution.py:518
  102.0 1.7 %shard_map.151 = f32[64,5760]{1,0:T(8,128)} custom-call(f32[64,5760]{1,0:T(8,128)S(1)} %copy-done, f32[4,64,768]{2,1,0:T(8,128)S(1)} %get-tuple-element.132.own_ref.ser_own.x_own, f32[8,768]{1,0:T(8,128)S(1)} %add.87.ss_ref.refs_4_, f32[32,256]{1,0:T(8,128)S(1)} %add.106.in_own, f32[32,256]{1,0:T(8,128)S(1)} %collective-permute-done.38.in_rec, ...), custom_call_target="tpu_custom_call" | custom-call | flops 61849 | bytes 61849 | tf_op jit(solution)/shard_map/pallas_call | solution.py:432
  109.8 1.6 %shard_map.153 = f32[64,5760]{1,0:T(8,128)} custom-call(f32[64,5760]{1,0:T(8,128)S(1)} %copy-done.1, f32[2,64,768]{2,1,0:T(8,128)S(1)} %get-tuple-element.244.refs_0_, f32[1,64,768]{2,1,0:T(8,128)S(1)} %get-tuple-element.245.refs_1_, f32[1,64,768]{2,1,0:T(8,128)S(1)} %get-tuple-element.246.refs_2_, f32[2,64,768]{2,1,0:T(8,128)S(1)} %collective-permute-done.37.refs_3_, ...), custom_call_target="tpu_custom_call" | custom-call | flops 4521984 | bytes 4521984 | tf_op jit(solution)/shard_map/pallas_call | solution.py:432
  111.4 1.7 %collective-permute-done.44.rec_ref = f32[8,256]{1,0:T(8,128)S(1)} collective-permute-done((f32[8,256]{1,0:T(8,128)S(1)}, f32[8,256]{1,0:T(8,128)S(1)}, u32[]{:S(2)}, u32[]{:S(2)}) %collective-permute-start.44) | collective-permute-done | bytes 8224 | tf_op jit(solution)/shard_map/stats_2/ppermute | solution.py:518
  (126 shorter events, 32.4 us)
Async XLA Ops:
  1.9 9.4 %collective-permute-start = (f32[48,768]{1,0:T(8,128)S(1)}, f32[48,768]{1,0:T(8,128)S(1)}, u32[]{:S(2)}, u32[]{:S(2)}) collective-permute-start(f32[48,768]{1,0:T(8,128)S(1)} %get-tuple-element.128.own_ref), channel_id=1, source_target_pairs={{0,1},{1,0},{2,3},{3,2},{4,5},{5,4},{6,7},{7,6},{8,9},{9,8},{10,11... | collective-permute-start | bytes 442376 | tf_op jit(solution)/shard_map/message_x/ppermute | solution.py:518
  6.9 9.4 %collective-permute-start.2 = (f32[1,64,768]{2,1,0:T(8,128)S(1)}, f32[1,64,768]{2,1,0:T(8,128)S(1)}, u32[]{:S(2)}, u32[]{:S(2)}) collective-permute-start(f32[1,64,768]{2,1,0:T(8,128)S(1)} %get-tuple-element.138), channel_id=1, source_target_pairs={{0,1},{1,0},{2,3},{3,2},{4,5},{5,4},{6,7},{7,6},{8,9},{9,8},{10,11... | collective-permute-start | bytes 589832 | tf_op jit(solution)/shard_map/cot_x/ppermute | solution.py:518
  11.2 8.1 %collective-permute-start.1 = (f32[1,64,768]{2,1,0:T(8,128)S(1)}, f32[1,64,768]{2,1,0:T(8,128)S(1)}, u32[]{:S(2)}, u32[]{:S(2)}) collective-permute-start(f32[1,64,768]{2,1,0:T(8,128)S(1)} %get-tuple-element.137), channel_id=1, source_target_pairs={{0,1},{1,0},{2,3},{3,2},{4,5},{5,4},{6,7},{7,6},{8,9},{9,8},{10,11... | collective-permute-start | bytes 589832 | tf_op jit(solution)/shard_map/cot_x/ppermute | solution.py:518
  17.2 7.7 %collective-permute-start.9 = (f32[256,256]{1,0:T(8,128)S(1)}, f32[256,256]{1,0:T(8,128)S(1)}, u32[]{:S(2)}, u32[]{:S(2)}) collective-permute-start(f32[256,256]{1,0:T(8,128)S(1)} %shard_map.140), channel_id=1, source_target_pairs={{0,2},{1,3},{2,0},{3,1},{4,6},{5,7},{6,4},{7,5},{8,10},{9,11},{10,... | collective-permute-start | bytes 786440 | tf_op jit(solution)/shard_map/e0/ppermute | solution.py:518
  17.7 9.0 %collective-permute-start.8 = (f32[1,64,768]{2,1,0:T(8,128)S(1)}, f32[1,64,768]{2,1,0:T(8,128)S(1)}, u32[]{:S(2)}, u32[]{:S(2)}) collective-permute-start(f32[1,64,768]{2,1,0:T(8,128)S(1)} %get-tuple-element.150), channel_id=1, source_target_pairs={{0,1},{1,0},{2,3},{3,2},{4,5},{5,4},{6,7},{7,6},{8,9},{9,8},{10,11... | collective-permute-start | bytes 589832 | tf_op jit(solution)/shard_map/cot_x/ppermute | solution.py:518
  20.2 7.4 %collective-permute-start.7 = (f32[8,768]{1,0:T(8,128)S(1)}, f32[8,768]{1,0:T(8,128)S(1)}, u32[]{:S(2)}, u32[]{:S(2)}) collective-permute-start(f32[8,768]{1,0:T(8,128)S(1)} %add.85), channel_id=1, source_target_pairs={{0,4},{1,5},{2,6},{3,7},{4,0},{5,1},{6,2},{7,3},{8,12},{9,13},{10,... | collective-permute-start | bytes 73736 | tf_op jit(solution)/shard_map/squares_z2/ppermute | solution.py:518
  22.6 9.5 %collective-permute-start.6 = (f32[256,256]{1,0:T(8,128)S(1)}, f32[256,256]{1,0:T(8,128)S(1)}, u32[]{:S(2)}, u32[]{:S(2)}) collective-permute-start(f32[256,256]{1,0:T(8,128)S(1)} %shard_map.141), channel_id=1, source_target_pairs={{0,2},{1,3},{2,0},{3,1},{4,6},{5,7},{6,4},{7,5},{8,10},{9,11},{10,... | collective-permute-start | bytes 786440 | tf_op jit(solution)/shard_map/e1/ppermute | solution.py:518
  24.2 8.0 %collective-permute-start.5 = (f32[1,64,768]{2,1,0:T(8,128)S(1)}, f32[1,64,768]{2,1,0:T(8,128)S(1)}, u32[]{:S(2)}, u32[]{:S(2)}) collective-permute-start(f32[1,64,768]{2,1,0:T(8,128)S(1)} %get-tuple-element.148), channel_id=1, source_target_pairs={{0,1},{1,0},{2,3},{3,2},{4,5},{5,4},{6,7},{7,6},{8,9},{9,8},{10,11... | collective-permute-start | bytes 589832 | tf_op jit(solution)/shard_map/cot_x/ppermute | solution.py:518
  24.9 12.9 %collective-permute-start.11 = (f32[2,64,768]{2,1,0:T(8,128)S(1)}, f32[2,64,768]{2,1,0:T(8,128)S(1)}, u32[]{:S(2)}, u32[]{:S(2)}) collective-permute-start(f32[2,64,768]{2,1,0:T(8,128)S(1)} %get-tuple-element.160.refs_4_), channel_id=1, source_target_pairs={{0,1},{1,0},{2,3},{3,2},{4,5},{5,4},{6,7},{7,6},{8,9},{9,8},{10,11... | collective-permute-start | bytes 1179656 | tf_op jit(solution)/shard_map/ser_x/ppermute | solution.py:518
  27.6 10.1 %collective-permute-start.12 = (f32[256,256]{1,0:T(8,128)S(1)}, f32[256,256]{1,0:T(8,128)S(1)}, u32[]{:S(2)}, u32[]{:S(2)}) collective-permute-start(f32[256,256]{1,0:T(8,128)S(1)} %shard_map.142), channel_id=1, source_target_pairs={{0,2},{1,3},{2,0},{3,1},{4,6},{5,7},{6,4},{7,5},{8,10},{9,11},{10,... | collective-permute-start | bytes 786440 | tf_op jit(solution)/shard_map/e2/ppermute | solution.py:518
  32.1 7.8 %collective-permute-start.16 = (f32[256,256]{1,0:T(8,128)S(1)}, f32[256,256]{1,0:T(8,128)S(1)}, u32[]{:S(2)}, u32[]{:S(2)}) collective-permute-start(f32[256,256]{1,0:T(8,128)S(1)} %add.88), channel_id=1, source_target_pairs={{0,8},{1,9},{2,4},{3,5},{4,2},{5,3},{6,14},{7,15},{8,0},{9,1},{10,... | collective-permute-start | bytes 786440 | tf_op jit(solution)/shard_map/m1/ppermute | solution.py:542
  33.1 14.7 %collective-permute-start.10 = (f32[2,64,768]{2,1,0:T(8,128)S(1)}, f32[2,64,768]{2,1,0:T(8,128)S(1)}, u32[]{:S(2)}, u32[]{:S(2)}) collective-permute-start(f32[2,64,768]{2,1,0:T(8,128)S(1)} %get-tuple-element.157.refs_5_), channel_id=1, source_target_pairs={{0,1},{1,0},{2,3},{3,2},{4,5},{5,4},{6,7},{7,6},{8,9},{9,8},{10,11... | collective-permute-start | bytes 1179656 | tf_op jit(solution)/shard_map/ser_x/ppermute | solution.py:518
  33.8 9.4 %collective-permute-start.15 = (f32[256,256]{1,0:T(8,128)S(1)}, f32[256,256]{1,0:T(8,128)S(1)}, u32[]{:S(2)}, u32[]{:S(2)}) collective-permute-start(f32[256,256]{1,0:T(8,128)S(1)} %add_select_fusion.4.refs_0_), channel_id=1, source_target_pairs={{0,2},{1,3},{2,0},{3,1},{4,6},{5,7},{6,4},{7,5},{8,10},{9,11},{10,... | collective-permute-start | bytes 786440 | tf_op jit(solution)/shard_map/e3/ppermute | solution.py:518
  40.0 10.5 %collective-permute-start.17 = (f32[256,256]{1,0:T(8,128)S(1)}, f32[256,256]{1,0:T(8,128)S(1)}, u32[]{:S(2)}, u32[]{:S(2)}) collective-permute-start(f32[256,256]{1,0:T(8,128)S(1)} %add_select_fusion.3.refs_1_), channel_id=1, source_target_pairs={{0,2},{1,3},{2,0},{3,1},{4,6},{5,7},{6,4},{7,5},{8,10},{9,11},{10,... | collective-permute-start | bytes 786440 | tf_op jit(solution)/shard_map/e4/ppermute | solution.py:518
  43.3 7.3 %collective-permute-start.20 = (f32[256,256]{1,0:T(8,128)S(1)}, f32[256,256]{1,0:T(8,128)S(1)}, u32[]{:S(2)}, u32[]{:S(2)}) collective-permute-start(f32[256,256]{1,0:T(8,128)S(1)} %add.92), channel_id=1, source_target_pairs={{0,8},{1,9},{2,4},{3,5},{4,2},{5,3},{6,14},{7,15},{8,0},{9,1},{10,... | collective-permute-start | bytes 786440 | tf_op jit(solution)/shard_map/m3/ppermute | solution.py:542
  43.4 11.5 %collective-permute-start.19 = (f32[256,256]{1,0:T(8,128)S(1)}, f32[256,256]{1,0:T(8,128)S(1)}, u32[]{:S(2)}, u32[]{:S(2)}) collective-permute-start(f32[256,256]{1,0:T(8,128)S(1)} %add_select_fusion.2.refs_0_), channel_id=1, source_target_pairs={{0,2},{1,3},{2,0},{3,1},{4,6},{5,7},{6,4},{7,5},{8,10},{9,11},{10,... | collective-permute-start | bytes 786440 | tf_op jit(solution)/shard_map/e5/ppermute | solution.py:518
  50.5 9.0 %collective-permute-start.18 = (f32[256,256]{1,0:T(8,128)S(1)}, f32[256,256]{1,0:T(8,128)S(1)}, u32[]{:S(2)}, u32[]{:S(2)}) collective-permute-start(f32[256,256]{1,0:T(8,128)S(1)} %add.94), channel_id=1, source_target_pairs={{0,8},{1,9},{2,4},{3,5},{4,2},{5,3},{6,14},{7,15},{8,0},{9,1},{10,... | collective-permute-start | bytes 786440 | tf_op jit(solution)/shard_map/m4/ppermute | solution.py:542
  50.7 12.8 %collective-permute-start.23 = (f32[256,256]{1,0:T(8,128)S(1)}, f32[256,256]{1,0:T(8,128)S(1)}, u32[]{:S(2)}, u32[]{:S(2)}) collective-permute-start(f32[256,256]{1,0:T(8,128)S(1)} %add_select_fusion.1.refs_1_), channel_id=1, source_target_pairs={{0,2},{1,3},{2,0},{3,1},{4,6},{5,7},{6,4},{7,5},{8,10},{9,11},{10,... | collective-permute-start | bytes 786440 | tf_op jit(solution)/shard_map/e6/ppermute | solution.py:518
  54.9 12.5 %collective-permute-start.22 = (f32[256,256]{1,0:T(8,128)S(1)}, f32[256,256]{1,0:T(8,128)S(1)}, u32[]{:S(2)}, u32[]{:S(2)}) collective-permute-start(f32[256,256]{1,0:T(8,128)S(1)} %add.96), channel_id=1, source_target_pairs={{0,8},{1,9},{2,4},{3,5},{4,2},{5,3},{6,14},{7,15},{8,0},{9,1},{10,... | collective-permute-start | bytes 786440 | tf_op jit(solution)/shard_map/m5/ppermute | solution.py:542
  58.7 16.2 %collective-permute-start.25 = (f32[2,64,768]{2,1,0:T(8,128)S(1)}, f32[2,64,768]{2,1,0:T(8,128)S(1)}, u32[]{:S(2)}, u32[]{:S(2)}) collective-permute-start(f32[2,64,768]{2,1,0:T(8,128)S(1)} %get-tuple-element.191), channel_id=1, source_target_pairs={{0,1},{1,0},{2,3},{3,2},{4,5},{5,4},{6,7},{7,6},{8,9},{9,8},{10,11... | collective-permute-start | bytes 1179656 | tf_op jit(solution)/shard_map/scaled0/ppermute | solution.py:518
  59.6 8.5 %collective-permute-start.21 = (f32[256,256]{1,0:T(8,128)S(1)}, f32[256,256]{1,0:T(8,128)S(1)}, u32[]{:S(2)}, u32[]{:S(2)}) collective-permute-start(f32[256,256]{1,0:T(8,128)S(1)} %add_select_fusion.refs_0_), channel_id=1, source_target_pairs={{0,2},{1,3},{2,0},{3,1},{4,6},{5,7},{6,4},{7,5},{8,10},{9,11},{10,... | collective-permute-start | bytes 786440 | tf_op jit(solution)/shard_map/e7/ppermute | solution.py:518
  67.5 9.2 %collective-permute-start.28 = (f32[256,256]{1,0:T(8,128)S(1)}, f32[256,256]{1,0:T(8,128)S(1)}, u32[]{:S(2)}, u32[]{:S(2)}) collective-permute-start(f32[256,256]{1,0:T(8,128)S(1)} %add.99.refs_1_), channel_id=1, source_target_pairs={{0,2},{1,3},{2,0},{3,1},{4,6},{5,7},{6,4},{7,5},{8,10},{9,11},{10,... | collective-permute-start | bytes 786440 | tf_op jit(solution)/shard_map/e8/ppermute | solution.py:518
  68.1 12.6 %collective-permute-start.24 = (f32[256,256]{1,0:T(8,128)S(1)}, f32[256,256]{1,0:T(8,128)S(1)}, u32[]{:S(2)}, u32[]{:S(2)}) collective-permute-start(f32[256,256]{1,0:T(8,128)S(1)} %add.100), channel_id=1, source_target_pairs={{0,8},{1,9},{2,4},{3,5},{4,2},{5,3},{6,14},{7,15},{8,0},{9,1},{10,... | collective-permute-start | bytes 786440 | tf_op jit(solution)/shard_map/m7/ppermute | solution.py:542
  69.8 13.1 %collective-permute-start.34 = (f32[256,256]{1,0:T(8,128)S(1)}, f32[256,256]{1,0:T(8,128)S(1)}, u32[]{:S(2)}, u32[]{:S(2)}) collective-permute-start(f32[256,256]{1,0:T(8,128)S(1)} %add.101.refs_0_), channel_id=1, source_target_pairs={{0,2},{1,3},{2,0},{3,1},{4,6},{5,7},{6,4},{7,5},{8,10},{9,11},{10,... | collective-permute-start | bytes 786440 | tf_op jit(solution)/shard_map/e9/ppermute | solution.py:518
  72.7 9.9 %collective-permute-start.30 = (f32[32,256]{1,0:T(8,128)S(1)}, f32[32,256]{1,0:T(8,128)S(1)}, u32[]{:S(2)}, u32[]{:S(2)}) collective-permute-start(f32[32,256]{1,0:T(8,128)S(1)} %pad_maximum_fusion.3), channel_id=1, source_target_pairs={{0,2},{1,3},{2,0},{3,1},{4,6},{5,7},{6,4},{7,5},{8,10},{9,11},{10,... | collective-permute-start | bytes 98312 | tf_op jit(solution)/shard_map/inner_z1/ppermute | solution.py:518
  74.9 13.8 %collective-permute-start.32 = (f32[64,256]{1,0:T(8,128)S(1)}, f32[64,256]{1,0:T(8,128)S(1)}, u32[]{:S(2)}, u32[]{:S(2)}) collective-permute-start(f32[64,256]{1,0:T(8,128)S(1)} %add.102), channel_id=1, source_target_pairs={{0,8},{8,0},{16,24},{24,16},{1,9},{9,1},{17,25},{25,17},{2,10},{10... | collective-permute-start | bytes 196616 | tf_op jit(solution)/shard_map/r_c/ppermute | solution.py:518
  76.7 12.1 %collective-permute-start.33 = (f32[2,64,768]{2,1,0:T(8,128)S(1)}, f32[2,64,768]{2,1,0:T(8,128)S(1)}, u32[]{:S(2)}, u32[]{:S(2)}) collective-permute-start(f32[2,64,768]{2,1,0:T(8,128)S(1)} %get-tuple-element.207), channel_id=1, source_target_pairs={{0,1},{1,0},{2,3},{3,2},{4,5},{5,4},{6,7},{7,6},{8,9},{9,8},{10,11... | collective-permute-start | bytes 1179656 | tf_op jit(solution)/shard_map/scaled1/ppermute | solution.py:518
  80.7 18.3 %collective-permute-start.37 = (f32[2,64,768]{2,1,0:T(8,128)S(1)}, f32[2,64,768]{2,1,0:T(8,128)S(1)}, u32[]{:S(2)}, u32[]{:S(2)}) collective-permute-start(f32[2,64,768]{2,1,0:T(8,128)S(1)} %get-tuple-element.224), channel_id=1, source_target_pairs={{0,1},{1,0},{2,3},{3,2},{4,5},{5,4},{6,7},{7,6},{8,9},{9,8},{10,11... | collective-permute-start | bytes 1179656 | tf_op jit(solution)/shard_map/branch0/ppermute | solution.py:518
  82.6 8.6 %collective-permute-start.29 = (f32[256,256]{1,0:T(8,128)S(1)}, f32[256,256]{1,0:T(8,128)S(1)}, u32[]{:S(2)}, u32[]{:S(2)}) collective-permute-start(f32[256,256]{1,0:T(8,128)S(1)} %add.103.refs_0_), channel_id=1, source_target_pairs={{0,2},{1,3},{2,0},{3,1},{4,6},{5,7},{6,4},{7,5},{8,10},{9,11},{10,... | collective-permute-start | bytes 786440 | tf_op jit(solution)/shard_map/e10/ppermute | solution.py:518
  82.9 7.4 %collective-permute-start.31 = (f32[32,256]{1,0:T(8,128)S(1)}, f32[32,256]{1,0:T(8,128)S(1)}, u32[]{:S(2)}, u32[]{:S(2)}) collective-permute-start(f32[32,256]{1,0:T(8,128)S(1)} %fusion.1), channel_id=1, source_target_pairs={{0,4},{1,5},{2,6},{3,7},{4,0},{5,1},{6,2},{7,3},{8,12},{9,13},{10,... | collective-permute-start | bytes 98312 | tf_op jit(solution)/shard_map/inner_z2/ppermute | solution.py:518
  95.2 8.5 %collective-permute-start.41 = (f32[1,64,768]{2,1,0:T(8,128)S(1)}, f32[1,64,768]{2,1,0:T(8,128)S(1)}, u32[]{:S(2)}, u32[]{:S(2)}) collective-permute-start(f32[1,64,768]{2,1,0:T(8,128)S(1)} %get-tuple-element.230), channel_id=1, source_target_pairs={{0,1},{1,0},{2,3},{3,2},{4,5},{5,4},{6,7},{7,6},{8,9},{9,8},{10,11... | collective-permute-start | bytes 589832 | tf_op jit(solution)/shard_map/branch1/ppermute | solution.py:518
  96.8 9.4 %collective-permute-start.43 = (f32[1,64,768]{2,1,0:T(8,128)S(1)}, f32[1,64,768]{2,1,0:T(8,128)S(1)}, u32[]{:S(2)}, u32[]{:S(2)}) collective-permute-start(f32[1,64,768]{2,1,0:T(8,128)S(1)} %get-tuple-element.238), channel_id=1, source_target_pairs={{0,1},{1,0},{2,3},{3,2},{4,5},{5,4},{6,7},{7,6},{8,9},{9,8},{10,11... | collective-permute-start | bytes 589832 | tf_op jit(solution)/shard_map/branch2/ppermute | solution.py:518
  (21 other events, 118.5 us)
